TPU v7x, 32 devices: a whole 2x2x4 slice. The times are simulated.
32 devices in a mesh: groups: 2 (over y), dom: 4 (over z), ens: 4 (over x, core).
Axes of the slice: x: 2, y: 2, z: 4, core: 2. Of those that a mesh axis runs over, the one named last changes fastest.
Arguments:
- state: float32 [16, 256, 512], P('ens', ('groups', 'dom')), parts along dimension 1, may hold values from -8 to 8, as said below
- coords: float32 [3, 2048], P(None, ('groups', 'dom')), parts along dimension 1, may hold values from -1 to 1
- owner_local: int32 [2048], P(('groups', 'dom')), parts along dimension 0, may hold values from 0 to 31
- counts: int32 [8, 4], P(('groups', 'dom')), parts along dimension 0, may hold values from 32 to 64, as said below
- obs_value: float32 [2048], P(('groups', 'dom')), parts along dimension 0, may hold values from 0.5 to 3.5
- obs_weight: float32 [2048], P(('groups', 'dom')), parts along dimension 0, as said below
Outputs:
- analysis: float32 [16, 256, 512], P('ens', ('groups', 'dom')), parts along dimension 1
There are 2 independent parts, one for each index of `groups`. A program takes and returns all parts, laid end to end along the dimension named above; each array names one. Nothing has to cross between parts.
Inputs may be any that keep to these rules, and one draw needn't show every extreme that they name: `state`: each member is an independent field plus an offset of its own. The sensors of one block are stored in order of owner block: the first counts[d, 0] slots belong to owner block 0, the next counts[d, 1] to block 1, and so on; slots after the last of them are unused. For one owner block, chosen by the draw, every row holds exactly 64. `obs_weight`: Positive.
All inputs are finite; a program needn't handle non-finite values.
Results may differ from a plain program's by a relative error of at most 0.00028.
Values sent between devices are 32-bit elements; how exact they have to be, the bound alone decides.
No kernel may reach another device: no remote copies, remote signals or barrier semaphores. Data moves between devices by JAX's collectives and lax.ppermute only.
A program may use at most 64 MiB of HBM per device.

v0:
```python
import jax
import jax.numpy as jnp
from jax import lax
from jax.sharding import PartitionSpec as P

CAP = 64
NS_ITERS = 8


GLL_POINTS = (
    -1.0,
    -0.8717401485096066,
    -0.5917001814331423,
    -0.2092992179024789,
    0.2092992179024789,
    0.5917001814331423,
    0.8717401485096066,
    1.0,
)
INFLATION = 1.1


def lagrange(position):
    basis_rows = []
    for node_index in range(8):
        product = jnp.ones_like(position)
        for other_node in range(8):
            if other_node != node_index:
                product = (
                    product
                    * (position - GLL_POINTS[other_node])
                    / (GLL_POINTS[node_index] - GLL_POINTS[other_node])
                )
        basis_rows.append(product)
    return jnp.stack(basis_rows, 0)


def node_weights(sensor_coords):
    along_r = lagrange(sensor_coords[0]).T
    along_s = lagrange(sensor_coords[1]).T
    along_t = lagrange(sensor_coords[2]).T
    node_table = along_t[:, :, None, None] * along_s[:, None, :, None] * along_r[:, None, None, :]
    return node_table.reshape(sensor_coords.shape[1], 512)


def analysis_weights(cross_terms, project):
    highest = lax.Precision.HIGHEST
    members = cross_terms.shape[0]
    identity = jnp.eye(members, dtype=jnp.float32)
    system = cross_terms + (members - 1) / INFLATION * identity
    trace_value = jnp.trace(system)
    iterate = system / trace_value
    inverse_root = identity
    for sweep in range(NS_ITERS):
        middle = 0.5 * (3.0 * identity - jnp.dot(inverse_root, iterate, precision=highest))
        iterate = jnp.dot(iterate, middle, precision=highest)
        inverse_root = jnp.dot(middle, inverse_root, precision=highest)
    mean_weights = (
        jnp.dot(inverse_root, jnp.dot(inverse_root, project, precision=highest), precision=highest)
        / trace_value
    )
    transform = inverse_root * jnp.sqrt((members - 1) / trace_value) + mean_weights[:, None]
    return transform - jnp.mean(transform, axis=0, keepdims=True) + 1.0 / members


def on_device(state, coords, owner_local, counts, obs_value, obs_weight):
    highest = lax.Precision.HIGHEST
    local_members, local_elements, node_count = state.shape
    row_counts = counts[0]
    starts = jnp.cumsum(row_counts) - row_counts
    column = jnp.arange(CAP, dtype=jnp.int32)
    in_use = column[None, :] < row_counts[:, None]
    slot_index = jnp.minimum(starts[:, None] + column[None, :], coords.shape[1] - 1)
    tile_coords = coords[:, slot_index]
    tile_owner = owner_local[slot_index][None]
    tile_obs = obs_value[slot_index]
    tile_weight = jnp.where(in_use, obs_weight[slot_index], jnp.zeros_like(tile_obs))
    node_major = state.transpose(2, 0, 1).reshape(node_count, local_members * local_elements)
    element_ids = jnp.arange(local_elements, dtype=jnp.int32)
    sensor_coords = lax.all_to_all(tile_coords, "dom", split_axis=1, concat_axis=1, tiled=True)
    sources = sensor_coords.shape[1]
    item_count = sensor_coords.shape[2]
    node_table = node_weights(sensor_coords.reshape(3, sources * item_count))
    partial_values = jnp.dot(node_table, node_major, precision=highest)
    partial_values = partial_values.reshape(sources * item_count, local_members, local_elements)
    selector = (
        lax.all_to_all(tile_owner, "dom", split_axis=1, concat_axis=1, tiled=True).reshape(
            sources * item_count, 1
        )
        == element_ids[None, :]
    ).astype(jnp.float32)
    chosen = jnp.sum(partial_values * selector[:, None, :], axis=2)
    owner_values = chosen.T.reshape(local_members, sources, item_count)
    member_part = lax.all_to_all(owner_values, "dom", split_axis=1, concat_axis=1, tiled=True)
    all_values = lax.all_gather(member_part, "ens", axis=0, tiled=True)
    members = all_values.shape[0]
    flat_values = all_values.reshape(members, -1)
    mean_value = jnp.mean(flat_values, axis=0)
    anomaly = flat_values - mean_value[None, :]
    weighted = anomaly * tile_weight.reshape(-1)[None, :]
    cross_terms = jnp.dot(weighted, anomaly.T, precision=highest)
    project = jnp.dot(weighted, tile_obs.reshape(-1) - mean_value, precision=highest)
    cross_terms, project = lax.psum((cross_terms, project), "dom")
    mixing = analysis_weights(cross_terms, project)
    grouped = lax.all_to_all(state, "ens", split_axis=1, concat_axis=0, tiled=True)
    member_total = grouped.shape[0]
    mixed = jnp.dot(mixing.T, grouped.reshape(member_total, -1), precision=highest).reshape(
        grouped.shape
    )
    return lax.all_to_all(mixed, "ens", split_axis=0, concat_axis=1, tiled=True)


def solution(mesh):
    return jax.shard_map(
        on_device,
        mesh=mesh,
        in_specs=(
            P("ens", ("groups", "dom"), None),
            P(None, ("groups", "dom")),
            P(("groups", "dom")),
            P(("groups", "dom"), None),
            P(("groups", "dom")),
            P(("groups", "dom")),
        ),
        out_specs=P("ens", ("groups", "dom"), None),
        check_vma=False,
    )
```

profile of v0, /device:TPU:0, one launch (start us, length us, event | category | flops | bytes accessed | tf_op | source)
XLA Modules:
  0.0 76.4 jit_solution(562660524366019711)
XLA Ops:
  0.0 0.7 copy-done.5
  0.7 0.2 reduce-window.8
  1.0 1.9 %gather_fusion.1 = s32[256]{0:T(256)S(1)} fusion(s32[256]{0:T(256)S(1)} %copy-done, s32[1024]{0:T(1024)S(1)} %pad_clamp_fusion), kind=kCustom, calls=%fused_computation.1 | custom fusion | bytes 3072 | tf_op jit(solution)/shard_map/gather | solution.py:75
  3.0 0.7 broadcast_in_dim.5
  3.7 6.3 %all-to-all-start.1 = ((s32[1,4,64]{2,0,1:T(1,128)}), s32[1,4,64]{2,0,1:T(1,128)S(1)}, u32[]{:S(2)}, u32[]{:S(2)}) async-start(s32[1,4,64]{2,0,1:T(1,128)} %broadcast_in_dim.5), calls=%async_computation.1 | async-start | bytes 4096 | tf_op jit(solution)/shard_map/all_to_all | solution.py:87
  10.2 0.7 gather_fusion
  11.0 0.7 reshape.2397
  11.7 1.9 %gather_fusion.2 = f32[256]{0:T(256)S(1)} fusion(f32[256]{0:T(256)S(1)} %copy-done.1, s32[1024]{0:T(1024)S(1)} %pad_clamp_fusion), kind=kCustom, calls=%fused_computation.2 | custom fusion | bytes 3072 | tf_op jit(solution)/shard_map/gather | solution.py:77
  13.7 1.7 %all-to-all-done.1 = s32[1,4,64]{2,0,1:T(1,128)S(1)} async-done(((s32[1,4,64]{2,0,1:T(1,128)}), s32[1,4,64]{2,0,1:T(1,128)S(1)}, u32[]{:S(2)}, u32[]{:S(2)}) %all-to-all-start.1) | async-done | bytes 1056 | tf_op jit(solution)/shard_map/all_to_all | solution.py:87
  15.4 3.4 %all-to-all-start = ((f32[4,1,192]{2,1,0:T(1,128)}), f32[4,1,192]{2,1,0:T(1,128)S(1)}, u32[]{:S(2)}, u32[]{:S(2)}) async-start(f32[4,1,192]{2,1,0:T(1,128)} %reshape.2397), calls=%async_computation | async-start | bytes 8192 | tf_op jit(solution)/shard_map/all_to_all | solution.py:80
  18.8 0.6 broadcast.3262
  19.4 0.7 reduce.4
  20.2 4.2 %all-to-all-done = f32[4,1,192]{2,1,0:T(1,128)S(1)} async-done(((f32[4,1,192]{2,1,0:T(1,128)}), f32[4,1,192]{2,1,0:T(1,128)S(1)}, u32[]{:S(2)}, u32[]{:S(2)}) %all-to-all-start) | async-done | bytes 3104 | tf_op jit(solution)/shard_map/all_to_all | solution.py:80
  24.4 0.5 broadcast.3265
  24.9 0.6 reduce.5
  27.8 0.9 %copy-done.3 = f32[4,32,512]{2,1,0:T(8,128)S(1)} copy-done((f32[4,32,512]{2,1,0:T(8,128)S(1)}, f32[4,32,512]{2,1,0:T(8,128)}, u32[]{:S(2)}) %copy-start.3) | copy-done | bytes 262168
  28.7 0.5 fusion
  29.2 0.7 reshape.2399
  29.9 3.2 %all-to-all-start.2 = ((f32[4,1,256]{2,1,0:T(1,128)}), f32[4,1,256]{2,1,0:T(1,128)S(1)}, u32[]{:S(2)}, u32[]{:S(2)}) async-start(f32[4,1,256]{2,1,0:T(1,128)} %reshape.2399), calls=%async_computation.2 | async-start | bytes 8192 | tf_op jit(solution)/shard_map/all_to_all | solution.py:94
  33.2 0.9 %copy.45 = f32[4,32,512]{2,0,1:T(4,128)} copy(f32[4,32,512]{2,1,0:T(8,128)S(1)} %copy-done.3) | data formatting | bytes 524288 | tf_op args[0]
  34.1 1.9 %gather_fusion.3 = f32[256]{0:T(256)S(1)} fusion(f32[256]{0:T(256)S(1)} %copy-done.2, s32[1024]{0:T(1024)S(1)} %pad_clamp_fusion), kind=kCustom, calls=%fused_computation.3 | custom fusion | bytes 3072 | tf_op jit(solution)/shard_map/gather | solution.py:76
  36.1 2.6 %all-to-all-done.2 = f32[4,1,256]{2,1,0:T(1,128)S(1)} async-done(((f32[4,1,256]{2,1,0:T(1,128)}), f32[4,1,256]{2,1,0:T(1,128)S(1)}, u32[]{:S(2)}, u32[]{:S(2)}) %all-to-all-start.2) | async-done | bytes 4128 | tf_op jit(solution)/shard_map/all_to_all | solution.py:94
  38.7 3.4 %all-to-all-start.3 = ((f32[4,32,512]{2,0,1:T(4,128)}), f32[4,32,512]{2,0,1:T(4,128)S(1)}, u32[]{:S(2)}, u32[]{:S(2)}) async-start(f32[4,32,512]{2,0,1:T(4,128)} %copy.45), calls=%async_computation.3 | async-start | bytes 524288 | tf_op jit(solution)/shard_map/all_to_all | solution.py:105
  42.1 0.6 reduce.6
  42.8 6.3 %all_gather.3 = f32[16,4,64]{2,1,0:T(4,128)S(1)} all-gather(f32[4,4,64]{2,1,0:T(4,128)S(1)} %copy.42), channel_id=1, replica_groups=mesh['groups'=2,'dom'=4,'ens'=4] {'ens'}, dimensions={0}, use_global_device_ids=true | all-gather | bytes 20480 | tf_op jit(solution)/shard_map/all_gather | solution.py:95
  49.3 0.2 convolution_bitcast_fusion
  49.5 9.9 %all-reduce = (f32[16,16]{1,0:T(8,128)S(1)}, f32[16]{0:T(128)S(1)}) all-reduce(f32[16,16]{1,0:T(8,128)S(1)} %convolution_bitcast_fusion, f32[16]{0:T(128)S(1)} %convolution_bitcast_fusion.1), channel_id=1, replica_groups=mesh['groups'=2,'dom'=4,'ens'=4] {'dom'}, use_global_device_ids=true, to_apply=%region_3.4 | all-reduce | flops 272 | bytes 2176 | tf_op jit(solution)/shard_map/psum | solution.py:103
  59.4 0.7 select_reduce_fusion
  60.1 0.8 %fusion.8 = f32[16,16]{1,0:T(8,128)S(1)} fusion(f32[16,16]{1,0:T(8,128)S(1)} %get-tuple-element.5, f32[]{:T(128)} %select_reduce_fusion), kind=kOutput, calls=%fused_computation.21 | convolution fusion | flops 51456 | bytes 2052 | tf_op jit(solution)/shard_map/dot_general | solution.py:55
  60.9 0.8 %fusion.28 = f32[16,16]{1,0:T(8,128)S(1)} fusion(f32[16,16]{1,0:T(8,128)S(1)} %fusion.8, f32[16,16]{1,0:T(8,128)S(1)} %get-tuple-element.5, f32[]{:T(128)} %select_reduce_fusion), kind=kOutput, calls=%fused_computation.82 | convolution fusion | flops 50176 | bytes 3076 | tf_op jit(solution)/shard_map/dot_general | solution.py:56
  61.9 0.1 fusion.7
  62.0 0.1 fusion.40
  62.3 0.1 fusion.6
  62.4 0.1 fusion.42
  62.7 0.1 fusion.5
  62.8 0.1 fusion.44
  63.1 0.1 fusion.4
  63.3 0.1 fusion.46
  63.5 0.1 fusion.3
  64.0 0.1 fusion.2
  64.1 0.1 fusion.50
  64.4 0.1 fusion.1
  64.7 0.1 convolution_bitcast_fusion.3
  64.8 0.8 %fusion.9 = f32[16]{0:T(128)S(1)} fusion(f32[16,16]{1,0:T(8,128)S(1)} %fusion.51, f32[16,1]{0,1:T(1,128)S(1)} %convolution_bitcast_fusion.3, f32[]{:T(128)} %select_reduce_fusion), kind=kOutput, calls=%fused_computation.26 | convolution fusion | flops 3088 | bytes 1156 | tf_op jit(solution)/shard_map/dot_general | solution.py:59
  66.6 0.6 fusion.10
  67.2 0.2 copy.49
  67.3 8.4 %all_to_all.48 = f32[16,8,512]{2,1,0:T(8,128)S(1)} all-to-all(f32[16,8,512]{2,1,0:T(8,128)S(1)} %copy.49), channel_id=1, replica_groups=mesh['groups'=2,'dom'=4,'ens'=4] {'ens'}, dimensions={0} | all-to-all | bytes 524288 | tf_op jit(solution)/shard_map/all_to_all | solution.py:110
  75.7 0.7 copy.76
  (79 shorter events, 4.8 us)
Async XLA Ops:
  0.0 1.0 %copy-start = (s32[256]{0:T(256)S(1)}, s32[256]{0:T(256)}, u32[]{:S(2)}) copy-start(s32[256]{0:T(256)} %param.8) | copy-start | bytes 3076
  0.0 0.7 copy-start.5
  3.0 7.0 %copy-start.4 = (f32[3,256]{1,0:T(4,128)S(1)}, f32[3,256]{1,0:T(4,128)}, u32[]{:S(2)}) copy-start(f32[3,256]{1,0:T(4,128)} %param.7) | copy-start | bytes 9220
  3.7 11.8 %all-to-all-start.1 = ((s32[1,4,64]{2,0,1:T(1,128)}), s32[1,4,64]{2,0,1:T(1,128)S(1)}, u32[]{:S(2)}, u32[]{:S(2)}) async-start(s32[1,4,64]{2,0,1:T(1,128)} %broadcast_in_dim.5), calls=%async_computation.1 | async-start | bytes 4096 | tf_op jit(solution)/shard_map/all_to_all | solution.py:87
  11.0 0.7 copy-start.1
  15.4 9.0 %all-to-all-start = ((f32[4,1,192]{2,1,0:T(1,128)}), f32[4,1,192]{2,1,0:T(1,128)S(1)}, u32[]{:S(2)}, u32[]{:S(2)}) async-start(f32[4,1,192]{2,1,0:T(1,128)} %reshape.2397), calls=%async_computation | async-start | bytes 8192 | tf_op jit(solution)/shard_map/all_to_all | solution.py:80
  27.7 1.0 %copy-start.3 = (f32[4,32,512]{2,1,0:T(8,128)S(1)}, f32[4,32,512]{2,1,0:T(8,128)}, u32[]{:S(2)}) copy-start(f32[4,32,512]{2,1,0:T(8,128)} %param.6) | copy-start | bytes 786436
  29.9 8.8 %all-to-all-start.2 = ((f32[4,1,256]{2,1,0:T(1,128)}), f32[4,1,256]{2,1,0:T(1,128)S(1)}, u32[]{:S(2)}, u32[]{:S(2)}) async-start(f32[4,1,256]{2,1,0:T(1,128)} %reshape.2399), calls=%async_computation.2 | async-start | bytes 8192 | tf_op jit(solution)/shard_map/all_to_all | solution.py:94
  33.2 0.9 %copy-start.2 = (f32[256]{0:T(256)S(1)}, f32[256]{0:T(256)}, u32[]{:S(2)}) copy-start(f32[256]{0:T(256)} %param.10) | copy-start | bytes 3076
  38.7 27.8 %all-to-all-start.3 = ((f32[4,32,512]{2,0,1:T(4,128)}), f32[4,32,512]{2,0,1:T(4,128)S(1)}, u32[]{:S(2)}, u32[]{:S(2)}) async-start(f32[4,32,512]{2,0,1:T(4,128)} %copy.45), calls=%async_computation.3 | async-start | bytes 524288 | tf_op jit(solution)/shard_map/all_to_all | solution.py:105
where the time goes:
time: 77 us; the launch traced here: 76.4 us
  blocking collectives  24.7 us (32%)
  starting transfers between devices  16.4 us (21%)
  local copies, waits for them, and re-layouts  16 us (21%)
  waiting for transfers between devices  8.47 us (11%)
  matrix products  6.82 us (9%)
  other arithmetic  3.14 us (4%)
  between operations  0.98 us (1%)
    psum x1, blocking collectives, on_device(): cross_terms, project = lax.psum((cross_terms, project), 'dom')  9.93 us
    all_to_all x1, blocking collectives, on_device(): return lax.all_to_all(mixed, 'ens', split_axis=0, concat_axis=1, tiled=True)  8.39 us
    all_to_all x1, starting transfers between devices, on_device(): lax.all_to_all(tile_owner, 'dom', split_axis=1, concat_axis=1, tiled=True)  6.35 us
    all_gather x1, blocking collectives, on_device(): all_values = lax.all_gather(member_part, 'ens', axis=0, tiled=True)  6.34 us
    all_to_all x1, waiting for transfers between devices, on_device(): lax.all_to_all(tile_coords, 'dom', split_axis=1, concat_axis=1, tiled=True)  4.19 us
    unnamed x21, local copies, waits for them, and re-layouts  4.14 us
    all_to_all x1, starting transfers between devices, on_device(): lax.all_to_all(state, 'ens', split_axis=1, concat_axis=0, tiled=True)  3.41 us
    all_to_all x1, starting transfers between devices, on_device(): lax.all_to_all(tile_coords, 'dom', split_axis=1, concat_axis=1, tiled=True)  3.38 us
  transfers between devices with their start and end apart: 4, of which 3 were waited for; matrix products, arithmetic and copies ran while one was open for 20% of the time, Pallas kernels for 0%

commit v1 on v0

v1 whole, which is shorter than its diff:
```python
import jax
import jax.numpy as jnp
from jax import lax
from jax.experimental import pallas as pl
from jax.experimental.pallas import tpu as pltpu
from jax.sharding import PartitionSpec as P

CAP = 64
NS_ITERS = 8


GLL_POINTS = (
    -1.0,
    -0.8717401485096066,
    -0.5917001814331423,
    -0.2092992179024789,
    0.2092992179024789,
    0.5917001814331423,
    0.8717401485096066,
    1.0,
)
INFLATION = 1.1
ORDER = len(GLL_POINTS)
F32 = jnp.float32
BF16 = jnp.bfloat16
DIRECT_DOM = 8


def lagrange_scale(index):
    product = 1.0
    for other in range(ORDER):
        if other != index:
            product *= GLL_POINTS[index] - GLL_POINTS[other]
    return 1.0 / product


def lagrange_rows(position):
    shape = (ORDER, position.shape[1])
    node = lax.broadcasted_iota(jnp.int32, shape, 0)
    product = jnp.full(shape, lagrange_scale(0), F32)
    for index in range(1, ORDER):
        product = jnp.where(node == index, lagrange_scale(index), product)
    for other in range(ORDER):
        product = product * jnp.where(node == other, 1.0, position - GLL_POINTS[other])
    return product


def split(value):
    high = value.astype(BF16)
    low = (value - high.astype(F32)).astype(BF16)
    return high, low


def pack_kernel(direct, counts, coords, owner, obs, weight, *rest):
    outs, block = rest[:-1], rest[-1]
    n_dom = counts.shape[1]
    slots = coords.shape[1]
    here = lax.axis_index("dom")
    block[...] = jnp.zeros(block.shape, F32)
    block[0:3, :] = coords[...]
    block[3:4, :] = owner[...].astype(F32)
    block[4:5, :] = obs[...]
    block[5:6, :] = weight[...]
    rows = block[...]
    column = lax.broadcasted_iota(jnp.int32, (8, 2 * CAP), 1)

    def tile(target, half):
        start = jnp.int32(0)
        for other in range(n_dom):
            start = start + jnp.where(other < target, counts[0, other], 0)
        count = counts[0, target]
        turned = pltpu.roll(rows, lax.rem(half - start + slots, slots), axis=1)[:, : 2 * CAP]
        return jnp.where((column >= half) & (column < half + count), turned, 0.0)

    if direct:
        for shift in range(n_dom):
            outs[shift][...] = tile(lax.rem(here + shift, n_dom), (shift % 2) * CAP)
    else:
        half = lax.rem(here, 2) * CAP

        def step(target, carry):
            outs[0][target] = tile(target, half)
            return carry

        lax.fori_loop(0, n_dom, step, 0)


def pick(state_rows, members, elements, high, low, chosen):
    rows_high, rows_low = split(state_rows)
    partial = (
        jnp.dot(rows_high, high, preferred_element_type=F32)
        + jnp.dot(rows_low, high, preferred_element_type=F32)
        + jnp.dot(rows_high, low, preferred_element_type=F32)
    )
    partial = partial.reshape(members, elements, partial.shape[1])
    return jnp.sum(jnp.where(chosen[None], partial, 0.0), axis=1)


def chosen_mask(sensors, elements):
    ids = lax.broadcasted_iota(jnp.int32, (elements, sensors.shape[1]), 0).astype(F32)
    return ids == sensors[3:4, :]


def values_kernel(tile_count, *refs):
    tiles, state_refs = refs[:tile_count], refs[tile_count:-4]
    sensors_out, high_out, low_out, values_out = refs[-4:]
    pairs = []
    for first in range(0, tile_count, 2):
        pair = tiles[first][...]
        if first + 1 < tile_count:
            pair = pair + tiles[first + 1][...]
        pairs.append(pair)
    sensors = jnp.concatenate(pairs, axis=1) if len(pairs) > 1 else pairs[0]
    sensors_out[...] = sensors
    along_r = lagrange_rows(sensors[0:1, :])
    along_s = lagrange_rows(sensors[1:2, :])
    along_t = lagrange_rows(sensors[2:3, :])
    for t in range(ORDER):
        for s in range(0, ORDER, 2):
            rows = [along_r * (along_t[t : t + 1, :] * along_s[k : k + 1, :]) for k in (s, s + 1)]
            high, low = split(jnp.concatenate(rows, axis=0))
            base = ORDER * ORDER * t + ORDER * s
            high_out[base : base + 2 * ORDER, :] = high
            low_out[base : base + 2 * ORDER, :] = low
    high, low = high_out[...], low_out[...]
    for index, ref in enumerate(state_refs):
        members, elements, nodes = ref.shape
        chosen = chosen_mask(sensors, elements)
        rows = ref[...].reshape(members * elements, nodes)
        values_out[index * members : (index + 1) * members, :] = pick(
            rows, members, elements, high, low, chosen
        )


def cross_kernel(sensors_ref, high_ref, low_ref, values_ref, *refs):
    state_refs, out = refs[:-1], refs[-1]
    high, low = high_ref[...], low_ref[...]
    sensors = sensors_ref[...]
    parts = [values_ref[...]]
    for ref in state_refs:
        members, elements, nodes = ref.shape
        chosen = chosen_mask(sensors, elements)
        rows = ref[...].reshape(members * elements, nodes)
        parts.append(pick(rows, members, elements, high, low, chosen))
    values = jnp.concatenate(parts, axis=0)
    total = values.shape[0]
    mean_value = jnp.sum(values, axis=0, keepdims=True) * (1.0 / total)
    anomaly = values - mean_value
    weighted = anomaly * sensors[5:6, :]
    innovation = sensors[4:5, :] - mean_value
    pad = jnp.zeros((out.shape[1] - total - 1, values.shape[1]), F32)
    right = jnp.concatenate([anomaly, innovation, pad], axis=0)
    out[...] = lax.dot_general(
        weighted,
        right,
        (((1,), (1,)), ((), ())),
        precision=lax.Precision.HIGHEST,
        preferred_element_type=F32,
    )


def mix_kernel(sum_count, *refs):
    sums, state_refs, out, splats = refs[:sum_count], refs[sum_count:-2], refs[-2], refs[-1]
    highest = lax.Precision.HIGHEST
    total_sum = sums[0][...]
    for ref in sums[1:]:
        total_sum = total_sum + ref[...]
    local_members, elements, nodes = out.shape
    members = local_members * len(state_refs)
    row = lax.broadcasted_iota(jnp.int32, (members, members), 0)
    col = lax.broadcasted_iota(jnp.int32, (members, members), 1)
    identity = (row == col).astype(F32)
    system = total_sum[:, :members] + (members - 1) / INFLATION * identity
    project = total_sum[:, members : members + 1]
    trace_value = jnp.sum(
        jnp.sum(jnp.where(row == col, system, 0.0), axis=1, keepdims=True), axis=0, keepdims=True
    )
    iterate = system / trace_value
    inverse_root = identity
    for sweep in range(NS_ITERS):
        if sweep:
            product = jnp.dot(inverse_root, iterate, precision=highest)
        else:
            product = iterate
        middle = 0.5 * (3.0 * identity - product)
        if sweep + 1 < NS_ITERS:
            iterate = jnp.dot(iterate, middle, precision=highest)
        inverse_root = jnp.dot(middle, inverse_root, precision=highest) if sweep else middle
    mean_weights = (
        jnp.dot(inverse_root, jnp.dot(inverse_root, project, precision=highest), precision=highest)
        / trace_value
    )
    transform = inverse_root * jnp.sqrt((members - 1) / trace_value) + mean_weights
    mixing = transform - jnp.mean(transform, axis=0, keepdims=True) + 1.0 / members
    for j in range(members):
        for k in range(local_members):
            splats[j * local_members + k] = jnp.broadcast_to(mixing[j : j + 1, k : k + 1], (8, 128))
    for block in range(elements // 8):
        span = slice(8 * block, 8 * block + 8)
        for lane in range(nodes // 128):
            lanes = slice(128 * lane, 128 * lane + 128)
            totals = [None] * local_members
            for j in range(members):
                value = state_refs[j // local_members][j % local_members, span, lanes]
                for k in range(local_members):
                    term = splats[j * local_members + k] * value
                    totals[k] = term if totals[k] is None else totals[k] + term
            for k in range(local_members):
                out[k, span, lanes] = totals[k]


def exchange(value, axis, pairs):
    return lax.ppermute(value, axis, pairs)


def gather_members(state, n_ens):
    pieces = {0: state}
    if n_ens & (n_ens - 1) == 0:
        bit = n_ens >> 1
        while bit:
            pairs = [(e, e ^ bit) for e in range(n_ens)]
            for key in list(pieces):
                pieces[key ^ bit] = exchange(pieces[key], "ens", pairs)
            bit >>= 1
    else:
        for shift in range(1, n_ens):
            pairs = [(e, (e + shift) % n_ens) for e in range(n_ens)]
            pieces[shift] = exchange(state, "ens", pairs)
    return [pieces[key] for key in sorted(pieces)]


def make_on_device(n_dom, n_ens):
    vmem = pl.BlockSpec(memory_space=pltpu.VMEM)
    smem = pl.BlockSpec(memory_space=pltpu.SMEM)
    direct = n_dom <= DIRECT_DOM

    def call(kernel, name, out_shape, operands, specs=None, scratch=()):
        many = isinstance(out_shape, (list, tuple))
        return pl.pallas_call(
            kernel,
            name=name,
            out_shape=out_shape,
            in_specs=specs or [vmem] * len(operands),
            out_specs=[vmem] * len(out_shape) if many else vmem,
            scratch_shapes=list(scratch),
        )(*operands)

    def shape(dims, dtype=F32):
        return jax.ShapeDtypeStruct(dims, dtype)

    def on_device(state, coords, owner_local, counts, obs_value, obs_weight):
        local_members, elements, nodes = state.shape
        slots = coords.shape[1]
        members = local_members * n_ens
        pieces = gather_members(state, n_ens)
        tile_shape = (8, 2 * CAP)
        tiles = list(call(
            lambda *refs: pack_kernel(direct, *refs),
            "pack",
            [shape(tile_shape)] * n_dom if direct else [shape((n_dom,) + tile_shape)],
            [counts, coords, owner_local[None], obs_value[None], obs_weight[None]],
            [smem] + [vmem] * 4,
            [pltpu.VMEM((8, slots), F32)],
        ))
        if direct:
            for shift in range(1, n_dom):
                pairs = [(d, (d + shift) % n_dom) for d in range(n_dom)]
                tiles[shift] = exchange(tiles[shift], "dom", pairs)
        else:
            moved = lax.all_to_all(tiles[0], "dom", split_axis=0, concat_axis=0, tiled=True)
            tiles = [moved[d] for d in range(n_dom)]
        sensor_count = CAP * (n_dom + n_dom % 2)
        early = max(1, n_ens // 2)
        sensors, high, low, values = call(
            lambda *refs: values_kernel(n_dom, *refs),
            "values",
            [
                shape((8, sensor_count)),
                shape((nodes, sensor_count), BF16),
                shape((nodes, sensor_count), BF16),
                shape((early * local_members, sensor_count)),
            ],
            list(tiles) + pieces[:early],
        )
        partial_sum = call(
            cross_kernel,
            "cross",
            shape((members, members + 8)),
            [sensors, high, low, values] + pieces[early:],
        )
        if direct:
            sums = [partial_sum]
            for shift in range(1, n_dom):
                pairs = [(d, (d + shift) % n_dom) for d in range(n_dom)]
                sums.append(exchange(partial_sum, "dom", pairs))
        else:
            sums = [lax.psum(partial_sum, "dom")]
        return call(
            lambda *refs: mix_kernel(len(sums), *refs),
            "mix",
            shape(state.shape),
            sums + pieces,
            None,
            [pltpu.VMEM((members * local_members, 8, 128), F32)],
        )

    return on_device


def solution(mesh):
    return jax.shard_map(
        make_on_device(mesh.shape["dom"], mesh.shape["ens"]),
        mesh=mesh,
        in_specs=(
            P("ens", ("groups", "dom"), None),
            P(None, ("groups", "dom")),
            P(("groups", "dom")),
            P(("groups", "dom"), None),
            P(("groups", "dom")),
            P(("groups", "dom")),
        ),
        out_specs=P("ens", ("groups", "dom"), None),
        check_vma=False,
    )
```

time: 77 us -> 38.3 us (0.50)
  blocking collectives: 24.7 us -> 0 us
  local copies, waits for them, and re-layouts: 16 us -> 1.99 us
  Pallas kernels: 0 us -> 10.9 us
  matrix products: 6.82 us -> 0 us
  waiting for transfers between devices: 8.47 us -> 12.3 us
  starting transfers between devices: 16.4 us -> 12.8 us
  other arithmetic: 3.14 us -> 0 us
  between operations: 0.98 us -> 0.04 us
    all_to_all x4 -> x0, starting transfers between devices: 16.4 us -> none  [the longest x1 6.35 us: on_device(): lax.all_to_all(tile_owner, 'dom', split_axis=1, concat_axis=1, tiled=True)]
    ppermute x0 -> x9, starting transfers between devices: none -> 12.8 us  [exchange(): return lax.ppermute(value, axis, pairs)]
    ppermute x0 -> x9, waiting for transfers between devices: none -> 12.3 us  [exchange(): return lax.ppermute(value, axis, pairs)]
    pallas_call x0 -> x4, Pallas kernels: none -> 10.9 us  [call(): pl.pallas_call(kernel, name=name, out_shape=out_shape, in_specs=specs or...]
    psum x1 -> x0, blocking collectives: 9.93 us -> none  [on_device(): cross_terms, project = lax.psum((cross_terms, project), 'dom')]
    all_to_all x4 -> x0, waiting for transfers between devices: 8.47 us -> none  [the longest x1 4.19 us: on_device(): lax.all_to_all(tile_coords, 'dom', split_axis=1, concat_axis=1, tiled=True)]
    all_to_all x1 -> x0, blocking collectives: 8.39 us -> none  [on_device(): return lax.all_to_all(mixed, 'ens', split_axis=0, concat_axis=1, tiled=True)]
    dot_general x29 -> x0, matrix products: 6.82 us -> none  [the longest x8 1.8 us: analysis_weights(): jnp.dot(inverse_root, iterate, precision=highest)]
  transfers between devices with their start and end apart: 4 -> 9, of which waited for: 3 -> 5; matrix products, arithmetic and copies ran while one was open for 20% -> 0% of each run, Pallas kernels for 0% -> 9%
where the time goes in v1:
time: 38.3 us; the launch traced here: 38 us
  starting transfers between devices  12.8 us (33%)
  waiting for transfers between devices  12.3 us (32%)
  Pallas kernels  10.9 us (28%)
  local copies, waits for them, and re-layouts  1.99 us (5%)
    ppermute x9, starting transfers between devices, exchange(): return lax.ppermute(value, axis, pairs)  12.8 us
    ppermute x9, waiting for transfers between devices, exchange(): return lax.ppermute(value, axis, pairs)  12.3 us
    pallas_call x4, Pallas kernels, call(): pl.pallas_call(kernel, name=name, out_shape=out_shape, in_specs=specs or...  10.9 us
    unnamed x20, local copies, waits for them, and re-layouts  1.99 us
  transfers between devices with their start and end apart: 9, of which 5 were waited for; matrix products, arithmetic and copies ran while one was open for 0% of the time, Pallas kernels for 9%

profile of v1, /device:TPU:0, one launch (start us, length us, event | category | flops | bytes accessed | tf_op | source)
XLA Modules:
  0.0 38.0 jit_solution(8867774816322348799)
XLA Ops:
  0.0 3.0 %collective-permute-start.4 = (f32[4,32,512]{2,1,0:T(8,128)}, f32[4,32,512]{2,1,0:T(8,128)S(1)}, u32[]{:S(2)}, u32[]{:S(2)}) collective-permute-start(f32[4,32,512]{2,1,0:T(8,128)} %refs_4_.3), channel_id=1, source_target_pairs={{0,2},{1,3},{2,0},{3,1},{4,6},{5,7},{6,4},{7,5},{8,10},{9,11},{10,... | collective-permute-start | bytes 786440 | tf_op jit(solution)/shard_map/ppermute | solution.py:213
  3.0 0.0 collective-permute-start.3
  3.0 6.5 %collective-permute-done.4.refs_0_.refs_6_ = f32[4,32,512]{2,1,0:T(8,128)S(1)} collective-permute-done((f32[4,32,512]{2,1,0:T(8,128)}, f32[4,32,512]{2,1,0:T(8,128)S(1)}, u32[]{:S(2)}, u32[]{:S(2)}) %collective-permute-start.4) | collective-permute-done | bytes 262176 | tf_op jit(solution)/shard_map/ppermute | solution.py:213
  9.5 0.0 copy-start.1
  9.5 0.0 collective-permute-start.5
  9.5 1.5 %pack.1 = (f32[8,128]{1,0:T(8,128)}, f32[8,128]{1,0:T(8,128)}, f32[8,128]{1,0:T(8,128)}, f32[8,128]{1,0:T(8,128)}) custom-call(s32[1,4]{1,0:T(1,128)} %refs_0_.1, f32[3,256]{1,0:T(4,128)} %refs_1_.1, s32[1,256]{1,0:T(1,128)} %bitcast.3, f32[1,256]{1,0:T(1,128)} %bitcast.4, f32[1,256]{1,0:T(1,128)} %bitcast.5), custom_call_target="tpu_custom_call" | custom-call | tf_op jit(solution)/shard_map/pack/pallas_call | solution.py:239
  11.0 0.0 copy-start.9
  11.0 1.8 %collective-permute-start = (f32[8,128]{1,0:T(8,128)}, f32[8,128]{1,0:T(8,128)S(1)}, u32[]{:S(2)}, u32[]{:S(2)}) collective-permute-start(f32[8,128]{1,0:T(8,128)} %get-tuple-element.14), channel_id=1, source_target_pairs={{0,4},{4,8},{8,12},{12,0},{1,5},{5,9},{9,13},{13,1},{2,6},{6,10},{... | collective-permute-start | bytes 12296 | tf_op jit(solution)/shard_map/ppermute | solution.py:213
  12.9 2.6 %collective-permute-start.1 = (f32[8,128]{1,0:T(8,128)}, f32[8,128]{1,0:T(8,128)S(1)}, u32[]{:S(2)}, u32[]{:S(2)}) collective-permute-start(f32[8,128]{1,0:T(8,128)} %get-tuple-element.15), channel_id=1, source_target_pairs={{0,8},{4,12},{8,0},{12,4},{1,9},{5,13},{9,1},{13,5},{2,10},{6,14},... | collective-permute-start | bytes 12296 | tf_op jit(solution)/shard_map/ppermute | solution.py:213
  15.4 0.0 copy-done.9
  15.4 1.3 %collective-permute-start.2 = (f32[8,128]{1,0:T(8,128)S(1)}, f32[8,128]{1,0:T(8,128)S(1)}, u32[]{:S(2)}, u32[]{:S(2)}) collective-permute-start(f32[8,128]{1,0:T(8,128)S(1)} %copy-done.9), channel_id=1, source_target_pairs={{0,12},{4,0},{8,4},{12,8},{1,13},{5,1},{9,5},{13,9},{2,14},{6,2},{... | collective-permute-start | bytes 12296 | tf_op jit(solution)/shard_map/ppermute | solution.py:213
  16.8 0.0 collective-permute-done.refs_1_
  16.8 0.0 copy-start.6
  16.8 0.8 %collective-permute-done.1.refs_2_ = f32[8,128]{1,0:T(8,128)S(1)} collective-permute-done((f32[8,128]{1,0:T(8,128)}, f32[8,128]{1,0:T(8,128)S(1)}, u32[]{:S(2)}, u32[]{:S(2)}) %collective-permute-start.1) | collective-permute-done | bytes 4128 | tf_op jit(solution)/shard_map/ppermute | solution.py:213
  17.6 0.0 copy-start.7
  17.6 1.5 %collective-permute-done.2.refs_3_ = f32[8,128]{1,0:T(8,128)S(1)} collective-permute-done((f32[8,128]{1,0:T(8,128)S(1)}, f32[8,128]{1,0:T(8,128)S(1)}, u32[]{:S(2)}, u32[]{:S(2)}) %collective-permute-start.2) | collective-permute-done | bytes 4128 | tf_op jit(solution)/shard_map/ppermute | solution.py:213
  19.1 0.0 copy-start.8
  19.1 0.0 collective-permute-done.3.refs_5_
  19.1 0.0 copy-start
  19.1 0.0 copy-done.6
  19.1 0.0 copy-done.7
  19.1 0.6 %copy-done.8 = f32[8,128]{1,0:T(8,128)} copy-done((f32[8,128]{1,0:T(8,128)}, f32[8,128]{1,0:T(8,128)S(1)}, u32[]{:S(2)}) %copy-start.8) | copy-done | bytes 4120
  19.6 0.1 copy-done
  19.8 2.1 %values.1 = (f32[8,256]{1,0:T(8,128)}, bf16[512,256]{1,0:T(8,128)(2,1)}, bf16[512,256]{1,0:T(8,128)(2,1)}, f32[8,256]{1,0:T(8,128)}) custom-call(f32[8,128]{1,0:T(8,128)} %get-tuple-element.13.refs_0_, f32[8,128]{1,0:T(8,128)} %copy-done.6, f32[8,128]{1,0:T(8,128)} %copy-done.7, f32[8,128]{1,0:T(8,128)} %copy-done.8, f32[4,32,512]{2,1,0:T(8,128)} %refs_4_.3, ...), custom_call_target="tpu_custom_call" | custom-call | tf_op jit(solution)/shard_map/values/pallas_call | solution.py:239
  21.8 0.0 collective-permute-done.5.refs_1_.refs_7_
  21.8 0.0 copy-start.2
  21.8 0.0 copy-done.1
  21.8 0.7 %copy-done.2 = f32[4,32,512]{2,1,0:T(8,128)} copy-done((f32[4,32,512]{2,1,0:T(8,128)}, f32[4,32,512]{2,1,0:T(8,128)S(1)}, u32[]{:S(2)}) %copy-start.2) | copy-done | bytes 262168
  22.5 2.4 %cross.1.refs_0_ = f32[16,24]{1,0:T(8,128)} custom-call(f32[8,256]{1,0:T(8,128)} %get-tuple-element.17.sensors_ref, bf16[512,256]{1,0:T(8,128)(2,1)} %get-tuple-element.18.high_ref, bf16[512,256]{1,0:T(8,128)(2,1)} %get-tuple-element.19.low_ref, f32[8,256]{1,0:T(8,128)} %get-tuple-element.20.values_ref, f32[4,32,512]{2,1,0:T(8,128)} %copy-done.1, ...), custom_call_target="tpu_custom_call" | custom-call | tf_op jit(solution)/shard_map/cross/pallas_call | solution.py:239
  24.9 0.1 collective-permute-start.6
  25.0 3.6 %collective-permute-start.7 = (f32[16,24]{1,0:T(8,128)}, f32[16,24]{1,0:T(8,128)S(1)}, u32[]{:S(2)}, u32[]{:S(2)}) collective-permute-start(f32[16,24]{1,0:T(8,128)} %cross.1.refs_0_), channel_id=1, source_target_pairs={{0,8},{4,12},{8,0},{12,4},{1,9},{5,13},{9,1},{13,5},{2,10},{6,14},... | collective-permute-start | bytes 4616 | tf_op jit(solution)/shard_map/ppermute | solution.py:213
  28.6 0.3 collective-permute-start.8
  28.9 1.6 %collective-permute-done.6.refs_1_ = f32[16,24]{1,0:T(8,128)S(1)} collective-permute-done((f32[16,24]{1,0:T(8,128)}, f32[16,24]{1,0:T(8,128)S(1)}, u32[]{:S(2)}, u32[]{:S(2)}) %collective-permute-start.6) | collective-permute-done | bytes 1568 | tf_op jit(solution)/shard_map/ppermute | solution.py:213
  30.6 0.0 copy-start.3
  30.6 0.0 collective-permute-done.7.refs_2_
  30.6 0.0 copy-start.4
  30.6 1.9 %collective-permute-done.8.refs_3_ = f32[16,24]{1,0:T(8,128)S(1)} collective-permute-done((f32[16,24]{1,0:T(8,128)}, f32[16,24]{1,0:T(8,128)S(1)}, u32[]{:S(2)}, u32[]{:S(2)}) %collective-permute-start.8) | collective-permute-done | bytes 1568 | tf_op jit(solution)/shard_map/ppermute | solution.py:213
  32.5 0.0 copy-done.3
  32.5 0.0 copy-done.4
  32.5 0.0 copy-start.5
  32.5 0.6 %copy-done.5 = f32[16,24]{1,0:T(8,128)} copy-done((f32[16,24]{1,0:T(8,128)}, f32[16,24]{1,0:T(8,128)S(1)}, u32[]{:S(2)}) %copy-start.5) | copy-done | bytes 1560
  33.1 5.0 %mix.1 = f32[4,32,512]{2,1,0:T(8,128)} custom-call(f32[16,24]{1,0:T(8,128)} %cross.1.refs_0_, f32[16,24]{1,0:T(8,128)} %copy-done.3, f32[16,24]{1,0:T(8,128)} %copy-done.4, f32[16,24]{1,0:T(8,128)} %copy-done.5, f32[4,32,512]{2,1,0:T(8,128)} %refs_4_.3, f32[4,32,512]{2,1,0:T(8,128)} %copy-done, f32[4,32,512]{2,1,0:T(8,128)} %copy-done.1, f32[4,32,512]{2,1,0:T(8,128)} %copy-done.2), custom_call_target="tpu_custom_call" | custom-call | tf_op jit(solution)/shard_map/mix/pallas_call | solution.py:239
Async XLA Ops:
  0.0 9.5 %collective-permute-start.4 = (f32[4,32,512]{2,1,0:T(8,128)}, f32[4,32,512]{2,1,0:T(8,128)S(1)}, u32[]{:S(2)}, u32[]{:S(2)}) collective-permute-start(f32[4,32,512]{2,1,0:T(8,128)} %refs_4_.3), channel_id=1, source_target_pairs={{0,2},{1,3},{2,0},{3,1},{4,6},{5,7},{6,4},{7,5},{8,10},{9,11},{10,... | collective-permute-start | bytes 786440 | tf_op jit(solution)/shard_map/ppermute | solution.py:213
  3.0 16.1 %collective-permute-start.3 = (f32[4,32,512]{2,1,0:T(8,128)}, f32[4,32,512]{2,1,0:T(8,128)S(1)}, u32[]{:S(2)}, u32[]{:S(2)}) collective-permute-start(f32[4,32,512]{2,1,0:T(8,128)} %refs_4_.3), channel_id=1, source_target_pairs={{0,1},{1,0},{2,3},{3,2},{4,5},{5,4},{6,7},{7,6},{8,9},{9,8},{10,11... | collective-permute-start | bytes 786440 | tf_op jit(solution)/shard_map/ppermute | solution.py:213
  9.5 12.3 %copy-start.1 = (f32[4,32,512]{2,1,0:T(8,128)}, f32[4,32,512]{2,1,0:T(8,128)S(1)}, u32[]{:S(2)}) copy-start(f32[4,32,512]{2,1,0:T(8,128)S(1)} %collective-permute-done.4.refs_0_.refs_6_) | copy-start | bytes 786436
  9.5 12.3 %collective-permute-start.5 = (f32[4,32,512]{2,1,0:T(8,128)S(1)}, f32[4,32,512]{2,1,0:T(8,128)S(1)}, u32[]{:S(2)}, u32[]{:S(2)}) collective-permute-start(f32[4,32,512]{2,1,0:T(8,128)S(1)} %collective-permute-done.4.refs_0_.refs_6_), channel_id=1, source_target_pairs={{0,1},{1,0},{2,3},{3,2},{4,5},{5,4},{6,7},{7,6},{8,9},{9,8},{10,11... | collective-permute-start | bytes 786440 | tf_op jit(solution)/shard_map/ppermute | solution.py:213
  11.0 4.4 %copy-start.9 = (f32[8,128]{1,0:T(8,128)S(1)}, f32[8,128]{1,0:T(8,128)}, u32[]{:S(2)}) copy-start(f32[8,128]{1,0:T(8,128)} %get-tuple-element.16) | copy-start | bytes 12292
  11.0 5.8 %collective-permute-start = (f32[8,128]{1,0:T(8,128)}, f32[8,128]{1,0:T(8,128)S(1)}, u32[]{:S(2)}, u32[]{:S(2)}) collective-permute-start(f32[8,128]{1,0:T(8,128)} %get-tuple-element.14), channel_id=1, source_target_pairs={{0,4},{4,8},{8,12},{12,0},{1,5},{5,9},{9,13},{13,1},{2,6},{6,10},{... | collective-permute-start | bytes 12296 | tf_op jit(solution)/shard_map/ppermute | solution.py:213
  12.9 4.7 %collective-permute-start.1 = (f32[8,128]{1,0:T(8,128)}, f32[8,128]{1,0:T(8,128)S(1)}, u32[]{:S(2)}, u32[]{:S(2)}) collective-permute-start(f32[8,128]{1,0:T(8,128)} %get-tuple-element.15), channel_id=1, source_target_pairs={{0,8},{4,12},{8,0},{12,4},{1,9},{5,13},{9,1},{13,5},{2,10},{6,14},... | collective-permute-start | bytes 12296 | tf_op jit(solution)/shard_map/ppermute | solution.py:213
  15.4 3.6 %collective-permute-start.2 = (f32[8,128]{1,0:T(8,128)S(1)}, f32[8,128]{1,0:T(8,128)S(1)}, u32[]{:S(2)}, u32[]{:S(2)}) collective-permute-start(f32[8,128]{1,0:T(8,128)S(1)} %copy-done.9), channel_id=1, source_target_pairs={{0,12},{4,0},{8,4},{12,8},{1,13},{5,1},{9,5},{13,9},{2,14},{6,2},{... | collective-permute-start | bytes 12296 | tf_op jit(solution)/shard_map/ppermute | solution.py:213
  16.8 2.3 %copy-start.6 = (f32[8,128]{1,0:T(8,128)}, f32[8,128]{1,0:T(8,128)S(1)}, u32[]{:S(2)}) copy-start(f32[8,128]{1,0:T(8,128)S(1)} %collective-permute-done.refs_1_) | copy-start | bytes 12292
  17.6 1.5 %copy-start.7 = (f32[8,128]{1,0:T(8,128)}, f32[8,128]{1,0:T(8,128)S(1)}, u32[]{:S(2)}) copy-start(f32[8,128]{1,0:T(8,128)S(1)} %collective-permute-done.1.refs_2_) | copy-start | bytes 12292
  19.1 0.6 %copy-start.8 = (f32[8,128]{1,0:T(8,128)}, f32[8,128]{1,0:T(8,128)S(1)}, u32[]{:S(2)}) copy-start(f32[8,128]{1,0:T(8,128)S(1)} %collective-permute-done.2.refs_3_) | copy-start | bytes 12292
  19.1 0.7 %copy-start = (f32[4,32,512]{2,1,0:T(8,128)}, f32[4,32,512]{2,1,0:T(8,128)S(1)}, u32[]{:S(2)}) copy-start(f32[4,32,512]{2,1,0:T(8,128)S(1)} %collective-permute-done.3.refs_5_) | copy-start | bytes 786436
  21.8 0.7 %copy-start.2 = (f32[4,32,512]{2,1,0:T(8,128)}, f32[4,32,512]{2,1,0:T(8,128)S(1)}, u32[]{:S(2)}) copy-start(f32[4,32,512]{2,1,0:T(8,128)S(1)} %collective-permute-done.5.refs_1_.refs_7_) | copy-start | bytes 786436
  24.9 5.7 %collective-permute-start.6 = (f32[16,24]{1,0:T(8,128)}, f32[16,24]{1,0:T(8,128)S(1)}, u32[]{:S(2)}, u32[]{:S(2)}) collective-permute-start(f32[16,24]{1,0:T(8,128)} %cross.1.refs_0_), channel_id=1, source_target_pairs={{0,4},{4,8},{8,12},{12,0},{1,5},{5,9},{9,13},{13,1},{2,6},{6,10},{... | collective-permute-start | bytes 4616 | tf_op jit(solution)/shard_map/ppermute | solution.py:213
  25.0 5.5 %collective-permute-start.7 = (f32[16,24]{1,0:T(8,128)}, f32[16,24]{1,0:T(8,128)S(1)}, u32[]{:S(2)}, u32[]{:S(2)}) collective-permute-start(f32[16,24]{1,0:T(8,128)} %cross.1.refs_0_), channel_id=1, source_target_pairs={{0,8},{4,12},{8,0},{12,4},{1,9},{5,13},{9,1},{13,5},{2,10},{6,14},... | collective-permute-start | bytes 4616 | tf_op jit(solution)/shard_map/ppermute | solution.py:213
  28.6 3.9 %collective-permute-start.8 = (f32[16,24]{1,0:T(8,128)}, f32[16,24]{1,0:T(8,128)S(1)}, u32[]{:S(2)}, u32[]{:S(2)}) collective-permute-start(f32[16,24]{1,0:T(8,128)} %cross.1.refs_0_), channel_id=1, source_target_pairs={{0,12},{4,0},{8,4},{12,8},{1,13},{5,1},{9,5},{13,9},{2,14},{6,2},{... | collective-permute-start | bytes 4616 | tf_op jit(solution)/shard_map/ppermute | solution.py:213
  30.6 1.9 %copy-start.3 = (f32[16,24]{1,0:T(8,128)}, f32[16,24]{1,0:T(8,128)S(1)}, u32[]{:S(2)}) copy-start(f32[16,24]{1,0:T(8,128)S(1)} %collective-permute-done.6.refs_1_) | copy-start | bytes 4612
  30.6 1.9 %copy-start.4 = (f32[16,24]{1,0:T(8,128)}, f32[16,24]{1,0:T(8,128)S(1)}, u32[]{:S(2)}) copy-start(f32[16,24]{1,0:T(8,128)S(1)} %collective-permute-done.7.refs_2_) | copy-start | bytes 4612
  32.5 0.6 %copy-start.5 = (f32[16,24]{1,0:T(8,128)}, f32[16,24]{1,0:T(8,128)S(1)}, u32[]{:S(2)}) copy-start(f32[16,24]{1,0:T(8,128)S(1)} %collective-permute-done.8.refs_3_) | copy-start | bytes 4612

commit v2 on v1

--- a/solution.py
+++ b/solution.py
@@ -24,6 +24,7 @@
 F32 = jnp.float32
 BF16 = jnp.bfloat16
 DIRECT_DOM = 8
+VMEM_LIMIT = 8 * 1024 * 1024
 
 
 def lagrange_scale(index):
@@ -51,7 +52,7 @@
     return high, low
 
 
-def pack_kernel(direct, counts, coords, owner, obs, weight, *rest):
+def pack_kernel(direct, paired, counts, coords, owner, obs, weight, *rest):
     outs, block = rest[:-1], rest[-1]
     n_dom = counts.shape[1]
     slots = coords.shape[1]
@@ -72,7 +73,11 @@
         turned = pltpu.roll(rows, lax.rem(half - start + slots, slots), axis=1)[:, : 2 * CAP]
         return jnp.where((column >= half) & (column < half + count), turned, 0.0)
 
-    if direct:
+    if paired:
+        near = jnp.where(lax.rem(lax.axis_index("ens"), 2) == 0, 1, 3)
+        for out, shift, half in zip(outs, (0, near, 2), (0, CAP, 0)):
+            out[...] = tile(lax.rem(here + shift, n_dom), half)
+    elif direct:
         for shift in range(n_dom):
             outs[shift][...] = tile(lax.rem(here + shift, n_dom), (shift % 2) * CAP)
     else:
@@ -132,7 +137,11 @@
         )
 
 
-def cross_kernel(sensors_ref, high_ref, low_ref, values_ref, *refs):
+def is_odd(paired):
+    return lax.rem(lax.axis_index("ens"), 2) if paired else 0
+
+
+def cross_kernel(paired, sensors_ref, high_ref, low_ref, values_ref, *refs):
     state_refs, out = refs[:-1], refs[-1]
     high, low = high_ref[...], low_ref[...]
     sensors = sensors_ref[...]
@@ -144,6 +153,11 @@
         parts.append(pick(rows, members, elements, high, low, chosen))
     values = jnp.concatenate(parts, axis=0)
     total = values.shape[0]
+    if paired:
+        size = total // (len(parts) + 1)
+        blocks = [values[first : first + size] for first in range(0, total, size)]
+        turned = [blocks[index ^ 1] for index in range(len(blocks))]
+        values = jnp.where(is_odd(paired) == 1, jnp.concatenate(turned, axis=0), values)
     mean_value = jnp.sum(values, axis=0, keepdims=True) * (1.0 / total)
     anomaly = values - mean_value
     weighted = anomaly * sensors[5:6, :]
@@ -159,7 +173,7 @@
     )
 
 
-def mix_kernel(sum_count, *refs):
+def mix_kernel(paired, sum_count, *refs):
     sums, state_refs, out, splats = refs[:sum_count], refs[sum_count:-2], refs[-2], refs[-1]
     highest = lax.Precision.HIGHEST
     total_sum = sums[0][...]
@@ -192,6 +206,11 @@
     )
     transform = inverse_root * jnp.sqrt((members - 1) / trace_value) + mean_weights
     mixing = transform - jnp.mean(transform, axis=0, keepdims=True) + 1.0 / members
+    odd = is_odd(paired)
+    if paired:
+        mixing = jnp.where(
+            odd == 1, mixing[:, local_members : 2 * local_members], mixing[:, :local_members]
+        )
     for j in range(members):
         for k in range(local_members):
             splats[j * local_members + k] = jnp.broadcast_to(mixing[j : j + 1, k : k + 1], (8, 128))
@@ -201,9 +220,11 @@
             lanes = slice(128 * lane, 128 * lane + 128)
             totals = [None] * local_members
             for j in range(members):
-                value = state_refs[j // local_members][j % local_members, span, lanes]
+                piece, member = divmod(j, local_members)
+                value = state_refs[piece][member, span, lanes]
+                place = piece + odd * (1 - 2 * (piece % 2))
                 for k in range(local_members):
-                    term = splats[j * local_members + k] * value
+                    term = splats[(place * local_members + member) * local_members + k] * value
                     totals[k] = term if totals[k] is None else totals[k] + term
             for k in range(local_members):
                 out[k, span, lanes] = totals[k]
@@ -213,26 +234,61 @@
     return lax.ppermute(value, axis, pairs)
 
 
-def gather_members(state, n_ens):
+def shifted(value, n_dom, shift):
+    return exchange(value, "dom", [(d, (d + shift) % n_dom) for d in range(n_dom)])
+
+
+def swapped(value, n_ens):
+    return exchange(value, "ens", [(e, e ^ 1) for e in range(n_ens)])
+
+
+def is_paired(n_dom, n_ens):
+    return n_dom == 4 and n_ens % 2 == 0
+
+
+def spread(values, n_dom, n_ens):
+    if not is_paired(n_dom, n_ens):
+        return [values[0]] + [shifted(values[s], n_dom, s) for s in range(1, n_dom)]
+    here, near, far = values
+    pairs = []
+    for d in range(n_dom):
+        for e in range(n_ens):
+            target = (d + (3 if e % 2 else 1)) % n_dom
+            pairs.append((d * n_ens + e, target * n_ens + e))
+    near = exchange(near, ("dom", "ens"), pairs)
+    far = shifted(far, n_dom, 2)
+    return [here, near, far, swapped(near, n_ens)]
+
+
+def gather_early(state, n_ens):
     pieces = {0: state}
     if n_ens & (n_ens - 1) == 0:
-        bit = n_ens >> 1
-        while bit:
-            pairs = [(e, e ^ bit) for e in range(n_ens)]
-            for key in list(pieces):
-                pieces[key ^ bit] = exchange(pieces[key], "ens", pairs)
-            bit >>= 1
+        for bit in {1, n_ens >> 1} - {0}:
+            pieces[bit] = exchange(state, "ens", [(e, e ^ bit) for e in range(n_ens)])
     else:
         for shift in range(1, n_ens):
             pairs = [(e, (e + shift) % n_ens) for e in range(n_ens)]
             pieces[shift] = exchange(state, "ens", pairs)
-    return [pieces[key] for key in sorted(pieces)]
+    return pieces
+
+
+def gather_late(pieces, n_ens, after):
+    bit = n_ens >> 2
+    while bit and len(pieces) < n_ens:
+        for key in list(pieces):
+            if key ^ bit not in pieces:
+                source = lax.optimization_barrier((pieces[key], after))[0]
+                pieces[key ^ bit] = exchange(source, "ens", [(e, e ^ bit) for e in range(n_ens)])
+        bit >>= 1
+    return pieces
 
 
 def make_on_device(n_dom, n_ens):
     vmem = pl.BlockSpec(memory_space=pltpu.VMEM)
     smem = pl.BlockSpec(memory_space=pltpu.SMEM)
     direct = n_dom <= DIRECT_DOM
+    paired = is_paired(n_dom, n_ens)
+    limit = VMEM_LIMIT if direct else None
 
     def call(kernel, name, out_shape, operands, specs=None, scratch=()):
         many = isinstance(out_shape, (list, tuple))
@@ -243,6 +299,7 @@
             in_specs=specs or [vmem] * len(operands),
             out_specs=[vmem] * len(out_shape) if many else vmem,
             scratch_shapes=list(scratch),
+            compiler_params=pltpu.CompilerParams(vmem_limit_bytes=limit),
         )(*operands)
 
     def shape(dims, dtype=F32):
@@ -252,25 +309,25 @@
         local_members, elements, nodes = state.shape
         slots = coords.shape[1]
         members = local_members * n_ens
-        pieces = gather_members(state, n_ens)
         tile_shape = (8, 2 * CAP)
         tiles = list(call(
-            lambda *refs: pack_kernel(direct, *refs),
+            lambda *refs: pack_kernel(direct, paired, *refs),
             "pack",
-            [shape(tile_shape)] * n_dom if direct else [shape((n_dom,) + tile_shape)],
+            [shape(tile_shape)] * (3 if paired else n_dom)
+            if direct
+            else [shape((n_dom,) + tile_shape)],
             [counts, coords, owner_local[None], obs_value[None], obs_weight[None]],
             [smem] + [vmem] * 4,
             [pltpu.VMEM((8, slots), F32)],
         ))
         if direct:
-            for shift in range(1, n_dom):
-                pairs = [(d, (d + shift) % n_dom) for d in range(n_dom)]
-                tiles[shift] = exchange(tiles[shift], "dom", pairs)
+            tiles = spread(tiles, n_dom, n_ens)
         else:
             moved = lax.all_to_all(tiles[0], "dom", split_axis=0, concat_axis=0, tiled=True)
             tiles = [moved[d] for d in range(n_dom)]
+        pieces = gather_early(state, n_ens)
         sensor_count = CAP * (n_dom + n_dom % 2)
-        early = max(1, n_ens // 2)
+        early = min(2, n_ens)
         sensors, high, low, values = call(
             lambda *refs: values_kernel(n_dom, *refs),
             "values",
@@ -280,23 +337,22 @@
                 shape((nodes, sensor_count), BF16),
                 shape((early * local_members, sensor_count)),
             ],
-            list(tiles) + pieces[:early],
-        )
+            list(tiles) + [pieces[key] for key in range(early)],
+        )
+        pieces = gather_late(pieces, n_ens, sensors)
+        pieces = [pieces[key] for key in range(n_ens)]
         partial_sum = call(
-            cross_kernel,
+            lambda *refs: cross_kernel(paired, *refs),
             "cross",
             shape((members, members + 8)),
             [sensors, high, low, values] + pieces[early:],
         )
         if direct:
-            sums = [partial_sum]
-            for shift in range(1, n_dom):
-                pairs = [(d, (d + shift) % n_dom) for d in range(n_dom)]
-                sums.append(exchange(partial_sum, "dom", pairs))
+            sums = spread([partial_sum] * (3 if paired else n_dom), n_dom, n_ens)
         else:
             sums = [lax.psum(partial_sum, "dom")]
         return call(
-            lambda *refs: mix_kernel(len(sums), *refs),
+            lambda *refs: mix_kernel(paired, len(sums), *refs),
             "mix",
             shape(state.shape),
             sums + pieces,

time: 38.3 us -> 26.6 us (0.69)
  Pallas kernels: 10.9 us -> 5.47 us
  waiting for transfers between devices: 12.3 us -> 7.44 us
  starting transfers between devices: 12.8 us -> 10.5 us
  local copies, waits for them, and re-layouts: 1.99 us -> 2.99 us
    pallas_call x4, Pallas kernels: 10.9 us -> 5.47 us  [call(): pl.pallas_call(kernel, name=name, out_shape=out_shape, in_specs=specs or...]
    ppermute x9, waiting for transfers between devices: 12.3 us -> 7.44 us  [exchange(): return lax.ppermute(value, axis, pairs)]
    ppermute x9, starting transfers between devices: 12.8 us -> 10.5 us  [exchange(): return lax.ppermute(value, axis, pairs)]
    unnamed x20 -> x14, local copies, waits for them, and re-layouts: 1.99 us -> 2.99 us
  transfers between devices with their start and end apart: 9 -> 9, of which waited for: 5 -> 7; matrix products, arithmetic and copies ran while one was open for 0% -> 0% of each run, Pallas kernels for 9% -> 4%
where the time goes in v2:
time: 26.6 us; the launch traced here: 26.4 us
  starting transfers between devices  10.5 us (39%)
  waiting for transfers between devices  7.44 us (28%)
  Pallas kernels  5.47 us (21%)
  local copies, waits for them, and re-layouts  2.99 us (11%)
    ppermute x9, starting transfers between devices, exchange(): return lax.ppermute(value, axis, pairs)  10.5 us
    ppermute x9, waiting for transfers between devices, exchange(): return lax.ppermute(value, axis, pairs)  7.44 us
    pallas_call x4, Pallas kernels, call(): pl.pallas_call(kernel, name=name, out_shape=out_shape, in_specs=specs or...  5.47 us
    unnamed x14, local copies, waits for them, and re-layouts  2.99 us
  transfers between devices with their start and end apart: 9, of which 7 were waited for; matrix products, arithmetic and copies ran while one was open for 0% of the time, Pallas kernels for 4%

profile of v2, /device:TPU:0, one launch (start us, length us, event | category | flops | bytes accessed | tf_op | source)
XLA Modules:
  0.0 26.4 jit_solution(12456391477960333768)
XLA Ops:
  0.0 0.0 copy-start.2
  0.0 0.5 %collective-permute-start.3 = (f32[4,32,512]{2,1,0:T(8,128)}, f32[4,32,512]{2,1,0:T(8,128)S(1)}, u32[]{:S(2)}, u32[]{:S(2)}) collective-permute-start(f32[4,32,512]{2,1,0:T(8,128)} %refs_4_.3), channel_id=1, source_target_pairs={{0,1},{1,0},{2,3},{3,2},{4,5},{5,4},{6,7},{7,6},{8,9},{9,8},{10,11... | collective-permute-start | bytes 786440 | tf_op jit(solution)/shard_map/ppermute | solution.py:234
  0.5 2.5 %collective-permute-start.4 = (f32[4,32,512]{2,1,0:T(8,128)}, f32[4,32,512]{2,1,0:T(8,128)S(1)}, u32[]{:S(2)}, u32[]{:S(2)}) collective-permute-start(f32[4,32,512]{2,1,0:T(8,128)} %refs_4_.3), channel_id=1, source_target_pairs={{0,2},{1,3},{2,0},{3,1},{4,6},{5,7},{6,4},{7,5},{8,10},{9,11},{10,... | collective-permute-start | bytes 786440 | tf_op jit(solution)/shard_map/ppermute | solution.py:234
  3.0 0.0 copy-start.3
  3.0 0.0 copy-start.6
  3.0 0.0 copy-done.2
  3.0 0.7 %copy-done.3 = s32[256]{0:T(256)S(1)} copy-done((s32[256]{0:T(256)S(1)}, s32[256]{0:T(256)}, u32[]{:S(2)}) %copy-start.3) | copy-done | bytes 1048
  3.7 0.0 copy-done.6
  3.7 0.0 copy-start.4
  3.7 0.7 %copy-done.4 = f32[256]{0:T(256)S(1)} copy-done((f32[256]{0:T(256)S(1)}, f32[256]{0:T(256)}, u32[]{:S(2)}) %copy-start.4) | copy-done | bytes 1048
  4.4 0.0 copy-start.5
  4.4 0.7 %copy-done.5 = f32[256]{0:T(256)S(1)} copy-done((f32[256]{0:T(256)S(1)}, f32[256]{0:T(256)}, u32[]{:S(2)}) %copy-start.5) | copy-done | bytes 1048
  5.1 0.6 %pack.1 = (f32[8,128]{1,0:T(8,128)S(1)}, f32[8,128]{1,0:T(8,128)S(1)}, f32[8,128]{1,0:T(8,128)S(1)}) custom-call(s32[1,4]{1,0:T(1,128)S(1)} %copy-done.6, f32[3,256]{1,0:T(4,128)S(1)} %copy-done.2, s32[1,256]{1,0:T(1,128)S(1)} %bitcast.3, f32[1,256]{1,0:T(1,128)S(1)} %bitcast.4, f32[1,256]{1,0:T(1,128)S(1)} %bitcast.5), custom_call_target="tpu_custom_call" | custom-call | tf_op jit(solution)/shard_map/pack/pallas_call | solution.py:295
  5.7 1.6 %collective-permute-start = (f32[8,128]{1,0:T(8,128)S(1)}, f32[8,128]{1,0:T(8,128)S(1)}, u32[]{:S(2)}, u32[]{:S(2)}) collective-permute-start(f32[8,128]{1,0:T(8,128)S(1)} %get-tuple-element.14), channel_id=1, source_target_pairs={{0,4},{1,13},{2,6},{3,15},{4,8},{5,1},{6,10},{7,3},{8,12},{9,5},{1... | collective-permute-start | bytes 12296 | tf_op jit(solution)/shard_map/ppermute | solution.py:234
  7.3 2.6 %collective-permute-start.1 = (f32[8,128]{1,0:T(8,128)S(1)}, f32[8,128]{1,0:T(8,128)S(1)}, u32[]{:S(2)}, u32[]{:S(2)}) collective-permute-start(f32[8,128]{1,0:T(8,128)S(1)} %get-tuple-element.15), channel_id=1, source_target_pairs={{0,8},{4,12},{8,0},{12,4},{1,9},{5,13},{9,1},{13,5},{2,10},{6,14},... | collective-permute-start | bytes 12296 | tf_op jit(solution)/shard_map/ppermute | solution.py:234
  9.9 1.2 %collective-permute-done.refs_1_ = f32[8,128]{1,0:T(8,128)S(1)} collective-permute-done((f32[8,128]{1,0:T(8,128)S(1)}, f32[8,128]{1,0:T(8,128)S(1)}, u32[]{:S(2)}, u32[]{:S(2)}) %collective-permute-start) | collective-permute-done | bytes 4128 | tf_op jit(solution)/shard_map/ppermute | solution.py:234
  11.2 0.0 collective-permute-start.2
  11.2 0.7 %collective-permute-done.1.refs_2_ = f32[8,128]{1,0:T(8,128)S(1)} collective-permute-done((f32[8,128]{1,0:T(8,128)S(1)}, f32[8,128]{1,0:T(8,128)S(1)}, u32[]{:S(2)}, u32[]{:S(2)}) %collective-permute-start.1) | collective-permute-done | bytes 4128 | tf_op jit(solution)/shard_map/ppermute | solution.py:234
  11.9 0.5 %collective-permute-done.2.refs_3_ = f32[8,128]{1,0:T(8,128)S(1)} collective-permute-done((f32[8,128]{1,0:T(8,128)S(1)}, f32[8,128]{1,0:T(8,128)S(1)}, u32[]{:S(2)}, u32[]{:S(2)}) %collective-permute-start.2) | collective-permute-done | bytes 4128 | tf_op jit(solution)/shard_map/ppermute | solution.py:234
  12.3 0.0 collective-permute-done.3.refs_5_
  12.3 0.0 copy-start
  12.3 0.9 %copy-done = f32[4,32,512]{2,1,0:T(8,128)S(1)} copy-done((f32[4,32,512]{2,1,0:T(8,128)S(1)}, f32[4,32,512]{2,1,0:T(8,128)}, u32[]{:S(2)}) %copy-start) | copy-done | bytes 262168
  13.3 0.4 %values.1 = (f32[8,256]{1,0:T(8,128)S(1)}, bf16[512,256]{1,0:T(8,128)(2,1)S(1)}, bf16[512,256]{1,0:T(8,128)(2,1)S(1)}, f32[8,256]{1,0:T(8,128)S(1)}) custom-call(f32[8,128]{1,0:T(8,128)S(1)} %get-tuple-element.13.refs_0_, f32[8,128]{1,0:T(8,128)S(1)} %collective-permute-done.refs_1_, f32[8,128]{1,0:T(8,128)S(1)} %collective-permute-done.1.refs_2_, ...), custom_call_target="tpu_custom_call" | custom-call | tf_op jit(solution)/shard_map/values/pallas_call | solution.py:295
  13.7 0.0 collective-permute-done.4.refs_4_.refs_6_
  13.7 0.3 %collective-permute-start.5 = (f32[4,32,512]{2,1,0:T(8,128)S(1)}, f32[4,32,512]{2,1,0:T(8,128)S(1)}, u32[]{:S(2)}, u32[]{:S(2)}) collective-permute-start(f32[4,32,512]{2,1,0:T(8,128)S(1)} %collective-permute-done.4.refs_4_.refs_6_), channel_id=1, source_target_pairs={{0,1},{1,0},{2,3},{3,2},{4,5},{5,4},{6,7},{7,6},{8,9},{9,8},{10,11... | collective-permute-start | bytes 786440 | tf_op jit(solution)/shard_map/ppermute | solution.py:234
  14.1 1.3 %collective-permute-done.5.refs_5_.refs_7_ = f32[4,32,512]{2,1,0:T(8,128)S(1)} collective-permute-done((f32[4,32,512]{2,1,0:T(8,128)S(1)}, f32[4,32,512]{2,1,0:T(8,128)S(1)}, u32[]{:S(2)}, u32[]{:S(2)}) %collective-permute-start.5) | collective-permute-done | bytes 262176 | tf_op jit(solution)/shard_map/ppermute | solution.py:234
  15.3 0.0 copy-start.1
  15.3 0.5 %cross.1.refs_0_ = f32[16,24]{1,0:T(8,128)S(1)} custom-call(f32[8,256]{1,0:T(8,128)S(1)} %get-tuple-element.16.refs_0_, bf16[512,256]{1,0:T(8,128)(2,1)S(1)} %get-tuple-element.17.refs_1_, bf16[512,256]{1,0:T(8,128)(2,1)S(1)} %get-tuple-element.18.refs_2_, f32[8,256]{1,0:T(8,128)S(1)} %get-tuple-element.19.refs_3_, ...), custom_call_target="tpu_custom_call" | custom-call | tf_op jit(solution)/shard_map/cross/pallas_call | solution.py:295
  15.9 1.1 %collective-permute-start.6 = (f32[16,24]{1,0:T(8,128)S(1)}, f32[16,24]{1,0:T(8,128)S(1)}, u32[]{:S(2)}, u32[]{:S(2)}) collective-permute-start(f32[16,24]{1,0:T(8,128)S(1)} %cross.1.refs_0_), channel_id=1, source_target_pairs={{0,4},{1,13},{2,6},{3,15},{4,8},{5,1},{6,10},{7,3},{8,12},{9,5},{1... | collective-permute-start | bytes 4616 | tf_op jit(solution)/shard_map/ppermute | solution.py:234
  17.0 1.8 %collective-permute-start.7 = (f32[16,24]{1,0:T(8,128)S(1)}, f32[16,24]{1,0:T(8,128)S(1)}, u32[]{:S(2)}, u32[]{:S(2)}) collective-permute-start(f32[16,24]{1,0:T(8,128)S(1)} %cross.1.refs_0_), channel_id=1, source_target_pairs={{0,8},{4,12},{8,0},{12,4},{1,9},{5,13},{9,1},{13,5},{2,10},{6,14},... | collective-permute-start | bytes 4616 | tf_op jit(solution)/shard_map/ppermute | solution.py:234
  18.7 2.6 %collective-permute-done.6.refs_1_ = f32[16,24]{1,0:T(8,128)S(1)} collective-permute-done((f32[16,24]{1,0:T(8,128)S(1)}, f32[16,24]{1,0:T(8,128)S(1)}, u32[]{:S(2)}, u32[]{:S(2)}) %collective-permute-start.6) | collective-permute-done | bytes 1568 | tf_op jit(solution)/shard_map/ppermute | solution.py:234
  21.3 0.0 collective-permute-start.8
  21.4 0.2 collective-permute-done.7.refs_2_
  21.5 1.0 %collective-permute-done.8.refs_3_ = f32[16,24]{1,0:T(8,128)S(1)} collective-permute-done((f32[16,24]{1,0:T(8,128)S(1)}, f32[16,24]{1,0:T(8,128)S(1)}, u32[]{:S(2)}, u32[]{:S(2)}) %collective-permute-start.8) | collective-permute-done | bytes 1568 | tf_op jit(solution)/shard_map/ppermute | solution.py:234
  22.5 0.0 copy-done.1
  22.5 3.9 %mix.1 = f32[4,32,512]{2,1,0:T(8,128)} custom-call(f32[16,24]{1,0:T(8,128)S(1)} %cross.1.refs_0_, f32[16,24]{1,0:T(8,128)S(1)} %collective-permute-done.6.refs_1_, f32[16,24]{1,0:T(8,128)S(1)} %collective-permute-done.7.refs_2_, f32[16,24]{1,0:T(8,128)S(1)} %collective-permute-done.8.refs_3_, f32[4,32,512]{2,1,0:T(8,128)S(1)} %copy-done.1, ...), custom_call_target="tpu_custom_call" | custom-call | tf_op jit(solution)/shard_map/mix/pallas_call | solution.py:295
Async XLA Ops:
  0.0 3.0 %copy-start.2 = (f32[3,256]{1,0:T(4,128)S(1)}, f32[3,256]{1,0:T(4,128)}, u32[]{:S(2)}) copy-start(f32[3,256]{1,0:T(4,128)} %refs_1_.1) | copy-start | bytes 9220
  0.0 12.3 %collective-permute-start.3 = (f32[4,32,512]{2,1,0:T(8,128)}, f32[4,32,512]{2,1,0:T(8,128)S(1)}, u32[]{:S(2)}, u32[]{:S(2)}) collective-permute-start(f32[4,32,512]{2,1,0:T(8,128)} %refs_4_.3), channel_id=1, source_target_pairs={{0,1},{1,0},{2,3},{3,2},{4,5},{5,4},{6,7},{7,6},{8,9},{9,8},{10,11... | collective-permute-start | bytes 786440 | tf_op jit(solution)/shard_map/ppermute | solution.py:234
  0.5 13.2 %collective-permute-start.4 = (f32[4,32,512]{2,1,0:T(8,128)}, f32[4,32,512]{2,1,0:T(8,128)S(1)}, u32[]{:S(2)}, u32[]{:S(2)}) collective-permute-start(f32[4,32,512]{2,1,0:T(8,128)} %refs_4_.3), channel_id=1, source_target_pairs={{0,2},{1,3},{2,0},{3,1},{4,6},{5,7},{6,4},{7,5},{8,10},{9,11},{10,... | collective-permute-start | bytes 786440 | tf_op jit(solution)/shard_map/ppermute | solution.py:234
  3.0 0.7 %copy-start.3 = (s32[256]{0:T(256)S(1)}, s32[256]{0:T(256)}, u32[]{:S(2)}) copy-start(s32[256]{0:T(256)} %param.8) | copy-start | bytes 3076
  3.0 0.7 %copy-start.6 = (s32[1,4]{1,0:T(1,128)S(1)}, s32[1,4]{1,0:T(1,128)}, u32[]{:S(2)}) copy-start(s32[1,4]{1,0:T(1,128)} %refs_0_.1) | copy-start | bytes 52
  3.7 0.7 %copy-start.4 = (f32[256]{0:T(256)S(1)}, f32[256]{0:T(256)}, u32[]{:S(2)}) copy-start(f32[256]{0:T(256)} %param.10) | copy-start | bytes 3076
  4.4 0.7 %copy-start.5 = (f32[256]{0:T(256)S(1)}, f32[256]{0:T(256)}, u32[]{:S(2)}) copy-start(f32[256]{0:T(256)} %param.11) | copy-start | bytes 3076
  5.7 5.5 %collective-permute-start = (f32[8,128]{1,0:T(8,128)S(1)}, f32[8,128]{1,0:T(8,128)S(1)}, u32[]{:S(2)}, u32[]{:S(2)}) collective-permute-start(f32[8,128]{1,0:T(8,128)S(1)} %get-tuple-element.14), channel_id=1, source_target_pairs={{0,4},{1,13},{2,6},{3,15},{4,8},{5,1},{6,10},{7,3},{8,12},{9,5},{1... | collective-permute-start | bytes 12296 | tf_op jit(solution)/shard_map/ppermute | solution.py:234
  7.3 4.5 %collective-permute-start.1 = (f32[8,128]{1,0:T(8,128)S(1)}, f32[8,128]{1,0:T(8,128)S(1)}, u32[]{:S(2)}, u32[]{:S(2)}) collective-permute-start(f32[8,128]{1,0:T(8,128)S(1)} %get-tuple-element.15), channel_id=1, source_target_pairs={{0,8},{4,12},{8,0},{12,4},{1,9},{5,13},{9,1},{13,5},{2,10},{6,14},... | collective-permute-start | bytes 12296 | tf_op jit(solution)/shard_map/ppermute | solution.py:234
  11.2 1.2 %collective-permute-start.2 = (f32[8,128]{1,0:T(8,128)S(1)}, f32[8,128]{1,0:T(8,128)S(1)}, u32[]{:S(2)}, u32[]{:S(2)}) collective-permute-start(f32[8,128]{1,0:T(8,128)S(1)} %collective-permute-done.refs_1_), channel_id=1, source_target_pairs={{0,1},{1,0},{2,3},{3,2},{4,5},{5,4},{6,7},{7,6},{8,9},{9,8},{10,11... | collective-permute-start | bytes 12296 | tf_op jit(solution)/shard_map/ppermute | solution.py:234
  12.3 1.0 %copy-start = (f32[4,32,512]{2,1,0:T(8,128)S(1)}, f32[4,32,512]{2,1,0:T(8,128)}, u32[]{:S(2)}) copy-start(f32[4,32,512]{2,1,0:T(8,128)} %refs_4_.3) | copy-start | bytes 786436
  13.7 1.6 %collective-permute-start.5 = (f32[4,32,512]{2,1,0:T(8,128)S(1)}, f32[4,32,512]{2,1,0:T(8,128)S(1)}, u32[]{:S(2)}, u32[]{:S(2)}) collective-permute-start(f32[4,32,512]{2,1,0:T(8,128)S(1)} %collective-permute-done.4.refs_4_.refs_6_), channel_id=1, source_target_pairs={{0,1},{1,0},{2,3},{3,2},{4,5},{5,4},{6,7},{7,6},{8,9},{9,8},{10,11... | collective-permute-start | bytes 786440 | tf_op jit(solution)/shard_map/ppermute | solution.py:234
  15.3 7.2 %copy-start.1 = (f32[4,32,512]{2,1,0:T(8,128)S(1)}, f32[4,32,512]{2,1,0:T(8,128)}, u32[]{:S(2)}) copy-start(f32[4,32,512]{2,1,0:T(8,128)} %refs_4_.3) | copy-start | bytes 786436
  15.9 5.5 %collective-permute-start.6 = (f32[16,24]{1,0:T(8,128)S(1)}, f32[16,24]{1,0:T(8,128)S(1)}, u32[]{:S(2)}, u32[]{:S(2)}) collective-permute-start(f32[16,24]{1,0:T(8,128)S(1)} %cross.1.refs_0_), channel_id=1, source_target_pairs={{0,4},{1,13},{2,6},{3,15},{4,8},{5,1},{6,10},{7,3},{8,12},{9,5},{1... | collective-permute-start | bytes 4616 | tf_op jit(solution)/shard_map/ppermute | solution.py:234
  17.0 4.5 %collective-permute-start.7 = (f32[16,24]{1,0:T(8,128)S(1)}, f32[16,24]{1,0:T(8,128)S(1)}, u32[]{:S(2)}, u32[]{:S(2)}) collective-permute-start(f32[16,24]{1,0:T(8,128)S(1)} %cross.1.refs_0_), channel_id=1, source_target_pairs={{0,8},{4,12},{8,0},{12,4},{1,9},{5,13},{9,1},{13,5},{2,10},{6,14},... | collective-permute-start | bytes 4616 | tf_op jit(solution)/shard_map/ppermute | solution.py:234
  21.3 1.2 %collective-permute-start.8 = (f32[16,24]{1,0:T(8,128)S(1)}, f32[16,24]{1,0:T(8,128)S(1)}, u32[]{:S(2)}, u32[]{:S(2)}) collective-permute-start(f32[16,24]{1,0:T(8,128)S(1)} %collective-permute-done.6.refs_1_), channel_id=1, source_target_pairs={{0,1},{1,0},{2,3},{3,2},{4,5},{5,4},{6,7},{7,6},{8,9},{9,8},{10,11... | collective-permute-start | bytes 4616 | tf_op jit(solution)/shard_map/ppermute | solution.py:234

commit v3 on v2

--- a/solution.py
+++ b/solution.py
@@ -4,6 +4,7 @@
 from jax.experimental import pallas as pl
 from jax.experimental.pallas import tpu as pltpu
 from jax.sharding import PartitionSpec as P
+
 
 CAP = 64
 NS_ITERS = 8
@@ -52,31 +53,49 @@
     return high, low
 
 
-def pack_kernel(direct, paired, counts, coords, owner, obs, weight, *rest):
-    outs, block = rest[:-1], rest[-1]
+def is_odd(paired):
+    return lax.rem(lax.axis_index("ens"), 2) if paired else 0
+
+
+def pack_kernel(direct, paired, state, counts, coords, owner, obs, weight, *rest):
+    own, outs = rest[0], rest[1:-8]
+    count_box, coord_box, owner_box, obs_box, weight_box, block, state_sem, sems = rest[-8:]
+    state_copy = pltpu.make_async_copy(state, own, state_sem)
+    pairs = zip(
+        (counts, coords, owner, obs, weight), (count_box, coord_box, owner_box, obs_box, weight_box)
+    )
+    copies = [
+        pltpu.make_async_copy(source, target, sems.at[index])
+        for index, (source, target) in enumerate(pairs)
+    ]
+    for copy in copies:
+        copy.start()
+    state_copy.start()
     n_dom = counts.shape[1]
     slots = coords.shape[1]
     here = lax.axis_index("dom")
     block[...] = jnp.zeros(block.shape, F32)
-    block[0:3, :] = coords[...]
-    block[3:4, :] = owner[...].astype(F32)
-    block[4:5, :] = obs[...]
-    block[5:6, :] = weight[...]
+    column = lax.broadcasted_iota(jnp.int32, (8, 2 * CAP), 1)
+    for copy in copies:
+        copy.wait()
+    block[0:3, :] = coord_box[...]
+    block[3:4, :] = owner_box[...].astype(F32)
+    block[4:5, :] = obs_box[...]
+    block[5:6, :] = weight_box[...]
     rows = block[...]
-    column = lax.broadcasted_iota(jnp.int32, (8, 2 * CAP), 1)
 
     def tile(target, half):
         start = jnp.int32(0)
         for other in range(n_dom):
-            start = start + jnp.where(other < target, counts[0, other], 0)
-        count = counts[0, target]
+            start = start + jnp.where(other < target, count_box[0, other], 0)
+        count = count_box[0, target]
         turned = pltpu.roll(rows, lax.rem(half - start + slots, slots), axis=1)[:, : 2 * CAP]
         return jnp.where((column >= half) & (column < half + count), turned, 0.0)
 
     if paired:
-        near = jnp.where(lax.rem(lax.axis_index("ens"), 2) == 0, 1, 3)
-        for out, shift, half in zip(outs, (0, near, 2), (0, CAP, 0)):
-            out[...] = tile(lax.rem(here + shift, n_dom), half)
+        near = jnp.where(is_odd(paired) == 0, 1, 3)
+        for out, bits, half in zip(outs, (0, near, 2), (0, CAP, 0)):
+            out[...] = tile(jnp.bitwise_xor(here, bits), half)
     elif direct:
         for shift in range(n_dom):
             outs[shift][...] = tile(lax.rem(here + shift, n_dom), (shift % 2) * CAP)
@@ -88,6 +107,7 @@
             return carry
 
         lax.fori_loop(0, n_dom, step, 0)
+    state_copy.wait()
 
 
 def pick(state_rows, members, elements, high, low, chosen):
@@ -135,10 +155,6 @@
         values_out[index * members : (index + 1) * members, :] = pick(
             rows, members, elements, high, low, chosen
         )
-
-
-def is_odd(paired):
-    return lax.rem(lax.axis_index("ens"), 2) if paired else 0
 
 
 def cross_kernel(paired, sensors_ref, high_ref, low_ref, values_ref, *refs):
@@ -230,57 +246,41 @@
                 out[k, span, lanes] = totals[k]
 
 
-def exchange(value, axis, pairs):
-    return lax.ppermute(value, axis, pairs)
-
-
-def shifted(value, n_dom, shift):
-    return exchange(value, "dom", [(d, (d + shift) % n_dom) for d in range(n_dom)])
-
-
-def swapped(value, n_ens):
-    return exchange(value, "ens", [(e, e ^ 1) for e in range(n_ens)])
-
-
 def is_paired(n_dom, n_ens):
     return n_dom == 4 and n_ens % 2 == 0
 
 
 def spread(values, n_dom, n_ens):
     if not is_paired(n_dom, n_ens):
-        return [values[0]] + [shifted(values[s], n_dom, s) for s in range(1, n_dom)]
+        return [values[0]] + [
+            lax.ppermute(values[s], "dom", [(d, (d + s) % n_dom) for d in range(n_dom)])
+            for s in range(1, n_dom)
+        ]
     here, near, far = values
     pairs = []
     for d in range(n_dom):
         for e in range(n_ens):
-            target = (d + (3 if e % 2 else 1)) % n_dom
-            pairs.append((d * n_ens + e, target * n_ens + e))
-    near = exchange(near, ("dom", "ens"), pairs)
-    far = shifted(far, n_dom, 2)
-    return [here, near, far, swapped(near, n_ens)]
-
-
-def gather_early(state, n_ens):
+            pairs.append((d * n_ens + e, (d ^ (3 if e % 2 else 1)) * n_ens + e))
+    near = lax.ppermute(near, ("dom", "ens"), pairs)
+    far = lax.ppermute(far, "dom", [(d, d ^ 2) for d in range(n_dom)])
+    other = lax.ppermute(near, "ens", [(e, e ^ 1) for e in range(n_ens)])
+    return [here, near, far, other]
+
+
+def gather_members(state, n_ens):
     pieces = {0: state}
-    if n_ens & (n_ens - 1) == 0:
-        for bit in {1, n_ens >> 1} - {0}:
-            pieces[bit] = exchange(state, "ens", [(e, e ^ bit) for e in range(n_ens)])
-    else:
+    if n_ens & (n_ens - 1):
         for shift in range(1, n_ens):
             pairs = [(e, (e + shift) % n_ens) for e in range(n_ens)]
-            pieces[shift] = exchange(state, "ens", pairs)
-    return pieces
-
-
-def gather_late(pieces, n_ens, after):
-    bit = n_ens >> 2
-    while bit and len(pieces) < n_ens:
+            pieces[shift] = lax.ppermute(state, "ens", pairs)
+        return [pieces[key] for key in range(n_ens)]
+    bit = n_ens >> 1
+    while bit:
         for key in list(pieces):
-            if key ^ bit not in pieces:
-                source = lax.optimization_barrier((pieces[key], after))[0]
-                pieces[key ^ bit] = exchange(source, "ens", [(e, e ^ bit) for e in range(n_ens)])
+            pairs = [(e, e ^ bit) for e in range(n_ens)]
+            pieces[key ^ bit] = lax.ppermute(pieces[key], "ens", pairs)
         bit >>= 1
-    return pieces
+    return [pieces[key] for key in range(n_ens)]
 
 
 def make_on_device(n_dom, n_ens):
@@ -290,11 +290,10 @@
     paired = is_paired(n_dom, n_ens)
     limit = VMEM_LIMIT if direct else None
 
-    def call(kernel, name, out_shape, operands, specs=None, scratch=()):
+    def call(kernel, out_shape, operands, specs=None, scratch=()):
         many = isinstance(out_shape, (list, tuple))
         return pl.pallas_call(
             kernel,
-            name=name,
             out_shape=out_shape,
             in_specs=specs or [vmem] * len(operands),
             out_specs=[vmem] * len(out_shape) if many else vmem,
@@ -306,31 +305,53 @@
         return jax.ShapeDtypeStruct(dims, dtype)
 
     def on_device(state, coords, owner_local, counts, obs_value, obs_weight):
-        local_members, elements, nodes = state.shape
+        local_members, _, nodes = state.shape
         slots = coords.shape[1]
         members = local_members * n_ens
         tile_shape = (8, 2 * CAP)
-        tiles = list(call(
+        hbm = [
+            pltpu.with_memory_space_constraint(value, pltpu.HBM)
+            for value in (
+                state,
+                counts,
+                coords,
+                owner_local[None],
+                obs_value[None],
+                obs_weight[None],
+            )
+        ]
+        own, *tiles = call(
             lambda *refs: pack_kernel(direct, paired, *refs),
-            "pack",
-            [shape(tile_shape)] * (3 if paired else n_dom)
-            if direct
-            else [shape((n_dom,) + tile_shape)],
-            [counts, coords, owner_local[None], obs_value[None], obs_weight[None]],
-            [smem] + [vmem] * 4,
-            [pltpu.VMEM((8, slots), F32)],
-        ))
+            [shape(state.shape)]
+            + (
+                [shape(tile_shape)] * (3 if paired else n_dom)
+                if direct
+                else [shape((n_dom,) + tile_shape)]
+            ),
+            hbm,
+            [pl.BlockSpec(memory_space=pltpu.HBM)] * len(hbm),
+            [
+                pltpu.SMEM(counts.shape, jnp.int32),
+                pltpu.VMEM(coords.shape, F32),
+                pltpu.VMEM((1, slots), jnp.int32),
+                pltpu.VMEM((1, slots), F32),
+                pltpu.VMEM((1, slots), F32),
+                pltpu.VMEM((8, slots), F32),
+                pltpu.SemaphoreType.DMA(()),
+                pltpu.SemaphoreType.DMA((5,)),
+            ],
+        )
         if direct:
             tiles = spread(tiles, n_dom, n_ens)
         else:
             moved = lax.all_to_all(tiles[0], "dom", split_axis=0, concat_axis=0, tiled=True)
             tiles = [moved[d] for d in range(n_dom)]
-        pieces = gather_early(state, n_ens)
+        pieces = gather_members(state, n_ens)
+        pieces[0] = own
         sensor_count = CAP * (n_dom + n_dom % 2)
         early = min(2, n_ens)
         sensors, high, low, values = call(
             lambda *refs: values_kernel(n_dom, *refs),
-            "values",
             [
                 shape((8, sensor_count)),
                 shape((nodes, sensor_count), BF16),
@@ -339,11 +360,8 @@
             ],
             list(tiles) + [pieces[key] for key in range(early)],
         )
-        pieces = gather_late(pieces, n_ens, sensors)
-        pieces = [pieces[key] for key in range(n_ens)]
         partial_sum = call(
             lambda *refs: cross_kernel(paired, *refs),
-            "cross",
             shape((members, members + 8)),
             [sensors, high, low, values] + pieces[early:],
         )
@@ -353,7 +371,6 @@
             sums = [lax.psum(partial_sum, "dom")]
         return call(
             lambda *refs: mix_kernel(paired, len(sums), *refs),
-            "mix",
             shape(state.shape),
             sums + pieces,
             None,
@@ -364,8 +381,9 @@
 
 
 def solution(mesh):
+    n_dom, n_ens = mesh.shape["dom"], mesh.shape["ens"]
     return jax.shard_map(
-        make_on_device(mesh.shape["dom"], mesh.shape["ens"]),
+        make_on_device(n_dom, n_ens),
         mesh=mesh,
         in_specs=(
             P("ens", ("groups", "dom"), None),

time: 26.6 us -> 28.2 us (1.060)
  starting transfers between devices: 10.5 us -> 13.5 us
  local copies, waits for them, and re-layouts: 2.99 us -> 0 us
  waiting for transfers between devices: 7.44 us -> 8.61 us
  Pallas kernels: 5.47 us -> 5.9 us
    ppermute x9, starting transfers between devices: 10.5 us -> 13.5 us  [the longest x2 5.98 us: spread(): far = lax.ppermute(far, 'dom', [(d, d ^ 2) for d in range(n_dom)])]
    unnamed x14 -> x0, local copies, waits for them, and re-layouts: 2.99 us -> none
    ppermute x9, waiting for transfers between devices: 7.44 us -> 8.61 us  [the longest x3 6.51 us: gather_members(): pieces[key ^ bit] = lax.ppermute(pieces[key], 'ens', pairs)]
    pallas_call x4, Pallas kernels: 5.47 us -> 5.9 us  [call(): pl.pallas_call(kernel, out_shape=out_shape, in_specs=specs or [vmem] * le...]
  transfers between devices with their start and end apart: 9 -> 9, of which waited for: 7 -> 3; matrix products, arithmetic and copies ran while one was open for 0% -> 0% of each run, Pallas kernels for 4% -> 5%
where the time goes in v3:
time: 28.2 us; the launch traced here: 28.1 us
  starting transfers between devices  13.5 us (48%)
  waiting for transfers between devices  8.61 us (31%)
  Pallas kernels  5.9 us (21%)
    ppermute x3, waiting for transfers between devices, gather_members(): pieces[key ^ bit] = lax.ppermute(pieces[key], 'ens', pairs)  6.51 us
    ppermute x2, starting transfers between devices, spread(): far = lax.ppermute(far, 'dom', [(d, d ^ 2) for d in range(n_dom)])  5.98 us
    pallas_call x4, Pallas kernels, call(): pl.pallas_call(kernel, out_shape=out_shape, in_specs=specs or [vmem] * le...  5.9 us
    ppermute x3, starting transfers between devices, gather_members(): pieces[key ^ bit] = lax.ppermute(pieces[key], 'ens', pairs)  2.97 us
    ppermute x2, starting transfers between devices, spread(): other = lax.ppermute(near, 'ens', [(e, e ^ 1) for e in range(n_ens)])  2.4 us
    ppermute x2, starting transfers between devices, spread(): near = lax.ppermute(near, ('dom', 'ens'), pairs)  2.18 us
    ppermute x2, waiting for transfers between devices, spread(): far = lax.ppermute(far, 'dom', [(d, d ^ 2) for d in range(n_dom)])  1.26 us
    ppermute x2, waiting for transfers between devices, spread(): other = lax.ppermute(near, 'ens', [(e, e ^ 1) for e in range(n_ens)])  0.83 us
  transfers between devices with their start and end apart: 9, of which 3 were waited for; matrix products, arithmetic and copies ran while one was open for 0% of the time, Pallas kernels for 5%

profile of v3, /device:TPU:0, one launch (start us, length us, event | category | flops | bytes accessed | tf_op | source)
XLA Modules:
  0.0 28.1 jit_solution(14654775091934901015)
XLA Ops:
  0.0 3.0 %collective-permute-start.4 = (f32[4,32,512]{2,1,0:T(8,128)}, f32[4,32,512]{2,1,0:T(8,128)S(1)}, u32[]{:S(2)}, u32[]{:S(2)}) collective-permute-start(f32[4,32,512]{2,1,0:T(8,128)} %refs_0_.1), channel_id=1, source_target_pairs={{0,2},{1,3},{2,0},{3,1},{4,6},{5,7},{6,4},{7,5},{8,10},{9,11},{10,... | collective-permute-start | bytes 786440 | tf_op jit(solution)/shard_map/ppermute | solution.py:281
  3.0 0.0 collective-permute-start.3
  3.0 6.5 %collective-permute-done.4.refs_4_.refs_6_ = f32[4,32,512]{2,1,0:T(8,128)S(1)} collective-permute-done((f32[4,32,512]{2,1,0:T(8,128)}, f32[4,32,512]{2,1,0:T(8,128)S(1)}, u32[]{:S(2)}, u32[]{:S(2)}) %collective-permute-start.4) | collective-permute-done | bytes 262176 | tf_op jit(solution)/shard_map/ppermute | solution.py:281
  9.5 0.0 collective-permute-start.5
  9.5 1.1 %shard_map.64 = (f32[4,32,512]{2,1,0:T(8,128)S(1)}, f32[8,128]{1,0:T(8,128)S(1)}, f32[8,128]{1,0:T(8,128)S(1)}, f32[8,128]{1,0:T(8,128)S(1)}) custom-call(f32[4,32,512]{2,1,0:T(8,128)} %refs_0_.1, s32[1,4]{1,0:T(1,128)} %refs_1_.1, f32[3,256]{1,0:T(4,128)} %refs_2_.1, s32[1,256]{1,0:T(1,128)} %bitcast.3, f32[1,256]{1,0:T(1,128)} %bitcast.4, f32[1,256]{1,0:T(1,128)} %bitcast.5), custom_call_target="tpu_custom_call" | custom-call | tf_op jit(solution)/shard_map/pallas_call | solution.py:295
  10.6 1.9 %collective-permute-start = (f32[8,128]{1,0:T(8,128)S(1)}, f32[8,128]{1,0:T(8,128)S(1)}, u32[]{:S(2)}, u32[]{:S(2)}) collective-permute-start(f32[8,128]{1,0:T(8,128)S(1)} %get-tuple-element.14), channel_id=1, source_target_pairs={{0,4},{1,13},{2,6},{3,15},{4,0},{5,9},{6,2},{7,11},{8,12},{9,5},{1... | collective-permute-start | bytes 12296 | tf_op jit(solution)/shard_map/ppermute | solution.py:264
  12.5 2.6 %collective-permute-start.1 = (f32[8,128]{1,0:T(8,128)S(1)}, f32[8,128]{1,0:T(8,128)S(1)}, u32[]{:S(2)}, u32[]{:S(2)}) collective-permute-start(f32[8,128]{1,0:T(8,128)S(1)} %get-tuple-element.15), channel_id=1, source_target_pairs={{0,8},{4,12},{8,0},{12,4},{1,9},{5,13},{9,1},{13,5},{2,10},{6,14},... | collective-permute-start | bytes 12296 | tf_op jit(solution)/shard_map/ppermute | solution.py:265
  15.0 0.0 collective-permute-done.refs_1_
  15.0 0.7 %collective-permute-start.2 = (f32[8,128]{1,0:T(8,128)S(1)}, f32[8,128]{1,0:T(8,128)S(1)}, u32[]{:S(2)}, u32[]{:S(2)}) collective-permute-start(f32[8,128]{1,0:T(8,128)S(1)} %collective-permute-done.refs_1_), channel_id=1, source_target_pairs={{0,1},{1,0},{2,3},{3,2},{4,5},{5,4},{6,7},{7,6},{8,9},{9,8},{10,11... | collective-permute-start | bytes 12296 | tf_op jit(solution)/shard_map/ppermute | solution.py:266
  15.7 1.3 %collective-permute-done.1.refs_2_ = f32[8,128]{1,0:T(8,128)S(1)} collective-permute-done((f32[8,128]{1,0:T(8,128)S(1)}, f32[8,128]{1,0:T(8,128)S(1)}, u32[]{:S(2)}, u32[]{:S(2)}) %collective-permute-start.1) | collective-permute-done | bytes 4128 | tf_op jit(solution)/shard_map/ppermute | solution.py:265
  17.0 0.0 collective-permute-done.2.refs_3_
  17.0 0.0 collective-permute-done.3.refs_5_
  17.0 0.4 %shard_map.65 = (f32[8,256]{1,0:T(8,128)S(1)}, bf16[512,256]{1,0:T(8,128)(2,1)S(1)}, bf16[512,256]{1,0:T(8,128)(2,1)S(1)}, f32[8,256]{1,0:T(8,128)S(1)}) custom-call(f32[8,128]{1,0:T(8,128)S(1)} %get-tuple-element.13.refs_0_, f32[8,128]{1,0:T(8,128)S(1)} %collective-permute-done.refs_1_, f32[8,128]{1,0:T(8,128)S(1)} %collective-permute-done.1.refs_2_, ...), custom_call_target="tpu_custom_call" | custom-call | tf_op jit(solution)/shard_map/pallas_call | solution.py:295
  17.4 0.0 collective-permute-done.5.refs_5_.refs_7_
  17.4 0.5 %shard_map.66.refs_0_ = f32[16,24]{1,0:T(8,128)S(1)} custom-call(f32[8,256]{1,0:T(8,128)S(1)} %get-tuple-element.17.refs_0_, bf16[512,256]{1,0:T(8,128)(2,1)S(1)} %get-tuple-element.18.refs_1_, bf16[512,256]{1,0:T(8,128)(2,1)S(1)} %get-tuple-element.19.refs_2_, f32[8,256]{1,0:T(8,128)S(1)} %get-tuple-element.20.refs_3_, ...), custom_call_target="tpu_custom_call" | custom-call | tf_op jit(solution)/shard_map/pallas_call | solution.py:295
  18.0 0.3 %collective-permute-start.6 = (f32[16,24]{1,0:T(8,128)S(1)}, f32[16,24]{1,0:T(8,128)S(1)}, u32[]{:S(2)}, u32[]{:S(2)}) collective-permute-start(f32[16,24]{1,0:T(8,128)S(1)} %shard_map.66.refs_0_), channel_id=1, source_target_pairs={{0,4},{1,13},{2,6},{3,15},{4,0},{5,9},{6,2},{7,11},{8,12},{9,5},{1... | collective-permute-start | bytes 4616 | tf_op jit(solution)/shard_map/ppermute | solution.py:264
  18.2 3.4 %collective-permute-start.7 = (f32[16,24]{1,0:T(8,128)S(1)}, f32[16,24]{1,0:T(8,128)S(1)}, u32[]{:S(2)}, u32[]{:S(2)}) collective-permute-start(f32[16,24]{1,0:T(8,128)S(1)} %shard_map.66.refs_0_), channel_id=1, source_target_pairs={{0,8},{4,12},{8,0},{12,4},{1,9},{5,13},{9,1},{13,5},{2,10},{6,14},... | collective-permute-start | bytes 4616 | tf_op jit(solution)/shard_map/ppermute | solution.py:265
  21.6 0.0 collective-permute-done.6.refs_1_
  21.6 1.7 %collective-permute-start.8 = (f32[16,24]{1,0:T(8,128)S(1)}, f32[16,24]{1,0:T(8,128)S(1)}, u32[]{:S(2)}, u32[]{:S(2)}) collective-permute-start(f32[16,24]{1,0:T(8,128)S(1)} %collective-permute-done.6.refs_1_), channel_id=1, source_target_pairs={{0,1},{1,0},{2,3},{3,2},{4,5},{5,4},{6,7},{7,6},{8,9},{9,8},{10,11... | collective-permute-start | bytes 4616 | tf_op jit(solution)/shard_map/ppermute | solution.py:266
  23.4 0.0 collective-permute-done.7.refs_2_
  23.4 0.8 %collective-permute-done.8.refs_3_ = f32[16,24]{1,0:T(8,128)S(1)} collective-permute-done((f32[16,24]{1,0:T(8,128)S(1)}, f32[16,24]{1,0:T(8,128)S(1)}, u32[]{:S(2)}, u32[]{:S(2)}) %collective-permute-start.8) | collective-permute-done | bytes 1568 | tf_op jit(solution)/shard_map/ppermute | solution.py:266
  24.2 3.9 %shard_map.67 = f32[4,32,512]{2,1,0:T(8,128)} custom-call(f32[16,24]{1,0:T(8,128)S(1)} %shard_map.66.refs_0_, f32[16,24]{1,0:T(8,128)S(1)} %collective-permute-done.6.refs_1_, f32[16,24]{1,0:T(8,128)S(1)} %collective-permute-done.7.refs_2_, f32[16,24]{1,0:T(8,128)S(1)} %collective-permute-done.8.refs_3_, f32[4,32,512]{2,1,0:T(8,128)S(1)} %get-tuple-element.16.refs_4_, ...), custom_call_target="tpu_custom_call" | custom-call | tf_op jit(solution)/shard_map/pallas_call | solution.py:295
Async XLA Ops:
  0.0 9.5 %collective-permute-start.4 = (f32[4,32,512]{2,1,0:T(8,128)}, f32[4,32,512]{2,1,0:T(8,128)S(1)}, u32[]{:S(2)}, u32[]{:S(2)}) collective-permute-start(f32[4,32,512]{2,1,0:T(8,128)} %refs_0_.1), channel_id=1, source_target_pairs={{0,2},{1,3},{2,0},{3,1},{4,6},{5,7},{6,4},{7,5},{8,10},{9,11},{10,... | collective-permute-start | bytes 786440 | tf_op jit(solution)/shard_map/ppermute | solution.py:281
  3.0 14.0 %collective-permute-start.3 = (f32[4,32,512]{2,1,0:T(8,128)}, f32[4,32,512]{2,1,0:T(8,128)S(1)}, u32[]{:S(2)}, u32[]{:S(2)}) collective-permute-start(f32[4,32,512]{2,1,0:T(8,128)} %refs_0_.1), channel_id=1, source_target_pairs={{0,1},{1,0},{2,3},{3,2},{4,5},{5,4},{6,7},{7,6},{8,9},{9,8},{10,11... | collective-permute-start | bytes 786440 | tf_op jit(solution)/shard_map/ppermute | solution.py:281
  9.5 7.9 %collective-permute-start.5 = (f32[4,32,512]{2,1,0:T(8,128)S(1)}, f32[4,32,512]{2,1,0:T(8,128)S(1)}, u32[]{:S(2)}, u32[]{:S(2)}) collective-permute-start(f32[4,32,512]{2,1,0:T(8,128)S(1)} %collective-permute-done.4.refs_4_.refs_6_), channel_id=1, source_target_pairs={{0,1},{1,0},{2,3},{3,2},{4,5},{5,4},{6,7},{7,6},{8,9},{9,8},{10,11... | collective-permute-start | bytes 786440 | tf_op jit(solution)/shard_map/ppermute | solution.py:281
  10.6 4.5 %collective-permute-start = (f32[8,128]{1,0:T(8,128)S(1)}, f32[8,128]{1,0:T(8,128)S(1)}, u32[]{:S(2)}, u32[]{:S(2)}) collective-permute-start(f32[8,128]{1,0:T(8,128)S(1)} %get-tuple-element.14), channel_id=1, source_target_pairs={{0,4},{1,13},{2,6},{3,15},{4,0},{5,9},{6,2},{7,11},{8,12},{9,5},{1... | collective-permute-start | bytes 12296 | tf_op jit(solution)/shard_map/ppermute | solution.py:264
  12.5 4.5 %collective-permute-start.1 = (f32[8,128]{1,0:T(8,128)S(1)}, f32[8,128]{1,0:T(8,128)S(1)}, u32[]{:S(2)}, u32[]{:S(2)}) collective-permute-start(f32[8,128]{1,0:T(8,128)S(1)} %get-tuple-element.15), channel_id=1, source_target_pairs={{0,8},{4,12},{8,0},{12,4},{1,9},{5,13},{9,1},{13,5},{2,10},{6,14},... | collective-permute-start | bytes 12296 | tf_op jit(solution)/shard_map/ppermute | solution.py:265
  15.0 1.9 %collective-permute-start.2 = (f32[8,128]{1,0:T(8,128)S(1)}, f32[8,128]{1,0:T(8,128)S(1)}, u32[]{:S(2)}, u32[]{:S(2)}) collective-permute-start(f32[8,128]{1,0:T(8,128)S(1)} %collective-permute-done.refs_1_), channel_id=1, source_target_pairs={{0,1},{1,0},{2,3},{3,2},{4,5},{5,4},{6,7},{7,6},{8,9},{9,8},{10,11... | collective-permute-start | bytes 12296 | tf_op jit(solution)/shard_map/ppermute | solution.py:266
  18.0 3.7 %collective-permute-start.6 = (f32[16,24]{1,0:T(8,128)S(1)}, f32[16,24]{1,0:T(8,128)S(1)}, u32[]{:S(2)}, u32[]{:S(2)}) collective-permute-start(f32[16,24]{1,0:T(8,128)S(1)} %shard_map.66.refs_0_), channel_id=1, source_target_pairs={{0,4},{1,13},{2,6},{3,15},{4,0},{5,9},{6,2},{7,11},{8,12},{9,5},{1... | collective-permute-start | bytes 4616 | tf_op jit(solution)/shard_map/ppermute | solution.py:264
  18.2 5.1 %collective-permute-start.7 = (f32[16,24]{1,0:T(8,128)S(1)}, f32[16,24]{1,0:T(8,128)S(1)}, u32[]{:S(2)}, u32[]{:S(2)}) collective-permute-start(f32[16,24]{1,0:T(8,128)S(1)} %shard_map.66.refs_0_), channel_id=1, source_target_pairs={{0,8},{4,12},{8,0},{12,4},{1,9},{5,13},{9,1},{13,5},{2,10},{6,14},... | collective-permute-start | bytes 4616 | tf_op jit(solution)/shard_map/ppermute | solution.py:265
  21.6 2.6 %collective-permute-start.8 = (f32[16,24]{1,0:T(8,128)S(1)}, f32[16,24]{1,0:T(8,128)S(1)}, u32[]{:S(2)}, u32[]{:S(2)}) collective-permute-start(f32[16,24]{1,0:T(8,128)S(1)} %collective-permute-done.6.refs_1_), channel_id=1, source_target_pairs={{0,1},{1,0},{2,3},{3,2},{4,5},{5,4},{6,7},{7,6},{8,9},{9,8},{10,11... | collective-permute-start | bytes 4616 | tf_op jit(solution)/shard_map/ppermute | solution.py:266

commit v4 on v3

--- a/solution.py
+++ b/solution.py
@@ -26,6 +26,7 @@
 BF16 = jnp.bfloat16
 DIRECT_DOM = 8
 VMEM_LIMIT = 8 * 1024 * 1024
+LANES = 128
 
 
 def lagrange_scale(index):
@@ -177,59 +178,102 @@
     mean_value = jnp.sum(values, axis=0, keepdims=True) * (1.0 / total)
     anomaly = values - mean_value
     weighted = anomaly * sensors[5:6, :]
-    innovation = sensors[4:5, :] - mean_value
-    pad = jnp.zeros((out.shape[1] - total - 1, values.shape[1]), F32)
-    right = jnp.concatenate([anomaly, innovation, pad], axis=0)
-    out[...] = lax.dot_general(
-        weighted,
-        right,
+    innovation = sensors[5:6, :] * (sensors[4:5, :] - mean_value)
+    copies = LANES // total
+    left = jnp.concatenate([weighted, jnp.broadcast_to(innovation, (8, innovation.shape[1]))], axis=0)
+    products = lax.dot_general(
+        left,
+        jnp.concatenate([anomaly] * copies, axis=0),
         (((1,), (1,)), ((), ())),
         precision=lax.Precision.HIGHEST,
         preferred_element_type=F32,
     )
+    own_row = lax.broadcasted_iota(jnp.int32, (copies, LANES), 0)
+    group = lax.broadcasted_iota(jnp.int32, (copies, LANES), 1) // total
+    for half in range(total // copies):
+        rows = products[half * copies : (half + 1) * copies, :]
+        out[half : half + 1, :] = jnp.sum(
+            jnp.where(own_row == group, rows, 0.0), axis=0, keepdims=True
+        )
+    out[2:3, :] = products[total : total + 1, :]
+    trace_part = jnp.sum(jnp.sum(weighted * anomaly, axis=0, keepdims=True), axis=1, keepdims=True)
+    out[3:4, :] = jnp.broadcast_to(trace_part, (1, LANES))
+    out[4:8, :] = jnp.zeros((4, LANES), F32)
+
+
+def lane_gather(value, lanes):
+    return jnp.take_along_axis(value, lanes, axis=1, mode="promise_in_bounds")
+
+
+def sublane_total(value):
+    for shift in (4, 2, 1):
+        value = value + pltpu.roll(value, shift, axis=0)
+    return value
 
 
 def mix_kernel(paired, sum_count, *refs):
-    sums, state_refs, out, splats = refs[:sum_count], refs[sum_count:-2], refs[-2], refs[-1]
-    highest = lax.Precision.HIGHEST
+    sums, state_refs = refs[:sum_count], refs[sum_count:-4]
+    out, staged, splats, sems = refs[-4:]
+    local_members, elements, nodes = out.shape
+    members = local_members * len(state_refs)
+    tile = (8, LANES)
+    sub = lax.broadcasted_iota(jnp.int32, tile, 0)
+    lane = lax.broadcasted_iota(jnp.int32, tile, 1)
+    left_lanes = [(lane // members) * members + (sub + 8 * g) for g in range(2)]
+    right_lanes = sub * members + lane % members
+    identity = [(lane // members + 8 * h == lane % members).astype(F32) for h in range(2)]
+
+    def as_left(matrix):
+        return [[lane_gather(matrix[h], left_lanes[g]) for g in range(2)] for h in range(2)]
+
+    def as_right(matrix):
+        return [lane_gather(matrix[g], right_lanes) for g in range(2)]
+
+    def product(left, right):
+        return [sublane_total(left[h][0] * right[0] + left[h][1] * right[1]) for h in range(2)]
+
     total_sum = sums[0][...]
     for ref in sums[1:]:
         total_sum = total_sum + ref[...]
-    local_members, elements, nodes = out.shape
-    members = local_members * len(state_refs)
-    row = lax.broadcasted_iota(jnp.int32, (members, members), 0)
-    col = lax.broadcasted_iota(jnp.int32, (members, members), 1)
-    identity = (row == col).astype(F32)
-    system = total_sum[:, :members] + (members - 1) / INFLATION * identity
-    project = total_sum[:, members : members + 1]
-    trace_value = jnp.sum(
-        jnp.sum(jnp.where(row == col, system, 0.0), axis=1, keepdims=True), axis=0, keepdims=True
-    )
-    iterate = system / trace_value
-    inverse_root = identity
+    trace_value = total_sum[3:4, :] + members * ((members - 1) / INFLATION)
+    scale = 1.0 / trace_value
+    project_row = jnp.broadcast_to(total_sum[2:3, :], tile)
+    project = [lane_gather(project_row, sub + 8 * g) for g in range(2)]
+    iterate = [
+        (total_sum[h : h + 1, :] + (members - 1) / INFLATION * identity[h]) * scale
+        for h in range(2)
+    ]
+    inverse_left = inverse_right = None
+    solved = None
     for sweep in range(NS_ITERS):
+        last = sweep + 1 == NS_ITERS
         if sweep:
-            product = jnp.dot(inverse_root, iterate, precision=highest)
+            step = product(inverse_left, as_right(iterate))
         else:
-            product = iterate
-        middle = 0.5 * (3.0 * identity - product)
-        if sweep + 1 < NS_ITERS:
-            iterate = jnp.dot(iterate, middle, precision=highest)
-        inverse_root = jnp.dot(middle, inverse_root, precision=highest) if sweep else middle
-    mean_weights = (
-        jnp.dot(inverse_root, jnp.dot(inverse_root, project, precision=highest), precision=highest)
-        / trace_value
-    )
-    transform = inverse_root * jnp.sqrt((members - 1) / trace_value) + mean_weights
-    mixing = transform - jnp.mean(transform, axis=0, keepdims=True) + 1.0 / members
+            step = iterate
+        middle = [1.5 * identity[h] - 0.5 * step[h] for h in range(2)]
+        if last:
+            middle_left = as_left(middle)
+            solved = product(middle_left, as_right(product(inverse_left, project)))
+            inverse_root = product(middle_left, inverse_right)
+            break
+        iterate = product(as_left(iterate), as_right(middle))
+        inverse_root = product(as_left(middle), inverse_right) if sweep else middle
+        inverse_left, inverse_right = as_left(inverse_root), as_right(inverse_root)
+    mean_weights = product(as_left(inverse_root), as_right(solved))
+    root_scale = jnp.sqrt((members - 1) * scale)
+    transform = [inverse_root[h] * root_scale + mean_weights[h] * scale for h in range(2)]
+    transform_right = as_right(transform)
+    column_mean = sublane_total(transform_right[0] + transform_right[1]) * (1.0 / members)
+    mixing = [transform[h] - column_mean + 1.0 / members for h in range(2)]
     odd = is_odd(paired)
-    if paired:
-        mixing = jnp.where(
-            odd == 1, mixing[:, local_members : 2 * local_members], mixing[:, :local_members]
-        )
-    for j in range(members):
-        for k in range(local_members):
-            splats[j * local_members + k] = jnp.broadcast_to(mixing[j : j + 1, k : k + 1], (8, 128))
+    for k in range(local_members):
+        lanes = sub * members + (k + local_members * odd)
+        for h in range(2):
+            column = lane_gather(mixing[h], lanes)
+            for i in range(8):
+                splats[(8 * h + i) * local_members + k] = jnp.broadcast_to(column[i : i + 1, :], tile)
+    copies = []
     for block in range(elements // 8):
         span = slice(8 * block, 8 * block + 8)
         for lane in range(nodes // 128):
@@ -243,7 +287,13 @@
                     term = splats[(place * local_members + member) * local_members + k] * value
                     totals[k] = term if totals[k] is None else totals[k] + term
             for k in range(local_members):
-                out[k, span, lanes] = totals[k]
+                staged[k, span, lanes] = totals[k]
+        place = pl.ds(8 * block, 8)
+        copy = pltpu.make_async_copy(staged.at[:, place], out.at[:, place], sems.at[block])
+        copy.start()
+        copies.append(copy)
+    for copy in copies:
+        copy.wait()
 
 
 def is_paired(n_dom, n_ens):
@@ -290,13 +340,13 @@
     paired = is_paired(n_dom, n_ens)
     limit = VMEM_LIMIT if direct else None
 
-    def call(kernel, out_shape, operands, specs=None, scratch=()):
+    def call(kernel, out_shape, operands, specs=None, scratch=(), out_spec=vmem):
         many = isinstance(out_shape, (list, tuple))
         return pl.pallas_call(
             kernel,
             out_shape=out_shape,
             in_specs=specs or [vmem] * len(operands),
-            out_specs=[vmem] * len(out_shape) if many else vmem,
+            out_specs=[out_spec] * len(out_shape) if many else out_spec,
             scratch_shapes=list(scratch),
             compiler_params=pltpu.CompilerParams(vmem_limit_bytes=limit),
         )(*operands)
@@ -305,7 +355,7 @@
         return jax.ShapeDtypeStruct(dims, dtype)
 
     def on_device(state, coords, owner_local, counts, obs_value, obs_weight):
-        local_members, _, nodes = state.shape
+        local_members, elements, nodes = state.shape
         slots = coords.shape[1]
         members = local_members * n_ens
         tile_shape = (8, 2 * CAP)
@@ -362,7 +412,7 @@
         )
         partial_sum = call(
             lambda *refs: cross_kernel(paired, *refs),
-            shape((members, members + 8)),
+            shape((8, LANES)),
             [sensors, high, low, values] + pieces[early:],
         )
         if direct:
@@ -374,7 +424,12 @@
             shape(state.shape),
             sums + pieces,
             None,
-            [pltpu.VMEM((members * local_members, 8, 128), F32)],
+            [
+                pltpu.VMEM(state.shape, F32),
+                pltpu.VMEM((members * local_members, 8, 128), F32),
+                pltpu.SemaphoreType.DMA((elements // 8,)),
+            ],
+            pl.BlockSpec(memory_space=pltpu.HBM),
         )
 
     return on_device

time: 28.2 us -> 27 us (0.957)
  Pallas kernels: 5.9 us -> 4.75 us
    pallas_call x4, Pallas kernels: 5.9 us -> 4.75 us  [call(): pl.pallas_call(kernel, out_shape=out_shape, in_specs=specs or [vmem] * le...]
  transfers between devices with their start and end apart: 9 -> 9, of which waited for: 3 -> 3; matrix products, arithmetic and copies ran while one was open for 0% -> 0% of each run, Pallas kernels for 5% -> 6%
where the time goes in v4:
time: 27 us; the launch traced here: 26.9 us
  starting transfers between devices  13.5 us (50%)
  waiting for transfers between devices  8.6 us (32%)
  Pallas kernels  4.75 us (18%)
    ppermute x3, waiting for transfers between devices, gather_members(): pieces[key ^ bit] = lax.ppermute(pieces[key], 'ens', pairs)  6.51 us
    ppermute x2, starting transfers between devices, spread(): far = lax.ppermute(far, 'dom', [(d, d ^ 2) for d in range(n_dom)])  5.99 us
    pallas_call x4, Pallas kernels, call(): pl.pallas_call(kernel, out_shape=out_shape, in_specs=specs or [vmem] * le...  4.75 us
    ppermute x3, starting transfers between devices, gather_members(): pieces[key ^ bit] = lax.ppermute(pieces[key], 'ens', pairs)  2.97 us
    ppermute x2, starting transfers between devices, spread(): other = lax.ppermute(near, 'ens', [(e, e ^ 1) for e in range(n_ens)])  2.35 us
    ppermute x2, starting transfers between devices, spread(): near = lax.ppermute(near, ('dom', 'ens'), pairs)  2.19 us
    ppermute x2, waiting for transfers between devices, spread(): far = lax.ppermute(far, 'dom', [(d, d ^ 2) for d in range(n_dom)])  1.26 us
    ppermute x2, waiting for transfers between devices, spread(): other = lax.ppermute(near, 'ens', [(e, e ^ 1) for e in range(n_ens)])  0.82 us
  transfers between devices with their start and end apart: 9, of which 3 were waited for; matrix products, arithmetic and copies ran while one was open for 0% of the time, Pallas kernels for 6%

profile of v4, /device:TPU:0, one launch (start us, length us, event | category | flops | bytes accessed | tf_op | source)
XLA Modules:
  0.0 26.9 jit_solution(7413702664708703194)
XLA Ops:
  0.0 3.0 %collective-permute-start.4 = (f32[4,32,512]{2,1,0:T(8,128)}, f32[4,32,512]{2,1,0:T(8,128)S(1)}, u32[]{:S(2)}, u32[]{:S(2)}) collective-permute-start(f32[4,32,512]{2,1,0:T(8,128)} %refs_0_.1), channel_id=1, source_target_pairs={{0,2},{1,3},{2,0},{3,1},{4,6},{5,7},{6,4},{7,5},{8,10},{9,11},{10,... | collective-permute-start | bytes 786440 | tf_op jit(solution)/shard_map/ppermute | solution.py:331
  3.0 0.0 collective-permute-start.3
  3.0 6.5 %collective-permute-done.4.refs_4_.refs_6_ = f32[4,32,512]{2,1,0:T(8,128)S(1)} collective-permute-done((f32[4,32,512]{2,1,0:T(8,128)}, f32[4,32,512]{2,1,0:T(8,128)S(1)}, u32[]{:S(2)}, u32[]{:S(2)}) %collective-permute-start.4) | collective-permute-done | bytes 262176 | tf_op jit(solution)/shard_map/ppermute | solution.py:331
  9.5 0.0 collective-permute-start.5
  9.5 1.1 %shard_map.64 = (f32[4,32,512]{2,1,0:T(8,128)S(1)}, f32[8,128]{1,0:T(8,128)S(1)}, f32[8,128]{1,0:T(8,128)S(1)}, f32[8,128]{1,0:T(8,128)S(1)}) custom-call(f32[4,32,512]{2,1,0:T(8,128)} %refs_0_.1, s32[1,4]{1,0:T(1,128)} %refs_1_.1, f32[3,256]{1,0:T(4,128)} %refs_2_.1, s32[1,256]{1,0:T(1,128)} %bitcast.3, f32[1,256]{1,0:T(1,128)} %bitcast.4, f32[1,256]{1,0:T(1,128)} %bitcast.5), custom_call_target="tpu_custom_call" | custom-call | tf_op jit(solution)/shard_map/pallas_call | solution.py:345
  10.6 1.9 %collective-permute-start = (f32[8,128]{1,0:T(8,128)S(1)}, f32[8,128]{1,0:T(8,128)S(1)}, u32[]{:S(2)}, u32[]{:S(2)}) collective-permute-start(f32[8,128]{1,0:T(8,128)S(1)} %get-tuple-element.14), channel_id=1, source_target_pairs={{0,4},{1,13},{2,6},{3,15},{4,0},{5,9},{6,2},{7,11},{8,12},{9,5},{1... | collective-permute-start | bytes 12296 | tf_op jit(solution)/shard_map/ppermute | solution.py:314
  12.5 2.6 %collective-permute-start.1 = (f32[8,128]{1,0:T(8,128)S(1)}, f32[8,128]{1,0:T(8,128)S(1)}, u32[]{:S(2)}, u32[]{:S(2)}) collective-permute-start(f32[8,128]{1,0:T(8,128)S(1)} %get-tuple-element.15), channel_id=1, source_target_pairs={{0,8},{4,12},{8,0},{12,4},{1,9},{5,13},{9,1},{13,5},{2,10},{6,14},... | collective-permute-start | bytes 12296 | tf_op jit(solution)/shard_map/ppermute | solution.py:315
  15.0 0.0 collective-permute-done.refs_1_
  15.0 0.7 %collective-permute-start.2 = (f32[8,128]{1,0:T(8,128)S(1)}, f32[8,128]{1,0:T(8,128)S(1)}, u32[]{:S(2)}, u32[]{:S(2)}) collective-permute-start(f32[8,128]{1,0:T(8,128)S(1)} %collective-permute-done.refs_1_), channel_id=1, source_target_pairs={{0,1},{1,0},{2,3},{3,2},{4,5},{5,4},{6,7},{7,6},{8,9},{9,8},{10,11... | collective-permute-start | bytes 12296 | tf_op jit(solution)/shard_map/ppermute | solution.py:316
  15.7 1.3 %collective-permute-done.1.refs_2_ = f32[8,128]{1,0:T(8,128)S(1)} collective-permute-done((f32[8,128]{1,0:T(8,128)S(1)}, f32[8,128]{1,0:T(8,128)S(1)}, u32[]{:S(2)}, u32[]{:S(2)}) %collective-permute-start.1) | collective-permute-done | bytes 4128 | tf_op jit(solution)/shard_map/ppermute | solution.py:315
  17.0 0.0 collective-permute-done.2.refs_3_
  17.0 0.0 collective-permute-done.3.refs_5_
  17.0 0.4 %shard_map.65 = (f32[8,256]{1,0:T(8,128)S(1)}, bf16[512,256]{1,0:T(8,128)(2,1)S(1)}, bf16[512,256]{1,0:T(8,128)(2,1)S(1)}, f32[8,256]{1,0:T(8,128)S(1)}) custom-call(f32[8,128]{1,0:T(8,128)S(1)} %get-tuple-element.13.refs_0_, f32[8,128]{1,0:T(8,128)S(1)} %collective-permute-done.refs_1_, f32[8,128]{1,0:T(8,128)S(1)} %collective-permute-done.1.refs_2_, ...), custom_call_target="tpu_custom_call" | custom-call | tf_op jit(solution)/shard_map/pallas_call | solution.py:345
  17.4 0.0 collective-permute-done.5.refs_5_.refs_7_
  17.4 0.8 %shard_map.66.refs_0_ = f32[8,128]{1,0:T(8,128)S(1)} custom-call(f32[8,256]{1,0:T(8,128)S(1)} %get-tuple-element.17.refs_0_, bf16[512,256]{1,0:T(8,128)(2,1)S(1)} %get-tuple-element.18.refs_1_, bf16[512,256]{1,0:T(8,128)(2,1)S(1)} %get-tuple-element.19.refs_2_, f32[8,256]{1,0:T(8,128)S(1)} %get-tuple-element.20.refs_3_, ...), custom_call_target="tpu_custom_call" | custom-call | tf_op jit(solution)/shard_map/pallas_call | solution.py:345
  18.2 0.3 %collective-permute-start.6 = (f32[8,128]{1,0:T(8,128)S(1)}, f32[8,128]{1,0:T(8,128)S(1)}, u32[]{:S(2)}, u32[]{:S(2)}) collective-permute-start(f32[8,128]{1,0:T(8,128)S(1)} %shard_map.66.refs_0_), channel_id=1, source_target_pairs={{0,4},{1,13},{2,6},{3,15},{4,0},{5,9},{6,2},{7,11},{8,12},{9,5},{1... | collective-permute-start | bytes 12296 | tf_op jit(solution)/shard_map/ppermute | solution.py:314
  18.5 3.4 %collective-permute-start.7 = (f32[8,128]{1,0:T(8,128)S(1)}, f32[8,128]{1,0:T(8,128)S(1)}, u32[]{:S(2)}, u32[]{:S(2)}) collective-permute-start(f32[8,128]{1,0:T(8,128)S(1)} %shard_map.66.refs_0_), channel_id=1, source_target_pairs={{0,8},{4,12},{8,0},{12,4},{1,9},{5,13},{9,1},{13,5},{2,10},{6,14},... | collective-permute-start | bytes 12296 | tf_op jit(solution)/shard_map/ppermute | solution.py:315
  21.9 0.0 collective-permute-done.6.refs_1_
  21.9 1.7 %collective-permute-start.8 = (f32[8,128]{1,0:T(8,128)S(1)}, f32[8,128]{1,0:T(8,128)S(1)}, u32[]{:S(2)}, u32[]{:S(2)}) collective-permute-start(f32[8,128]{1,0:T(8,128)S(1)} %collective-permute-done.6.refs_1_), channel_id=1, source_target_pairs={{0,1},{1,0},{2,3},{3,2},{4,5},{5,4},{6,7},{7,6},{8,9},{9,8},{10,11... | collective-permute-start | bytes 12296 | tf_op jit(solution)/shard_map/ppermute | solution.py:316
  23.6 0.0 collective-permute-done.7.refs_2_
  23.6 0.8 %collective-permute-done.8.refs_3_ = f32[8,128]{1,0:T(8,128)S(1)} collective-permute-done((f32[8,128]{1,0:T(8,128)S(1)}, f32[8,128]{1,0:T(8,128)S(1)}, u32[]{:S(2)}, u32[]{:S(2)}) %collective-permute-start.8) | collective-permute-done | bytes 4128 | tf_op jit(solution)/shard_map/ppermute | solution.py:316
  24.4 2.5 %shard_map.67 = f32[4,32,512]{2,1,0:T(8,128)} custom-call(f32[8,128]{1,0:T(8,128)S(1)} %shard_map.66.refs_0_, f32[8,128]{1,0:T(8,128)S(1)} %collective-permute-done.6.refs_1_, f32[8,128]{1,0:T(8,128)S(1)} %collective-permute-done.7.refs_2_, f32[8,128]{1,0:T(8,128)S(1)} %collective-permute-done.8.refs_3_, f32[4,32,512]{2,1,0:T(8,128)S(1)} %get-tuple-element.16.refs_4_, ...), custom_call_target="tpu_custom_call" | custom-call | tf_op jit(solution)/shard_map/pallas_call | solution.py:345
Async XLA Ops:
  0.0 9.5 %collective-permute-start.4 = (f32[4,32,512]{2,1,0:T(8,128)}, f32[4,32,512]{2,1,0:T(8,128)S(1)}, u32[]{:S(2)}, u32[]{:S(2)}) collective-permute-start(f32[4,32,512]{2,1,0:T(8,128)} %refs_0_.1), channel_id=1, source_target_pairs={{0,2},{1,3},{2,0},{3,1},{4,6},{5,7},{6,4},{7,5},{8,10},{9,11},{10,... | collective-permute-start | bytes 786440 | tf_op jit(solution)/shard_map/ppermute | solution.py:331
  3.0 14.0 %collective-permute-start.3 = (f32[4,32,512]{2,1,0:T(8,128)}, f32[4,32,512]{2,1,0:T(8,128)S(1)}, u32[]{:S(2)}, u32[]{:S(2)}) collective-permute-start(f32[4,32,512]{2,1,0:T(8,128)} %refs_0_.1), channel_id=1, source_target_pairs={{0,1},{1,0},{2,3},{3,2},{4,5},{5,4},{6,7},{7,6},{8,9},{9,8},{10,11... | collective-permute-start | bytes 786440 | tf_op jit(solution)/shard_map/ppermute | solution.py:331
  9.5 7.9 %collective-permute-start.5 = (f32[4,32,512]{2,1,0:T(8,128)S(1)}, f32[4,32,512]{2,1,0:T(8,128)S(1)}, u32[]{:S(2)}, u32[]{:S(2)}) collective-permute-start(f32[4,32,512]{2,1,0:T(8,128)S(1)} %collective-permute-done.4.refs_4_.refs_6_), channel_id=1, source_target_pairs={{0,1},{1,0},{2,3},{3,2},{4,5},{5,4},{6,7},{7,6},{8,9},{9,8},{10,11... | collective-permute-start | bytes 786440 | tf_op jit(solution)/shard_map/ppermute | solution.py:331
  10.6 4.5 %collective-permute-start = (f32[8,128]{1,0:T(8,128)S(1)}, f32[8,128]{1,0:T(8,128)S(1)}, u32[]{:S(2)}, u32[]{:S(2)}) collective-permute-start(f32[8,128]{1,0:T(8,128)S(1)} %get-tuple-element.14), channel_id=1, source_target_pairs={{0,4},{1,13},{2,6},{3,15},{4,0},{5,9},{6,2},{7,11},{8,12},{9,5},{1... | collective-permute-start | bytes 12296 | tf_op jit(solution)/shard_map/ppermute | solution.py:314
  12.5 4.5 %collective-permute-start.1 = (f32[8,128]{1,0:T(8,128)S(1)}, f32[8,128]{1,0:T(8,128)S(1)}, u32[]{:S(2)}, u32[]{:S(2)}) collective-permute-start(f32[8,128]{1,0:T(8,128)S(1)} %get-tuple-element.15), channel_id=1, source_target_pairs={{0,8},{4,12},{8,0},{12,4},{1,9},{5,13},{9,1},{13,5},{2,10},{6,14},... | collective-permute-start | bytes 12296 | tf_op jit(solution)/shard_map/ppermute | solution.py:315
  15.0 1.9 %collective-permute-start.2 = (f32[8,128]{1,0:T(8,128)S(1)}, f32[8,128]{1,0:T(8,128)S(1)}, u32[]{:S(2)}, u32[]{:S(2)}) collective-permute-start(f32[8,128]{1,0:T(8,128)S(1)} %collective-permute-done.refs_1_), channel_id=1, source_target_pairs={{0,1},{1,0},{2,3},{3,2},{4,5},{5,4},{6,7},{7,6},{8,9},{9,8},{10,11... | collective-permute-start | bytes 12296 | tf_op jit(solution)/shard_map/ppermute | solution.py:316
  18.2 3.7 %collective-permute-start.6 = (f32[8,128]{1,0:T(8,128)S(1)}, f32[8,128]{1,0:T(8,128)S(1)}, u32[]{:S(2)}, u32[]{:S(2)}) collective-permute-start(f32[8,128]{1,0:T(8,128)S(1)} %shard_map.66.refs_0_), channel_id=1, source_target_pairs={{0,4},{1,13},{2,6},{3,15},{4,0},{5,9},{6,2},{7,11},{8,12},{9,5},{1... | collective-permute-start | bytes 12296 | tf_op jit(solution)/shard_map/ppermute | solution.py:314
  18.5 5.1 %collective-permute-start.7 = (f32[8,128]{1,0:T(8,128)S(1)}, f32[8,128]{1,0:T(8,128)S(1)}, u32[]{:S(2)}, u32[]{:S(2)}) collective-permute-start(f32[8,128]{1,0:T(8,128)S(1)} %shard_map.66.refs_0_), channel_id=1, source_target_pairs={{0,8},{4,12},{8,0},{12,4},{1,9},{5,13},{9,1},{13,5},{2,10},{6,14},... | collective-permute-start | bytes 12296 | tf_op jit(solution)/shard_map/ppermute | solution.py:315
  21.9 2.5 %collective-permute-start.8 = (f32[8,128]{1,0:T(8,128)S(1)}, f32[8,128]{1,0:T(8,128)S(1)}, u32[]{:S(2)}, u32[]{:S(2)}) collective-permute-start(f32[8,128]{1,0:T(8,128)S(1)} %collective-permute-done.6.refs_1_), channel_id=1, source_target_pairs={{0,1},{1,0},{2,3},{3,2},{4,5},{5,4},{6,7},{7,6},{8,9},{9,8},{10,11... | collective-permute-start | bytes 12296 | tf_op jit(solution)/shard_map/ppermute | solution.py:316

commit v5 on v4

--- a/solution.py
+++ b/solution.py
@@ -27,6 +27,8 @@
 DIRECT_DOM = 8
 VMEM_LIMIT = 8 * 1024 * 1024
 LANES = 128
+PROJECT_LANES = 8
+TRACE_LANE = 64
 
 
 def lagrange_scale(index):
@@ -58,10 +60,9 @@
     return lax.rem(lax.axis_index("ens"), 2) if paired else 0
 
 
-def pack_kernel(direct, paired, state, counts, coords, owner, obs, weight, *rest):
-    own, outs = rest[0], rest[1:-8]
-    count_box, coord_box, owner_box, obs_box, weight_box, block, state_sem, sems = rest[-8:]
-    state_copy = pltpu.make_async_copy(state, own, state_sem)
+def pack_kernel(direct, paired, counts, coords, owner, obs, weight, *rest):
+    outs = rest[:-7]
+    count_box, coord_box, owner_box, obs_box, weight_box, block, sems = rest[-7:]
     pairs = zip(
         (counts, coords, owner, obs, weight), (count_box, coord_box, owner_box, obs_box, weight_box)
     )
@@ -71,7 +72,6 @@
     ]
     for copy in copies:
         copy.start()
-    state_copy.start()
     n_dom = counts.shape[1]
     slots = coords.shape[1]
     here = lax.axis_index("dom")
@@ -108,28 +108,30 @@
             return carry
 
         lax.fori_loop(0, n_dom, step, 0)
-    state_copy.wait()
-
-
-def pick(state_rows, members, elements, high, low, chosen):
-    rows_high, rows_low = split(state_rows)
+
+
+def pick(refs, sensors, high, low):
+    members, elements, nodes = refs[0].shape
+    rows = jnp.concatenate([ref[...].reshape(members * elements, nodes) for ref in refs], axis=0)
+    rows_high, rows_low = split(rows)
+    both = jnp.dot(
+        jnp.concatenate([rows_high, rows_low], axis=0), high, preferred_element_type=F32
+    )
     partial = (
-        jnp.dot(rows_high, high, preferred_element_type=F32)
-        + jnp.dot(rows_low, high, preferred_element_type=F32)
+        both[: rows.shape[0]]
+        + both[rows.shape[0] :]
         + jnp.dot(rows_high, low, preferred_element_type=F32)
     )
-    partial = partial.reshape(members, elements, partial.shape[1])
-    return jnp.sum(jnp.where(chosen[None], partial, 0.0), axis=1)
-
-
-def chosen_mask(sensors, elements):
     ids = lax.broadcasted_iota(jnp.int32, (elements, sensors.shape[1]), 0).astype(F32)
-    return ids == sensors[3:4, :]
+    partial = partial.reshape(len(refs) * members, elements, partial.shape[1])
+    return jnp.sum(jnp.where((ids == sensors[3:4, :])[None], partial, 0.0), axis=1)
 
 
 def values_kernel(tile_count, *refs):
-    tiles, state_refs = refs[:tile_count], refs[tile_count:-4]
-    sensors_out, high_out, low_out, values_out = refs[-4:]
+    tiles, state, state_refs = refs[:tile_count], refs[tile_count], refs[tile_count + 1 : -6]
+    sensors_out, high_out, low_out, values_out, own, sem = refs[-6:]
+    copy = pltpu.make_async_copy(state, own, sem)
+    copy.start()
     pairs = []
     for first in range(0, tile_count, 2):
         pair = tiles[first][...]
@@ -148,57 +150,47 @@
             base = ORDER * ORDER * t + ORDER * s
             high_out[base : base + 2 * ORDER, :] = high
             low_out[base : base + 2 * ORDER, :] = low
-    high, low = high_out[...], low_out[...]
-    for index, ref in enumerate(state_refs):
-        members, elements, nodes = ref.shape
-        chosen = chosen_mask(sensors, elements)
-        rows = ref[...].reshape(members * elements, nodes)
-        values_out[index * members : (index + 1) * members, :] = pick(
-            rows, members, elements, high, low, chosen
-        )
+    members = own.shape[0]
+    if state_refs:
+        values_out[members:, :] = pick(state_refs, sensors, high_out[...], low_out[...])
+    copy.wait()
+    values_out[:members, :] = pick([own], sensors, high_out[...], low_out[...])
 
 
 def cross_kernel(paired, sensors_ref, high_ref, low_ref, values_ref, *refs):
     state_refs, out = refs[:-1], refs[-1]
-    high, low = high_ref[...], low_ref[...]
     sensors = sensors_ref[...]
-    parts = [values_ref[...]]
-    for ref in state_refs:
-        members, elements, nodes = ref.shape
-        chosen = chosen_mask(sensors, elements)
-        rows = ref[...].reshape(members * elements, nodes)
-        parts.append(pick(rows, members, elements, high, low, chosen))
-    values = jnp.concatenate(parts, axis=0)
+    values = jnp.concatenate(
+        [values_ref[...], pick(state_refs, sensors, high_ref[...], low_ref[...])], axis=0
+    )
     total = values.shape[0]
     if paired:
-        size = total // (len(parts) + 1)
+        size = state_refs[0].shape[0]
         blocks = [values[first : first + size] for first in range(0, total, size)]
         turned = [blocks[index ^ 1] for index in range(len(blocks))]
         values = jnp.where(is_odd(paired) == 1, jnp.concatenate(turned, axis=0), values)
     mean_value = jnp.sum(values, axis=0, keepdims=True) * (1.0 / total)
     anomaly = values - mean_value
     weighted = anomaly * sensors[5:6, :]
-    innovation = sensors[5:6, :] * (sensors[4:5, :] - mean_value)
-    copies = LANES // total
-    left = jnp.concatenate([weighted, jnp.broadcast_to(innovation, (8, innovation.shape[1]))], axis=0)
-    products = lax.dot_general(
-        left,
-        jnp.concatenate([anomaly] * copies, axis=0),
-        (((1,), (1,)), ((), ())),
-        precision=lax.Precision.HIGHEST,
+    innovation = sensors[4:5, :] - mean_value
+    pad = jnp.zeros((PROJECT_LANES - 1, values.shape[1]), F32)
+    right = jnp.concatenate([anomaly, innovation, pad], axis=0)
+    left_high, left_low = split(weighted)
+    right_high, right_low = split(right)
+    across = (((1,), (1,)), ((), ()))
+    both = lax.dot_general(
+        jnp.concatenate([left_high, left_low], axis=0),
+        right_high,
+        across,
         preferred_element_type=F32,
     )
-    own_row = lax.broadcasted_iota(jnp.int32, (copies, LANES), 0)
-    group = lax.broadcasted_iota(jnp.int32, (copies, LANES), 1) // total
-    for half in range(total // copies):
-        rows = products[half * copies : (half + 1) * copies, :]
-        out[half : half + 1, :] = jnp.sum(
-            jnp.where(own_row == group, rows, 0.0), axis=0, keepdims=True
-        )
-    out[2:3, :] = products[total : total + 1, :]
+    out[:, : total + PROJECT_LANES] = (
+        both[:total]
+        + both[total:]
+        + lax.dot_general(left_high, right_low, across, preferred_element_type=F32)
+    )
     trace_part = jnp.sum(jnp.sum(weighted * anomaly, axis=0, keepdims=True), axis=1, keepdims=True)
-    out[3:4, :] = jnp.broadcast_to(trace_part, (1, LANES))
-    out[4:8, :] = jnp.zeros((4, LANES), F32)
+    out[:, TRACE_LANE:] = jnp.broadcast_to(trace_part, (total, LANES - TRACE_LANE))
 
 
 def lane_gather(value, lanes):
@@ -235,31 +227,38 @@
     total_sum = sums[0][...]
     for ref in sums[1:]:
         total_sum = total_sum + ref[...]
-    trace_value = total_sum[3:4, :] + members * ((members - 1) / INFLATION)
-    scale = 1.0 / trace_value
-    project_row = jnp.broadcast_to(total_sum[2:3, :], tile)
-    project = [lane_gather(project_row, sub + 8 * g) for g in range(2)]
-    iterate = [
-        (total_sum[h : h + 1, :] + (members - 1) / INFLATION * identity[h]) * scale
+    rows = [total_sum[8 * g : 8 * g + 8, :] for g in range(2)]
+    project = [lane_gather(rows[g], jnp.full(tile, members, jnp.int32)) for g in range(2)]
+    trace_value = lane_gather(rows[0], jnp.full(tile, TRACE_LANE, jnp.int32))
+    scale = 1.0 / (trace_value + members * ((members - 1) / INFLATION))
+    diagonal = (members - 1) / INFLATION
+    unit_left = [[(lane // members + 8 * h == sub + 8 * g).astype(F32) for g in range(2)] for h in range(2)]
+    unit_right = [(lane % members == sub + 8 * g).astype(F32) for g in range(2)]
+    system_left = [
+        [
+            (lane_gather(rows[g], lane // members + 8 * h) + diagonal * unit_left[h][g]) * scale
+            for g in range(2)
+        ]
         for h in range(2)
     ]
-    inverse_left = inverse_right = None
-    solved = None
-    for sweep in range(NS_ITERS):
-        last = sweep + 1 == NS_ITERS
-        if sweep:
-            step = product(inverse_left, as_right(iterate))
+    system_right = [
+        (lane_gather(rows[g], lane % members) + diagonal * unit_right[g]) * scale for g in range(2)
+    ]
+    inverse_left = [
+        [1.5 * unit_left[h][g] - 0.5 * system_left[h][g] for g in range(2)] for h in range(2)
+    ]
+    inverse_right = [1.5 * unit_right[g] - 0.5 * system_right[g] for g in range(2)]
+    iterate = product(system_left, inverse_right)
+    for sweep in range(1, NS_ITERS):
+        step = product(inverse_left, as_right(iterate))
+        middle = [1.5 * identity[h] - 0.5 * step[h] for h in range(2)]
+        middle_left = as_left(middle)
+        inverse_root = product(middle_left, inverse_right)
+        if sweep + 1 < NS_ITERS:
+            iterate = product(as_left(iterate), as_right(middle))
+            inverse_left, inverse_right = as_left(inverse_root), as_right(inverse_root)
         else:
-            step = iterate
-        middle = [1.5 * identity[h] - 0.5 * step[h] for h in range(2)]
-        if last:
-            middle_left = as_left(middle)
             solved = product(middle_left, as_right(product(inverse_left, project)))
-            inverse_root = product(middle_left, inverse_right)
-            break
-        iterate = product(as_left(iterate), as_right(middle))
-        inverse_root = product(as_left(middle), inverse_right) if sweep else middle
-        inverse_left, inverse_right = as_left(inverse_root), as_right(inverse_root)
     mean_weights = product(as_left(inverse_root), as_right(solved))
     root_scale = jnp.sqrt((members - 1) * scale)
     transform = [inverse_root[h] * root_scale + mean_weights[h] * scale for h in range(2)]
@@ -335,7 +334,7 @@
 
 def make_on_device(n_dom, n_ens):
     vmem = pl.BlockSpec(memory_space=pltpu.VMEM)
-    smem = pl.BlockSpec(memory_space=pltpu.SMEM)
+    hbm = pl.BlockSpec(memory_space=pltpu.HBM)
     direct = n_dom <= DIRECT_DOM
     paired = is_paired(n_dom, n_ens)
     limit = VMEM_LIMIT if direct else None
@@ -351,6 +350,9 @@
             compiler_params=pltpu.CompilerParams(vmem_limit_bytes=limit),
         )(*operands)
 
+    def in_hbm(value):
+        return pltpu.with_memory_space_constraint(value, pltpu.HBM)
+
     def shape(dims, dtype=F32):
         return jax.ShapeDtypeStruct(dims, dtype)
 
@@ -359,27 +361,14 @@
         slots = coords.shape[1]
         members = local_members * n_ens
         tile_shape = (8, 2 * CAP)
-        hbm = [
-            pltpu.with_memory_space_constraint(value, pltpu.HBM)
-            for value in (
-                state,
-                counts,
-                coords,
-                owner_local[None],
-                obs_value[None],
-                obs_weight[None],
-            )
-        ]
-        own, *tiles = call(
+        inputs = [counts, coords, owner_local[None], obs_value[None], obs_weight[None]]
+        tiles = call(
             lambda *refs: pack_kernel(direct, paired, *refs),
-            [shape(state.shape)]
-            + (
-                [shape(tile_shape)] * (3 if paired else n_dom)
-                if direct
-                else [shape((n_dom,) + tile_shape)]
-            ),
-            hbm,
-            [pl.BlockSpec(memory_space=pltpu.HBM)] * len(hbm),
+            [shape(tile_shape)] * (3 if paired else n_dom)
+            if direct
+            else [shape((n_dom,) + tile_shape)],
+            [in_hbm(value) for value in inputs],
+            [hbm] * len(inputs),
             [
                 pltpu.SMEM(counts.shape, jnp.int32),
                 pltpu.VMEM(coords.shape, F32),
@@ -387,7 +376,6 @@
                 pltpu.VMEM((1, slots), F32),
                 pltpu.VMEM((1, slots), F32),
                 pltpu.VMEM((8, slots), F32),
-                pltpu.SemaphoreType.DMA(()),
                 pltpu.SemaphoreType.DMA((5,)),
             ],
         )
@@ -397,22 +385,24 @@
             moved = lax.all_to_all(tiles[0], "dom", split_axis=0, concat_axis=0, tiled=True)
             tiles = [moved[d] for d in range(n_dom)]
         pieces = gather_members(state, n_ens)
-        pieces[0] = own
         sensor_count = CAP * (n_dom + n_dom % 2)
-        early = min(2, n_ens)
-        sensors, high, low, values = call(
+        early = n_ens - 1
+        sensors, high, low, values, pieces[0] = call(
             lambda *refs: values_kernel(n_dom, *refs),
             [
                 shape((8, sensor_count)),
                 shape((nodes, sensor_count), BF16),
                 shape((nodes, sensor_count), BF16),
                 shape((early * local_members, sensor_count)),
+                shape(state.shape),
             ],
-            list(tiles) + [pieces[key] for key in range(early)],
+            list(tiles) + [in_hbm(state)] + pieces[1:early],
+            [vmem] * n_dom + [hbm] + [vmem] * (early - 1),
+            [pltpu.SemaphoreType.DMA(())],
         )
         partial_sum = call(
             lambda *refs: cross_kernel(paired, *refs),
-            shape((8, LANES)),
+            shape((members, LANES)),
             [sensors, high, low, values] + pieces[early:],
         )
         if direct:
@@ -429,7 +419,7 @@
                 pltpu.VMEM((members * local_members, 8, 128), F32),
                 pltpu.SemaphoreType.DMA((elements // 8,)),
             ],
-            pl.BlockSpec(memory_space=pltpu.HBM),
+            hbm,
         )
 
     return on_device

time: 27 us -> 27.6 us (1.022)
  Pallas kernels: 4.75 us -> 5.22 us
    pallas_call x4, Pallas kernels: 4.75 us -> 5.22 us  [call(): pl.pallas_call(kernel, out_shape=out_shape, in_specs=specs or [vmem] * le...]
  transfers between devices with their start and end apart: 9 -> 9, of which waited for: 3 -> 3; matrix products, arithmetic and copies ran while one was open for 0% -> 0% of each run, Pallas kernels for 6% -> 9%
where the time goes in v5:
time: 27.6 us; the launch traced here: 27.4 us
  starting transfers between devices  13.6 us (49%)
  waiting for transfers between devices  8.61 us (31%)
  Pallas kernels  5.22 us (19%)
    ppermute x3, waiting for transfers between devices, gather_members(): pieces[key ^ bit] = lax.ppermute(pieces[key], 'ens', pairs)  6.51 us
    ppermute x2, starting transfers between devices, spread(): far = lax.ppermute(far, 'dom', [(d, d ^ 2) for d in range(n_dom)])  5.99 us
    pallas_call x4, Pallas kernels, call(): pl.pallas_call(kernel, out_shape=out_shape, in_specs=specs or [vmem] * le...  5.22 us
    ppermute x3, starting transfers between devices, gather_members(): pieces[key ^ bit] = lax.ppermute(pieces[key], 'ens', pairs)  2.97 us
    ppermute x2, starting transfers between devices, spread(): other = lax.ppermute(near, 'ens', [(e, e ^ 1) for e in range(n_ens)])  2.4 us
    ppermute x2, starting transfers between devices, spread(): near = lax.ppermute(near, ('dom', 'ens'), pairs)  2.22 us
    ppermute x2, waiting for transfers between devices, spread(): far = lax.ppermute(far, 'dom', [(d, d ^ 2) for d in range(n_dom)])  1.26 us
    ppermute x2, waiting for transfers between devices, spread(): other = lax.ppermute(near, 'ens', [(e, e ^ 1) for e in range(n_ens)])  0.83 us
  transfers between devices with their start and end apart: 9, of which 3 were waited for; matrix products, arithmetic and copies ran while one was open for 0% of the time, Pallas kernels for 9%

profile of v5, /device:TPU:0, one launch (start us, length us, event | category | flops | bytes accessed | tf_op | source)
XLA Modules:
  0.0 27.4 jit_solution(1403835034298299352)
XLA Ops:
  0.0 3.0 %collective-permute-start.4 = (f32[4,32,512]{2,1,0:T(8,128)}, f32[4,32,512]{2,1,0:T(8,128)S(1)}, u32[]{:S(2)}, u32[]{:S(2)}) collective-permute-start(f32[4,32,512]{2,1,0:T(8,128)} %refs_4_.1), channel_id=1, source_target_pairs={{0,2},{1,3},{2,0},{3,1},{4,6},{5,7},{6,4},{7,5},{8,10},{9,11},{10,... | collective-permute-start | bytes 786440 | tf_op jit(solution)/shard_map/ppermute | solution.py:330
  3.0 0.0 collective-permute-start.3
  3.0 6.5 %collective-permute-done.4.refs_6_ = f32[4,32,512]{2,1,0:T(8,128)S(1)} collective-permute-done((f32[4,32,512]{2,1,0:T(8,128)}, f32[4,32,512]{2,1,0:T(8,128)S(1)}, u32[]{:S(2)}, u32[]{:S(2)}) %collective-permute-start.4) | collective-permute-done | bytes 262176 | tf_op jit(solution)/shard_map/ppermute | solution.py:330
  9.5 0.0 collective-permute-start.5
  9.5 0.9 %shard_map.64 = (f32[8,128]{1,0:T(8,128)S(1)}, f32[8,128]{1,0:T(8,128)S(1)}, f32[8,128]{1,0:T(8,128)S(1)}) custom-call(s32[1,4]{1,0:T(1,128)} %refs_0_.1, f32[3,256]{1,0:T(4,128)} %refs_1_.1, s32[1,256]{1,0:T(1,128)} %bitcast.3, f32[1,256]{1,0:T(1,128)} %bitcast.4, f32[1,256]{1,0:T(1,128)} %bitcast.5), custom_call_target="tpu_custom_call" | custom-call | tf_op jit(solution)/shard_map/pallas_call | solution.py:344
  10.4 1.9 %collective-permute-start = (f32[8,128]{1,0:T(8,128)S(1)}, f32[8,128]{1,0:T(8,128)S(1)}, u32[]{:S(2)}, u32[]{:S(2)}) collective-permute-start(f32[8,128]{1,0:T(8,128)S(1)} %get-tuple-element.14), channel_id=1, source_target_pairs={{0,4},{1,13},{2,6},{3,15},{4,0},{5,9},{6,2},{7,11},{8,12},{9,5},{1... | collective-permute-start | bytes 12296 | tf_op jit(solution)/shard_map/ppermute | solution.py:313
  12.2 2.6 %collective-permute-start.1 = (f32[8,128]{1,0:T(8,128)S(1)}, f32[8,128]{1,0:T(8,128)S(1)}, u32[]{:S(2)}, u32[]{:S(2)}) collective-permute-start(f32[8,128]{1,0:T(8,128)S(1)} %get-tuple-element.15), channel_id=1, source_target_pairs={{0,8},{4,12},{8,0},{12,4},{1,9},{5,13},{9,1},{13,5},{2,10},{6,14},... | collective-permute-start | bytes 12296 | tf_op jit(solution)/shard_map/ppermute | solution.py:314
  14.8 0.0 collective-permute-done.refs_1_
  14.8 0.7 %collective-permute-start.2 = (f32[8,128]{1,0:T(8,128)S(1)}, f32[8,128]{1,0:T(8,128)S(1)}, u32[]{:S(2)}, u32[]{:S(2)}) collective-permute-start(f32[8,128]{1,0:T(8,128)S(1)} %collective-permute-done.refs_1_), channel_id=1, source_target_pairs={{0,1},{1,0},{2,3},{3,2},{4,5},{5,4},{6,7},{7,6},{8,9},{9,8},{10,11... | collective-permute-start | bytes 12296 | tf_op jit(solution)/shard_map/ppermute | solution.py:315
  15.5 1.3 %collective-permute-done.1.refs_2_ = f32[8,128]{1,0:T(8,128)S(1)} collective-permute-done((f32[8,128]{1,0:T(8,128)S(1)}, f32[8,128]{1,0:T(8,128)S(1)}, u32[]{:S(2)}, u32[]{:S(2)}) %collective-permute-start.1) | collective-permute-done | bytes 4128 | tf_op jit(solution)/shard_map/ppermute | solution.py:314
  16.8 0.0 collective-permute-done.2.refs_3_
  16.8 0.0 collective-permute-done.3.refs_5_
  16.8 1.5 %shard_map.65 = (f32[8,256]{1,0:T(8,128)S(1)}, bf16[512,256]{1,0:T(8,128)(2,1)S(1)}, bf16[512,256]{1,0:T(8,128)(2,1)S(1)}, f32[12,256]{1,0:T(8,128)S(1)}, f32[4,32,512]{2,1,0:T(8,128)S(1)}) custom-call(f32[8,128]{1,0:T(8,128)S(1)} %get-tuple-element.13.refs_0_, f32[8,128]{1,0:T(8,128)S(1)} %collective-permute-done.refs_1_, ...), custom_call_target="tpu_custom_call" | custom-call | tf_op jit(solution)/shard_map/pallas_call | solution.py:344
  18.2 0.0 collective-permute-done.5.refs_4_.refs_7_
  18.3 0.4 %shard_map.66.refs_0_ = f32[16,128]{1,0:T(8,128)S(1)} custom-call(f32[8,256]{1,0:T(8,128)S(1)} %get-tuple-element.16.refs_0_, bf16[512,256]{1,0:T(8,128)(2,1)S(1)} %get-tuple-element.17.refs_1_, bf16[512,256]{1,0:T(8,128)(2,1)S(1)} %get-tuple-element.18.refs_2_, f32[12,256]{1,0:T(8,128)S(1)} %get-tuple-element.19.refs_3_, ...), custom_call_target="tpu_custom_call" | custom-call | tf_op jit(solution)/shard_map/pallas_call | solution.py:344
  18.6 0.3 %collective-permute-start.6 = (f32[16,128]{1,0:T(8,128)S(1)}, f32[16,128]{1,0:T(8,128)S(1)}, u32[]{:S(2)}, u32[]{:S(2)}) collective-permute-start(f32[16,128]{1,0:T(8,128)S(1)} %shard_map.66.refs_0_), channel_id=1, source_target_pairs={{0,4},{1,13},{2,6},{3,15},{4,0},{5,9},{6,2},{7,11},{8,12},{9,5},{1... | collective-permute-start | bytes 24584 | tf_op jit(solution)/shard_map/ppermute | solution.py:313
  19.0 3.4 %collective-permute-start.7 = (f32[16,128]{1,0:T(8,128)S(1)}, f32[16,128]{1,0:T(8,128)S(1)}, u32[]{:S(2)}, u32[]{:S(2)}) collective-permute-start(f32[16,128]{1,0:T(8,128)S(1)} %shard_map.66.refs_0_), channel_id=1, source_target_pairs={{0,8},{4,12},{8,0},{12,4},{1,9},{5,13},{9,1},{13,5},{2,10},{6,14},... | collective-permute-start | bytes 24584 | tf_op jit(solution)/shard_map/ppermute | solution.py:314
  22.4 0.0 collective-permute-done.6.refs_1_
  22.4 1.7 %collective-permute-start.8 = (f32[16,128]{1,0:T(8,128)S(1)}, f32[16,128]{1,0:T(8,128)S(1)}, u32[]{:S(2)}, u32[]{:S(2)}) collective-permute-start(f32[16,128]{1,0:T(8,128)S(1)} %collective-permute-done.6.refs_1_), channel_id=1, source_target_pairs={{0,1},{1,0},{2,3},{3,2},{4,5},{5,4},{6,7},{7,6},{8,9},{9,8},{10,11... | collective-permute-start | bytes 24584 | tf_op jit(solution)/shard_map/ppermute | solution.py:315
  24.1 0.0 collective-permute-done.7.refs_2_
  24.1 0.8 %collective-permute-done.8.refs_3_ = f32[16,128]{1,0:T(8,128)S(1)} collective-permute-done((f32[16,128]{1,0:T(8,128)S(1)}, f32[16,128]{1,0:T(8,128)S(1)}, u32[]{:S(2)}, u32[]{:S(2)}) %collective-permute-start.8) | collective-permute-done | bytes 8224 | tf_op jit(solution)/shard_map/ppermute | solution.py:315
  24.9 2.5 %shard_map.67 = f32[4,32,512]{2,1,0:T(8,128)} custom-call(f32[16,128]{1,0:T(8,128)S(1)} %shard_map.66.refs_0_, f32[16,128]{1,0:T(8,128)S(1)} %collective-permute-done.6.refs_1_, f32[16,128]{1,0:T(8,128)S(1)} %collective-permute-done.7.refs_2_, f32[16,128]{1,0:T(8,128)S(1)} %collective-permute-done.8.refs_3_, f32[4,32,512]{2,1,0:T(8,128)S(1)} %get-tuple-element.20.refs_4_, ...), custom_call_target="tpu_custom_call" | custom-call | tf_op jit(solution)/shard_map/pallas_call | solution.py:344
Async XLA Ops:
  0.0 9.5 %collective-permute-start.4 = (f32[4,32,512]{2,1,0:T(8,128)}, f32[4,32,512]{2,1,0:T(8,128)S(1)}, u32[]{:S(2)}, u32[]{:S(2)}) collective-permute-start(f32[4,32,512]{2,1,0:T(8,128)} %refs_4_.1), channel_id=1, source_target_pairs={{0,2},{1,3},{2,0},{3,1},{4,6},{5,7},{6,4},{7,5},{8,10},{9,11},{10,... | collective-permute-start | bytes 786440 | tf_op jit(solution)/shard_map/ppermute | solution.py:330
  3.0 13.8 %collective-permute-start.3 = (f32[4,32,512]{2,1,0:T(8,128)}, f32[4,32,512]{2,1,0:T(8,128)S(1)}, u32[]{:S(2)}, u32[]{:S(2)}) collective-permute-start(f32[4,32,512]{2,1,0:T(8,128)} %refs_4_.1), channel_id=1, source_target_pairs={{0,1},{1,0},{2,3},{3,2},{4,5},{5,4},{6,7},{7,6},{8,9},{9,8},{10,11... | collective-permute-start | bytes 786440 | tf_op jit(solution)/shard_map/ppermute | solution.py:330
  9.5 8.8 %collective-permute-start.5 = (f32[4,32,512]{2,1,0:T(8,128)S(1)}, f32[4,32,512]{2,1,0:T(8,128)S(1)}, u32[]{:S(2)}, u32[]{:S(2)}) collective-permute-start(f32[4,32,512]{2,1,0:T(8,128)S(1)} %collective-permute-done.4.refs_6_), channel_id=1, source_target_pairs={{0,1},{1,0},{2,3},{3,2},{4,5},{5,4},{6,7},{7,6},{8,9},{9,8},{10,11... | collective-permute-start | bytes 786440 | tf_op jit(solution)/shard_map/ppermute | solution.py:330
  10.4 4.5 %collective-permute-start = (f32[8,128]{1,0:T(8,128)S(1)}, f32[8,128]{1,0:T(8,128)S(1)}, u32[]{:S(2)}, u32[]{:S(2)}) collective-permute-start(f32[8,128]{1,0:T(8,128)S(1)} %get-tuple-element.14), channel_id=1, source_target_pairs={{0,4},{1,13},{2,6},{3,15},{4,0},{5,9},{6,2},{7,11},{8,12},{9,5},{1... | collective-permute-start | bytes 12296 | tf_op jit(solution)/shard_map/ppermute | solution.py:313
  12.2 4.5 %collective-permute-start.1 = (f32[8,128]{1,0:T(8,128)S(1)}, f32[8,128]{1,0:T(8,128)S(1)}, u32[]{:S(2)}, u32[]{:S(2)}) collective-permute-start(f32[8,128]{1,0:T(8,128)S(1)} %get-tuple-element.15), channel_id=1, source_target_pairs={{0,8},{4,12},{8,0},{12,4},{1,9},{5,13},{9,1},{13,5},{2,10},{6,14},... | collective-permute-start | bytes 12296 | tf_op jit(solution)/shard_map/ppermute | solution.py:314
  14.8 1.9 %collective-permute-start.2 = (f32[8,128]{1,0:T(8,128)S(1)}, f32[8,128]{1,0:T(8,128)S(1)}, u32[]{:S(2)}, u32[]{:S(2)}) collective-permute-start(f32[8,128]{1,0:T(8,128)S(1)} %collective-permute-done.refs_1_), channel_id=1, source_target_pairs={{0,1},{1,0},{2,3},{3,2},{4,5},{5,4},{6,7},{7,6},{8,9},{9,8},{10,11... | collective-permute-start | bytes 12296 | tf_op jit(solution)/shard_map/ppermute | solution.py:315
  18.6 3.7 %collective-permute-start.6 = (f32[16,128]{1,0:T(8,128)S(1)}, f32[16,128]{1,0:T(8,128)S(1)}, u32[]{:S(2)}, u32[]{:S(2)}) collective-permute-start(f32[16,128]{1,0:T(8,128)S(1)} %shard_map.66.refs_0_), channel_id=1, source_target_pairs={{0,4},{1,13},{2,6},{3,15},{4,0},{5,9},{6,2},{7,11},{8,12},{9,5},{1... | collective-permute-start | bytes 24584 | tf_op jit(solution)/shard_map/ppermute | solution.py:313
  19.0 5.1 %collective-permute-start.7 = (f32[16,128]{1,0:T(8,128)S(1)}, f32[16,128]{1,0:T(8,128)S(1)}, u32[]{:S(2)}, u32[]{:S(2)}) collective-permute-start(f32[16,128]{1,0:T(8,128)S(1)} %shard_map.66.refs_0_), channel_id=1, source_target_pairs={{0,8},{4,12},{8,0},{12,4},{1,9},{5,13},{9,1},{13,5},{2,10},{6,14},... | collective-permute-start | bytes 24584 | tf_op jit(solution)/shard_map/ppermute | solution.py:314
  22.4 2.6 %collective-permute-start.8 = (f32[16,128]{1,0:T(8,128)S(1)}, f32[16,128]{1,0:T(8,128)S(1)}, u32[]{:S(2)}, u32[]{:S(2)}) collective-permute-start(f32[16,128]{1,0:T(8,128)S(1)} %collective-permute-done.6.refs_1_), channel_id=1, source_target_pairs={{0,1},{1,0},{2,3},{3,2},{4,5},{5,4},{6,7},{7,6},{8,9},{9,8},{10,11... | collective-permute-start | bytes 24584 | tf_op jit(solution)/shard_map/ppermute | solution.py:315

commit v6 on v5

--- a/solution.py
+++ b/solution.py
@@ -60,9 +60,10 @@
     return lax.rem(lax.axis_index("ens"), 2) if paired else 0
 
 
-def pack_kernel(direct, paired, counts, coords, owner, obs, weight, *rest):
-    outs = rest[:-7]
-    count_box, coord_box, owner_box, obs_box, weight_box, block, sems = rest[-7:]
+def pack_kernel(direct, paired, state, counts, coords, owner, obs, weight, *rest):
+    own, outs = rest[0], rest[1:-8]
+    count_box, coord_box, owner_box, obs_box, weight_box, block, state_sem, sems = rest[-8:]
+    state_copy = pltpu.make_async_copy(state, own, state_sem)
     pairs = zip(
         (counts, coords, owner, obs, weight), (count_box, coord_box, owner_box, obs_box, weight_box)
     )
@@ -72,6 +73,7 @@
     ]
     for copy in copies:
         copy.start()
+    state_copy.start()
     n_dom = counts.shape[1]
     slots = coords.shape[1]
     here = lax.axis_index("dom")
@@ -108,6 +110,7 @@
             return carry
 
         lax.fori_loop(0, n_dom, step, 0)
+    state_copy.wait()
 
 
 def pick(refs, sensors, high, low):
@@ -128,10 +131,8 @@
 
 
 def values_kernel(tile_count, *refs):
-    tiles, state, state_refs = refs[:tile_count], refs[tile_count], refs[tile_count + 1 : -6]
-    sensors_out, high_out, low_out, values_out, own, sem = refs[-6:]
-    copy = pltpu.make_async_copy(state, own, sem)
-    copy.start()
+    tiles, state_refs = refs[:tile_count], refs[tile_count:-4]
+    sensors_out, high_out, low_out, values_out = refs[-4:]
     pairs = []
     for first in range(0, tile_count, 2):
         pair = tiles[first][...]
@@ -150,11 +151,7 @@
             base = ORDER * ORDER * t + ORDER * s
             high_out[base : base + 2 * ORDER, :] = high
             low_out[base : base + 2 * ORDER, :] = low
-    members = own.shape[0]
-    if state_refs:
-        values_out[members:, :] = pick(state_refs, sensors, high_out[...], low_out[...])
-    copy.wait()
-    values_out[:members, :] = pick([own], sensors, high_out[...], low_out[...])
+    values_out[...] = pick(state_refs, sensors, high_out[...], low_out[...])
 
 
 def cross_kernel(paired, sensors_ref, high_ref, low_ref, values_ref, *refs):
@@ -361,12 +358,15 @@
         slots = coords.shape[1]
         members = local_members * n_ens
         tile_shape = (8, 2 * CAP)
-        inputs = [counts, coords, owner_local[None], obs_value[None], obs_weight[None]]
-        tiles = call(
+        inputs = [state, counts, coords, owner_local[None], obs_value[None], obs_weight[None]]
+        own, *tiles = call(
             lambda *refs: pack_kernel(direct, paired, *refs),
-            [shape(tile_shape)] * (3 if paired else n_dom)
-            if direct
-            else [shape((n_dom,) + tile_shape)],
+            [shape(state.shape)]
+            + (
+                [shape(tile_shape)] * (3 if paired else n_dom)
+                if direct
+                else [shape((n_dom,) + tile_shape)]
+            ),
             [in_hbm(value) for value in inputs],
             [hbm] * len(inputs),
             [
@@ -376,6 +376,7 @@
                 pltpu.VMEM((1, slots), F32),
                 pltpu.VMEM((1, slots), F32),
                 pltpu.VMEM((8, slots), F32),
+                pltpu.SemaphoreType.DMA(()),
                 pltpu.SemaphoreType.DMA((5,)),
             ],
         )
@@ -385,20 +386,18 @@
             moved = lax.all_to_all(tiles[0], "dom", split_axis=0, concat_axis=0, tiled=True)
             tiles = [moved[d] for d in range(n_dom)]
         pieces = gather_members(state, n_ens)
+        pieces[0] = own
         sensor_count = CAP * (n_dom + n_dom % 2)
         early = n_ens - 1
-        sensors, high, low, values, pieces[0] = call(
+        sensors, high, low, values = call(
             lambda *refs: values_kernel(n_dom, *refs),
             [
                 shape((8, sensor_count)),
                 shape((nodes, sensor_count), BF16),
                 shape((nodes, sensor_count), BF16),
                 shape((early * local_members, sensor_count)),
-                shape(state.shape),
             ],
-            list(tiles) + [in_hbm(state)] + pieces[1:early],
-            [vmem] * n_dom + [hbm] + [vmem] * (early - 1),
-            [pltpu.SemaphoreType.DMA(())],
+            list(tiles) + pieces[:early],
         )
         partial_sum = call(
             lambda *refs: cross_kernel(paired, *refs),

time: 27.6 us -> 26.9 us (0.975)
  Pallas kernels: 5.22 us -> 4.52 us
    pallas_call x4, Pallas kernels: 5.22 us -> 4.52 us  [call(): pl.pallas_call(kernel, out_shape=out_shape, in_specs=specs or [vmem] * le...]
  transfers between devices with their start and end apart: 9 -> 9, of which waited for: 3 -> 3; matrix products, arithmetic and copies ran while one was open for 0% -> 0% of each run, Pallas kernels for 9% -> 6%
where the time goes in v6:
time: 26.9 us; the launch traced here: 26.7 us
  starting transfers between devices  13.6 us (51%)
  waiting for transfers between devices  8.61 us (32%)
  Pallas kernels  4.52 us (17%)
    ppermute x3, waiting for transfers between devices, gather_members(): pieces[key ^ bit] = lax.ppermute(pieces[key], 'ens', pairs)  6.51 us
    ppermute x2, starting transfers between devices, spread(): far = lax.ppermute(far, 'dom', [(d, d ^ 2) for d in range(n_dom)])  5.99 us
    pallas_call x4, Pallas kernels, call(): pl.pallas_call(kernel, out_shape=out_shape, in_specs=specs or [vmem] * le...  4.52 us
    ppermute x3, starting transfers between devices, gather_members(): pieces[key ^ bit] = lax.ppermute(pieces[key], 'ens', pairs)  2.97 us
    ppermute x2, starting transfers between devices, spread(): other = lax.ppermute(near, 'ens', [(e, e ^ 1) for e in range(n_ens)])  2.39 us
    ppermute x2, starting transfers between devices, spread(): near = lax.ppermute(near, ('dom', 'ens'), pairs)  2.22 us
    ppermute x2, waiting for transfers between devices, spread(): far = lax.ppermute(far, 'dom', [(d, d ^ 2) for d in range(n_dom)])  1.26 us
    ppermute x2, waiting for transfers between devices, spread(): other = lax.ppermute(near, 'ens', [(e, e ^ 1) for e in range(n_ens)])  0.83 us
  transfers between devices with their start and end apart: 9, of which 3 were waited for; matrix products, arithmetic and copies ran while one was open for 0% of the time, Pallas kernels for 6%

profile of v6, /device:TPU:0, one launch (start us, length us, event | category | flops | bytes accessed | tf_op | source)
XLA Modules:
  0.0 26.7 jit_solution(17848919045128974048)
XLA Ops:
  0.0 3.0 %collective-permute-start.4 = (f32[4,32,512]{2,1,0:T(8,128)}, f32[4,32,512]{2,1,0:T(8,128)S(1)}, u32[]{:S(2)}, u32[]{:S(2)}) collective-permute-start(f32[4,32,512]{2,1,0:T(8,128)} %refs_0_.1), channel_id=1, source_target_pairs={{0,2},{1,3},{2,0},{3,1},{4,6},{5,7},{6,4},{7,5},{8,10},{9,11},{10,... | collective-permute-start | bytes 786440 | tf_op jit(solution)/shard_map/ppermute | solution.py:327
  3.0 0.0 collective-permute-start.3
  3.0 6.5 %collective-permute-done.4.refs_6_ = f32[4,32,512]{2,1,0:T(8,128)S(1)} collective-permute-done((f32[4,32,512]{2,1,0:T(8,128)}, f32[4,32,512]{2,1,0:T(8,128)S(1)}, u32[]{:S(2)}, u32[]{:S(2)}) %collective-permute-start.4) | collective-permute-done | bytes 262176 | tf_op jit(solution)/shard_map/ppermute | solution.py:327
  9.5 0.0 collective-permute-start.5
  9.5 1.1 %shard_map.64 = (f32[4,32,512]{2,1,0:T(8,128)S(1)}, f32[8,128]{1,0:T(8,128)S(1)}, f32[8,128]{1,0:T(8,128)S(1)}, f32[8,128]{1,0:T(8,128)S(1)}) custom-call(f32[4,32,512]{2,1,0:T(8,128)} %refs_0_.1, s32[1,4]{1,0:T(1,128)} %refs_1_.1, f32[3,256]{1,0:T(4,128)} %refs_2_.1, s32[1,256]{1,0:T(1,128)} %bitcast.3, f32[1,256]{1,0:T(1,128)} %bitcast.4, f32[1,256]{1,0:T(1,128)} %bitcast.5), custom_call_target="tpu_custom_call" | custom-call | tf_op jit(solution)/shard_map/pallas_call | solution.py:341
  10.6 1.9 %collective-permute-start = (f32[8,128]{1,0:T(8,128)S(1)}, f32[8,128]{1,0:T(8,128)S(1)}, u32[]{:S(2)}, u32[]{:S(2)}) collective-permute-start(f32[8,128]{1,0:T(8,128)S(1)} %get-tuple-element.14), channel_id=1, source_target_pairs={{0,4},{1,13},{2,6},{3,15},{4,0},{5,9},{6,2},{7,11},{8,12},{9,5},{1... | collective-permute-start | bytes 12296 | tf_op jit(solution)/shard_map/ppermute | solution.py:310
  12.5 2.6 %collective-permute-start.1 = (f32[8,128]{1,0:T(8,128)S(1)}, f32[8,128]{1,0:T(8,128)S(1)}, u32[]{:S(2)}, u32[]{:S(2)}) collective-permute-start(f32[8,128]{1,0:T(8,128)S(1)} %get-tuple-element.15), channel_id=1, source_target_pairs={{0,8},{4,12},{8,0},{12,4},{1,9},{5,13},{9,1},{13,5},{2,10},{6,14},... | collective-permute-start | bytes 12296 | tf_op jit(solution)/shard_map/ppermute | solution.py:311
  15.0 0.0 collective-permute-done.refs_1_
  15.0 0.7 %collective-permute-start.2 = (f32[8,128]{1,0:T(8,128)S(1)}, f32[8,128]{1,0:T(8,128)S(1)}, u32[]{:S(2)}, u32[]{:S(2)}) collective-permute-start(f32[8,128]{1,0:T(8,128)S(1)} %collective-permute-done.refs_1_), channel_id=1, source_target_pairs={{0,1},{1,0},{2,3},{3,2},{4,5},{5,4},{6,7},{7,6},{8,9},{9,8},{10,11... | collective-permute-start | bytes 12296 | tf_op jit(solution)/shard_map/ppermute | solution.py:312
  15.7 1.3 %collective-permute-done.1.refs_2_ = f32[8,128]{1,0:T(8,128)S(1)} collective-permute-done((f32[8,128]{1,0:T(8,128)S(1)}, f32[8,128]{1,0:T(8,128)S(1)}, u32[]{:S(2)}, u32[]{:S(2)}) %collective-permute-start.1) | collective-permute-done | bytes 4128 | tf_op jit(solution)/shard_map/ppermute | solution.py:311
  17.0 0.0 collective-permute-done.2.refs_3_
  17.0 0.0 collective-permute-done.3.refs_5_
  17.0 0.6 %shard_map.65 = (f32[8,256]{1,0:T(8,128)S(1)}, bf16[512,256]{1,0:T(8,128)(2,1)S(1)}, bf16[512,256]{1,0:T(8,128)(2,1)S(1)}, f32[12,256]{1,0:T(8,128)S(1)}) custom-call(f32[8,128]{1,0:T(8,128)S(1)} %get-tuple-element.13.refs_0_, f32[8,128]{1,0:T(8,128)S(1)} %collective-permute-done.refs_1_, f32[8,128]{1,0:T(8,128)S(1)} %collective-permute-done.1.refs_2_, ...), custom_call_target="tpu_custom_call" | custom-call | tf_op jit(solution)/shard_map/pallas_call | solution.py:341
  17.5 0.0 collective-permute-done.5.refs_4_.refs_7_
  17.6 0.4 %shard_map.66.refs_0_ = f32[16,128]{1,0:T(8,128)S(1)} custom-call(f32[8,256]{1,0:T(8,128)S(1)} %get-tuple-element.17.refs_0_, bf16[512,256]{1,0:T(8,128)(2,1)S(1)} %get-tuple-element.18.refs_1_, bf16[512,256]{1,0:T(8,128)(2,1)S(1)} %get-tuple-element.19.refs_2_, f32[12,256]{1,0:T(8,128)S(1)} %get-tuple-element.20.refs_3_, ...), custom_call_target="tpu_custom_call" | custom-call | tf_op jit(solution)/shard_map/pallas_call | solution.py:341
  17.9 0.3 %collective-permute-start.6 = (f32[16,128]{1,0:T(8,128)S(1)}, f32[16,128]{1,0:T(8,128)S(1)}, u32[]{:S(2)}, u32[]{:S(2)}) collective-permute-start(f32[16,128]{1,0:T(8,128)S(1)} %shard_map.66.refs_0_), channel_id=1, source_target_pairs={{0,4},{1,13},{2,6},{3,15},{4,0},{5,9},{6,2},{7,11},{8,12},{9,5},{1... | collective-permute-start | bytes 24584 | tf_op jit(solution)/shard_map/ppermute | solution.py:310
  18.3 3.4 %collective-permute-start.7 = (f32[16,128]{1,0:T(8,128)S(1)}, f32[16,128]{1,0:T(8,128)S(1)}, u32[]{:S(2)}, u32[]{:S(2)}) collective-permute-start(f32[16,128]{1,0:T(8,128)S(1)} %shard_map.66.refs_0_), channel_id=1, source_target_pairs={{0,8},{4,12},{8,0},{12,4},{1,9},{5,13},{9,1},{13,5},{2,10},{6,14},... | collective-permute-start | bytes 24584 | tf_op jit(solution)/shard_map/ppermute | solution.py:311
  21.7 0.0 collective-permute-done.6.refs_1_
  21.7 1.7 %collective-permute-start.8 = (f32[16,128]{1,0:T(8,128)S(1)}, f32[16,128]{1,0:T(8,128)S(1)}, u32[]{:S(2)}, u32[]{:S(2)}) collective-permute-start(f32[16,128]{1,0:T(8,128)S(1)} %collective-permute-done.6.refs_1_), channel_id=1, source_target_pairs={{0,1},{1,0},{2,3},{3,2},{4,5},{5,4},{6,7},{7,6},{8,9},{9,8},{10,11... | collective-permute-start | bytes 24584 | tf_op jit(solution)/shard_map/ppermute | solution.py:312
  23.4 0.0 collective-permute-done.7.refs_2_
  23.4 0.8 %collective-permute-done.8.refs_3_ = f32[16,128]{1,0:T(8,128)S(1)} collective-permute-done((f32[16,128]{1,0:T(8,128)S(1)}, f32[16,128]{1,0:T(8,128)S(1)}, u32[]{:S(2)}, u32[]{:S(2)}) %collective-permute-start.8) | collective-permute-done | bytes 8224 | tf_op jit(solution)/shard_map/ppermute | solution.py:312
  24.2 2.5 %shard_map.67 = f32[4,32,512]{2,1,0:T(8,128)} custom-call(f32[16,128]{1,0:T(8,128)S(1)} %shard_map.66.refs_0_, f32[16,128]{1,0:T(8,128)S(1)} %collective-permute-done.6.refs_1_, f32[16,128]{1,0:T(8,128)S(1)} %collective-permute-done.7.refs_2_, f32[16,128]{1,0:T(8,128)S(1)} %collective-permute-done.8.refs_3_, f32[4,32,512]{2,1,0:T(8,128)S(1)} %get-tuple-element.16.refs_4_, ...), custom_call_target="tpu_custom_call" | custom-call | tf_op jit(solution)/shard_map/pallas_call | solution.py:341
Async XLA Ops:
  0.0 9.5 %collective-permute-start.4 = (f32[4,32,512]{2,1,0:T(8,128)}, f32[4,32,512]{2,1,0:T(8,128)S(1)}, u32[]{:S(2)}, u32[]{:S(2)}) collective-permute-start(f32[4,32,512]{2,1,0:T(8,128)} %refs_0_.1), channel_id=1, source_target_pairs={{0,2},{1,3},{2,0},{3,1},{4,6},{5,7},{6,4},{7,5},{8,10},{9,11},{10,... | collective-permute-start | bytes 786440 | tf_op jit(solution)/shard_map/ppermute | solution.py:327
  3.0 14.0 %collective-permute-start.3 = (f32[4,32,512]{2,1,0:T(8,128)}, f32[4,32,512]{2,1,0:T(8,128)S(1)}, u32[]{:S(2)}, u32[]{:S(2)}) collective-permute-start(f32[4,32,512]{2,1,0:T(8,128)} %refs_0_.1), channel_id=1, source_target_pairs={{0,1},{1,0},{2,3},{3,2},{4,5},{5,4},{6,7},{7,6},{8,9},{9,8},{10,11... | collective-permute-start | bytes 786440 | tf_op jit(solution)/shard_map/ppermute | solution.py:327
  9.5 8.1 %collective-permute-start.5 = (f32[4,32,512]{2,1,0:T(8,128)S(1)}, f32[4,32,512]{2,1,0:T(8,128)S(1)}, u32[]{:S(2)}, u32[]{:S(2)}) collective-permute-start(f32[4,32,512]{2,1,0:T(8,128)S(1)} %collective-permute-done.4.refs_6_), channel_id=1, source_target_pairs={{0,1},{1,0},{2,3},{3,2},{4,5},{5,4},{6,7},{7,6},{8,9},{9,8},{10,11... | collective-permute-start | bytes 786440 | tf_op jit(solution)/shard_map/ppermute | solution.py:327
  10.6 4.5 %collective-permute-start = (f32[8,128]{1,0:T(8,128)S(1)}, f32[8,128]{1,0:T(8,128)S(1)}, u32[]{:S(2)}, u32[]{:S(2)}) collective-permute-start(f32[8,128]{1,0:T(8,128)S(1)} %get-tuple-element.14), channel_id=1, source_target_pairs={{0,4},{1,13},{2,6},{3,15},{4,0},{5,9},{6,2},{7,11},{8,12},{9,5},{1... | collective-permute-start | bytes 12296 | tf_op jit(solution)/shard_map/ppermute | solution.py:310
  12.5 4.5 %collective-permute-start.1 = (f32[8,128]{1,0:T(8,128)S(1)}, f32[8,128]{1,0:T(8,128)S(1)}, u32[]{:S(2)}, u32[]{:S(2)}) collective-permute-start(f32[8,128]{1,0:T(8,128)S(1)} %get-tuple-element.15), channel_id=1, source_target_pairs={{0,8},{4,12},{8,0},{12,4},{1,9},{5,13},{9,1},{13,5},{2,10},{6,14},... | collective-permute-start | bytes 12296 | tf_op jit(solution)/shard_map/ppermute | solution.py:311
  15.0 1.9 %collective-permute-start.2 = (f32[8,128]{1,0:T(8,128)S(1)}, f32[8,128]{1,0:T(8,128)S(1)}, u32[]{:S(2)}, u32[]{:S(2)}) collective-permute-start(f32[8,128]{1,0:T(8,128)S(1)} %collective-permute-done.refs_1_), channel_id=1, source_target_pairs={{0,1},{1,0},{2,3},{3,2},{4,5},{5,4},{6,7},{7,6},{8,9},{9,8},{10,11... | collective-permute-start | bytes 12296 | tf_op jit(solution)/shard_map/ppermute | solution.py:312
  17.9 3.7 %collective-permute-start.6 = (f32[16,128]{1,0:T(8,128)S(1)}, f32[16,128]{1,0:T(8,128)S(1)}, u32[]{:S(2)}, u32[]{:S(2)}) collective-permute-start(f32[16,128]{1,0:T(8,128)S(1)} %shard_map.66.refs_0_), channel_id=1, source_target_pairs={{0,4},{1,13},{2,6},{3,15},{4,0},{5,9},{6,2},{7,11},{8,12},{9,5},{1... | collective-permute-start | bytes 24584 | tf_op jit(solution)/shard_map/ppermute | solution.py:310
  18.3 5.1 %collective-permute-start.7 = (f32[16,128]{1,0:T(8,128)S(1)}, f32[16,128]{1,0:T(8,128)S(1)}, u32[]{:S(2)}, u32[]{:S(2)}) collective-permute-start(f32[16,128]{1,0:T(8,128)S(1)} %shard_map.66.refs_0_), channel_id=1, source_target_pairs={{0,8},{4,12},{8,0},{12,4},{1,9},{5,13},{9,1},{13,5},{2,10},{6,14},... | collective-permute-start | bytes 24584 | tf_op jit(solution)/shard_map/ppermute | solution.py:311
  21.7 2.6 %collective-permute-start.8 = (f32[16,128]{1,0:T(8,128)S(1)}, f32[16,128]{1,0:T(8,128)S(1)}, u32[]{:S(2)}, u32[]{:S(2)}) collective-permute-start(f32[16,128]{1,0:T(8,128)S(1)} %collective-permute-done.6.refs_1_), channel_id=1, source_target_pairs={{0,1},{1,0},{2,3},{3,2},{4,5},{5,4},{6,7},{7,6},{8,9},{9,8},{10,11... | collective-permute-start | bytes 24584 | tf_op jit(solution)/shard_map/ppermute | solution.py:312

commit v7 on v6

--- a/solution.py
+++ b/solution.py
@@ -56,8 +56,8 @@
     return high, low
 
 
-def is_odd(paired):
-    return lax.rem(lax.axis_index("ens"), 2) if paired else 0
+def is_odd(halves):
+    return lax.rem(lax.axis_index("ens"), 2) if halves else 0
 
 
 def pack_kernel(direct, paired, state, counts, coords, owner, obs, weight, *rest):
@@ -130,14 +130,19 @@
     return jnp.sum(jnp.where((ids == sensors[3:4, :])[None], partial, 0.0), axis=1)
 
 
-def values_kernel(tile_count, *refs):
+def values_kernel(paired, tile_count, *refs):
     tiles, state_refs = refs[:tile_count], refs[tile_count:-4]
     sensors_out, high_out, low_out, values_out = refs[-4:]
+    blocks = [ref[...] for ref in tiles]
+    if paired:
+        here, near, far, other = blocks
+        odd = is_odd(paired) == 1
+        blocks = [here, jnp.where(odd, other, near), far, jnp.where(odd, near, other)]
     pairs = []
     for first in range(0, tile_count, 2):
-        pair = tiles[first][...]
+        pair = blocks[first]
         if first + 1 < tile_count:
-            pair = pair + tiles[first + 1][...]
+            pair = pair + blocks[first + 1]
         pairs.append(pair)
     sensors = jnp.concatenate(pairs, axis=1) if len(pairs) > 1 else pairs[0]
     sensors_out[...] = sensors
@@ -154,18 +159,21 @@
     values_out[...] = pick(state_refs, sensors, high_out[...], low_out[...])
 
 
-def cross_kernel(paired, sensors_ref, high_ref, low_ref, values_ref, *refs):
+def reach_kernel(sensors_ref, high_ref, low_ref, values_ref, *refs):
     state_refs, out = refs[:-1], refs[-1]
+    first = values_ref.shape[0]
+    out[:first, :] = values_ref[...]
+    out[first:, :] = pick(state_refs, sensors_ref[...], high_ref[...], low_ref[...])
+
+
+def cross_kernel(halves, sensors_ref, *refs):
+    value_refs, out = refs[:-1], refs[-1]
     sensors = sensors_ref[...]
-    values = jnp.concatenate(
-        [values_ref[...], pick(state_refs, sensors, high_ref[...], low_ref[...])], axis=0
-    )
+    values = jnp.concatenate([ref[...] for ref in value_refs], axis=0)
     total = values.shape[0]
-    if paired:
-        size = state_refs[0].shape[0]
-        blocks = [values[first : first + size] for first in range(0, total, size)]
-        turned = [blocks[index ^ 1] for index in range(len(blocks))]
-        values = jnp.where(is_odd(paired) == 1, jnp.concatenate(turned, axis=0), values)
+    if halves:
+        turned = jnp.concatenate([ref[...] for ref in value_refs[::-1]], axis=0)
+        values = jnp.where(is_odd(halves) == 1, turned, values)
     mean_value = jnp.sum(values, axis=0, keepdims=True) * (1.0 / total)
     anomaly = values - mean_value
     weighted = anomaly * sensors[5:6, :]
@@ -200,7 +208,7 @@
     return value
 
 
-def mix_kernel(paired, sum_count, *refs):
+def mix_kernel(halves, sum_count, *refs):
     sums, state_refs = refs[:sum_count], refs[sum_count:-4]
     out, staged, splats, sems = refs[-4:]
     local_members, elements, nodes = out.shape
@@ -262,28 +270,36 @@
     transform_right = as_right(transform)
     column_mean = sublane_total(transform_right[0] + transform_right[1]) * (1.0 / members)
     mixing = [transform[h] - column_mean + 1.0 / members for h in range(2)]
-    odd = is_odd(paired)
+    odd = is_odd(halves)
+    order = key_order(len(state_refs))
+    own_place = odd * order.index(1) if halves else 0
     for k in range(local_members):
-        lanes = sub * members + (k + local_members * odd)
+        lanes = sub * members + (k + local_members * own_place)
         for h in range(2):
             column = lane_gather(mixing[h], lanes)
             for i in range(8):
                 splats[(8 * h + i) * local_members + k] = jnp.broadcast_to(column[i : i + 1, :], tile)
+    places = []
+    for piece in range(len(state_refs)):
+        place = order.index(piece)
+        places.append(place + odd * (order.index(piece ^ 1) - place) if halves else place)
     copies = []
     for block in range(elements // 8):
         span = slice(8 * block, 8 * block + 8)
-        for lane in range(nodes // 128):
-            lanes = slice(128 * lane, 128 * lane + 128)
-            totals = [None] * local_members
+        for first in range(0, nodes, 2 * LANES):
+            spans = [slice(first + LANES * u, first + LANES * (u + 1)) for u in range(2)]
+            totals = [[None, None] for _ in range(local_members)]
             for j in range(members):
                 piece, member = divmod(j, local_members)
-                value = state_refs[piece][member, span, lanes]
-                place = piece + odd * (1 - 2 * (piece % 2))
+                values = [state_refs[piece][member, span, lanes] for lanes in spans]
                 for k in range(local_members):
-                    term = splats[(place * local_members + member) * local_members + k] * value
-                    totals[k] = term if totals[k] is None else totals[k] + term
+                    factor = splats[(places[piece] * local_members + member) * local_members + k]
+                    for u in range(2):
+                        term = factor * values[u]
+                        totals[k][u] = term if j == 0 else totals[k][u] + term
             for k in range(local_members):
-                staged[k, span, lanes] = totals[k]
+                for u in range(2):
+                    staged[k, span, spans[u]] = totals[k][u]
         place = pl.ds(8 * block, 8)
         copy = pltpu.make_async_copy(staged.at[:, place], out.at[:, place], sems.at[block])
         copy.start()
@@ -292,8 +308,18 @@
         copy.wait()
 
 
+def has_halves(n_ens):
+    return n_ens > 1 and n_ens & (n_ens - 1) == 0
+
+
 def is_paired(n_dom, n_ens):
-    return n_dom == 4 and n_ens % 2 == 0
+    return n_dom == 4 and has_halves(n_ens)
+
+
+def key_order(n_ens):
+    if not has_halves(n_ens):
+        return list(range(n_ens))
+    return list(range(0, n_ens, 2)) + list(range(1, n_ens, 2))
 
 
 def spread(values, n_dom, n_ens):
@@ -313,20 +339,24 @@
     return [here, near, far, other]
 
 
-def gather_members(state, n_ens):
+def gather_members(state, own, n_ens):
     pieces = {0: state}
-    if n_ens & (n_ens - 1):
+    if not has_halves(n_ens):
         for shift in range(1, n_ens):
             pairs = [(e, (e + shift) % n_ens) for e in range(n_ens)]
             pieces[shift] = lax.ppermute(state, "ens", pairs)
-        return [pieces[key] for key in range(n_ens)]
+        pieces[0] = own
+        return pieces
     bit = n_ens >> 1
     while bit:
+        pairs = [(e, e ^ bit) for e in range(n_ens)]
         for key in list(pieces):
-            pairs = [(e, e ^ bit) for e in range(n_ens)]
             pieces[key ^ bit] = lax.ppermute(pieces[key], "ens", pairs)
         bit >>= 1
-    return [pieces[key] for key in range(n_ens)]
+        if bit == 1:
+            pieces[0] = own
+    pieces[0] = own
+    return pieces
 
 
 def make_on_device(n_dom, n_ens):
@@ -334,6 +364,7 @@
     hbm = pl.BlockSpec(memory_space=pltpu.HBM)
     direct = n_dom <= DIRECT_DOM
     paired = is_paired(n_dom, n_ens)
+    halves = has_halves(n_ens)
     limit = VMEM_LIMIT if direct else None
 
     def call(kernel, out_shape, operands, specs=None, scratch=(), out_spec=vmem):
@@ -385,33 +416,41 @@
         else:
             moved = lax.all_to_all(tiles[0], "dom", split_axis=0, concat_axis=0, tiled=True)
             tiles = [moved[d] for d in range(n_dom)]
-        pieces = gather_members(state, n_ens)
-        pieces[0] = own
+        pieces = gather_members(state, own, n_ens)
         sensor_count = CAP * (n_dom + n_dom % 2)
-        early = n_ens - 1
+        order = key_order(n_ens)
+        local = order[: n_ens // 2] if halves else order
         sensors, high, low, values = call(
-            lambda *refs: values_kernel(n_dom, *refs),
+            lambda *refs: values_kernel(paired, n_dom, *refs),
             [
                 shape((8, sensor_count)),
                 shape((nodes, sensor_count), BF16),
                 shape((nodes, sensor_count), BF16),
-                shape((early * local_members, sensor_count)),
+                shape((local_members, sensor_count)),
             ],
-            list(tiles) + pieces[:early],
+            list(tiles) + [pieces[0]],
         )
+        if len(local) > 1:
+            values = call(
+                reach_kernel,
+                shape((len(local) * local_members, sensor_count)),
+                [sensors, high, low, values] + [pieces[key] for key in local[1:]],
+            )
+        values = [values]
+        if halves:
+            pairs = [(e, e ^ 1) for e in range(n_ens)]
+            values.append(lax.ppermute(values[0], "ens", pairs))
         partial_sum = call(
-            lambda *refs: cross_kernel(paired, *refs),
-            shape((members, LANES)),
-            [sensors, high, low, values] + pieces[early:],
+            lambda *refs: cross_kernel(halves, *refs), shape((members, LANES)), [sensors] + values
         )
         if direct:
             sums = spread([partial_sum] * (3 if paired else n_dom), n_dom, n_ens)
         else:
             sums = [lax.psum(partial_sum, "dom")]
         return call(
-            lambda *refs: mix_kernel(paired, len(sums), *refs),
+            lambda *refs: mix_kernel(halves, len(sums), *refs),
             shape(state.shape),
-            sums + pieces,
+            sums + [pieces[key] for key in range(n_ens)],
             None,
             [
                 pltpu.VMEM(state.shape, F32),

time: 26.9 us -> 26.7 us (level)
  waiting for transfers between devices: 8.61 us -> 9.02 us
  starting transfers between devices: 13.6 us -> 13.2 us
    ppermute x0 -> x1, starting transfers between devices: none -> 1.17 us  [on_device(): values.append(lax.ppermute(values[0], 'ens', pairs))]
    ppermute x3, waiting for transfers between devices: 6.51 us -> 5.36 us  [gather_members(): pieces[key ^ bit] = lax.ppermute(pieces[key], 'ens', pairs)]
    ppermute x0 -> x1, waiting for transfers between devices: none -> 0.83 us  [on_device(): values.append(lax.ppermute(values[0], 'ens', pairs))]
    ppermute x2, starting transfers between devices: 2.39 us -> 1.65 us  [spread(): other = lax.ppermute(near, 'ens', [(e, e ^ 1) for e in range(n_ens)])]
    ppermute x2, waiting for transfers between devices: 0.01 us -> 0.75 us  [spread(): near = lax.ppermute(near, ('dom', 'ens'), pairs)]
    ppermute x2, starting transfers between devices: 5.99 us -> 5.53 us  [spread(): far = lax.ppermute(far, 'dom', [(d, d ^ 2) for d in range(n_dom)])]
    ppermute x2, starting transfers between devices: 2.22 us -> 1.83 us  [spread(): near = lax.ppermute(near, ('dom', 'ens'), pairs)]
    pallas_call x4 -> x5, Pallas kernels: 4.52 us -> 4.28 us  [call(): pl.pallas_call(kernel, out_shape=out_shape, in_specs=specs or [vmem] * le...]
  transfers between devices with their start and end apart: 9 -> 10, of which waited for: 3 -> 5; matrix products, arithmetic and copies ran while one was open for 0% -> 0% of each run, Pallas kernels for 6% -> 7%
where the time goes in v7:
time: 26.7 us; the launch traced here: 26.6 us
  starting transfers between devices  13.2 us (49%)
  waiting for transfers between devices  9.02 us (34%)
  Pallas kernels  4.28 us (16%)
    ppermute x2, starting transfers between devices, spread(): far = lax.ppermute(far, 'dom', [(d, d ^ 2) for d in range(n_dom)])  5.53 us
    ppermute x3, waiting for transfers between devices, gather_members(): pieces[key ^ bit] = lax.ppermute(pieces[key], 'ens', pairs)  5.36 us
    pallas_call x5, Pallas kernels, call(): pl.pallas_call(kernel, out_shape=out_shape, in_specs=specs or [vmem] * le...  4.28 us
    ppermute x3, starting transfers between devices, gather_members(): pieces[key ^ bit] = lax.ppermute(pieces[key], 'ens', pairs)  3.04 us
    ppermute x2, starting transfers between devices, spread(): near = lax.ppermute(near, ('dom', 'ens'), pairs)  1.83 us
    ppermute x2, starting transfers between devices, spread(): other = lax.ppermute(near, 'ens', [(e, e ^ 1) for e in range(n_ens)])  1.65 us
    ppermute x2, waiting for transfers between devices, spread(): far = lax.ppermute(far, 'dom', [(d, d ^ 2) for d in range(n_dom)])  1.26 us
    ppermute x1, starting transfers between devices, on_device(): values.append(lax.ppermute(values[0], 'ens', pairs))  1.17 us
  transfers between devices with their start and end apart: 10, of which 5 were waited for; matrix products, arithmetic and copies ran while one was open for 0% of the time, Pallas kernels for 7%

profile of v7, /device:TPU:0, one launch (start us, length us, event | category | flops | bytes accessed | tf_op | source)
XLA Modules:
  0.0 26.6 jit_solution(17790573487132640423)
XLA Ops:
  0.0 3.0 %collective-permute-start.3 = (f32[4,32,512]{2,1,0:T(8,128)}, f32[4,32,512]{2,1,0:T(8,128)S(1)}, u32[]{:S(2)}, u32[]{:S(2)}) collective-permute-start(f32[4,32,512]{2,1,0:T(8,128)} %refs_0_.1), channel_id=1, source_target_pairs={{0,2},{1,3},{2,0},{3,1},{4,6},{5,7},{6,4},{7,5},{8,10},{9,11},{10,... | collective-permute-start | bytes 786440 | tf_op jit(solution)/shard_map/ppermute | solution.py:354
  3.0 1.1 %shard_map.64 = (f32[4,32,512]{2,1,0:T(8,128)S(1)}, f32[8,128]{1,0:T(8,128)S(1)}, f32[8,128]{1,0:T(8,128)S(1)}, f32[8,128]{1,0:T(8,128)S(1)}) custom-call(f32[4,32,512]{2,1,0:T(8,128)} %refs_0_.1, s32[1,4]{1,0:T(1,128)} %refs_1_.1, f32[3,256]{1,0:T(4,128)} %refs_2_.1, s32[1,256]{1,0:T(1,128)} %bitcast.3, f32[1,256]{1,0:T(1,128)} %bitcast.4, f32[1,256]{1,0:T(1,128)} %bitcast.5), custom_call_target="tpu_custom_call" | custom-call | tf_op jit(solution)/shard_map/pallas_call | solution.py:372
  4.1 0.1 collective-permute-start.8
  4.1 5.4 %collective-permute-done.3.refs_0_.refs_6_ = f32[4,32,512]{2,1,0:T(8,128)S(1)} collective-permute-done((f32[4,32,512]{2,1,0:T(8,128)}, f32[4,32,512]{2,1,0:T(8,128)S(1)}, u32[]{:S(2)}, u32[]{:S(2)}) %collective-permute-start.3) | collective-permute-done | bytes 262176 | tf_op jit(solution)/shard_map/ppermute | solution.py:354
  9.5 0.0 collective-permute-start.9
  9.5 1.8 %collective-permute-start = (f32[8,128]{1,0:T(8,128)S(1)}, f32[8,128]{1,0:T(8,128)S(1)}, u32[]{:S(2)}, u32[]{:S(2)}) collective-permute-start(f32[8,128]{1,0:T(8,128)S(1)} %get-tuple-element.14), channel_id=1, source_target_pairs={{0,4},{1,13},{2,6},{3,15},{4,0},{5,9},{6,2},{7,11},{8,12},{9,5},{1... | collective-permute-start | bytes 12296 | tf_op jit(solution)/shard_map/ppermute | solution.py:336
  11.3 2.6 %collective-permute-start.1 = (f32[8,128]{1,0:T(8,128)S(1)}, f32[8,128]{1,0:T(8,128)S(1)}, u32[]{:S(2)}, u32[]{:S(2)}) collective-permute-start(f32[8,128]{1,0:T(8,128)S(1)} %get-tuple-element.15), channel_id=1, source_target_pairs={{0,8},{4,12},{8,0},{12,4},{1,9},{5,13},{9,1},{13,5},{2,10},{6,14},... | collective-permute-start | bytes 12296 | tf_op jit(solution)/shard_map/ppermute | solution.py:337
  13.9 0.0 collective-permute-done.refs_1_
  13.9 0.7 %collective-permute-start.2 = (f32[8,128]{1,0:T(8,128)S(1)}, f32[8,128]{1,0:T(8,128)S(1)}, u32[]{:S(2)}, u32[]{:S(2)}) collective-permute-start(f32[8,128]{1,0:T(8,128)S(1)} %collective-permute-done.refs_1_), channel_id=1, source_target_pairs={{0,1},{1,0},{2,3},{3,2},{4,5},{5,4},{6,7},{7,6},{8,9},{9,8},{10,11... | collective-permute-start | bytes 12296 | tf_op jit(solution)/shard_map/ppermute | solution.py:338
  14.6 1.3 %collective-permute-done.1.refs_2_ = f32[8,128]{1,0:T(8,128)S(1)} collective-permute-done((f32[8,128]{1,0:T(8,128)S(1)}, f32[8,128]{1,0:T(8,128)S(1)}, u32[]{:S(2)}, u32[]{:S(2)}) %collective-permute-start.1) | collective-permute-done | bytes 4128 | tf_op jit(solution)/shard_map/ppermute | solution.py:337
  15.8 0.0 collective-permute-done.2.refs_3_
  15.8 0.4 %shard_map.65 = (f32[8,256]{1,0:T(8,128)S(1)}, bf16[512,256]{1,0:T(8,128)(2,1)S(1)}, bf16[512,256]{1,0:T(8,128)(2,1)S(1)}, f32[4,256]{1,0:T(4,128)S(1)}) custom-call(f32[8,128]{1,0:T(8,128)S(1)} %get-tuple-element.13.refs_0_, f32[8,128]{1,0:T(8,128)S(1)} %collective-permute-done.refs_1_, f32[8,128]{1,0:T(8,128)S(1)} %collective-permute-done.1.refs_2_, ...), custom_call_target="tpu_custom_call" | custom-call | tf_op jit(solution)/shard_map/pallas_call | solution.py:372
  16.2 0.3 %shard_map.66.refs_1_ = f32[8,256]{1,0:T(8,128)S(1)} custom-call(f32[8,256]{1,0:T(8,128)S(1)} %get-tuple-element.17.sensors_ref.refs_0_, bf16[512,256]{1,0:T(8,128)(2,1)S(1)} %get-tuple-element.18.high_ref, bf16[512,256]{1,0:T(8,128)(2,1)S(1)} %get-tuple-element.19.low_ref, f32[4,256]{1,0:T(4,128)S(1)} %get-tuple-element.20.values_ref, ...), custom_call_target="tpu_custom_call" | custom-call | tf_op jit(solution)/shard_map/pallas_call | solution.py:372
  16.5 1.2 %collective-permute-start.4 = (f32[8,256]{1,0:T(8,128)S(1)}, f32[8,256]{1,0:T(8,128)S(1)}, u32[]{:S(2)}, u32[]{:S(2)}) collective-permute-start(f32[8,256]{1,0:T(8,128)S(1)} %shard_map.66.refs_1_), channel_id=1, source_target_pairs={{0,1},{1,0},{2,3},{3,2},{4,5},{5,4},{6,7},{7,6},{8,9},{9,8},{10,11... | collective-permute-start | bytes 24584 | tf_op jit(solution)/shard_map/ppermute | solution.py:442
  17.6 0.8 %collective-permute-done.4.refs_2_ = f32[8,256]{1,0:T(8,128)S(1)} collective-permute-done((f32[8,256]{1,0:T(8,128)S(1)}, f32[8,256]{1,0:T(8,128)S(1)}, u32[]{:S(2)}, u32[]{:S(2)}) %collective-permute-start.4) | collective-permute-done | bytes 8224 | tf_op jit(solution)/shard_map/ppermute | solution.py:442
  18.5 0.1 shard_map.67.refs_0_
  18.6 0.0 collective-permute-start.5
  18.6 2.9 %collective-permute-start.6 = (f32[16,128]{1,0:T(8,128)S(1)}, f32[16,128]{1,0:T(8,128)S(1)}, u32[]{:S(2)}, u32[]{:S(2)}) collective-permute-start(f32[16,128]{1,0:T(8,128)S(1)} %shard_map.67.refs_0_), channel_id=1, source_target_pairs={{0,8},{4,12},{8,0},{12,4},{1,9},{5,13},{9,1},{13,5},{2,10},{6,14},... | collective-permute-start | bytes 24584 | tf_op jit(solution)/shard_map/ppermute | solution.py:337
  21.5 0.7 %collective-permute-done.5.refs_1_ = f32[16,128]{1,0:T(8,128)S(1)} collective-permute-done((f32[16,128]{1,0:T(8,128)S(1)}, f32[16,128]{1,0:T(8,128)S(1)}, u32[]{:S(2)}, u32[]{:S(2)}) %collective-permute-start.5) | collective-permute-done | bytes 8224 | tf_op jit(solution)/shard_map/ppermute | solution.py:336
  22.3 1.0 %collective-permute-start.7 = (f32[16,128]{1,0:T(8,128)S(1)}, f32[16,128]{1,0:T(8,128)S(1)}, u32[]{:S(2)}, u32[]{:S(2)}) collective-permute-start(f32[16,128]{1,0:T(8,128)S(1)} %collective-permute-done.5.refs_1_), channel_id=1, source_target_pairs={{0,1},{1,0},{2,3},{3,2},{4,5},{5,4},{6,7},{7,6},{8,9},{9,8},{10,11... | collective-permute-start | bytes 24584 | tf_op jit(solution)/shard_map/ppermute | solution.py:338
  23.3 0.0 collective-permute-done.8.refs_5_
  23.3 0.0 collective-permute-done.6.refs_2_
  23.3 0.8 %collective-permute-done.7.refs_3_ = f32[16,128]{1,0:T(8,128)S(1)} collective-permute-done((f32[16,128]{1,0:T(8,128)S(1)}, f32[16,128]{1,0:T(8,128)S(1)}, u32[]{:S(2)}, u32[]{:S(2)}) %collective-permute-start.7) | collective-permute-done | bytes 8224 | tf_op jit(solution)/shard_map/ppermute | solution.py:338
  24.1 0.0 collective-permute-done.9.refs_7_
  24.1 2.5 %shard_map.68 = f32[4,32,512]{2,1,0:T(8,128)} custom-call(f32[16,128]{1,0:T(8,128)S(1)} %shard_map.67.refs_0_, f32[16,128]{1,0:T(8,128)S(1)} %collective-permute-done.5.refs_1_, f32[16,128]{1,0:T(8,128)S(1)} %collective-permute-done.6.refs_2_, f32[16,128]{1,0:T(8,128)S(1)} %collective-permute-done.7.refs_3_, f32[4,32,512]{2,1,0:T(8,128)S(1)} %get-tuple-element.16.refs_4_, ...), custom_call_target="tpu_custom_call" | custom-call | tf_op jit(solution)/shard_map/pallas_call | solution.py:372
Async XLA Ops:
  0.0 9.5 %collective-permute-start.3 = (f32[4,32,512]{2,1,0:T(8,128)}, f32[4,32,512]{2,1,0:T(8,128)S(1)}, u32[]{:S(2)}, u32[]{:S(2)}) collective-permute-start(f32[4,32,512]{2,1,0:T(8,128)} %refs_0_.1), channel_id=1, source_target_pairs={{0,2},{1,3},{2,0},{3,1},{4,6},{5,7},{6,4},{7,5},{8,10},{9,11},{10,... | collective-permute-start | bytes 786440 | tf_op jit(solution)/shard_map/ppermute | solution.py:354
  4.1 19.2 %collective-permute-start.8 = (f32[4,32,512]{2,1,0:T(8,128)S(1)}, f32[4,32,512]{2,1,0:T(8,128)S(1)}, u32[]{:S(2)}, u32[]{:S(2)}) collective-permute-start(f32[4,32,512]{2,1,0:T(8,128)S(1)} %get-tuple-element.16.refs_4_), channel_id=1, source_target_pairs={{0,1},{1,0},{2,3},{3,2},{4,5},{5,4},{6,7},{7,6},{8,9},{9,8},{10,11... | collective-permute-start | bytes 786440 | tf_op jit(solution)/shard_map/ppermute | solution.py:354
  9.5 14.6 %collective-permute-start.9 = (f32[4,32,512]{2,1,0:T(8,128)S(1)}, f32[4,32,512]{2,1,0:T(8,128)S(1)}, u32[]{:S(2)}, u32[]{:S(2)}) collective-permute-start(f32[4,32,512]{2,1,0:T(8,128)S(1)} %collective-permute-done.3.refs_0_.refs_6_), channel_id=1, source_target_pairs={{0,1},{1,0},{2,3},{3,2},{4,5},{5,4},{6,7},{7,6},{8,9},{9,8},{10,11... | collective-permute-start | bytes 786440 | tf_op jit(solution)/shard_map/ppermute | solution.py:354
  9.5 4.4 %collective-permute-start = (f32[8,128]{1,0:T(8,128)S(1)}, f32[8,128]{1,0:T(8,128)S(1)}, u32[]{:S(2)}, u32[]{:S(2)}) collective-permute-start(f32[8,128]{1,0:T(8,128)S(1)} %get-tuple-element.14), channel_id=1, source_target_pairs={{0,4},{1,13},{2,6},{3,15},{4,0},{5,9},{6,2},{7,11},{8,12},{9,5},{1... | collective-permute-start | bytes 12296 | tf_op jit(solution)/shard_map/ppermute | solution.py:336
  11.3 4.5 %collective-permute-start.1 = (f32[8,128]{1,0:T(8,128)S(1)}, f32[8,128]{1,0:T(8,128)S(1)}, u32[]{:S(2)}, u32[]{:S(2)}) collective-permute-start(f32[8,128]{1,0:T(8,128)S(1)} %get-tuple-element.15), channel_id=1, source_target_pairs={{0,8},{4,12},{8,0},{12,4},{1,9},{5,13},{9,1},{13,5},{2,10},{6,14},... | collective-permute-start | bytes 12296 | tf_op jit(solution)/shard_map/ppermute | solution.py:337
  13.9 1.9 %collective-permute-start.2 = (f32[8,128]{1,0:T(8,128)S(1)}, f32[8,128]{1,0:T(8,128)S(1)}, u32[]{:S(2)}, u32[]{:S(2)}) collective-permute-start(f32[8,128]{1,0:T(8,128)S(1)} %collective-permute-done.refs_1_), channel_id=1, source_target_pairs={{0,1},{1,0},{2,3},{3,2},{4,5},{5,4},{6,7},{7,6},{8,9},{9,8},{10,11... | collective-permute-start | bytes 12296 | tf_op jit(solution)/shard_map/ppermute | solution.py:338
  16.5 2.0 %collective-permute-start.4 = (f32[8,256]{1,0:T(8,128)S(1)}, f32[8,256]{1,0:T(8,128)S(1)}, u32[]{:S(2)}, u32[]{:S(2)}) collective-permute-start(f32[8,256]{1,0:T(8,128)S(1)} %shard_map.66.refs_1_), channel_id=1, source_target_pairs={{0,1},{1,0},{2,3},{3,2},{4,5},{5,4},{6,7},{7,6},{8,9},{9,8},{10,11... | collective-permute-start | bytes 24584 | tf_op jit(solution)/shard_map/ppermute | solution.py:442
  18.6 3.7 %collective-permute-start.5 = (f32[16,128]{1,0:T(8,128)S(1)}, f32[16,128]{1,0:T(8,128)S(1)}, u32[]{:S(2)}, u32[]{:S(2)}) collective-permute-start(f32[16,128]{1,0:T(8,128)S(1)} %shard_map.67.refs_0_), channel_id=1, source_target_pairs={{0,4},{1,13},{2,6},{3,15},{4,0},{5,9},{6,2},{7,11},{8,12},{9,5},{1... | collective-permute-start | bytes 24584 | tf_op jit(solution)/shard_map/ppermute | solution.py:336
  18.6 4.7 %collective-permute-start.6 = (f32[16,128]{1,0:T(8,128)S(1)}, f32[16,128]{1,0:T(8,128)S(1)}, u32[]{:S(2)}, u32[]{:S(2)}) collective-permute-start(f32[16,128]{1,0:T(8,128)S(1)} %shard_map.67.refs_0_), channel_id=1, source_target_pairs={{0,8},{4,12},{8,0},{12,4},{1,9},{5,13},{9,1},{13,5},{2,10},{6,14},... | collective-permute-start | bytes 24584 | tf_op jit(solution)/shard_map/ppermute | solution.py:337
  22.3 1.8 %collective-permute-start.7 = (f32[16,128]{1,0:T(8,128)S(1)}, f32[16,128]{1,0:T(8,128)S(1)}, u32[]{:S(2)}, u32[]{:S(2)}) collective-permute-start(f32[16,128]{1,0:T(8,128)S(1)} %collective-permute-done.5.refs_1_), channel_id=1, source_target_pairs={{0,1},{1,0},{2,3},{3,2},{4,5},{5,4},{6,7},{7,6},{8,9},{9,8},{10,11... | collective-permute-start | bytes 24584 | tf_op jit(solution)/shard_map/ppermute | solution.py:338

commit v8 on v7

--- a/solution.py
+++ b/solution.py
@@ -60,10 +60,15 @@
     return lax.rem(lax.axis_index("ens"), 2) if halves else 0
 
 
-def pack_kernel(direct, paired, state, counts, coords, owner, obs, weight, *rest):
-    own, outs = rest[0], rest[1:-8]
-    count_box, coord_box, owner_box, obs_box, weight_box, block, state_sem, sems = rest[-8:]
-    state_copy = pltpu.make_async_copy(state, own, state_sem)
+def fetch_kernel(state, own, sem):
+    copy = pltpu.make_async_copy(state, own, sem)
+    copy.start()
+    copy.wait()
+
+
+def pack_kernel(direct, paired, counts, coords, owner, obs, weight, *rest):
+    outs = rest[:-7]
+    count_box, coord_box, owner_box, obs_box, weight_box, block, sems = rest[-7:]
     pairs = zip(
         (counts, coords, owner, obs, weight), (count_box, coord_box, owner_box, obs_box, weight_box)
     )
@@ -73,7 +78,6 @@
     ]
     for copy in copies:
         copy.start()
-    state_copy.start()
     n_dom = counts.shape[1]
     slots = coords.shape[1]
     here = lax.axis_index("dom")
@@ -110,7 +114,6 @@
             return carry
 
         lax.fori_loop(0, n_dom, step, 0)
-    state_copy.wait()
 
 
 def pick(refs, sensors, high, low):
@@ -329,12 +332,13 @@
             for s in range(1, n_dom)
         ]
     here, near, far = values
-    pairs = []
+    pairs, cross = [], []
     for d in range(n_dom):
         for e in range(n_ens):
             pairs.append((d * n_ens + e, (d ^ (3 if e % 2 else 1)) * n_ens + e))
+            cross.append((d * n_ens + e, (d ^ 2) * n_ens + (e ^ 1)))
     near = lax.ppermute(near, ("dom", "ens"), pairs)
-    far = lax.ppermute(far, "dom", [(d, d ^ 2) for d in range(n_dom)])
+    far = lax.ppermute(far, ("dom", "ens"), cross)
     other = lax.ppermute(near, "ens", [(e, e ^ 1) for e in range(n_ens)])
     return [here, near, far, other]
 
@@ -389,15 +393,12 @@
         slots = coords.shape[1]
         members = local_members * n_ens
         tile_shape = (8, 2 * CAP)
-        inputs = [state, counts, coords, owner_local[None], obs_value[None], obs_weight[None]]
-        own, *tiles = call(
+        inputs = [counts, coords, owner_local[None], obs_value[None], obs_weight[None]]
+        tiles = call(
             lambda *refs: pack_kernel(direct, paired, *refs),
-            [shape(state.shape)]
-            + (
-                [shape(tile_shape)] * (3 if paired else n_dom)
-                if direct
-                else [shape((n_dom,) + tile_shape)]
-            ),
+            [shape(tile_shape)] * (3 if paired else n_dom)
+            if direct
+            else [shape((n_dom,) + tile_shape)],
             [in_hbm(value) for value in inputs],
             [hbm] * len(inputs),
             [
@@ -407,7 +408,6 @@
                 pltpu.VMEM((1, slots), F32),
                 pltpu.VMEM((1, slots), F32),
                 pltpu.VMEM((8, slots), F32),
-                pltpu.SemaphoreType.DMA(()),
                 pltpu.SemaphoreType.DMA((5,)),
             ],
         )
@@ -416,6 +416,9 @@
         else:
             moved = lax.all_to_all(tiles[0], "dom", split_axis=0, concat_axis=0, tiled=True)
             tiles = [moved[d] for d in range(n_dom)]
+        own = call(
+            fetch_kernel, shape(state.shape), [in_hbm(state)], [hbm], [pltpu.SemaphoreType.DMA(())]
+        )
         pieces = gather_members(state, own, n_ens)
         sensor_count = CAP * (n_dom + n_dom % 2)
         order = key_order(n_ens)

time: 26.7 us -> 28.2 us (1.056)
  waiting for transfers between devices: 9.02 us -> 11.4 us
  starting transfers between devices: 13.2 us -> 11.6 us
  Pallas kernels: 4.28 us -> 5.05 us
    ppermute x2, starting transfers between devices: 5.53 us -> 2.01 us  [spread(): far = lax.ppermute(far, ('dom', 'ens'), cross)]
    ppermute x2, waiting for transfers between devices: 0.75 us -> 3.45 us  [spread(): near = lax.ppermute(near, ('dom', 'ens'), pairs)]
    ppermute x1, starting transfers between devices: 1.17 us -> 2.18 us  [on_device(): values.append(lax.ppermute(values[0], 'ens', pairs))]
    ppermute x2, starting transfers between devices: 1.65 us -> 2.46 us  [spread(): other = lax.ppermute(near, 'ens', [(e, e ^ 1) for e in range(n_ens)])]
    pallas_call x5 -> x6, Pallas kernels: 4.28 us -> 5.05 us  [call(): pl.pallas_call(kernel, out_shape=out_shape, in_specs=specs or [vmem] * le...]
    ppermute x2, waiting for transfers between devices: 1.26 us -> 0.68 us  [spread(): far = lax.ppermute(far, ('dom', 'ens'), cross)]
  transfers between devices with their start and end apart: 10 -> 10, of which waited for: 5 -> 7; matrix products, arithmetic and copies ran while one was open for 0% -> 0% of each run, Pallas kernels for 7% -> 9%
where the time goes in v8:
time: 28.2 us; the launch traced here: 28.1 us
  starting transfers between devices  11.6 us (41%)
  waiting for transfers between devices  11.4 us (40%)
  Pallas kernels  5.05 us (18%)
    ppermute x3, waiting for transfers between devices, gather_members(): pieces[key ^ bit] = lax.ppermute(pieces[key], 'ens', pairs)  5.44 us
    pallas_call x6, Pallas kernels, call(): pl.pallas_call(kernel, out_shape=out_shape, in_specs=specs or [vmem] * le...  5.05 us
    ppermute x2, waiting for transfers between devices, spread(): near = lax.ppermute(near, ('dom', 'ens'), pairs)  3.45 us
    ppermute x3, starting transfers between devices, gather_members(): pieces[key ^ bit] = lax.ppermute(pieces[key], 'ens', pairs)  3.04 us
    ppermute x2, starting transfers between devices, spread(): other = lax.ppermute(near, 'ens', [(e, e ^ 1) for e in range(n_ens)])  2.46 us
    ppermute x1, starting transfers between devices, on_device(): values.append(lax.ppermute(values[0], 'ens', pairs))  2.18 us
    ppermute x2, starting transfers between devices, spread(): far = lax.ppermute(far, ('dom', 'ens'), cross)  2.01 us
    ppermute x2, starting transfers between devices, spread(): near = lax.ppermute(near, ('dom', 'ens'), pairs)  1.9 us
  transfers between devices with their start and end apart: 10, of which 7 were waited for; matrix products, arithmetic and copies ran while one was open for 0% of the time, Pallas kernels for 9%

profile of v8, /device:TPU:0, one launch (start us, length us, event | category | flops | bytes accessed | tf_op | source)
XLA Modules:
  0.0 28.1 jit_solution(15506408705678191159)
XLA Ops:
  0.0 3.0 %collective-permute-start.3 = (f32[4,32,512]{2,1,0:T(8,128)}, f32[4,32,512]{2,1,0:T(8,128)S(1)}, u32[]{:S(2)}, u32[]{:S(2)}) collective-permute-start(f32[4,32,512]{2,1,0:T(8,128)} %state.1), channel_id=1, source_target_pairs={{0,2},{1,3},{2,0},{3,1},{4,6},{5,7},{6,4},{7,5},{8,10},{9,11},{10,... | collective-permute-start | bytes 786440 | tf_op jit(solution)/shard_map/ppermute | solution.py:358
  3.0 1.0 %shard_map.65.refs_4_ = f32[4,32,512]{2,1,0:T(8,128)S(1)} custom-call(f32[4,32,512]{2,1,0:T(8,128)} %state.1), custom_call_target="tpu_custom_call" | custom-call | tf_op jit(solution)/shard_map/pallas_call | solution.py:376
  4.0 0.1 collective-permute-start.8
  4.0 5.4 %collective-permute-done.3.refs_0_.refs_6_ = f32[4,32,512]{2,1,0:T(8,128)S(1)} collective-permute-done((f32[4,32,512]{2,1,0:T(8,128)}, f32[4,32,512]{2,1,0:T(8,128)S(1)}, u32[]{:S(2)}, u32[]{:S(2)}) %collective-permute-start.3) | collective-permute-done | bytes 262176 | tf_op jit(solution)/shard_map/ppermute | solution.py:358
  9.5 0.0 collective-permute-start.9
  9.5 0.9 %shard_map.64 = (f32[8,128]{1,0:T(8,128)S(1)}, f32[8,128]{1,0:T(8,128)S(1)}, f32[8,128]{1,0:T(8,128)S(1)}) custom-call(s32[1,4]{1,0:T(1,128)} %refs_0_.1, f32[3,256]{1,0:T(4,128)} %refs_1_.1, s32[1,256]{1,0:T(1,128)} %bitcast.3, f32[1,256]{1,0:T(1,128)} %bitcast.4, f32[1,256]{1,0:T(1,128)} %bitcast.5), custom_call_target="tpu_custom_call" | custom-call | tf_op jit(solution)/shard_map/pallas_call | solution.py:376
  10.4 1.9 %collective-permute-start = (f32[8,128]{1,0:T(8,128)S(1)}, f32[8,128]{1,0:T(8,128)S(1)}, u32[]{:S(2)}, u32[]{:S(2)}) collective-permute-start(f32[8,128]{1,0:T(8,128)S(1)} %get-tuple-element.13), channel_id=1, source_target_pairs={{0,4},{1,13},{2,6},{3,15},{4,0},{5,9},{6,2},{7,11},{8,12},{9,5},{1... | collective-permute-start | bytes 12296 | tf_op jit(solution)/shard_map/ppermute | solution.py:340
  12.2 1.3 %collective-permute-start.1 = (f32[8,128]{1,0:T(8,128)S(1)}, f32[8,128]{1,0:T(8,128)S(1)}, u32[]{:S(2)}, u32[]{:S(2)}) collective-permute-start(f32[8,128]{1,0:T(8,128)S(1)} %get-tuple-element.14), channel_id=1, source_target_pairs={{0,9},{1,8},{2,11},{3,10},{4,13},{5,12},{6,15},{7,14},{8,1},{9,0},... | collective-permute-start | bytes 12296 | tf_op jit(solution)/shard_map/ppermute | solution.py:341
  13.5 0.5 %collective-permute-done.refs_1_ = f32[8,128]{1,0:T(8,128)S(1)} collective-permute-done((f32[8,128]{1,0:T(8,128)S(1)}, f32[8,128]{1,0:T(8,128)S(1)}, u32[]{:S(2)}, u32[]{:S(2)}) %collective-permute-start) | collective-permute-done | bytes 4128 | tf_op jit(solution)/shard_map/ppermute | solution.py:340
  14.0 1.5 %collective-permute-start.2 = (f32[8,128]{1,0:T(8,128)S(1)}, f32[8,128]{1,0:T(8,128)S(1)}, u32[]{:S(2)}, u32[]{:S(2)}) collective-permute-start(f32[8,128]{1,0:T(8,128)S(1)} %collective-permute-done.refs_1_), channel_id=1, source_target_pairs={{0,1},{1,0},{2,3},{3,2},{4,5},{5,4},{6,7},{7,6},{8,9},{9,8},{10,11... | collective-permute-start | bytes 12296 | tf_op jit(solution)/shard_map/ppermute | solution.py:342
  15.5 0.7 %collective-permute-done.1.refs_2_ = f32[8,128]{1,0:T(8,128)S(1)} collective-permute-done((f32[8,128]{1,0:T(8,128)S(1)}, f32[8,128]{1,0:T(8,128)S(1)}, u32[]{:S(2)}, u32[]{:S(2)}) %collective-permute-start.1) | collective-permute-done | bytes 4128 | tf_op jit(solution)/shard_map/ppermute | solution.py:341
  16.2 0.1 collective-permute-done.2.refs_3_
  16.3 0.3 %shard_map.66 = (f32[8,256]{1,0:T(8,128)S(1)}, bf16[512,256]{1,0:T(8,128)(2,1)S(1)}, bf16[512,256]{1,0:T(8,128)(2,1)S(1)}, f32[4,256]{1,0:T(4,128)S(1)}) custom-call(f32[8,128]{1,0:T(8,128)S(1)} %get-tuple-element.12.refs_0_, f32[8,128]{1,0:T(8,128)S(1)} %collective-permute-done.refs_1_, f32[8,128]{1,0:T(8,128)S(1)} %collective-permute-done.1.refs_2_, ...), custom_call_target="tpu_custom_call" | custom-call | tf_op jit(solution)/shard_map/pallas_call | solution.py:376
  16.7 0.3 %shard_map.67.refs_1_ = f32[8,256]{1,0:T(8,128)S(1)} custom-call(f32[8,256]{1,0:T(8,128)S(1)} %get-tuple-element.15.sensors_ref.refs_0_, bf16[512,256]{1,0:T(8,128)(2,1)S(1)} %get-tuple-element.16.high_ref, bf16[512,256]{1,0:T(8,128)(2,1)S(1)} %get-tuple-element.17.low_ref, f32[4,256]{1,0:T(4,128)S(1)} %get-tuple-element.18.values_ref, ...), custom_call_target="tpu_custom_call" | custom-call | tf_op jit(solution)/shard_map/pallas_call | solution.py:376
  17.0 2.2 %collective-permute-start.4 = (f32[8,256]{1,0:T(8,128)S(1)}, f32[8,256]{1,0:T(8,128)S(1)}, u32[]{:S(2)}, u32[]{:S(2)}) collective-permute-start(f32[8,256]{1,0:T(8,128)S(1)} %shard_map.67.refs_1_), channel_id=1, source_target_pairs={{0,1},{1,0},{2,3},{3,2},{4,5},{5,4},{6,7},{7,6},{8,9},{9,8},{10,11... | collective-permute-start | bytes 24584 | tf_op jit(solution)/shard_map/ppermute | solution.py:445
  19.1 0.8 %collective-permute-done.4.refs_2_ = f32[8,256]{1,0:T(8,128)S(1)} collective-permute-done((f32[8,256]{1,0:T(8,128)S(1)}, f32[8,256]{1,0:T(8,128)S(1)}, u32[]{:S(2)}, u32[]{:S(2)}) %collective-permute-start.4) | collective-permute-done | bytes 8224 | tf_op jit(solution)/shard_map/ppermute | solution.py:445
  20.0 0.1 shard_map.68.refs_0_
  20.1 0.0 collective-permute-start.5
  20.1 0.7 %collective-permute-start.6 = (f32[16,128]{1,0:T(8,128)S(1)}, f32[16,128]{1,0:T(8,128)S(1)}, u32[]{:S(2)}, u32[]{:S(2)}) collective-permute-start(f32[16,128]{1,0:T(8,128)S(1)} %shard_map.68.refs_0_), channel_id=1, source_target_pairs={{0,9},{1,8},{2,11},{3,10},{4,13},{5,12},{6,15},{7,14},{8,1},{9,0},... | collective-permute-start | bytes 24584 | tf_op jit(solution)/shard_map/ppermute | solution.py:341
  20.8 3.0 %collective-permute-done.5.refs_1_ = f32[16,128]{1,0:T(8,128)S(1)} collective-permute-done((f32[16,128]{1,0:T(8,128)S(1)}, f32[16,128]{1,0:T(8,128)S(1)}, u32[]{:S(2)}, u32[]{:S(2)}) %collective-permute-start.5) | collective-permute-done | bytes 8224 | tf_op jit(solution)/shard_map/ppermute | solution.py:340
  23.8 1.0 %collective-permute-start.7 = (f32[16,128]{1,0:T(8,128)S(1)}, f32[16,128]{1,0:T(8,128)S(1)}, u32[]{:S(2)}, u32[]{:S(2)}) collective-permute-start(f32[16,128]{1,0:T(8,128)S(1)} %collective-permute-done.5.refs_1_), channel_id=1, source_target_pairs={{0,1},{1,0},{2,3},{3,2},{4,5},{5,4},{6,7},{7,6},{8,9},{9,8},{10,11... | collective-permute-start | bytes 24584 | tf_op jit(solution)/shard_map/ppermute | solution.py:342
  24.8 0.0 collective-permute-done.8.refs_5_
  24.8 0.0 collective-permute-done.6.refs_2_
  24.8 0.8 %collective-permute-done.7.refs_3_ = f32[16,128]{1,0:T(8,128)S(1)} collective-permute-done((f32[16,128]{1,0:T(8,128)S(1)}, f32[16,128]{1,0:T(8,128)S(1)}, u32[]{:S(2)}, u32[]{:S(2)}) %collective-permute-start.7) | collective-permute-done | bytes 8224 | tf_op jit(solution)/shard_map/ppermute | solution.py:342
  25.6 0.0 collective-permute-done.9.refs_7_
  25.6 2.5 %shard_map.69 = f32[4,32,512]{2,1,0:T(8,128)} custom-call(f32[16,128]{1,0:T(8,128)S(1)} %shard_map.68.refs_0_, f32[16,128]{1,0:T(8,128)S(1)} %collective-permute-done.5.refs_1_, f32[16,128]{1,0:T(8,128)S(1)} %collective-permute-done.6.refs_2_, f32[16,128]{1,0:T(8,128)S(1)} %collective-permute-done.7.refs_3_, f32[4,32,512]{2,1,0:T(8,128)S(1)} %shard_map.65.refs_4_, ...), custom_call_target="tpu_custom_call" | custom-call | tf_op jit(solution)/shard_map/pallas_call | solution.py:376
Async XLA Ops:
  0.0 9.5 %collective-permute-start.3 = (f32[4,32,512]{2,1,0:T(8,128)}, f32[4,32,512]{2,1,0:T(8,128)S(1)}, u32[]{:S(2)}, u32[]{:S(2)}) collective-permute-start(f32[4,32,512]{2,1,0:T(8,128)} %state.1), channel_id=1, source_target_pairs={{0,2},{1,3},{2,0},{3,1},{4,6},{5,7},{6,4},{7,5},{8,10},{9,11},{10,... | collective-permute-start | bytes 786440 | tf_op jit(solution)/shard_map/ppermute | solution.py:358
  4.0 20.8 %collective-permute-start.8 = (f32[4,32,512]{2,1,0:T(8,128)S(1)}, f32[4,32,512]{2,1,0:T(8,128)S(1)}, u32[]{:S(2)}, u32[]{:S(2)}) collective-permute-start(f32[4,32,512]{2,1,0:T(8,128)S(1)} %shard_map.65.refs_4_), channel_id=1, source_target_pairs={{0,1},{1,0},{2,3},{3,2},{4,5},{5,4},{6,7},{7,6},{8,9},{9,8},{10,11... | collective-permute-start | bytes 786440 | tf_op jit(solution)/shard_map/ppermute | solution.py:358
  9.5 16.1 %collective-permute-start.9 = (f32[4,32,512]{2,1,0:T(8,128)S(1)}, f32[4,32,512]{2,1,0:T(8,128)S(1)}, u32[]{:S(2)}, u32[]{:S(2)}) collective-permute-start(f32[4,32,512]{2,1,0:T(8,128)S(1)} %collective-permute-done.3.refs_0_.refs_6_), channel_id=1, source_target_pairs={{0,1},{1,0},{2,3},{3,2},{4,5},{5,4},{6,7},{7,6},{8,9},{9,8},{10,11... | collective-permute-start | bytes 786440 | tf_op jit(solution)/shard_map/ppermute | solution.py:358
  10.4 3.7 %collective-permute-start = (f32[8,128]{1,0:T(8,128)S(1)}, f32[8,128]{1,0:T(8,128)S(1)}, u32[]{:S(2)}, u32[]{:S(2)}) collective-permute-start(f32[8,128]{1,0:T(8,128)S(1)} %get-tuple-element.13), channel_id=1, source_target_pairs={{0,4},{1,13},{2,6},{3,15},{4,0},{5,9},{6,2},{7,11},{8,12},{9,5},{1... | collective-permute-start | bytes 12296 | tf_op jit(solution)/shard_map/ppermute | solution.py:340
  12.2 3.9 %collective-permute-start.1 = (f32[8,128]{1,0:T(8,128)S(1)}, f32[8,128]{1,0:T(8,128)S(1)}, u32[]{:S(2)}, u32[]{:S(2)}) collective-permute-start(f32[8,128]{1,0:T(8,128)S(1)} %get-tuple-element.14), channel_id=1, source_target_pairs={{0,9},{1,8},{2,11},{3,10},{4,13},{5,12},{6,15},{7,14},{8,1},{9,0},... | collective-permute-start | bytes 12296 | tf_op jit(solution)/shard_map/ppermute | solution.py:341
  14.0 2.3 %collective-permute-start.2 = (f32[8,128]{1,0:T(8,128)S(1)}, f32[8,128]{1,0:T(8,128)S(1)}, u32[]{:S(2)}, u32[]{:S(2)}) collective-permute-start(f32[8,128]{1,0:T(8,128)S(1)} %collective-permute-done.refs_1_), channel_id=1, source_target_pairs={{0,1},{1,0},{2,3},{3,2},{4,5},{5,4},{6,7},{7,6},{8,9},{9,8},{10,11... | collective-permute-start | bytes 12296 | tf_op jit(solution)/shard_map/ppermute | solution.py:342
  17.0 3.0 %collective-permute-start.4 = (f32[8,256]{1,0:T(8,128)S(1)}, f32[8,256]{1,0:T(8,128)S(1)}, u32[]{:S(2)}, u32[]{:S(2)}) collective-permute-start(f32[8,256]{1,0:T(8,128)S(1)} %shard_map.67.refs_1_), channel_id=1, source_target_pairs={{0,1},{1,0},{2,3},{3,2},{4,5},{5,4},{6,7},{7,6},{8,9},{9,8},{10,11... | collective-permute-start | bytes 24584 | tf_op jit(solution)/shard_map/ppermute | solution.py:445
  20.1 3.7 %collective-permute-start.5 = (f32[16,128]{1,0:T(8,128)S(1)}, f32[16,128]{1,0:T(8,128)S(1)}, u32[]{:S(2)}, u32[]{:S(2)}) collective-permute-start(f32[16,128]{1,0:T(8,128)S(1)} %shard_map.68.refs_0_), channel_id=1, source_target_pairs={{0,4},{1,13},{2,6},{3,15},{4,0},{5,9},{6,2},{7,11},{8,12},{9,5},{1... | collective-permute-start | bytes 24584 | tf_op jit(solution)/shard_map/ppermute | solution.py:340
  20.1 4.7 %collective-permute-start.6 = (f32[16,128]{1,0:T(8,128)S(1)}, f32[16,128]{1,0:T(8,128)S(1)}, u32[]{:S(2)}, u32[]{:S(2)}) collective-permute-start(f32[16,128]{1,0:T(8,128)S(1)} %shard_map.68.refs_0_), channel_id=1, source_target_pairs={{0,9},{1,8},{2,11},{3,10},{4,13},{5,12},{6,15},{7,14},{8,1},{9,0},... | collective-permute-start | bytes 24584 | tf_op jit(solution)/shard_map/ppermute | solution.py:341
  23.8 1.8 %collective-permute-start.7 = (f32[16,128]{1,0:T(8,128)S(1)}, f32[16,128]{1,0:T(8,128)S(1)}, u32[]{:S(2)}, u32[]{:S(2)}) collective-permute-start(f32[16,128]{1,0:T(8,128)S(1)} %collective-permute-done.5.refs_1_), channel_id=1, source_target_pairs={{0,1},{1,0},{2,3},{3,2},{4,5},{5,4},{6,7},{7,6},{8,9},{9,8},{10,11... | collective-permute-start | bytes 24584 | tf_op jit(solution)/shard_map/ppermute | solution.py:342

commit v9 on v8

--- a/solution.py
+++ b/solution.py
@@ -332,13 +332,12 @@
             for s in range(1, n_dom)
         ]
     here, near, far = values
-    pairs, cross = [], []
+    pairs = []
     for d in range(n_dom):
         for e in range(n_ens):
             pairs.append((d * n_ens + e, (d ^ (3 if e % 2 else 1)) * n_ens + e))
-            cross.append((d * n_ens + e, (d ^ 2) * n_ens + (e ^ 1)))
     near = lax.ppermute(near, ("dom", "ens"), pairs)
-    far = lax.ppermute(far, ("dom", "ens"), cross)
+    far = lax.ppermute(far, "dom", [(d, d ^ 2) for d in range(n_dom)])
     other = lax.ppermute(near, "ens", [(e, e ^ 1) for e in range(n_ens)])
     return [here, near, far, other]
 

time: 28.2 us -> 27.7 us (0.982)
  waiting for transfers between devices: 11.4 us -> 9.09 us
  starting transfers between devices: 11.6 us -> 13.3 us
    ppermute x2, starting transfers between devices: 2.01 us -> 5.53 us  [spread(): far = lax.ppermute(far, 'dom', [(d, d ^ 2) for d in range(n_dom)])]
    ppermute x2, waiting for transfers between devices: 3.45 us -> 0.74 us  [spread(): near = lax.ppermute(near, ('dom', 'ens'), pairs)]
    ppermute x1, starting transfers between devices: 2.18 us -> 1.17 us  [on_device(): values.append(lax.ppermute(values[0], 'ens', pairs))]
    ppermute x2, starting transfers between devices: 2.46 us -> 1.65 us  [spread(): other = lax.ppermute(near, 'ens', [(e, e ^ 1) for e in range(n_ens)])]
    ppermute x2, waiting for transfers between devices: 0.68 us -> 1.26 us  [spread(): far = lax.ppermute(far, 'dom', [(d, d ^ 2) for d in range(n_dom)])]
  transfers between devices with their start and end apart: 10 -> 10, of which waited for: 7 -> 5; matrix products, arithmetic and copies ran while one was open for 0% -> 0% of each run, Pallas kernels for 9% -> 9%
where the time goes in v9:
time: 27.7 us; the launch traced here: 27.5 us
  starting transfers between devices  13.3 us (48%)
  waiting for transfers between devices  9.09 us (33%)
  Pallas kernels  5.05 us (18%)
    ppermute x2, starting transfers between devices, spread(): far = lax.ppermute(far, 'dom', [(d, d ^ 2) for d in range(n_dom)])  5.53 us
    ppermute x3, waiting for transfers between devices, gather_members(): pieces[key ^ bit] = lax.ppermute(pieces[key], 'ens', pairs)  5.44 us
    pallas_call x6, Pallas kernels, call(): pl.pallas_call(kernel, out_shape=out_shape, in_specs=specs or [vmem] * le...  5.05 us
    ppermute x3, starting transfers between devices, gather_members(): pieces[key ^ bit] = lax.ppermute(pieces[key], 'ens', pairs)  3.04 us
    ppermute x2, starting transfers between devices, spread(): near = lax.ppermute(near, ('dom', 'ens'), pairs)  1.9 us
    ppermute x2, starting transfers between devices, spread(): other = lax.ppermute(near, 'ens', [(e, e ^ 1) for e in range(n_ens)])  1.65 us
    ppermute x2, waiting for transfers between devices, spread(): far = lax.ppermute(far, 'dom', [(d, d ^ 2) for d in range(n_dom)])  1.26 us
    ppermute x1, starting transfers between devices, on_device(): values.append(lax.ppermute(values[0], 'ens', pairs))  1.17 us
  transfers between devices with their start and end apart: 10, of which 5 were waited for; matrix products, arithmetic and copies ran while one was open for 0% of the time, Pallas kernels for 9%

profile of v9, /device:TPU:0, one launch (start us, length us, event | category | flops | bytes accessed | tf_op | source)
XLA Modules:
  0.0 27.5 jit_solution(6049228374544365637)
XLA Ops:
  0.0 3.0 %collective-permute-start.3 = (f32[4,32,512]{2,1,0:T(8,128)}, f32[4,32,512]{2,1,0:T(8,128)S(1)}, u32[]{:S(2)}, u32[]{:S(2)}) collective-permute-start(f32[4,32,512]{2,1,0:T(8,128)} %state.1), channel_id=1, source_target_pairs={{0,2},{1,3},{2,0},{3,1},{4,6},{5,7},{6,4},{7,5},{8,10},{9,11},{10,... | collective-permute-start | bytes 786440 | tf_op jit(solution)/shard_map/ppermute | solution.py:357
  3.0 1.0 %shard_map.65.refs_4_ = f32[4,32,512]{2,1,0:T(8,128)S(1)} custom-call(f32[4,32,512]{2,1,0:T(8,128)} %state.1), custom_call_target="tpu_custom_call" | custom-call | tf_op jit(solution)/shard_map/pallas_call | solution.py:375
  4.0 0.1 collective-permute-start.8
  4.0 5.4 %collective-permute-done.3.refs_0_.refs_6_ = f32[4,32,512]{2,1,0:T(8,128)S(1)} collective-permute-done((f32[4,32,512]{2,1,0:T(8,128)}, f32[4,32,512]{2,1,0:T(8,128)S(1)}, u32[]{:S(2)}, u32[]{:S(2)}) %collective-permute-start.3) | collective-permute-done | bytes 262176 | tf_op jit(solution)/shard_map/ppermute | solution.py:357
  9.5 0.0 collective-permute-start.9
  9.5 0.9 %shard_map.64 = (f32[8,128]{1,0:T(8,128)S(1)}, f32[8,128]{1,0:T(8,128)S(1)}, f32[8,128]{1,0:T(8,128)S(1)}) custom-call(s32[1,4]{1,0:T(1,128)} %refs_0_.1, f32[3,256]{1,0:T(4,128)} %refs_1_.1, s32[1,256]{1,0:T(1,128)} %bitcast.3, f32[1,256]{1,0:T(1,128)} %bitcast.4, f32[1,256]{1,0:T(1,128)} %bitcast.5), custom_call_target="tpu_custom_call" | custom-call | tf_op jit(solution)/shard_map/pallas_call | solution.py:375
  10.4 1.9 %collective-permute-start = (f32[8,128]{1,0:T(8,128)S(1)}, f32[8,128]{1,0:T(8,128)S(1)}, u32[]{:S(2)}, u32[]{:S(2)}) collective-permute-start(f32[8,128]{1,0:T(8,128)S(1)} %get-tuple-element.13), channel_id=1, source_target_pairs={{0,4},{1,13},{2,6},{3,15},{4,0},{5,9},{6,2},{7,11},{8,12},{9,5},{1... | collective-permute-start | bytes 12296 | tf_op jit(solution)/shard_map/ppermute | solution.py:339
  12.2 2.6 %collective-permute-start.1 = (f32[8,128]{1,0:T(8,128)S(1)}, f32[8,128]{1,0:T(8,128)S(1)}, u32[]{:S(2)}, u32[]{:S(2)}) collective-permute-start(f32[8,128]{1,0:T(8,128)S(1)} %get-tuple-element.14), channel_id=1, source_target_pairs={{0,8},{4,12},{8,0},{12,4},{1,9},{5,13},{9,1},{13,5},{2,10},{6,14},... | collective-permute-start | bytes 12296 | tf_op jit(solution)/shard_map/ppermute | solution.py:340
  14.8 0.0 collective-permute-done.refs_1_
  14.8 0.7 %collective-permute-start.2 = (f32[8,128]{1,0:T(8,128)S(1)}, f32[8,128]{1,0:T(8,128)S(1)}, u32[]{:S(2)}, u32[]{:S(2)}) collective-permute-start(f32[8,128]{1,0:T(8,128)S(1)} %collective-permute-done.refs_1_), channel_id=1, source_target_pairs={{0,1},{1,0},{2,3},{3,2},{4,5},{5,4},{6,7},{7,6},{8,9},{9,8},{10,11... | collective-permute-start | bytes 12296 | tf_op jit(solution)/shard_map/ppermute | solution.py:341
  15.5 1.3 %collective-permute-done.1.refs_2_ = f32[8,128]{1,0:T(8,128)S(1)} collective-permute-done((f32[8,128]{1,0:T(8,128)S(1)}, f32[8,128]{1,0:T(8,128)S(1)}, u32[]{:S(2)}, u32[]{:S(2)}) %collective-permute-start.1) | collective-permute-done | bytes 4128 | tf_op jit(solution)/shard_map/ppermute | solution.py:340
  16.8 0.0 collective-permute-done.2.refs_3_
  16.8 0.4 %shard_map.66 = (f32[8,256]{1,0:T(8,128)S(1)}, bf16[512,256]{1,0:T(8,128)(2,1)S(1)}, bf16[512,256]{1,0:T(8,128)(2,1)S(1)}, f32[4,256]{1,0:T(4,128)S(1)}) custom-call(f32[8,128]{1,0:T(8,128)S(1)} %get-tuple-element.12.refs_0_, f32[8,128]{1,0:T(8,128)S(1)} %collective-permute-done.refs_1_, f32[8,128]{1,0:T(8,128)S(1)} %collective-permute-done.1.refs_2_, ...), custom_call_target="tpu_custom_call" | custom-call | tf_op jit(solution)/shard_map/pallas_call | solution.py:375
  17.1 0.3 %shard_map.67.refs_1_ = f32[8,256]{1,0:T(8,128)S(1)} custom-call(f32[8,256]{1,0:T(8,128)S(1)} %get-tuple-element.15.sensors_ref.refs_0_, bf16[512,256]{1,0:T(8,128)(2,1)S(1)} %get-tuple-element.16.high_ref, bf16[512,256]{1,0:T(8,128)(2,1)S(1)} %get-tuple-element.17.low_ref, f32[4,256]{1,0:T(4,128)S(1)} %get-tuple-element.18.values_ref, ...), custom_call_target="tpu_custom_call" | custom-call | tf_op jit(solution)/shard_map/pallas_call | solution.py:375
  17.4 1.2 %collective-permute-start.4 = (f32[8,256]{1,0:T(8,128)S(1)}, f32[8,256]{1,0:T(8,128)S(1)}, u32[]{:S(2)}, u32[]{:S(2)}) collective-permute-start(f32[8,256]{1,0:T(8,128)S(1)} %shard_map.67.refs_1_), channel_id=1, source_target_pairs={{0,1},{1,0},{2,3},{3,2},{4,5},{5,4},{6,7},{7,6},{8,9},{9,8},{10,11... | collective-permute-start | bytes 24584 | tf_op jit(solution)/shard_map/ppermute | solution.py:444
  18.6 0.8 %collective-permute-done.4.refs_2_ = f32[8,256]{1,0:T(8,128)S(1)} collective-permute-done((f32[8,256]{1,0:T(8,128)S(1)}, f32[8,256]{1,0:T(8,128)S(1)}, u32[]{:S(2)}, u32[]{:S(2)}) %collective-permute-start.4) | collective-permute-done | bytes 8224 | tf_op jit(solution)/shard_map/ppermute | solution.py:444
  19.4 0.1 shard_map.68.refs_0_
  19.5 0.0 collective-permute-start.5
  19.5 2.9 %collective-permute-start.6 = (f32[16,128]{1,0:T(8,128)S(1)}, f32[16,128]{1,0:T(8,128)S(1)}, u32[]{:S(2)}, u32[]{:S(2)}) collective-permute-start(f32[16,128]{1,0:T(8,128)S(1)} %shard_map.68.refs_0_), channel_id=1, source_target_pairs={{0,8},{4,12},{8,0},{12,4},{1,9},{5,13},{9,1},{13,5},{2,10},{6,14},... | collective-permute-start | bytes 24584 | tf_op jit(solution)/shard_map/ppermute | solution.py:340
  22.5 0.7 %collective-permute-done.5.refs_1_ = f32[16,128]{1,0:T(8,128)S(1)} collective-permute-done((f32[16,128]{1,0:T(8,128)S(1)}, f32[16,128]{1,0:T(8,128)S(1)}, u32[]{:S(2)}, u32[]{:S(2)}) %collective-permute-start.5) | collective-permute-done | bytes 8224 | tf_op jit(solution)/shard_map/ppermute | solution.py:339
  23.2 1.0 %collective-permute-start.7 = (f32[16,128]{1,0:T(8,128)S(1)}, f32[16,128]{1,0:T(8,128)S(1)}, u32[]{:S(2)}, u32[]{:S(2)}) collective-permute-start(f32[16,128]{1,0:T(8,128)S(1)} %collective-permute-done.5.refs_1_), channel_id=1, source_target_pairs={{0,1},{1,0},{2,3},{3,2},{4,5},{5,4},{6,7},{7,6},{8,9},{9,8},{10,11... | collective-permute-start | bytes 24584 | tf_op jit(solution)/shard_map/ppermute | solution.py:341
  24.2 0.0 collective-permute-done.8.refs_5_
  24.2 0.0 collective-permute-done.6.refs_2_
  24.2 0.8 %collective-permute-done.7.refs_3_ = f32[16,128]{1,0:T(8,128)S(1)} collective-permute-done((f32[16,128]{1,0:T(8,128)S(1)}, f32[16,128]{1,0:T(8,128)S(1)}, u32[]{:S(2)}, u32[]{:S(2)}) %collective-permute-start.7) | collective-permute-done | bytes 8224 | tf_op jit(solution)/shard_map/ppermute | solution.py:341
  25.0 0.0 collective-permute-done.9.refs_7_
  25.0 2.5 %shard_map.69 = f32[4,32,512]{2,1,0:T(8,128)} custom-call(f32[16,128]{1,0:T(8,128)S(1)} %shard_map.68.refs_0_, f32[16,128]{1,0:T(8,128)S(1)} %collective-permute-done.5.refs_1_, f32[16,128]{1,0:T(8,128)S(1)} %collective-permute-done.6.refs_2_, f32[16,128]{1,0:T(8,128)S(1)} %collective-permute-done.7.refs_3_, f32[4,32,512]{2,1,0:T(8,128)S(1)} %shard_map.65.refs_4_, ...), custom_call_target="tpu_custom_call" | custom-call | tf_op jit(solution)/shard_map/pallas_call | solution.py:375
Async XLA Ops:
  0.0 9.5 %collective-permute-start.3 = (f32[4,32,512]{2,1,0:T(8,128)}, f32[4,32,512]{2,1,0:T(8,128)S(1)}, u32[]{:S(2)}, u32[]{:S(2)}) collective-permute-start(f32[4,32,512]{2,1,0:T(8,128)} %state.1), channel_id=1, source_target_pairs={{0,2},{1,3},{2,0},{3,1},{4,6},{5,7},{6,4},{7,5},{8,10},{9,11},{10,... | collective-permute-start | bytes 786440 | tf_op jit(solution)/shard_map/ppermute | solution.py:357
  4.0 20.2 %collective-permute-start.8 = (f32[4,32,512]{2,1,0:T(8,128)S(1)}, f32[4,32,512]{2,1,0:T(8,128)S(1)}, u32[]{:S(2)}, u32[]{:S(2)}) collective-permute-start(f32[4,32,512]{2,1,0:T(8,128)S(1)} %shard_map.65.refs_4_), channel_id=1, source_target_pairs={{0,1},{1,0},{2,3},{3,2},{4,5},{5,4},{6,7},{7,6},{8,9},{9,8},{10,11... | collective-permute-start | bytes 786440 | tf_op jit(solution)/shard_map/ppermute | solution.py:357
  9.5 15.5 %collective-permute-start.9 = (f32[4,32,512]{2,1,0:T(8,128)S(1)}, f32[4,32,512]{2,1,0:T(8,128)S(1)}, u32[]{:S(2)}, u32[]{:S(2)}) collective-permute-start(f32[4,32,512]{2,1,0:T(8,128)S(1)} %collective-permute-done.3.refs_0_.refs_6_), channel_id=1, source_target_pairs={{0,1},{1,0},{2,3},{3,2},{4,5},{5,4},{6,7},{7,6},{8,9},{9,8},{10,11... | collective-permute-start | bytes 786440 | tf_op jit(solution)/shard_map/ppermute | solution.py:357
  10.4 4.5 %collective-permute-start = (f32[8,128]{1,0:T(8,128)S(1)}, f32[8,128]{1,0:T(8,128)S(1)}, u32[]{:S(2)}, u32[]{:S(2)}) collective-permute-start(f32[8,128]{1,0:T(8,128)S(1)} %get-tuple-element.13), channel_id=1, source_target_pairs={{0,4},{1,13},{2,6},{3,15},{4,0},{5,9},{6,2},{7,11},{8,12},{9,5},{1... | collective-permute-start | bytes 12296 | tf_op jit(solution)/shard_map/ppermute | solution.py:339
  12.2 4.5 %collective-permute-start.1 = (f32[8,128]{1,0:T(8,128)S(1)}, f32[8,128]{1,0:T(8,128)S(1)}, u32[]{:S(2)}, u32[]{:S(2)}) collective-permute-start(f32[8,128]{1,0:T(8,128)S(1)} %get-tuple-element.14), channel_id=1, source_target_pairs={{0,8},{4,12},{8,0},{12,4},{1,9},{5,13},{9,1},{13,5},{2,10},{6,14},... | collective-permute-start | bytes 12296 | tf_op jit(solution)/shard_map/ppermute | solution.py:340
  14.8 1.9 %collective-permute-start.2 = (f32[8,128]{1,0:T(8,128)S(1)}, f32[8,128]{1,0:T(8,128)S(1)}, u32[]{:S(2)}, u32[]{:S(2)}) collective-permute-start(f32[8,128]{1,0:T(8,128)S(1)} %collective-permute-done.refs_1_), channel_id=1, source_target_pairs={{0,1},{1,0},{2,3},{3,2},{4,5},{5,4},{6,7},{7,6},{8,9},{9,8},{10,11... | collective-permute-start | bytes 12296 | tf_op jit(solution)/shard_map/ppermute | solution.py:341
  17.4 2.0 %collective-permute-start.4 = (f32[8,256]{1,0:T(8,128)S(1)}, f32[8,256]{1,0:T(8,128)S(1)}, u32[]{:S(2)}, u32[]{:S(2)}) collective-permute-start(f32[8,256]{1,0:T(8,128)S(1)} %shard_map.67.refs_1_), channel_id=1, source_target_pairs={{0,1},{1,0},{2,3},{3,2},{4,5},{5,4},{6,7},{7,6},{8,9},{9,8},{10,11... | collective-permute-start | bytes 24584 | tf_op jit(solution)/shard_map/ppermute | solution.py:444
  19.5 3.7 %collective-permute-start.5 = (f32[16,128]{1,0:T(8,128)S(1)}, f32[16,128]{1,0:T(8,128)S(1)}, u32[]{:S(2)}, u32[]{:S(2)}) collective-permute-start(f32[16,128]{1,0:T(8,128)S(1)} %shard_map.68.refs_0_), channel_id=1, source_target_pairs={{0,4},{1,13},{2,6},{3,15},{4,0},{5,9},{6,2},{7,11},{8,12},{9,5},{1... | collective-permute-start | bytes 24584 | tf_op jit(solution)/shard_map/ppermute | solution.py:339
  19.5 4.7 %collective-permute-start.6 = (f32[16,128]{1,0:T(8,128)S(1)}, f32[16,128]{1,0:T(8,128)S(1)}, u32[]{:S(2)}, u32[]{:S(2)}) collective-permute-start(f32[16,128]{1,0:T(8,128)S(1)} %shard_map.68.refs_0_), channel_id=1, source_target_pairs={{0,8},{4,12},{8,0},{12,4},{1,9},{5,13},{9,1},{13,5},{2,10},{6,14},... | collective-permute-start | bytes 24584 | tf_op jit(solution)/shard_map/ppermute | solution.py:340
  23.2 1.8 %collective-permute-start.7 = (f32[16,128]{1,0:T(8,128)S(1)}, f32[16,128]{1,0:T(8,128)S(1)}, u32[]{:S(2)}, u32[]{:S(2)}) collective-permute-start(f32[16,128]{1,0:T(8,128)S(1)} %collective-permute-done.5.refs_1_), channel_id=1, source_target_pairs={{0,1},{1,0},{2,3},{3,2},{4,5},{5,4},{6,7},{7,6},{8,9},{9,8},{10,11... | collective-permute-start | bytes 24584 | tf_op jit(solution)/shard_map/ppermute | solution.py:341

commit v10 on v8

--- a/solution.py
+++ b/solution.py
@@ -100,8 +100,8 @@
         return jnp.where((column >= half) & (column < half + count), turned, 0.0)
 
     if paired:
-        near = jnp.where(is_odd(paired) == 0, 1, 3)
-        for out, bits, half in zip(outs, (0, near, 2), (0, CAP, 0)):
+        near = jnp.where(is_odd(paired) == 0, 1, 2)
+        for out, bits, half in zip(outs, (0, near, 3), (0, CAP, 0)):
             out[...] = tile(jnp.bitwise_xor(here, bits), half)
     elif direct:
         for shift in range(n_dom):
@@ -335,8 +335,8 @@
     pairs, cross = [], []
     for d in range(n_dom):
         for e in range(n_ens):
-            pairs.append((d * n_ens + e, (d ^ (3 if e % 2 else 1)) * n_ens + e))
-            cross.append((d * n_ens + e, (d ^ 2) * n_ens + (e ^ 1)))
+            pairs.append((d * n_ens + e, (d ^ (2 if e % 2 else 1)) * n_ens + e))
+            cross.append((d * n_ens + e, (d ^ 3) * n_ens + (e ^ 1)))
     near = lax.ppermute(near, ("dom", "ens"), pairs)
     far = lax.ppermute(far, ("dom", "ens"), cross)
     other = lax.ppermute(near, "ens", [(e, e ^ 1) for e in range(n_ens)])

time: 28.2 us -> 27.6 us (0.979)
  starting transfers between devices: 11.6 us -> 10.8 us
    ppermute x2, waiting for transfers between devices: 0.68 us -> 3.41 us  [spread(): far = lax.ppermute(far, ('dom', 'ens'), cross)]
    ppermute x2, starting transfers between devices: 2.01 us -> 4.05 us  [spread(): far = lax.ppermute(far, ('dom', 'ens'), cross)]
    ppermute x2, starting transfers between devices: 2.46 us -> 0.47 us  [spread(): other = lax.ppermute(near, 'ens', [(e, e ^ 1) for e in range(n_ens)])]
    ppermute x2, waiting for transfers between devices: 3.45 us -> 1.85 us  [spread(): near = lax.ppermute(near, ('dom', 'ens'), pairs)]
    ppermute x2, waiting for transfers between devices: 0.96 us -> 0.01 us  [spread(): other = lax.ppermute(near, 'ens', [(e, e ^ 1) for e in range(n_ens)])]
    ppermute x1, starting transfers between devices: 2.18 us -> 1.31 us  [on_device(): values.append(lax.ppermute(values[0], 'ens', pairs))]
  transfers between devices with their start and end apart: 10 -> 10, of which waited for: 7 -> 5; matrix products, arithmetic and copies ran while one was open for 0% -> 0% of each run, Pallas kernels for 9% -> 9%
where the time goes in v10:
time: 27.6 us; the launch traced here: 27.4 us
  waiting for transfers between devices  11.5 us (42%)
  starting transfers between devices  10.8 us (39%)
  Pallas kernels  5.05 us (18%)
    ppermute x3, waiting for transfers between devices, gather_members(): pieces[key ^ bit] = lax.ppermute(pieces[key], 'ens', pairs)  5.44 us
    pallas_call x6, Pallas kernels, call(): pl.pallas_call(kernel, out_shape=out_shape, in_specs=specs or [vmem] * le...  5.05 us
    ppermute x2, starting transfers between devices, spread(): far = lax.ppermute(far, ('dom', 'ens'), cross)  4.05 us
    ppermute x2, waiting for transfers between devices, spread(): far = lax.ppermute(far, ('dom', 'ens'), cross)  3.41 us
    ppermute x3, starting transfers between devices, gather_members(): pieces[key ^ bit] = lax.ppermute(pieces[key], 'ens', pairs)  3.04 us
    ppermute x2, starting transfers between devices, spread(): near = lax.ppermute(near, ('dom', 'ens'), pairs)  1.9 us
    ppermute x2, waiting for transfers between devices, spread(): near = lax.ppermute(near, ('dom', 'ens'), pairs)  1.85 us
    ppermute x1, starting transfers between devices, on_device(): values.append(lax.ppermute(values[0], 'ens', pairs))  1.31 us
  transfers between devices with their start and end apart: 10, of which 5 were waited for; matrix products, arithmetic and copies ran while one was open for 0% of the time, Pallas kernels for 9%

profile of v10, /device:TPU:0, one launch (start us, length us, event | category | flops | bytes accessed | tf_op | source)
XLA Modules:
  0.0 27.4 jit_solution(9189047556305588630)
XLA Ops:
  0.0 3.0 %collective-permute-start.3 = (f32[4,32,512]{2,1,0:T(8,128)}, f32[4,32,512]{2,1,0:T(8,128)S(1)}, u32[]{:S(2)}, u32[]{:S(2)}) collective-permute-start(f32[4,32,512]{2,1,0:T(8,128)} %state.1), channel_id=1, source_target_pairs={{0,2},{1,3},{2,0},{3,1},{4,6},{5,7},{6,4},{7,5},{8,10},{9,11},{10,... | collective-permute-start | bytes 786440 | tf_op jit(solution)/shard_map/ppermute | solution.py:358
  3.0 1.0 %shard_map.65.refs_4_ = f32[4,32,512]{2,1,0:T(8,128)S(1)} custom-call(f32[4,32,512]{2,1,0:T(8,128)} %state.1), custom_call_target="tpu_custom_call" | custom-call | tf_op jit(solution)/shard_map/pallas_call | solution.py:376
  4.0 0.1 collective-permute-start.8
  4.0 5.4 %collective-permute-done.3.refs_0_.refs_6_ = f32[4,32,512]{2,1,0:T(8,128)S(1)} collective-permute-done((f32[4,32,512]{2,1,0:T(8,128)}, f32[4,32,512]{2,1,0:T(8,128)S(1)}, u32[]{:S(2)}, u32[]{:S(2)}) %collective-permute-start.3) | collective-permute-done | bytes 262176 | tf_op jit(solution)/shard_map/ppermute | solution.py:358
  9.5 0.0 collective-permute-start.9
  9.5 0.9 %shard_map.64 = (f32[8,128]{1,0:T(8,128)S(1)}, f32[8,128]{1,0:T(8,128)S(1)}, f32[8,128]{1,0:T(8,128)S(1)}) custom-call(s32[1,4]{1,0:T(1,128)} %refs_0_.1, f32[3,256]{1,0:T(4,128)} %refs_1_.1, s32[1,256]{1,0:T(1,128)} %bitcast.3, f32[1,256]{1,0:T(1,128)} %bitcast.4, f32[1,256]{1,0:T(1,128)} %bitcast.5), custom_call_target="tpu_custom_call" | custom-call | tf_op jit(solution)/shard_map/pallas_call | solution.py:376
  10.4 1.9 %collective-permute-start = (f32[8,128]{1,0:T(8,128)S(1)}, f32[8,128]{1,0:T(8,128)S(1)}, u32[]{:S(2)}, u32[]{:S(2)}) collective-permute-start(f32[8,128]{1,0:T(8,128)S(1)} %get-tuple-element.13), channel_id=1, source_target_pairs={{0,4},{1,9},{2,6},{3,11},{4,0},{5,13},{6,2},{7,15},{8,12},{9,1},{1... | collective-permute-start | bytes 12296 | tf_op jit(solution)/shard_map/ppermute | solution.py:340
  12.2 2.2 %collective-permute-start.1 = (f32[8,128]{1,0:T(8,128)S(1)}, f32[8,128]{1,0:T(8,128)S(1)}, u32[]{:S(2)}, u32[]{:S(2)}) collective-permute-start(f32[8,128]{1,0:T(8,128)S(1)} %get-tuple-element.14), channel_id=1, source_target_pairs={{0,13},{1,12},{2,15},{3,14},{4,9},{5,8},{6,11},{7,10},{8,5},{9,4},... | collective-permute-start | bytes 12296 | tf_op jit(solution)/shard_map/ppermute | solution.py:341
  14.5 0.0 collective-permute-done.refs_1_
  14.5 0.4 %collective-permute-start.2 = (f32[8,128]{1,0:T(8,128)S(1)}, f32[8,128]{1,0:T(8,128)S(1)}, u32[]{:S(2)}, u32[]{:S(2)}) collective-permute-start(f32[8,128]{1,0:T(8,128)S(1)} %collective-permute-done.refs_1_), channel_id=1, source_target_pairs={{0,1},{1,0},{2,3},{3,2},{4,5},{5,4},{6,7},{7,6},{8,9},{9,8},{10,11... | collective-permute-start | bytes 12296 | tf_op jit(solution)/shard_map/ppermute | solution.py:342
  14.8 2.2 %collective-permute-done.1.refs_2_ = f32[8,128]{1,0:T(8,128)S(1)} collective-permute-done((f32[8,128]{1,0:T(8,128)S(1)}, f32[8,128]{1,0:T(8,128)S(1)}, u32[]{:S(2)}, u32[]{:S(2)}) %collective-permute-start.1) | collective-permute-done | bytes 4128 | tf_op jit(solution)/shard_map/ppermute | solution.py:341
  17.1 0.0 collective-permute-done.2.refs_3_
  17.1 0.4 %shard_map.66 = (f32[8,256]{1,0:T(8,128)S(1)}, bf16[512,256]{1,0:T(8,128)(2,1)S(1)}, bf16[512,256]{1,0:T(8,128)(2,1)S(1)}, f32[4,256]{1,0:T(4,128)S(1)}) custom-call(f32[8,128]{1,0:T(8,128)S(1)} %get-tuple-element.12.refs_0_, f32[8,128]{1,0:T(8,128)S(1)} %collective-permute-done.refs_1_, f32[8,128]{1,0:T(8,128)S(1)} %collective-permute-done.1.refs_2_, ...), custom_call_target="tpu_custom_call" | custom-call | tf_op jit(solution)/shard_map/pallas_call | solution.py:376
  17.4 0.3 %shard_map.67.refs_1_ = f32[8,256]{1,0:T(8,128)S(1)} custom-call(f32[8,256]{1,0:T(8,128)S(1)} %get-tuple-element.15.sensors_ref.refs_0_, bf16[512,256]{1,0:T(8,128)(2,1)S(1)} %get-tuple-element.16.high_ref, bf16[512,256]{1,0:T(8,128)(2,1)S(1)} %get-tuple-element.17.low_ref, f32[4,256]{1,0:T(4,128)S(1)} %get-tuple-element.18.values_ref, ...), custom_call_target="tpu_custom_call" | custom-call | tf_op jit(solution)/shard_map/pallas_call | solution.py:376
  17.7 1.3 %collective-permute-start.4 = (f32[8,256]{1,0:T(8,128)S(1)}, f32[8,256]{1,0:T(8,128)S(1)}, u32[]{:S(2)}, u32[]{:S(2)}) collective-permute-start(f32[8,256]{1,0:T(8,128)S(1)} %shard_map.67.refs_1_), channel_id=1, source_target_pairs={{0,1},{1,0},{2,3},{3,2},{4,5},{5,4},{6,7},{7,6},{8,9},{9,8},{10,11... | collective-permute-start | bytes 24584 | tf_op jit(solution)/shard_map/ppermute | solution.py:445
  19.0 0.8 %collective-permute-done.4.refs_2_ = f32[8,256]{1,0:T(8,128)S(1)} collective-permute-done((f32[8,256]{1,0:T(8,128)S(1)}, f32[8,256]{1,0:T(8,128)S(1)}, u32[]{:S(2)}, u32[]{:S(2)}) %collective-permute-start.4) | collective-permute-done | bytes 8224 | tf_op jit(solution)/shard_map/ppermute | solution.py:445
  19.9 0.1 shard_map.68.refs_0_
  20.0 0.0 collective-permute-start.5
  20.0 1.8 %collective-permute-start.6 = (f32[16,128]{1,0:T(8,128)S(1)}, f32[16,128]{1,0:T(8,128)S(1)}, u32[]{:S(2)}, u32[]{:S(2)}) collective-permute-start(f32[16,128]{1,0:T(8,128)S(1)} %shard_map.68.refs_0_), channel_id=1, source_target_pairs={{0,13},{1,12},{2,15},{3,14},{4,9},{5,8},{6,11},{7,10},{8,5},{9,4},... | collective-permute-start | bytes 24584 | tf_op jit(solution)/shard_map/ppermute | solution.py:341
  21.8 1.8 %collective-permute-done.5.refs_1_ = f32[16,128]{1,0:T(8,128)S(1)} collective-permute-done((f32[16,128]{1,0:T(8,128)S(1)}, f32[16,128]{1,0:T(8,128)S(1)}, u32[]{:S(2)}, u32[]{:S(2)}) %collective-permute-start.5) | collective-permute-done | bytes 8224 | tf_op jit(solution)/shard_map/ppermute | solution.py:340
  23.7 0.1 collective-permute-start.7
  23.8 0.0 collective-permute-done.8.refs_5_
  23.8 1.2 %collective-permute-done.6.refs_2_ = f32[16,128]{1,0:T(8,128)S(1)} collective-permute-done((f32[16,128]{1,0:T(8,128)S(1)}, f32[16,128]{1,0:T(8,128)S(1)}, u32[]{:S(2)}, u32[]{:S(2)}) %collective-permute-start.6) | collective-permute-done | bytes 8224 | tf_op jit(solution)/shard_map/ppermute | solution.py:341
  24.9 0.0 collective-permute-done.7.refs_3_
  24.9 0.0 collective-permute-done.9.refs_7_
  24.9 2.5 %shard_map.69 = f32[4,32,512]{2,1,0:T(8,128)} custom-call(f32[16,128]{1,0:T(8,128)S(1)} %shard_map.68.refs_0_, f32[16,128]{1,0:T(8,128)S(1)} %collective-permute-done.5.refs_1_, f32[16,128]{1,0:T(8,128)S(1)} %collective-permute-done.6.refs_2_, f32[16,128]{1,0:T(8,128)S(1)} %collective-permute-done.7.refs_3_, f32[4,32,512]{2,1,0:T(8,128)S(1)} %shard_map.65.refs_4_, ...), custom_call_target="tpu_custom_call" | custom-call | tf_op jit(solution)/shard_map/pallas_call | solution.py:376
Async XLA Ops:
  0.0 9.5 %collective-permute-start.3 = (f32[4,32,512]{2,1,0:T(8,128)}, f32[4,32,512]{2,1,0:T(8,128)S(1)}, u32[]{:S(2)}, u32[]{:S(2)}) collective-permute-start(f32[4,32,512]{2,1,0:T(8,128)} %state.1), channel_id=1, source_target_pairs={{0,2},{1,3},{2,0},{3,1},{4,6},{5,7},{6,4},{7,5},{8,10},{9,11},{10,... | collective-permute-start | bytes 786440 | tf_op jit(solution)/shard_map/ppermute | solution.py:358
  4.0 19.8 %collective-permute-start.8 = (f32[4,32,512]{2,1,0:T(8,128)S(1)}, f32[4,32,512]{2,1,0:T(8,128)S(1)}, u32[]{:S(2)}, u32[]{:S(2)}) collective-permute-start(f32[4,32,512]{2,1,0:T(8,128)S(1)} %shard_map.65.refs_4_), channel_id=1, source_target_pairs={{0,1},{1,0},{2,3},{3,2},{4,5},{5,4},{6,7},{7,6},{8,9},{9,8},{10,11... | collective-permute-start | bytes 786440 | tf_op jit(solution)/shard_map/ppermute | solution.py:358
  9.5 15.5 %collective-permute-start.9 = (f32[4,32,512]{2,1,0:T(8,128)S(1)}, f32[4,32,512]{2,1,0:T(8,128)S(1)}, u32[]{:S(2)}, u32[]{:S(2)}) collective-permute-start(f32[4,32,512]{2,1,0:T(8,128)S(1)} %collective-permute-done.3.refs_0_.refs_6_), channel_id=1, source_target_pairs={{0,1},{1,0},{2,3},{3,2},{4,5},{5,4},{6,7},{7,6},{8,9},{9,8},{10,11... | collective-permute-start | bytes 786440 | tf_op jit(solution)/shard_map/ppermute | solution.py:358
  10.4 4.1 %collective-permute-start = (f32[8,128]{1,0:T(8,128)S(1)}, f32[8,128]{1,0:T(8,128)S(1)}, u32[]{:S(2)}, u32[]{:S(2)}) collective-permute-start(f32[8,128]{1,0:T(8,128)S(1)} %get-tuple-element.13), channel_id=1, source_target_pairs={{0,4},{1,9},{2,6},{3,11},{4,0},{5,13},{6,2},{7,15},{8,12},{9,1},{1... | collective-permute-start | bytes 12296 | tf_op jit(solution)/shard_map/ppermute | solution.py:340
  12.2 4.8 %collective-permute-start.1 = (f32[8,128]{1,0:T(8,128)S(1)}, f32[8,128]{1,0:T(8,128)S(1)}, u32[]{:S(2)}, u32[]{:S(2)}) collective-permute-start(f32[8,128]{1,0:T(8,128)S(1)} %get-tuple-element.14), channel_id=1, source_target_pairs={{0,13},{1,12},{2,15},{3,14},{4,9},{5,8},{6,11},{7,10},{8,5},{9,4},... | collective-permute-start | bytes 12296 | tf_op jit(solution)/shard_map/ppermute | solution.py:341
  14.5 2.6 %collective-permute-start.2 = (f32[8,128]{1,0:T(8,128)S(1)}, f32[8,128]{1,0:T(8,128)S(1)}, u32[]{:S(2)}, u32[]{:S(2)}) collective-permute-start(f32[8,128]{1,0:T(8,128)S(1)} %collective-permute-done.refs_1_), channel_id=1, source_target_pairs={{0,1},{1,0},{2,3},{3,2},{4,5},{5,4},{6,7},{7,6},{8,9},{9,8},{10,11... | collective-permute-start | bytes 12296 | tf_op jit(solution)/shard_map/ppermute | solution.py:342
  17.7 2.1 %collective-permute-start.4 = (f32[8,256]{1,0:T(8,128)S(1)}, f32[8,256]{1,0:T(8,128)S(1)}, u32[]{:S(2)}, u32[]{:S(2)}) collective-permute-start(f32[8,256]{1,0:T(8,128)S(1)} %shard_map.67.refs_1_), channel_id=1, source_target_pairs={{0,1},{1,0},{2,3},{3,2},{4,5},{5,4},{6,7},{7,6},{8,9},{9,8},{10,11... | collective-permute-start | bytes 24584 | tf_op jit(solution)/shard_map/ppermute | solution.py:445
  20.0 3.7 %collective-permute-start.5 = (f32[16,128]{1,0:T(8,128)S(1)}, f32[16,128]{1,0:T(8,128)S(1)}, u32[]{:S(2)}, u32[]{:S(2)}) collective-permute-start(f32[16,128]{1,0:T(8,128)S(1)} %shard_map.68.refs_0_), channel_id=1, source_target_pairs={{0,4},{1,9},{2,6},{3,11},{4,0},{5,13},{6,2},{7,15},{8,12},{9,1},{1... | collective-permute-start | bytes 24584 | tf_op jit(solution)/shard_map/ppermute | solution.py:340
  20.0 5.0 %collective-permute-start.6 = (f32[16,128]{1,0:T(8,128)S(1)}, f32[16,128]{1,0:T(8,128)S(1)}, u32[]{:S(2)}, u32[]{:S(2)}) collective-permute-start(f32[16,128]{1,0:T(8,128)S(1)} %shard_map.68.refs_0_), channel_id=1, source_target_pairs={{0,13},{1,12},{2,15},{3,14},{4,9},{5,8},{6,11},{7,10},{8,5},{9,4},... | collective-permute-start | bytes 24584 | tf_op jit(solution)/shard_map/ppermute | solution.py:341
  23.7 1.3 %collective-permute-start.7 = (f32[16,128]{1,0:T(8,128)S(1)}, f32[16,128]{1,0:T(8,128)S(1)}, u32[]{:S(2)}, u32[]{:S(2)}) collective-permute-start(f32[16,128]{1,0:T(8,128)S(1)} %collective-permute-done.5.refs_1_), channel_id=1, source_target_pairs={{0,1},{1,0},{2,3},{3,2},{4,5},{5,4},{6,7},{7,6},{8,9},{9,8},{10,11... | collective-permute-start | bytes 24584 | tf_op jit(solution)/shard_map/ppermute | solution.py:342

commit v11 on v9

--- a/solution.py
+++ b/solution.py
@@ -64,6 +64,26 @@
     copy = pltpu.make_async_copy(state, own, sem)
     copy.start()
     copy.wait()
+
+
+def early_kernel(*refs):
+    @pl.when(is_odd(True) == 1)
+    def _():
+        pack_kernel(True, True, *refs)
+
+
+def later_kernel(early_count, *refs):
+    early, refs = refs[:early_count], refs[early_count:]
+    odd = is_odd(True)
+
+    @pl.when(odd == 1)
+    def _():
+        for source, out in zip(early, refs[5 : 5 + early_count]):
+            out[...] = source[...]
+
+    @pl.when(odd == 0)
+    def _():
+        pack_kernel(True, True, *refs)
 
 
 def pack_kernel(direct, paired, counts, coords, owner, obs, weight, *rest):
@@ -393,23 +413,34 @@
         members = local_members * n_ens
         tile_shape = (8, 2 * CAP)
         inputs = [counts, coords, owner_local[None], obs_value[None], obs_weight[None]]
-        tiles = call(
-            lambda *refs: pack_kernel(direct, paired, *refs),
-            [shape(tile_shape)] * (3 if paired else n_dom)
-            if direct
-            else [shape((n_dom,) + tile_shape)],
-            [in_hbm(value) for value in inputs],
-            [hbm] * len(inputs),
-            [
-                pltpu.SMEM(counts.shape, jnp.int32),
-                pltpu.VMEM(coords.shape, F32),
-                pltpu.VMEM((1, slots), jnp.int32),
-                pltpu.VMEM((1, slots), F32),
-                pltpu.VMEM((1, slots), F32),
-                pltpu.VMEM((8, slots), F32),
-                pltpu.SemaphoreType.DMA((5,)),
-            ],
-        )
+        pack_scratch = [
+            pltpu.SMEM(counts.shape, jnp.int32),
+            pltpu.VMEM(coords.shape, F32),
+            pltpu.VMEM((1, slots), jnp.int32),
+            pltpu.VMEM((1, slots), F32),
+            pltpu.VMEM((1, slots), F32),
+            pltpu.VMEM((8, slots), F32),
+            pltpu.SemaphoreType.DMA((5,)),
+        ]
+        inputs = [in_hbm(value) for value in inputs]
+        if paired:
+            made = [shape(tile_shape)] * 3
+            tiles = call(early_kernel, made, inputs, [hbm] * len(inputs), pack_scratch)
+            tiles = call(
+                lambda *refs: later_kernel(len(made), *refs),
+                made,
+                list(tiles) + inputs,
+                [vmem] * len(made) + [hbm] * len(inputs),
+                pack_scratch,
+            )
+        else:
+            tiles = call(
+                lambda *refs: pack_kernel(direct, paired, *refs),
+                [shape(tile_shape)] * n_dom if direct else [shape((n_dom,) + tile_shape)],
+                inputs,
+                [hbm] * len(inputs),
+                pack_scratch,
+            )
         if direct:
             tiles = spread(tiles, n_dom, n_ens)
         else:

time: 27.7 us -> 27.7 us (level)
    pallas_call x6 -> x7, Pallas kernels: 5.05 us -> 5.11 us  [call(): pl.pallas_call(kernel, out_shape=out_shape, in_specs=specs or [vmem] * le...]
  transfers between devices with their start and end apart: 10 -> 10, of which waited for: 5 -> 5; matrix products, arithmetic and copies ran while one was open for 0% -> 0% of each run, Pallas kernels for 9% -> 10%
where the time goes in v11:
time: 27.7 us; the launch traced here: 27.6 us
  starting transfers between devices  13.3 us (48%)
  waiting for transfers between devices  9.1 us (33%)
  Pallas kernels  5.11 us (18%)
    ppermute x2, starting transfers between devices, spread(): far = lax.ppermute(far, 'dom', [(d, d ^ 2) for d in range(n_dom)])  5.52 us
    ppermute x3, waiting for transfers between devices, gather_members(): pieces[key ^ bit] = lax.ppermute(pieces[key], 'ens', pairs)  5.44 us
    pallas_call x7, Pallas kernels, call(): pl.pallas_call(kernel, out_shape=out_shape, in_specs=specs or [vmem] * le...  5.11 us
    ppermute x3, starting transfers between devices, gather_members(): pieces[key ^ bit] = lax.ppermute(pieces[key], 'ens', pairs)  3.04 us
    ppermute x2, starting transfers between devices, spread(): near = lax.ppermute(near, ('dom', 'ens'), pairs)  1.9 us
    ppermute x2, starting transfers between devices, spread(): other = lax.ppermute(near, 'ens', [(e, e ^ 1) for e in range(n_ens)])  1.65 us
    ppermute x2, waiting for transfers between devices, spread(): far = lax.ppermute(far, 'dom', [(d, d ^ 2) for d in range(n_dom)])  1.26 us
    ppermute x1, starting transfers between devices, on_device(): values.append(lax.ppermute(values[0], 'ens', pairs))  1.17 us
  transfers between devices with their start and end apart: 10, of which 5 were waited for; matrix products, arithmetic and copies ran while one was open for 0% of the time, Pallas kernels for 10%

profile of v11, /device:TPU:0, one launch (start us, length us, event | category | flops | bytes accessed | tf_op | source)
XLA Modules:
  0.0 27.6 jit_solution(8978260364689263148)
XLA Ops:
  0.0 3.0 %collective-permute-start.3 = (f32[4,32,512]{2,1,0:T(8,128)}, f32[4,32,512]{2,1,0:T(8,128)S(1)}, u32[]{:S(2)}, u32[]{:S(2)}) collective-permute-start(f32[4,32,512]{2,1,0:T(8,128)} %state.1), channel_id=1, source_target_pairs={{0,2},{1,3},{2,0},{3,1},{4,6},{5,7},{6,4},{7,5},{8,10},{9,11},{10,... | collective-permute-start | bytes 786440 | tf_op jit(solution)/shard_map/ppermute | solution.py:377
  3.0 1.0 %shard_map.66.refs_4_ = f32[4,32,512]{2,1,0:T(8,128)S(1)} custom-call(f32[4,32,512]{2,1,0:T(8,128)} %state.1), custom_call_target="tpu_custom_call" | custom-call | tf_op jit(solution)/shard_map/pallas_call | solution.py:395
  4.0 0.1 collective-permute-start.8
  4.0 5.4 %collective-permute-done.3.refs_0_.refs_6_ = f32[4,32,512]{2,1,0:T(8,128)S(1)} collective-permute-done((f32[4,32,512]{2,1,0:T(8,128)}, f32[4,32,512]{2,1,0:T(8,128)S(1)}, u32[]{:S(2)}, u32[]{:S(2)}) %collective-permute-start.3) | collective-permute-done | bytes 262176 | tf_op jit(solution)/shard_map/ppermute | solution.py:377
  9.5 0.0 collective-permute-start.9
  9.5 0.9 %shard_map.65 = (f32[8,128]{1,0:T(8,128)S(1)}, f32[8,128]{1,0:T(8,128)S(1)}, f32[8,128]{1,0:T(8,128)S(1)}) custom-call(f32[8,128]{1,0:T(8,128)S(1)} %get-tuple-element.15.refs_0_, f32[8,128]{1,0:T(8,128)S(1)} %get-tuple-element.16.refs_1_, f32[8,128]{1,0:T(8,128)S(1)} %get-tuple-element.17.refs_2_, s32[1,4]{1,0:T(1,128)} %refs_3_.1, f32[3,256]{1,0:T(4,128)} %refs_4_.1, ...), custom_call_target="tpu_custom_call" | custom-call | tf_op jit(solution)/shard_map/pallas_call | solution.py:395
  10.4 1.9 %collective-permute-start = (f32[8,128]{1,0:T(8,128)S(1)}, f32[8,128]{1,0:T(8,128)S(1)}, u32[]{:S(2)}, u32[]{:S(2)}) collective-permute-start(f32[8,128]{1,0:T(8,128)S(1)} %get-tuple-element.19), channel_id=1, source_target_pairs={{0,4},{1,13},{2,6},{3,15},{4,0},{5,9},{6,2},{7,11},{8,12},{9,5},{1... | collective-permute-start | bytes 12296 | tf_op jit(solution)/shard_map/ppermute | solution.py:359
  12.3 2.6 %collective-permute-start.1 = (f32[8,128]{1,0:T(8,128)S(1)}, f32[8,128]{1,0:T(8,128)S(1)}, u32[]{:S(2)}, u32[]{:S(2)}) collective-permute-start(f32[8,128]{1,0:T(8,128)S(1)} %get-tuple-element.20), channel_id=1, source_target_pairs={{0,8},{4,12},{8,0},{12,4},{1,9},{5,13},{9,1},{13,5},{2,10},{6,14},... | collective-permute-start | bytes 12296 | tf_op jit(solution)/shard_map/ppermute | solution.py:360
  14.9 0.0 collective-permute-done.refs_1_
  14.9 0.7 %collective-permute-start.2 = (f32[8,128]{1,0:T(8,128)S(1)}, f32[8,128]{1,0:T(8,128)S(1)}, u32[]{:S(2)}, u32[]{:S(2)}) collective-permute-start(f32[8,128]{1,0:T(8,128)S(1)} %collective-permute-done.refs_1_), channel_id=1, source_target_pairs={{0,1},{1,0},{2,3},{3,2},{4,5},{5,4},{6,7},{7,6},{8,9},{9,8},{10,11... | collective-permute-start | bytes 12296 | tf_op jit(solution)/shard_map/ppermute | solution.py:361
  15.6 1.3 %collective-permute-done.1.refs_2_ = f32[8,128]{1,0:T(8,128)S(1)} collective-permute-done((f32[8,128]{1,0:T(8,128)S(1)}, f32[8,128]{1,0:T(8,128)S(1)}, u32[]{:S(2)}, u32[]{:S(2)}) %collective-permute-start.1) | collective-permute-done | bytes 4128 | tf_op jit(solution)/shard_map/ppermute | solution.py:360
  16.8 0.0 collective-permute-done.2.refs_3_
  16.8 0.3 %shard_map.67 = (f32[8,256]{1,0:T(8,128)S(1)}, bf16[512,256]{1,0:T(8,128)(2,1)S(1)}, bf16[512,256]{1,0:T(8,128)(2,1)S(1)}, f32[4,256]{1,0:T(4,128)S(1)}) custom-call(f32[8,128]{1,0:T(8,128)S(1)} %get-tuple-element.18.refs_0_, f32[8,128]{1,0:T(8,128)S(1)} %collective-permute-done.refs_1_, f32[8,128]{1,0:T(8,128)S(1)} %collective-permute-done.1.refs_2_, ...), custom_call_target="tpu_custom_call" | custom-call | tf_op jit(solution)/shard_map/pallas_call | solution.py:395
  17.2 0.3 %shard_map.68.refs_1_ = f32[8,256]{1,0:T(8,128)S(1)} custom-call(f32[8,256]{1,0:T(8,128)S(1)} %get-tuple-element.21.sensors_ref.refs_0_, bf16[512,256]{1,0:T(8,128)(2,1)S(1)} %get-tuple-element.22.high_ref, bf16[512,256]{1,0:T(8,128)(2,1)S(1)} %get-tuple-element.23.low_ref, f32[4,256]{1,0:T(4,128)S(1)} %get-tuple-element.24.values_ref, ...), custom_call_target="tpu_custom_call" | custom-call | tf_op jit(solution)/shard_map/pallas_call | solution.py:395
  17.5 1.2 %collective-permute-start.4 = (f32[8,256]{1,0:T(8,128)S(1)}, f32[8,256]{1,0:T(8,128)S(1)}, u32[]{:S(2)}, u32[]{:S(2)}) collective-permute-start(f32[8,256]{1,0:T(8,128)S(1)} %shard_map.68.refs_1_), channel_id=1, source_target_pairs={{0,1},{1,0},{2,3},{3,2},{4,5},{5,4},{6,7},{7,6},{8,9},{9,8},{10,11... | collective-permute-start | bytes 24584 | tf_op jit(solution)/shard_map/ppermute | solution.py:475
  18.6 0.8 %collective-permute-done.4.refs_2_ = f32[8,256]{1,0:T(8,128)S(1)} collective-permute-done((f32[8,256]{1,0:T(8,128)S(1)}, f32[8,256]{1,0:T(8,128)S(1)}, u32[]{:S(2)}, u32[]{:S(2)}) %collective-permute-start.4) | collective-permute-done | bytes 8224 | tf_op jit(solution)/shard_map/ppermute | solution.py:475
  19.5 0.1 shard_map.69.refs_0_
  19.6 0.0 collective-permute-start.5
  19.6 2.9 %collective-permute-start.6 = (f32[16,128]{1,0:T(8,128)S(1)}, f32[16,128]{1,0:T(8,128)S(1)}, u32[]{:S(2)}, u32[]{:S(2)}) collective-permute-start(f32[16,128]{1,0:T(8,128)S(1)} %shard_map.69.refs_0_), channel_id=1, source_target_pairs={{0,8},{4,12},{8,0},{12,4},{1,9},{5,13},{9,1},{13,5},{2,10},{6,14},... | collective-permute-start | bytes 24584 | tf_op jit(solution)/shard_map/ppermute | solution.py:360
  22.5 0.7 %collective-permute-done.5.refs_1_ = f32[16,128]{1,0:T(8,128)S(1)} collective-permute-done((f32[16,128]{1,0:T(8,128)S(1)}, f32[16,128]{1,0:T(8,128)S(1)}, u32[]{:S(2)}, u32[]{:S(2)}) %collective-permute-start.5) | collective-permute-done | bytes 8224 | tf_op jit(solution)/shard_map/ppermute | solution.py:359
  23.3 1.0 %collective-permute-start.7 = (f32[16,128]{1,0:T(8,128)S(1)}, f32[16,128]{1,0:T(8,128)S(1)}, u32[]{:S(2)}, u32[]{:S(2)}) collective-permute-start(f32[16,128]{1,0:T(8,128)S(1)} %collective-permute-done.5.refs_1_), channel_id=1, source_target_pairs={{0,1},{1,0},{2,3},{3,2},{4,5},{5,4},{6,7},{7,6},{8,9},{9,8},{10,11... | collective-permute-start | bytes 24584 | tf_op jit(solution)/shard_map/ppermute | solution.py:361
  24.3 0.0 collective-permute-done.8.refs_5_
  24.3 0.0 collective-permute-done.6.refs_2_
  24.3 0.8 %collective-permute-done.7.refs_3_ = f32[16,128]{1,0:T(8,128)S(1)} collective-permute-done((f32[16,128]{1,0:T(8,128)S(1)}, f32[16,128]{1,0:T(8,128)S(1)}, u32[]{:S(2)}, u32[]{:S(2)}) %collective-permute-start.7) | collective-permute-done | bytes 8224 | tf_op jit(solution)/shard_map/ppermute | solution.py:361
  25.1 0.0 collective-permute-done.9.refs_7_
  25.1 2.5 %shard_map.70 = f32[4,32,512]{2,1,0:T(8,128)} custom-call(f32[16,128]{1,0:T(8,128)S(1)} %shard_map.69.refs_0_, f32[16,128]{1,0:T(8,128)S(1)} %collective-permute-done.5.refs_1_, f32[16,128]{1,0:T(8,128)S(1)} %collective-permute-done.6.refs_2_, f32[16,128]{1,0:T(8,128)S(1)} %collective-permute-done.7.refs_3_, f32[4,32,512]{2,1,0:T(8,128)S(1)} %shard_map.66.refs_4_, ...), custom_call_target="tpu_custom_call" | custom-call | tf_op jit(solution)/shard_map/pallas_call | solution.py:395
  (1 shorter events, 0.0 us)
Async XLA Ops:
  0.0 9.5 %collective-permute-start.3 = (f32[4,32,512]{2,1,0:T(8,128)}, f32[4,32,512]{2,1,0:T(8,128)S(1)}, u32[]{:S(2)}, u32[]{:S(2)}) collective-permute-start(f32[4,32,512]{2,1,0:T(8,128)} %state.1), channel_id=1, source_target_pairs={{0,2},{1,3},{2,0},{3,1},{4,6},{5,7},{6,4},{7,5},{8,10},{9,11},{10,... | collective-permute-start | bytes 786440 | tf_op jit(solution)/shard_map/ppermute | solution.py:377
  4.0 20.3 %collective-permute-start.8 = (f32[4,32,512]{2,1,0:T(8,128)S(1)}, f32[4,32,512]{2,1,0:T(8,128)S(1)}, u32[]{:S(2)}, u32[]{:S(2)}) collective-permute-start(f32[4,32,512]{2,1,0:T(8,128)S(1)} %shard_map.66.refs_4_), channel_id=1, source_target_pairs={{0,1},{1,0},{2,3},{3,2},{4,5},{5,4},{6,7},{7,6},{8,9},{9,8},{10,11... | collective-permute-start | bytes 786440 | tf_op jit(solution)/shard_map/ppermute | solution.py:377
  9.5 15.6 %collective-permute-start.9 = (f32[4,32,512]{2,1,0:T(8,128)S(1)}, f32[4,32,512]{2,1,0:T(8,128)S(1)}, u32[]{:S(2)}, u32[]{:S(2)}) collective-permute-start(f32[4,32,512]{2,1,0:T(8,128)S(1)} %collective-permute-done.3.refs_0_.refs_6_), channel_id=1, source_target_pairs={{0,1},{1,0},{2,3},{3,2},{4,5},{5,4},{6,7},{7,6},{8,9},{9,8},{10,11... | collective-permute-start | bytes 786440 | tf_op jit(solution)/shard_map/ppermute | solution.py:377
  10.4 4.5 %collective-permute-start = (f32[8,128]{1,0:T(8,128)S(1)}, f32[8,128]{1,0:T(8,128)S(1)}, u32[]{:S(2)}, u32[]{:S(2)}) collective-permute-start(f32[8,128]{1,0:T(8,128)S(1)} %get-tuple-element.19), channel_id=1, source_target_pairs={{0,4},{1,13},{2,6},{3,15},{4,0},{5,9},{6,2},{7,11},{8,12},{9,5},{1... | collective-permute-start | bytes 12296 | tf_op jit(solution)/shard_map/ppermute | solution.py:359
  12.3 4.5 %collective-permute-start.1 = (f32[8,128]{1,0:T(8,128)S(1)}, f32[8,128]{1,0:T(8,128)S(1)}, u32[]{:S(2)}, u32[]{:S(2)}) collective-permute-start(f32[8,128]{1,0:T(8,128)S(1)} %get-tuple-element.20), channel_id=1, source_target_pairs={{0,8},{4,12},{8,0},{12,4},{1,9},{5,13},{9,1},{13,5},{2,10},{6,14},... | collective-permute-start | bytes 12296 | tf_op jit(solution)/shard_map/ppermute | solution.py:360
  14.9 1.9 %collective-permute-start.2 = (f32[8,128]{1,0:T(8,128)S(1)}, f32[8,128]{1,0:T(8,128)S(1)}, u32[]{:S(2)}, u32[]{:S(2)}) collective-permute-start(f32[8,128]{1,0:T(8,128)S(1)} %collective-permute-done.refs_1_), channel_id=1, source_target_pairs={{0,1},{1,0},{2,3},{3,2},{4,5},{5,4},{6,7},{7,6},{8,9},{9,8},{10,11... | collective-permute-start | bytes 12296 | tf_op jit(solution)/shard_map/ppermute | solution.py:361
  17.5 2.0 %collective-permute-start.4 = (f32[8,256]{1,0:T(8,128)S(1)}, f32[8,256]{1,0:T(8,128)S(1)}, u32[]{:S(2)}, u32[]{:S(2)}) collective-permute-start(f32[8,256]{1,0:T(8,128)S(1)} %shard_map.68.refs_1_), channel_id=1, source_target_pairs={{0,1},{1,0},{2,3},{3,2},{4,5},{5,4},{6,7},{7,6},{8,9},{9,8},{10,11... | collective-permute-start | bytes 24584 | tf_op jit(solution)/shard_map/ppermute | solution.py:475
  19.6 3.7 %collective-permute-start.5 = (f32[16,128]{1,0:T(8,128)S(1)}, f32[16,128]{1,0:T(8,128)S(1)}, u32[]{:S(2)}, u32[]{:S(2)}) collective-permute-start(f32[16,128]{1,0:T(8,128)S(1)} %shard_map.69.refs_0_), channel_id=1, source_target_pairs={{0,4},{1,13},{2,6},{3,15},{4,0},{5,9},{6,2},{7,11},{8,12},{9,5},{1... | collective-permute-start | bytes 24584 | tf_op jit(solution)/shard_map/ppermute | solution.py:359
  19.6 4.7 %collective-permute-start.6 = (f32[16,128]{1,0:T(8,128)S(1)}, f32[16,128]{1,0:T(8,128)S(1)}, u32[]{:S(2)}, u32[]{:S(2)}) collective-permute-start(f32[16,128]{1,0:T(8,128)S(1)} %shard_map.69.refs_0_), channel_id=1, source_target_pairs={{0,8},{4,12},{8,0},{12,4},{1,9},{5,13},{9,1},{13,5},{2,10},{6,14},... | collective-permute-start | bytes 24584 | tf_op jit(solution)/shard_map/ppermute | solution.py:360
  23.3 1.8 %collective-permute-start.7 = (f32[16,128]{1,0:T(8,128)S(1)}, f32[16,128]{1,0:T(8,128)S(1)}, u32[]{:S(2)}, u32[]{:S(2)}) collective-permute-start(f32[16,128]{1,0:T(8,128)S(1)} %collective-permute-done.5.refs_1_), channel_id=1, source_target_pairs={{0,1},{1,0},{2,3},{3,2},{4,5},{5,4},{6,7},{7,6},{8,9},{9,8},{10,11... | collective-permute-start | bytes 24584 | tf_op jit(solution)/shard_map/ppermute | solution.py:361

commit v12 on v9

--- a/solution.py
+++ b/solution.py
@@ -325,19 +325,20 @@
     return list(range(0, n_ens, 2)) + list(range(1, n_ens, 2))
 
 
-def spread(values, n_dom, n_ens):
+def spread(values, n_dom, n_ens, bits=(1, 3, 2), crossing=0):
     if not is_paired(n_dom, n_ens):
         return [values[0]] + [
             lax.ppermute(values[s], "dom", [(d, (d + s) % n_dom) for d in range(n_dom)])
             for s in range(1, n_dom)
         ]
     here, near, far = values
-    pairs = []
+    near_pairs, far_pairs = [], []
     for d in range(n_dom):
         for e in range(n_ens):
-            pairs.append((d * n_ens + e, (d ^ (3 if e % 2 else 1)) * n_ens + e))
-    near = lax.ppermute(near, ("dom", "ens"), pairs)
-    far = lax.ppermute(far, "dom", [(d, d ^ 2) for d in range(n_dom)])
+            near_pairs.append((d * n_ens + e, (d ^ bits[e % 2]) * n_ens + e))
+            far_pairs.append((d * n_ens + e, (d ^ bits[2]) * n_ens + (e ^ crossing)))
+    near = lax.ppermute(near, ("dom", "ens"), near_pairs)
+    far = lax.ppermute(far, ("dom", "ens"), far_pairs)
     other = lax.ppermute(near, "ens", [(e, e ^ 1) for e in range(n_ens)])
     return [here, near, far, other]
 
@@ -446,7 +447,8 @@
             lambda *refs: cross_kernel(halves, *refs), shape((members, LANES)), [sensors] + values
         )
         if direct:
-            sums = spread([partial_sum] * (3 if paired else n_dom), n_dom, n_ens)
+            copies = [partial_sum] * (3 if paired else n_dom)
+            sums = spread(copies, n_dom, n_ens, bits=(2, 3, 1), crossing=1)
         else:
             sums = [lax.psum(partial_sum, "dom")]
         return call(

time: 27.7 us -> 27.9 us (level)
  waiting for transfers between devices: 9.09 us -> 11.3 us
  starting transfers between devices: 13.3 us -> 11.4 us
    ppermute x4, waiting for transfers between devices: 2 us -> 4.19 us  [the longest x2 2.67 us: spread(): near = lax.ppermute(near, ('dom', 'ens'), near_pairs)]
    ppermute x4, starting transfers between devices: 7.43 us -> 6.41 us  [the longest x2 3.76 us: spread(): near = lax.ppermute(near, ('dom', 'ens'), near_pairs)]
    ppermute x2, starting transfers between devices: 1.65 us -> 0.75 us  [spread(): other = lax.ppermute(near, 'ens', [(e, e ^ 1) for e in range(n_ens)])]
  transfers between devices with their start and end apart: 10 -> 10, of which waited for: 5 -> 6; matrix products, arithmetic and copies ran while one was open for 0% -> 0% of each run, Pallas kernels for 9% -> 9%
where the time goes in v12:
time: 27.9 us; the launch traced here: 27.7 us
  starting transfers between devices  11.4 us (41%)
  waiting for transfers between devices  11.3 us (41%)
  Pallas kernels  5.05 us (18%)
    ppermute x3, waiting for transfers between devices, gather_members(): pieces[key ^ bit] = lax.ppermute(pieces[key], 'ens', pairs)  5.44 us
    pallas_call x6, Pallas kernels, call(): pl.pallas_call(kernel, out_shape=out_shape, in_specs=specs or [vmem] * le...  5.05 us
    ppermute x2, starting transfers between devices, spread(): near = lax.ppermute(near, ('dom', 'ens'), near_pairs)  3.76 us
    ppermute x3, starting transfers between devices, gather_members(): pieces[key ^ bit] = lax.ppermute(pieces[key], 'ens', pairs)  3.04 us
    ppermute x2, waiting for transfers between devices, spread(): near = lax.ppermute(near, ('dom', 'ens'), near_pairs)  2.67 us
    ppermute x2, starting transfers between devices, spread(): far = lax.ppermute(far, ('dom', 'ens'), far_pairs)  2.64 us
    ppermute x2, waiting for transfers between devices, spread(): far = lax.ppermute(far, ('dom', 'ens'), far_pairs)  1.52 us
    ppermute x1, starting transfers between devices, on_device(): values.append(lax.ppermute(values[0], 'ens', pairs))  1.17 us
  transfers between devices with their start and end apart: 10, of which 6 were waited for; matrix products, arithmetic and copies ran while one was open for 0% of the time, Pallas kernels for 9%

profile of v12, /device:TPU:0, one launch (start us, length us, event | category | flops | bytes accessed | tf_op | source)
XLA Modules:
  0.0 27.7 jit_solution(6674263424799717581)
XLA Ops:
  0.0 3.0 %collective-permute-start.3 = (f32[4,32,512]{2,1,0:T(8,128)}, f32[4,32,512]{2,1,0:T(8,128)S(1)}, u32[]{:S(2)}, u32[]{:S(2)}) collective-permute-start(f32[4,32,512]{2,1,0:T(8,128)} %state.1), channel_id=1, source_target_pairs={{0,2},{1,3},{2,0},{3,1},{4,6},{5,7},{6,4},{7,5},{8,10},{9,11},{10,... | collective-permute-start | bytes 786440 | tf_op jit(solution)/shard_map/ppermute | solution.py:358
  3.0 1.0 %shard_map.65.refs_4_ = f32[4,32,512]{2,1,0:T(8,128)S(1)} custom-call(f32[4,32,512]{2,1,0:T(8,128)} %state.1), custom_call_target="tpu_custom_call" | custom-call | tf_op jit(solution)/shard_map/pallas_call | solution.py:376
  4.0 0.1 collective-permute-start.8
  4.0 5.4 %collective-permute-done.3.refs_0_.refs_6_ = f32[4,32,512]{2,1,0:T(8,128)S(1)} collective-permute-done((f32[4,32,512]{2,1,0:T(8,128)}, f32[4,32,512]{2,1,0:T(8,128)S(1)}, u32[]{:S(2)}, u32[]{:S(2)}) %collective-permute-start.3) | collective-permute-done | bytes 262176 | tf_op jit(solution)/shard_map/ppermute | solution.py:358
  9.5 0.0 collective-permute-start.9
  9.5 0.9 %shard_map.64 = (f32[8,128]{1,0:T(8,128)S(1)}, f32[8,128]{1,0:T(8,128)S(1)}, f32[8,128]{1,0:T(8,128)S(1)}) custom-call(s32[1,4]{1,0:T(1,128)} %refs_0_.1, f32[3,256]{1,0:T(4,128)} %refs_1_.1, s32[1,256]{1,0:T(1,128)} %bitcast.3, f32[1,256]{1,0:T(1,128)} %bitcast.4, f32[1,256]{1,0:T(1,128)} %bitcast.5), custom_call_target="tpu_custom_call" | custom-call | tf_op jit(solution)/shard_map/pallas_call | solution.py:376
  10.4 1.9 %collective-permute-start = (f32[8,128]{1,0:T(8,128)S(1)}, f32[8,128]{1,0:T(8,128)S(1)}, u32[]{:S(2)}, u32[]{:S(2)}) collective-permute-start(f32[8,128]{1,0:T(8,128)S(1)} %get-tuple-element.13), channel_id=1, source_target_pairs={{0,4},{1,13},{2,6},{3,15},{4,0},{5,9},{6,2},{7,11},{8,12},{9,5},{1... | collective-permute-start | bytes 12296 | tf_op jit(solution)/shard_map/ppermute | solution.py:340
  12.2 2.6 %collective-permute-start.1 = (f32[8,128]{1,0:T(8,128)S(1)}, f32[8,128]{1,0:T(8,128)S(1)}, u32[]{:S(2)}, u32[]{:S(2)}) collective-permute-start(f32[8,128]{1,0:T(8,128)S(1)} %get-tuple-element.14), channel_id=1, source_target_pairs={{0,8},{1,9},{2,10},{3,11},{4,12},{5,13},{6,14},{7,15},{8,0},{9,1},... | collective-permute-start | bytes 12296 | tf_op jit(solution)/shard_map/ppermute | solution.py:341
  14.8 0.0 collective-permute-done.refs_1_
  14.8 0.7 %collective-permute-start.2 = (f32[8,128]{1,0:T(8,128)S(1)}, f32[8,128]{1,0:T(8,128)S(1)}, u32[]{:S(2)}, u32[]{:S(2)}) collective-permute-start(f32[8,128]{1,0:T(8,128)S(1)} %collective-permute-done.refs_1_), channel_id=1, source_target_pairs={{0,1},{1,0},{2,3},{3,2},{4,5},{5,4},{6,7},{7,6},{8,9},{9,8},{10,11... | collective-permute-start | bytes 12296 | tf_op jit(solution)/shard_map/ppermute | solution.py:342
  15.5 1.3 %collective-permute-done.1.refs_2_ = f32[8,128]{1,0:T(8,128)S(1)} collective-permute-done((f32[8,128]{1,0:T(8,128)S(1)}, f32[8,128]{1,0:T(8,128)S(1)}, u32[]{:S(2)}, u32[]{:S(2)}) %collective-permute-start.1) | collective-permute-done | bytes 4128 | tf_op jit(solution)/shard_map/ppermute | solution.py:341
  16.8 0.0 collective-permute-done.2.refs_3_
  16.8 0.4 %shard_map.66 = (f32[8,256]{1,0:T(8,128)S(1)}, bf16[512,256]{1,0:T(8,128)(2,1)S(1)}, bf16[512,256]{1,0:T(8,128)(2,1)S(1)}, f32[4,256]{1,0:T(4,128)S(1)}) custom-call(f32[8,128]{1,0:T(8,128)S(1)} %get-tuple-element.12.refs_0_, f32[8,128]{1,0:T(8,128)S(1)} %collective-permute-done.refs_1_, f32[8,128]{1,0:T(8,128)S(1)} %collective-permute-done.1.refs_2_, ...), custom_call_target="tpu_custom_call" | custom-call | tf_op jit(solution)/shard_map/pallas_call | solution.py:376
  17.1 0.3 %shard_map.67.refs_1_ = f32[8,256]{1,0:T(8,128)S(1)} custom-call(f32[8,256]{1,0:T(8,128)S(1)} %get-tuple-element.15.sensors_ref.refs_0_, bf16[512,256]{1,0:T(8,128)(2,1)S(1)} %get-tuple-element.16.high_ref, bf16[512,256]{1,0:T(8,128)(2,1)S(1)} %get-tuple-element.17.low_ref, f32[4,256]{1,0:T(4,128)S(1)} %get-tuple-element.18.values_ref, ...), custom_call_target="tpu_custom_call" | custom-call | tf_op jit(solution)/shard_map/pallas_call | solution.py:376
  17.4 1.2 %collective-permute-start.4 = (f32[8,256]{1,0:T(8,128)S(1)}, f32[8,256]{1,0:T(8,128)S(1)}, u32[]{:S(2)}, u32[]{:S(2)}) collective-permute-start(f32[8,256]{1,0:T(8,128)S(1)} %shard_map.67.refs_1_), channel_id=1, source_target_pairs={{0,1},{1,0},{2,3},{3,2},{4,5},{5,4},{6,7},{7,6},{8,9},{9,8},{10,11... | collective-permute-start | bytes 24584 | tf_op jit(solution)/shard_map/ppermute | solution.py:445
  18.6 0.8 %collective-permute-done.4.refs_2_ = f32[8,256]{1,0:T(8,128)S(1)} collective-permute-done((f32[8,256]{1,0:T(8,128)S(1)}, f32[8,256]{1,0:T(8,128)S(1)}, u32[]{:S(2)}, u32[]{:S(2)}) %collective-permute-start.4) | collective-permute-done | bytes 8224 | tf_op jit(solution)/shard_map/ppermute | solution.py:445
  19.4 0.1 shard_map.68.refs_0_
  19.5 1.9 %collective-permute-start.5 = (f32[16,128]{1,0:T(8,128)S(1)}, f32[16,128]{1,0:T(8,128)S(1)}, u32[]{:S(2)}, u32[]{:S(2)}) collective-permute-start(f32[16,128]{1,0:T(8,128)S(1)} %shard_map.68.refs_0_), channel_id=1, source_target_pairs={{0,8},{1,13},{2,10},{3,15},{4,12},{5,9},{6,14},{7,11},{8,0},{9,5},... | collective-permute-start | bytes 24584 | tf_op jit(solution)/shard_map/ppermute | solution.py:340
  21.4 0.1 collective-permute-start.6
  21.4 2.7 %collective-permute-done.5.refs_1_ = f32[16,128]{1,0:T(8,128)S(1)} collective-permute-done((f32[16,128]{1,0:T(8,128)S(1)}, f32[16,128]{1,0:T(8,128)S(1)}, u32[]{:S(2)}, u32[]{:S(2)}) %collective-permute-start.5) | collective-permute-done | bytes 8224 | tf_op jit(solution)/shard_map/ppermute | solution.py:340
  24.1 0.1 collective-permute-start.7
  24.2 0.0 collective-permute-done.8.refs_5_
  24.2 0.3 collective-permute-done.6.refs_2_
  24.5 0.8 %collective-permute-done.7.refs_3_ = f32[16,128]{1,0:T(8,128)S(1)} collective-permute-done((f32[16,128]{1,0:T(8,128)S(1)}, f32[16,128]{1,0:T(8,128)S(1)}, u32[]{:S(2)}, u32[]{:S(2)}) %collective-permute-start.7) | collective-permute-done | bytes 8224 | tf_op jit(solution)/shard_map/ppermute | solution.py:342
  25.3 0.0 collective-permute-done.9.refs_7_
  25.3 2.5 %shard_map.69 = f32[4,32,512]{2,1,0:T(8,128)} custom-call(f32[16,128]{1,0:T(8,128)S(1)} %shard_map.68.refs_0_, f32[16,128]{1,0:T(8,128)S(1)} %collective-permute-done.5.refs_1_, f32[16,128]{1,0:T(8,128)S(1)} %collective-permute-done.6.refs_2_, f32[16,128]{1,0:T(8,128)S(1)} %collective-permute-done.7.refs_3_, f32[4,32,512]{2,1,0:T(8,128)S(1)} %shard_map.65.refs_4_, ...), custom_call_target="tpu_custom_call" | custom-call | tf_op jit(solution)/shard_map/pallas_call | solution.py:376
Async XLA Ops:
  0.0 9.5 %collective-permute-start.3 = (f32[4,32,512]{2,1,0:T(8,128)}, f32[4,32,512]{2,1,0:T(8,128)S(1)}, u32[]{:S(2)}, u32[]{:S(2)}) collective-permute-start(f32[4,32,512]{2,1,0:T(8,128)} %state.1), channel_id=1, source_target_pairs={{0,2},{1,3},{2,0},{3,1},{4,6},{5,7},{6,4},{7,5},{8,10},{9,11},{10,... | collective-permute-start | bytes 786440 | tf_op jit(solution)/shard_map/ppermute | solution.py:358
  4.0 20.2 %collective-permute-start.8 = (f32[4,32,512]{2,1,0:T(8,128)S(1)}, f32[4,32,512]{2,1,0:T(8,128)S(1)}, u32[]{:S(2)}, u32[]{:S(2)}) collective-permute-start(f32[4,32,512]{2,1,0:T(8,128)S(1)} %shard_map.65.refs_4_), channel_id=1, source_target_pairs={{0,1},{1,0},{2,3},{3,2},{4,5},{5,4},{6,7},{7,6},{8,9},{9,8},{10,11... | collective-permute-start | bytes 786440 | tf_op jit(solution)/shard_map/ppermute | solution.py:358
  9.5 15.8 %collective-permute-start.9 = (f32[4,32,512]{2,1,0:T(8,128)S(1)}, f32[4,32,512]{2,1,0:T(8,128)S(1)}, u32[]{:S(2)}, u32[]{:S(2)}) collective-permute-start(f32[4,32,512]{2,1,0:T(8,128)S(1)} %collective-permute-done.3.refs_0_.refs_6_), channel_id=1, source_target_pairs={{0,1},{1,0},{2,3},{3,2},{4,5},{5,4},{6,7},{7,6},{8,9},{9,8},{10,11... | collective-permute-start | bytes 786440 | tf_op jit(solution)/shard_map/ppermute | solution.py:358
  10.4 4.5 %collective-permute-start = (f32[8,128]{1,0:T(8,128)S(1)}, f32[8,128]{1,0:T(8,128)S(1)}, u32[]{:S(2)}, u32[]{:S(2)}) collective-permute-start(f32[8,128]{1,0:T(8,128)S(1)} %get-tuple-element.13), channel_id=1, source_target_pairs={{0,4},{1,13},{2,6},{3,15},{4,0},{5,9},{6,2},{7,11},{8,12},{9,5},{1... | collective-permute-start | bytes 12296 | tf_op jit(solution)/shard_map/ppermute | solution.py:340
  12.2 4.5 %collective-permute-start.1 = (f32[8,128]{1,0:T(8,128)S(1)}, f32[8,128]{1,0:T(8,128)S(1)}, u32[]{:S(2)}, u32[]{:S(2)}) collective-permute-start(f32[8,128]{1,0:T(8,128)S(1)} %get-tuple-element.14), channel_id=1, source_target_pairs={{0,8},{1,9},{2,10},{3,11},{4,12},{5,13},{6,14},{7,15},{8,0},{9,1},... | collective-permute-start | bytes 12296 | tf_op jit(solution)/shard_map/ppermute | solution.py:341
  14.8 1.9 %collective-permute-start.2 = (f32[8,128]{1,0:T(8,128)S(1)}, f32[8,128]{1,0:T(8,128)S(1)}, u32[]{:S(2)}, u32[]{:S(2)}) collective-permute-start(f32[8,128]{1,0:T(8,128)S(1)} %collective-permute-done.refs_1_), channel_id=1, source_target_pairs={{0,1},{1,0},{2,3},{3,2},{4,5},{5,4},{6,7},{7,6},{8,9},{9,8},{10,11... | collective-permute-start | bytes 12296 | tf_op jit(solution)/shard_map/ppermute | solution.py:342
  17.4 2.0 %collective-permute-start.4 = (f32[8,256]{1,0:T(8,128)S(1)}, f32[8,256]{1,0:T(8,128)S(1)}, u32[]{:S(2)}, u32[]{:S(2)}) collective-permute-start(f32[8,256]{1,0:T(8,128)S(1)} %shard_map.67.refs_1_), channel_id=1, source_target_pairs={{0,1},{1,0},{2,3},{3,2},{4,5},{5,4},{6,7},{7,6},{8,9},{9,8},{10,11... | collective-permute-start | bytes 24584 | tf_op jit(solution)/shard_map/ppermute | solution.py:445
  19.5 4.6 %collective-permute-start.5 = (f32[16,128]{1,0:T(8,128)S(1)}, f32[16,128]{1,0:T(8,128)S(1)}, u32[]{:S(2)}, u32[]{:S(2)}) collective-permute-start(f32[16,128]{1,0:T(8,128)S(1)} %shard_map.68.refs_0_), channel_id=1, source_target_pairs={{0,8},{1,13},{2,10},{3,15},{4,12},{5,9},{6,14},{7,11},{8,0},{9,5},... | collective-permute-start | bytes 24584 | tf_op jit(solution)/shard_map/ppermute | solution.py:340
  21.4 3.1 %collective-permute-start.6 = (f32[16,128]{1,0:T(8,128)S(1)}, f32[16,128]{1,0:T(8,128)S(1)}, u32[]{:S(2)}, u32[]{:S(2)}) collective-permute-start(f32[16,128]{1,0:T(8,128)S(1)} %shard_map.68.refs_0_), channel_id=1, source_target_pairs={{0,5},{1,4},{2,7},{3,6},{4,1},{5,0},{6,3},{7,2},{8,13},{9,12},{10,... | collective-permute-start | bytes 24584 | tf_op jit(solution)/shard_map/ppermute | solution.py:341
  24.1 1.2 %collective-permute-start.7 = (f32[16,128]{1,0:T(8,128)S(1)}, f32[16,128]{1,0:T(8,128)S(1)}, u32[]{:S(2)}, u32[]{:S(2)}) collective-permute-start(f32[16,128]{1,0:T(8,128)S(1)} %collective-permute-done.5.refs_1_), channel_id=1, source_target_pairs={{0,1},{1,0},{2,3},{3,2},{4,5},{5,4},{6,7},{7,6},{8,9},{9,8},{10,11... | collective-permute-start | bytes 24584 | tf_op jit(solution)/shard_map/ppermute | solution.py:342

commit v13 on v12

--- a/solution.py
+++ b/solution.py
@@ -322,7 +322,8 @@
 def key_order(n_ens):
     if not has_halves(n_ens):
         return list(range(n_ens))
-    return list(range(0, n_ens, 2)) + list(range(1, n_ens, 2))
+    local = [0] + [key + 1 for key in range(2, n_ens, 2)]
+    return local + [key ^ 1 for key in local]
 
 
 def spread(values, n_dom, n_ens, bits=(1, 3, 2), crossing=0):
@@ -351,15 +352,13 @@
             pieces[shift] = lax.ppermute(state, "ens", pairs)
         pieces[0] = own
         return pieces
-    bit = n_ens >> 1
-    while bit:
-        pairs = [(e, e ^ bit) for e in range(n_ens)]
-        for key in list(pieces):
-            pieces[key ^ bit] = lax.ppermute(pieces[key], "ens", pairs)
-        bit >>= 1
-        if bit == 1:
-            pieces[0] = own
+    for key in key_order(n_ens)[1 : n_ens // 2]:
+        pairs = [(e, e ^ key) for e in range(n_ens)]
+        pieces[key] = lax.ppermute(state, "ens", pairs)
     pieces[0] = own
+    for key in list(pieces):
+        pairs = [(e, e ^ 1) for e in range(n_ens)]
+        pieces[key ^ 1] = lax.ppermute(pieces[key], "ens", pairs)
     return pieces
 
 

time: 27.9 us -> 28.4 us (1.018)
  starting transfers between devices: 11.4 us -> 12.1 us
  waiting for transfers between devices: 11.3 us -> 11 us
    ppermute x2, starting transfers between devices: 3.76 us -> 4.49 us  [spread(): near = lax.ppermute(near, ('dom', 'ens'), near_pairs)]
where the time goes in v13:
time: 28.4 us; the launch traced here: 28.3 us
  starting transfers between devices  12.1 us (43%)
  waiting for transfers between devices  11 us (39%)
  Pallas kernels  5.05 us (18%)
    ppermute x1, waiting for transfers between devices, gather_members(): pieces[key] = lax.ppermute(state, 'ens', pairs)  5.26 us
    pallas_call x6, Pallas kernels, call(): pl.pallas_call(kernel, out_shape=out_shape, in_specs=specs or [vmem] * le...  5.05 us
    ppermute x2, starting transfers between devices, spread(): near = lax.ppermute(near, ('dom', 'ens'), near_pairs)  4.49 us
    ppermute x2, starting transfers between devices, spread(): far = lax.ppermute(far, ('dom', 'ens'), far_pairs)  2.64 us
    ppermute x2, waiting for transfers between devices, spread(): near = lax.ppermute(near, ('dom', 'ens'), near_pairs)  2.55 us
    ppermute x1, starting transfers between devices, gather_members(): pieces[key] = lax.ppermute(state, 'ens', pairs)  2.41 us
    ppermute x2, waiting for transfers between devices, spread(): far = lax.ppermute(far, ('dom', 'ens'), far_pairs)  1.69 us
    ppermute x1, starting transfers between devices, on_device(): values.append(lax.ppermute(values[0], 'ens', pairs))  1.05 us
  transfers between devices with their start and end apart: 10, of which 6 were waited for; matrix products, arithmetic and copies ran while one was open for 0% of the time, Pallas kernels for 9%

profile of v13, /device:TPU:0, one launch (start us, length us, event | category | flops | bytes accessed | tf_op | source)
XLA Modules:
  0.0 28.3 jit_solution(9038310758573891031)
XLA Ops:
  0.0 2.4 %collective-permute-start.3 = (f32[4,32,512]{2,1,0:T(8,128)}, f32[4,32,512]{2,1,0:T(8,128)S(1)}, u32[]{:S(2)}, u32[]{:S(2)}) collective-permute-start(f32[4,32,512]{2,1,0:T(8,128)} %state.1), channel_id=1, source_target_pairs={{0,3},{1,2},{2,1},{3,0},{4,7},{5,6},{6,5},{7,4},{8,11},{9,10},{10,... | collective-permute-start | bytes 786440 | tf_op jit(solution)/shard_map/ppermute | solution.py:357
  2.4 1.0 %shard_map.65.refs_4_ = f32[4,32,512]{2,1,0:T(8,128)S(1)} custom-call(f32[4,32,512]{2,1,0:T(8,128)} %state.1), custom_call_target="tpu_custom_call" | custom-call | tf_op jit(solution)/shard_map/pallas_call | solution.py:375
  3.4 0.7 %collective-permute-start.8 = (f32[4,32,512]{2,1,0:T(8,128)S(1)}, f32[4,32,512]{2,1,0:T(8,128)S(1)}, u32[]{:S(2)}, u32[]{:S(2)}) collective-permute-start(f32[4,32,512]{2,1,0:T(8,128)S(1)} %shard_map.65.refs_4_), channel_id=1, source_target_pairs={{0,1},{1,0},{2,3},{3,2},{4,5},{5,4},{6,7},{7,6},{8,9},{9,8},{10,11... | collective-permute-start | bytes 786440 | tf_op jit(solution)/shard_map/ppermute | solution.py:361
  4.1 5.3 %collective-permute-done.3.refs_0_.refs_7_ = f32[4,32,512]{2,1,0:T(8,128)S(1)} collective-permute-done((f32[4,32,512]{2,1,0:T(8,128)}, f32[4,32,512]{2,1,0:T(8,128)S(1)}, u32[]{:S(2)}, u32[]{:S(2)}) %collective-permute-start.3) | collective-permute-done | bytes 262176 | tf_op jit(solution)/shard_map/ppermute | solution.py:357
  9.4 0.1 collective-permute-start.9
  9.5 0.9 %shard_map.64 = (f32[8,128]{1,0:T(8,128)S(1)}, f32[8,128]{1,0:T(8,128)S(1)}, f32[8,128]{1,0:T(8,128)S(1)}) custom-call(s32[1,4]{1,0:T(1,128)} %refs_0_.1, f32[3,256]{1,0:T(4,128)} %refs_1_.1, s32[1,256]{1,0:T(1,128)} %bitcast.3, f32[1,256]{1,0:T(1,128)} %bitcast.4, f32[1,256]{1,0:T(1,128)} %bitcast.5), custom_call_target="tpu_custom_call" | custom-call | tf_op jit(solution)/shard_map/pallas_call | solution.py:375
  10.4 2.5 %collective-permute-start = (f32[8,128]{1,0:T(8,128)S(1)}, f32[8,128]{1,0:T(8,128)S(1)}, u32[]{:S(2)}, u32[]{:S(2)}) collective-permute-start(f32[8,128]{1,0:T(8,128)S(1)} %get-tuple-element.13), channel_id=1, source_target_pairs={{0,4},{1,13},{2,6},{3,15},{4,0},{5,9},{6,2},{7,11},{8,12},{9,5},{1... | collective-permute-start | bytes 12296 | tf_op jit(solution)/shard_map/ppermute | solution.py:341
  12.9 2.6 %collective-permute-start.1 = (f32[8,128]{1,0:T(8,128)S(1)}, f32[8,128]{1,0:T(8,128)S(1)}, u32[]{:S(2)}, u32[]{:S(2)}) collective-permute-start(f32[8,128]{1,0:T(8,128)S(1)} %get-tuple-element.14), channel_id=1, source_target_pairs={{0,8},{1,9},{2,10},{3,11},{4,12},{5,13},{6,14},{7,15},{8,0},{9,1},... | collective-permute-start | bytes 12296 | tf_op jit(solution)/shard_map/ppermute | solution.py:342
  15.5 0.0 collective-permute-done.refs_1_
  15.5 0.5 %collective-permute-start.2 = (f32[8,128]{1,0:T(8,128)S(1)}, f32[8,128]{1,0:T(8,128)S(1)}, u32[]{:S(2)}, u32[]{:S(2)}) collective-permute-start(f32[8,128]{1,0:T(8,128)S(1)} %collective-permute-done.refs_1_), channel_id=1, source_target_pairs={{0,1},{1,0},{2,3},{3,2},{4,5},{5,4},{6,7},{7,6},{8,9},{9,8},{10,11... | collective-permute-start | bytes 12296 | tf_op jit(solution)/shard_map/ppermute | solution.py:343
  16.0 1.4 %collective-permute-done.1.refs_2_ = f32[8,128]{1,0:T(8,128)S(1)} collective-permute-done((f32[8,128]{1,0:T(8,128)S(1)}, f32[8,128]{1,0:T(8,128)S(1)}, u32[]{:S(2)}, u32[]{:S(2)}) %collective-permute-start.1) | collective-permute-done | bytes 4128 | tf_op jit(solution)/shard_map/ppermute | solution.py:342
  17.4 0.0 collective-permute-done.2.refs_3_
  17.4 0.4 %shard_map.66 = (f32[8,256]{1,0:T(8,128)S(1)}, bf16[512,256]{1,0:T(8,128)(2,1)S(1)}, bf16[512,256]{1,0:T(8,128)(2,1)S(1)}, f32[4,256]{1,0:T(4,128)S(1)}) custom-call(f32[8,128]{1,0:T(8,128)S(1)} %get-tuple-element.12.refs_0_, f32[8,128]{1,0:T(8,128)S(1)} %collective-permute-done.refs_1_, f32[8,128]{1,0:T(8,128)S(1)} %collective-permute-done.1.refs_2_, ...), custom_call_target="tpu_custom_call" | custom-call | tf_op jit(solution)/shard_map/pallas_call | solution.py:375
  17.7 0.3 shard_map.67.refs_1_
  18.0 1.1 %collective-permute-start.4 = (f32[8,256]{1,0:T(8,128)S(1)}, f32[8,256]{1,0:T(8,128)S(1)}, u32[]{:S(2)}, u32[]{:S(2)}) collective-permute-start(f32[8,256]{1,0:T(8,128)S(1)} %shard_map.67.refs_1_), channel_id=1, source_target_pairs={{0,1},{1,0},{2,3},{3,2},{4,5},{5,4},{6,7},{7,6},{8,9},{9,8},{10,11... | collective-permute-start | bytes 24584 | tf_op jit(solution)/shard_map/ppermute | solution.py:444
  19.1 0.8 %collective-permute-done.4.refs_2_ = f32[8,256]{1,0:T(8,128)S(1)} collective-permute-done((f32[8,256]{1,0:T(8,128)S(1)}, f32[8,256]{1,0:T(8,128)S(1)}, u32[]{:S(2)}, u32[]{:S(2)}) %collective-permute-start.4) | collective-permute-done | bytes 8224 | tf_op jit(solution)/shard_map/ppermute | solution.py:444
  19.9 0.1 shard_map.68.refs_0_
  20.0 2.0 %collective-permute-start.5 = (f32[16,128]{1,0:T(8,128)S(1)}, f32[16,128]{1,0:T(8,128)S(1)}, u32[]{:S(2)}, u32[]{:S(2)}) collective-permute-start(f32[16,128]{1,0:T(8,128)S(1)} %shard_map.68.refs_0_), channel_id=1, source_target_pairs={{0,8},{1,13},{2,10},{3,15},{4,12},{5,9},{6,14},{7,11},{8,0},{9,5},... | collective-permute-start | bytes 24584 | tf_op jit(solution)/shard_map/ppermute | solution.py:341
  22.0 0.1 collective-permute-start.6
  22.1 2.5 %collective-permute-done.5.refs_1_ = f32[16,128]{1,0:T(8,128)S(1)} collective-permute-done((f32[16,128]{1,0:T(8,128)S(1)}, f32[16,128]{1,0:T(8,128)S(1)}, u32[]{:S(2)}, u32[]{:S(2)}) %collective-permute-start.5) | collective-permute-done | bytes 8224 | tf_op jit(solution)/shard_map/ppermute | solution.py:341
  24.6 0.1 collective-permute-start.7
  24.8 0.0 collective-permute-done.8.refs_5_
  24.8 0.3 %collective-permute-done.6.refs_2_ = f32[16,128]{1,0:T(8,128)S(1)} collective-permute-done((f32[16,128]{1,0:T(8,128)S(1)}, f32[16,128]{1,0:T(8,128)S(1)}, u32[]{:S(2)}, u32[]{:S(2)}) %collective-permute-start.6) | collective-permute-done | bytes 8224 | tf_op jit(solution)/shard_map/ppermute | solution.py:342
  25.1 0.7 %collective-permute-done.7.refs_3_ = f32[16,128]{1,0:T(8,128)S(1)} collective-permute-done((f32[16,128]{1,0:T(8,128)S(1)}, f32[16,128]{1,0:T(8,128)S(1)}, u32[]{:S(2)}, u32[]{:S(2)}) %collective-permute-start.7) | collective-permute-done | bytes 8224 | tf_op jit(solution)/shard_map/ppermute | solution.py:343
  25.8 0.0 collective-permute-done.9.refs_6_
  25.8 2.5 %shard_map.69 = f32[4,32,512]{2,1,0:T(8,128)} custom-call(f32[16,128]{1,0:T(8,128)S(1)} %shard_map.68.refs_0_, f32[16,128]{1,0:T(8,128)S(1)} %collective-permute-done.5.refs_1_, f32[16,128]{1,0:T(8,128)S(1)} %collective-permute-done.6.refs_2_, f32[16,128]{1,0:T(8,128)S(1)} %collective-permute-done.7.refs_3_, f32[4,32,512]{2,1,0:T(8,128)S(1)} %shard_map.65.refs_4_, ...), custom_call_target="tpu_custom_call" | custom-call | tf_op jit(solution)/shard_map/pallas_call | solution.py:375
Async XLA Ops:
  0.0 9.4 %collective-permute-start.3 = (f32[4,32,512]{2,1,0:T(8,128)}, f32[4,32,512]{2,1,0:T(8,128)S(1)}, u32[]{:S(2)}, u32[]{:S(2)}) collective-permute-start(f32[4,32,512]{2,1,0:T(8,128)} %state.1), channel_id=1, source_target_pairs={{0,3},{1,2},{2,1},{3,0},{4,7},{5,6},{6,5},{7,4},{8,11},{9,10},{10,... | collective-permute-start | bytes 786440 | tf_op jit(solution)/shard_map/ppermute | solution.py:357
  3.4 21.4 %collective-permute-start.8 = (f32[4,32,512]{2,1,0:T(8,128)S(1)}, f32[4,32,512]{2,1,0:T(8,128)S(1)}, u32[]{:S(2)}, u32[]{:S(2)}) collective-permute-start(f32[4,32,512]{2,1,0:T(8,128)S(1)} %shard_map.65.refs_4_), channel_id=1, source_target_pairs={{0,1},{1,0},{2,3},{3,2},{4,5},{5,4},{6,7},{7,6},{8,9},{9,8},{10,11... | collective-permute-start | bytes 786440 | tf_op jit(solution)/shard_map/ppermute | solution.py:361
  9.4 16.4 %collective-permute-start.9 = (f32[4,32,512]{2,1,0:T(8,128)S(1)}, f32[4,32,512]{2,1,0:T(8,128)S(1)}, u32[]{:S(2)}, u32[]{:S(2)}) collective-permute-start(f32[4,32,512]{2,1,0:T(8,128)S(1)} %collective-permute-done.3.refs_0_.refs_7_), channel_id=1, source_target_pairs={{0,1},{1,0},{2,3},{3,2},{4,5},{5,4},{6,7},{7,6},{8,9},{9,8},{10,11... | collective-permute-start | bytes 786440 | tf_op jit(solution)/shard_map/ppermute | solution.py:361
  10.4 5.1 %collective-permute-start = (f32[8,128]{1,0:T(8,128)S(1)}, f32[8,128]{1,0:T(8,128)S(1)}, u32[]{:S(2)}, u32[]{:S(2)}) collective-permute-start(f32[8,128]{1,0:T(8,128)S(1)} %get-tuple-element.13), channel_id=1, source_target_pairs={{0,4},{1,13},{2,6},{3,15},{4,0},{5,9},{6,2},{7,11},{8,12},{9,5},{1... | collective-permute-start | bytes 12296 | tf_op jit(solution)/shard_map/ppermute | solution.py:341
  12.9 4.5 %collective-permute-start.1 = (f32[8,128]{1,0:T(8,128)S(1)}, f32[8,128]{1,0:T(8,128)S(1)}, u32[]{:S(2)}, u32[]{:S(2)}) collective-permute-start(f32[8,128]{1,0:T(8,128)S(1)} %get-tuple-element.14), channel_id=1, source_target_pairs={{0,8},{1,9},{2,10},{3,11},{4,12},{5,13},{6,14},{7,15},{8,0},{9,1},... | collective-permute-start | bytes 12296 | tf_op jit(solution)/shard_map/ppermute | solution.py:342
  15.5 1.9 %collective-permute-start.2 = (f32[8,128]{1,0:T(8,128)S(1)}, f32[8,128]{1,0:T(8,128)S(1)}, u32[]{:S(2)}, u32[]{:S(2)}) collective-permute-start(f32[8,128]{1,0:T(8,128)S(1)} %collective-permute-done.refs_1_), channel_id=1, source_target_pairs={{0,1},{1,0},{2,3},{3,2},{4,5},{5,4},{6,7},{7,6},{8,9},{9,8},{10,11... | collective-permute-start | bytes 12296 | tf_op jit(solution)/shard_map/ppermute | solution.py:343
  18.0 1.9 %collective-permute-start.4 = (f32[8,256]{1,0:T(8,128)S(1)}, f32[8,256]{1,0:T(8,128)S(1)}, u32[]{:S(2)}, u32[]{:S(2)}) collective-permute-start(f32[8,256]{1,0:T(8,128)S(1)} %shard_map.67.refs_1_), channel_id=1, source_target_pairs={{0,1},{1,0},{2,3},{3,2},{4,5},{5,4},{6,7},{7,6},{8,9},{9,8},{10,11... | collective-permute-start | bytes 24584 | tf_op jit(solution)/shard_map/ppermute | solution.py:444
  20.0 4.6 %collective-permute-start.5 = (f32[16,128]{1,0:T(8,128)S(1)}, f32[16,128]{1,0:T(8,128)S(1)}, u32[]{:S(2)}, u32[]{:S(2)}) collective-permute-start(f32[16,128]{1,0:T(8,128)S(1)} %shard_map.68.refs_0_), channel_id=1, source_target_pairs={{0,8},{1,13},{2,10},{3,15},{4,12},{5,9},{6,14},{7,11},{8,0},{9,5},... | collective-permute-start | bytes 24584 | tf_op jit(solution)/shard_map/ppermute | solution.py:341
  22.0 3.1 %collective-permute-start.6 = (f32[16,128]{1,0:T(8,128)S(1)}, f32[16,128]{1,0:T(8,128)S(1)}, u32[]{:S(2)}, u32[]{:S(2)}) collective-permute-start(f32[16,128]{1,0:T(8,128)S(1)} %shard_map.68.refs_0_), channel_id=1, source_target_pairs={{0,5},{1,4},{2,7},{3,6},{4,1},{5,0},{6,3},{7,2},{8,13},{9,12},{10,... | collective-permute-start | bytes 24584 | tf_op jit(solution)/shard_map/ppermute | solution.py:342
  24.6 1.2 %collective-permute-start.7 = (f32[16,128]{1,0:T(8,128)S(1)}, f32[16,128]{1,0:T(8,128)S(1)}, u32[]{:S(2)}, u32[]{:S(2)}) collective-permute-start(f32[16,128]{1,0:T(8,128)S(1)} %collective-permute-done.5.refs_1_), channel_id=1, source_target_pairs={{0,1},{1,0},{2,3},{3,2},{4,5},{5,4},{6,7},{7,6},{8,9},{9,8},{10,11... | collective-permute-start | bytes 24584 | tf_op jit(solution)/shard_map/ppermute | solution.py:343

commit v14 on v12

--- a/solution.py
+++ b/solution.py
@@ -267,12 +267,17 @@
             inverse_left, inverse_right = as_left(inverse_root), as_right(inverse_root)
         else:
             solved = product(middle_left, as_right(product(inverse_left, project)))
-    mean_weights = product(as_left(inverse_root), as_right(solved))
+            ones = [jnp.ones(tile, F32)] * 2
+            row_sums = product(middle_left, as_right(product(inverse_left, ones)))
+    solved, row_sums, inverse_right = as_right(solved), as_right(row_sums), as_right(inverse_root)
+    mean_weights = product(as_left(inverse_root), solved)
     root_scale = jnp.sqrt((members - 1) * scale)
-    transform = [inverse_root[h] * root_scale + mean_weights[h] * scale for h in range(2)]
-    transform_right = as_right(transform)
-    column_mean = sublane_total(transform_right[0] + transform_right[1]) * (1.0 / members)
-    mixing = [transform[h] - column_mean + 1.0 / members for h in range(2)]
+    weights_mean = sublane_total(row_sums[0] * solved[0] + row_sums[1] * solved[1])
+    column_sum = sublane_total(inverse_right[0] + inverse_right[1])
+    shift = (1.0 - column_sum * root_scale - weights_mean * scale) * (1.0 / members)
+    mixing = [
+        inverse_root[h] * root_scale + mean_weights[h] * scale + shift for h in range(2)
+    ]
     odd = is_odd(halves)
     order = key_order(len(state_refs))
     own_place = odd * order.index(1) if halves else 0
@@ -286,9 +291,13 @@
     for piece in range(len(state_refs)):
         place = order.index(piece)
         places.append(place + odd * (order.index(piece ^ 1) - place) if halves else place)
-    copies = []
-    for block in range(elements // 8):
-        span = slice(8 * block, 8 * block + 8)
+
+    def output_copy(block):
+        place = pl.ds(pl.multiple_of(8 * block, 8), 8)
+        return pltpu.make_async_copy(staged.at[:, place], out.at[:, place], sems.at[block])
+
+    def mix_block(block, carry):
+        span = pl.ds(pl.multiple_of(8 * block, 8), 8)
         for first in range(0, nodes, 2 * LANES):
             spans = [slice(first + LANES * u, first + LANES * (u + 1)) for u in range(2)]
             totals = [[None, None] for _ in range(local_members)]
@@ -303,12 +312,15 @@
             for k in range(local_members):
                 for u in range(2):
                     staged[k, span, spans[u]] = totals[k][u]
-        place = pl.ds(8 * block, 8)
-        copy = pltpu.make_async_copy(staged.at[:, place], out.at[:, place], sems.at[block])
-        copy.start()
-        copies.append(copy)
-    for copy in copies:
-        copy.wait()
+        output_copy(block).start()
+        return carry
+
+    def wait_block(block, carry):
+        output_copy(block).wait()
+        return carry
+
+    lax.fori_loop(0, elements // 8, mix_block, 0)
+    lax.fori_loop(0, elements // 8, wait_block, 0)
 
 
 def has_halves(n_ens):
@@ -448,7 +460,7 @@
         )
         if direct:
             copies = [partial_sum] * (3 if paired else n_dom)
-            sums = spread(copies, n_dom, n_ens, bits=(2, 3, 1), crossing=1)
+            sums = spread(copies, n_dom, n_ens, bits=(2, 3, 1), crossing=0)
         else:
             sums = [lax.psum(partial_sum, "dom")]
         return call(

time: 27.9 us -> 27.9 us (level)
  waiting for transfers between devices: 11.3 us -> 10.2 us
  starting transfers between devices: 11.4 us -> 12.4 us
    ppermute x2, starting transfers between devices: 2.64 us -> 3.67 us  [spread(): far = lax.ppermute(far, ('dom', 'ens'), far_pairs)]
    ppermute x2, waiting for transfers between devices: 2.67 us -> 1.64 us  [spread(): near = lax.ppermute(near, ('dom', 'ens'), near_pairs)]
    ppermute x2, waiting for transfers between devices: 1.52 us -> 2.09 us  [spread(): far = lax.ppermute(far, ('dom', 'ens'), far_pairs)]
    ppermute x2, waiting for transfers between devices: 0.81 us -> 0.25 us  [spread(): other = lax.ppermute(near, 'ens', [(e, e ^ 1) for e in range(n_ens)])]
where the time goes in v14:
time: 27.9 us; the launch traced here: 27.7 us
  starting transfers between devices  12.4 us (44%)
  waiting for transfers between devices  10.2 us (37%)
  Pallas kernels  5.06 us (18%)
    ppermute x3, waiting for transfers between devices, gather_members(): pieces[key ^ bit] = lax.ppermute(pieces[key], 'ens', pairs)  5.44 us
    pallas_call x6, Pallas kernels, call(): pl.pallas_call(kernel, out_shape=out_shape, in_specs=specs or [vmem] * le...  5.06 us
    ppermute x2, starting transfers between devices, spread(): near = lax.ppermute(near, ('dom', 'ens'), near_pairs)  3.76 us
    ppermute x2, starting transfers between devices, spread(): far = lax.ppermute(far, ('dom', 'ens'), far_pairs)  3.67 us
    ppermute x3, starting transfers between devices, gather_members(): pieces[key ^ bit] = lax.ppermute(pieces[key], 'ens', pairs)  3.04 us
    ppermute x2, waiting for transfers between devices, spread(): far = lax.ppermute(far, ('dom', 'ens'), far_pairs)  2.09 us
    ppermute x2, waiting for transfers between devices, spread(): near = lax.ppermute(near, ('dom', 'ens'), near_pairs)  1.64 us
    ppermute x1, starting transfers between devices, on_device(): values.append(lax.ppermute(values[0], 'ens', pairs))  1.17 us
  transfers between devices with their start and end apart: 10, of which 6 were waited for; matrix products, arithmetic and copies ran while one was open for 0% of the time, Pallas kernels for 9%

profile of v14, /device:TPU:0, one launch (start us, length us, event | category | flops | bytes accessed | tf_op | source)
XLA Modules:
  0.0 27.7 jit_solution(12944962964864291573)
XLA Ops:
  0.0 3.0 %collective-permute-start.3 = (f32[4,32,512]{2,1,0:T(8,128)}, f32[4,32,512]{2,1,0:T(8,128)S(1)}, u32[]{:S(2)}, u32[]{:S(2)}) collective-permute-start(f32[4,32,512]{2,1,0:T(8,128)} %state.1), channel_id=1, source_target_pairs={{0,2},{1,3},{2,0},{3,1},{4,6},{5,7},{6,4},{7,5},{8,10},{9,11},{10,... | collective-permute-start | bytes 786440 | tf_op jit(solution)/shard_map/ppermute | solution.py:370
  3.0 1.0 %shard_map.65.refs_4_ = f32[4,32,512]{2,1,0:T(8,128)S(1)} custom-call(f32[4,32,512]{2,1,0:T(8,128)} %state.1), custom_call_target="tpu_custom_call" | custom-call | tf_op jit(solution)/shard_map/pallas_call | solution.py:388
  4.0 0.1 collective-permute-start.8
  4.0 5.4 %collective-permute-done.3.refs_0_.refs_6_ = f32[4,32,512]{2,1,0:T(8,128)S(1)} collective-permute-done((f32[4,32,512]{2,1,0:T(8,128)}, f32[4,32,512]{2,1,0:T(8,128)S(1)}, u32[]{:S(2)}, u32[]{:S(2)}) %collective-permute-start.3) | collective-permute-done | bytes 262176 | tf_op jit(solution)/shard_map/ppermute | solution.py:370
  9.5 0.0 collective-permute-start.9
  9.5 0.9 %shard_map.64 = (f32[8,128]{1,0:T(8,128)S(1)}, f32[8,128]{1,0:T(8,128)S(1)}, f32[8,128]{1,0:T(8,128)S(1)}) custom-call(s32[1,4]{1,0:T(1,128)} %refs_0_.1, f32[3,256]{1,0:T(4,128)} %refs_1_.1, s32[1,256]{1,0:T(1,128)} %bitcast.3, f32[1,256]{1,0:T(1,128)} %bitcast.4, f32[1,256]{1,0:T(1,128)} %bitcast.5), custom_call_target="tpu_custom_call" | custom-call | tf_op jit(solution)/shard_map/pallas_call | solution.py:388
  10.4 1.9 %collective-permute-start = (f32[8,128]{1,0:T(8,128)S(1)}, f32[8,128]{1,0:T(8,128)S(1)}, u32[]{:S(2)}, u32[]{:S(2)}) collective-permute-start(f32[8,128]{1,0:T(8,128)S(1)} %get-tuple-element.13), channel_id=1, source_target_pairs={{0,4},{1,13},{2,6},{3,15},{4,0},{5,9},{6,2},{7,11},{8,12},{9,5},{1... | collective-permute-start | bytes 12296 | tf_op jit(solution)/shard_map/ppermute | solution.py:352
  12.2 2.6 %collective-permute-start.1 = (f32[8,128]{1,0:T(8,128)S(1)}, f32[8,128]{1,0:T(8,128)S(1)}, u32[]{:S(2)}, u32[]{:S(2)}) collective-permute-start(f32[8,128]{1,0:T(8,128)S(1)} %get-tuple-element.14), channel_id=1, source_target_pairs={{0,8},{1,9},{2,10},{3,11},{4,12},{5,13},{6,14},{7,15},{8,0},{9,1},... | collective-permute-start | bytes 12296 | tf_op jit(solution)/shard_map/ppermute | solution.py:353
  14.8 0.0 collective-permute-done.refs_1_
  14.8 0.7 %collective-permute-start.2 = (f32[8,128]{1,0:T(8,128)S(1)}, f32[8,128]{1,0:T(8,128)S(1)}, u32[]{:S(2)}, u32[]{:S(2)}) collective-permute-start(f32[8,128]{1,0:T(8,128)S(1)} %collective-permute-done.refs_1_), channel_id=1, source_target_pairs={{0,1},{1,0},{2,3},{3,2},{4,5},{5,4},{6,7},{7,6},{8,9},{9,8},{10,11... | collective-permute-start | bytes 12296 | tf_op jit(solution)/shard_map/ppermute | solution.py:354
  15.5 1.3 %collective-permute-done.1.refs_2_ = f32[8,128]{1,0:T(8,128)S(1)} collective-permute-done((f32[8,128]{1,0:T(8,128)S(1)}, f32[8,128]{1,0:T(8,128)S(1)}, u32[]{:S(2)}, u32[]{:S(2)}) %collective-permute-start.1) | collective-permute-done | bytes 4128 | tf_op jit(solution)/shard_map/ppermute | solution.py:353
  16.8 0.0 collective-permute-done.2.refs_3_
  16.8 0.4 %shard_map.66 = (f32[8,256]{1,0:T(8,128)S(1)}, bf16[512,256]{1,0:T(8,128)(2,1)S(1)}, bf16[512,256]{1,0:T(8,128)(2,1)S(1)}, f32[4,256]{1,0:T(4,128)S(1)}) custom-call(f32[8,128]{1,0:T(8,128)S(1)} %get-tuple-element.12.refs_0_, f32[8,128]{1,0:T(8,128)S(1)} %collective-permute-done.refs_1_, f32[8,128]{1,0:T(8,128)S(1)} %collective-permute-done.1.refs_2_, ...), custom_call_target="tpu_custom_call" | custom-call | tf_op jit(solution)/shard_map/pallas_call | solution.py:388
  17.1 0.3 %shard_map.67.refs_1_ = f32[8,256]{1,0:T(8,128)S(1)} custom-call(f32[8,256]{1,0:T(8,128)S(1)} %get-tuple-element.15.sensors_ref.refs_0_, bf16[512,256]{1,0:T(8,128)(2,1)S(1)} %get-tuple-element.16.high_ref, bf16[512,256]{1,0:T(8,128)(2,1)S(1)} %get-tuple-element.17.low_ref, f32[4,256]{1,0:T(4,128)S(1)} %get-tuple-element.18.values_ref, ...), custom_call_target="tpu_custom_call" | custom-call | tf_op jit(solution)/shard_map/pallas_call | solution.py:388
  17.4 1.2 %collective-permute-start.4 = (f32[8,256]{1,0:T(8,128)S(1)}, f32[8,256]{1,0:T(8,128)S(1)}, u32[]{:S(2)}, u32[]{:S(2)}) collective-permute-start(f32[8,256]{1,0:T(8,128)S(1)} %shard_map.67.refs_1_), channel_id=1, source_target_pairs={{0,1},{1,0},{2,3},{3,2},{4,5},{5,4},{6,7},{7,6},{8,9},{9,8},{10,11... | collective-permute-start | bytes 24584 | tf_op jit(solution)/shard_map/ppermute | solution.py:457
  18.6 0.8 %collective-permute-done.4.refs_2_ = f32[8,256]{1,0:T(8,128)S(1)} collective-permute-done((f32[8,256]{1,0:T(8,128)S(1)}, f32[8,256]{1,0:T(8,128)S(1)}, u32[]{:S(2)}, u32[]{:S(2)}) %collective-permute-start.4) | collective-permute-done | bytes 8224 | tf_op jit(solution)/shard_map/ppermute | solution.py:457
  19.4 0.1 shard_map.68.refs_0_
  19.5 1.9 %collective-permute-start.5 = (f32[16,128]{1,0:T(8,128)S(1)}, f32[16,128]{1,0:T(8,128)S(1)}, u32[]{:S(2)}, u32[]{:S(2)}) collective-permute-start(f32[16,128]{1,0:T(8,128)S(1)} %shard_map.68.refs_0_), channel_id=1, source_target_pairs={{0,8},{1,13},{2,10},{3,15},{4,12},{5,9},{6,14},{7,11},{8,0},{9,5},... | collective-permute-start | bytes 24584 | tf_op jit(solution)/shard_map/ppermute | solution.py:352
  21.4 1.1 %collective-permute-start.6 = (f32[16,128]{1,0:T(8,128)S(1)}, f32[16,128]{1,0:T(8,128)S(1)}, u32[]{:S(2)}, u32[]{:S(2)}) collective-permute-start(f32[16,128]{1,0:T(8,128)S(1)} %shard_map.68.refs_0_), channel_id=1, source_target_pairs={{0,4},{1,5},{2,6},{3,7},{4,0},{5,1},{6,2},{7,3},{8,12},{9,13},{10,... | collective-permute-start | bytes 24584 | tf_op jit(solution)/shard_map/ppermute | solution.py:353
  22.5 1.6 %collective-permute-done.5.refs_1_ = f32[16,128]{1,0:T(8,128)S(1)} collective-permute-done((f32[16,128]{1,0:T(8,128)S(1)}, f32[16,128]{1,0:T(8,128)S(1)}, u32[]{:S(2)}, u32[]{:S(2)}) %collective-permute-start.5) | collective-permute-done | bytes 8224 | tf_op jit(solution)/shard_map/ppermute | solution.py:352
  24.1 0.1 collective-permute-start.7
  24.2 0.0 collective-permute-done.8.refs_5_
  24.2 0.8 %collective-permute-done.6.refs_2_ = f32[16,128]{1,0:T(8,128)S(1)} collective-permute-done((f32[16,128]{1,0:T(8,128)S(1)}, f32[16,128]{1,0:T(8,128)S(1)}, u32[]{:S(2)}, u32[]{:S(2)}) %collective-permute-start.6) | collective-permute-done | bytes 8224 | tf_op jit(solution)/shard_map/ppermute | solution.py:353
  25.0 0.2 collective-permute-done.7.refs_3_
  25.3 0.0 collective-permute-done.9.refs_7_
  25.3 2.5 %shard_map.69 = f32[4,32,512]{2,1,0:T(8,128)} custom-call(f32[16,128]{1,0:T(8,128)S(1)} %shard_map.68.refs_0_, f32[16,128]{1,0:T(8,128)S(1)} %collective-permute-done.5.refs_1_, f32[16,128]{1,0:T(8,128)S(1)} %collective-permute-done.6.refs_2_, f32[16,128]{1,0:T(8,128)S(1)} %collective-permute-done.7.refs_3_, f32[4,32,512]{2,1,0:T(8,128)S(1)} %shard_map.65.refs_4_, ...), custom_call_target="tpu_custom_call" | custom-call | tf_op jit(solution)/shard_map/pallas_call | solution.py:388
Async XLA Ops:
  0.0 9.5 %collective-permute-start.3 = (f32[4,32,512]{2,1,0:T(8,128)}, f32[4,32,512]{2,1,0:T(8,128)S(1)}, u32[]{:S(2)}, u32[]{:S(2)}) collective-permute-start(f32[4,32,512]{2,1,0:T(8,128)} %state.1), channel_id=1, source_target_pairs={{0,2},{1,3},{2,0},{3,1},{4,6},{5,7},{6,4},{7,5},{8,10},{9,11},{10,... | collective-permute-start | bytes 786440 | tf_op jit(solution)/shard_map/ppermute | solution.py:370
  4.0 20.2 %collective-permute-start.8 = (f32[4,32,512]{2,1,0:T(8,128)S(1)}, f32[4,32,512]{2,1,0:T(8,128)S(1)}, u32[]{:S(2)}, u32[]{:S(2)}) collective-permute-start(f32[4,32,512]{2,1,0:T(8,128)S(1)} %shard_map.65.refs_4_), channel_id=1, source_target_pairs={{0,1},{1,0},{2,3},{3,2},{4,5},{5,4},{6,7},{7,6},{8,9},{9,8},{10,11... | collective-permute-start | bytes 786440 | tf_op jit(solution)/shard_map/ppermute | solution.py:370
  9.5 15.8 %collective-permute-start.9 = (f32[4,32,512]{2,1,0:T(8,128)S(1)}, f32[4,32,512]{2,1,0:T(8,128)S(1)}, u32[]{:S(2)}, u32[]{:S(2)}) collective-permute-start(f32[4,32,512]{2,1,0:T(8,128)S(1)} %collective-permute-done.3.refs_0_.refs_6_), channel_id=1, source_target_pairs={{0,1},{1,0},{2,3},{3,2},{4,5},{5,4},{6,7},{7,6},{8,9},{9,8},{10,11... | collective-permute-start | bytes 786440 | tf_op jit(solution)/shard_map/ppermute | solution.py:370
  10.4 4.5 %collective-permute-start = (f32[8,128]{1,0:T(8,128)S(1)}, f32[8,128]{1,0:T(8,128)S(1)}, u32[]{:S(2)}, u32[]{:S(2)}) collective-permute-start(f32[8,128]{1,0:T(8,128)S(1)} %get-tuple-element.13), channel_id=1, source_target_pairs={{0,4},{1,13},{2,6},{3,15},{4,0},{5,9},{6,2},{7,11},{8,12},{9,5},{1... | collective-permute-start | bytes 12296 | tf_op jit(solution)/shard_map/ppermute | solution.py:352
  12.2 4.5 %collective-permute-start.1 = (f32[8,128]{1,0:T(8,128)S(1)}, f32[8,128]{1,0:T(8,128)S(1)}, u32[]{:S(2)}, u32[]{:S(2)}) collective-permute-start(f32[8,128]{1,0:T(8,128)S(1)} %get-tuple-element.14), channel_id=1, source_target_pairs={{0,8},{1,9},{2,10},{3,11},{4,12},{5,13},{6,14},{7,15},{8,0},{9,1},... | collective-permute-start | bytes 12296 | tf_op jit(solution)/shard_map/ppermute | solution.py:353
  14.8 1.9 %collective-permute-start.2 = (f32[8,128]{1,0:T(8,128)S(1)}, f32[8,128]{1,0:T(8,128)S(1)}, u32[]{:S(2)}, u32[]{:S(2)}) collective-permute-start(f32[8,128]{1,0:T(8,128)S(1)} %collective-permute-done.refs_1_), channel_id=1, source_target_pairs={{0,1},{1,0},{2,3},{3,2},{4,5},{5,4},{6,7},{7,6},{8,9},{9,8},{10,11... | collective-permute-start | bytes 12296 | tf_op jit(solution)/shard_map/ppermute | solution.py:354
  17.4 2.0 %collective-permute-start.4 = (f32[8,256]{1,0:T(8,128)S(1)}, f32[8,256]{1,0:T(8,128)S(1)}, u32[]{:S(2)}, u32[]{:S(2)}) collective-permute-start(f32[8,256]{1,0:T(8,128)S(1)} %shard_map.67.refs_1_), channel_id=1, source_target_pairs={{0,1},{1,0},{2,3},{3,2},{4,5},{5,4},{6,7},{7,6},{8,9},{9,8},{10,11... | collective-permute-start | bytes 24584 | tf_op jit(solution)/shard_map/ppermute | solution.py:457
  19.5 4.6 %collective-permute-start.5 = (f32[16,128]{1,0:T(8,128)S(1)}, f32[16,128]{1,0:T(8,128)S(1)}, u32[]{:S(2)}, u32[]{:S(2)}) collective-permute-start(f32[16,128]{1,0:T(8,128)S(1)} %shard_map.68.refs_0_), channel_id=1, source_target_pairs={{0,8},{1,13},{2,10},{3,15},{4,12},{5,9},{6,14},{7,11},{8,0},{9,5},... | collective-permute-start | bytes 24584 | tf_op jit(solution)/shard_map/ppermute | solution.py:352
  21.4 3.7 %collective-permute-start.6 = (f32[16,128]{1,0:T(8,128)S(1)}, f32[16,128]{1,0:T(8,128)S(1)}, u32[]{:S(2)}, u32[]{:S(2)}) collective-permute-start(f32[16,128]{1,0:T(8,128)S(1)} %shard_map.68.refs_0_), channel_id=1, source_target_pairs={{0,4},{1,5},{2,6},{3,7},{4,0},{5,1},{6,2},{7,3},{8,12},{9,13},{10,... | collective-permute-start | bytes 24584 | tf_op jit(solution)/shard_map/ppermute | solution.py:353
  24.1 1.2 %collective-permute-start.7 = (f32[16,128]{1,0:T(8,128)S(1)}, f32[16,128]{1,0:T(8,128)S(1)}, u32[]{:S(2)}, u32[]{:S(2)}) collective-permute-start(f32[16,128]{1,0:T(8,128)S(1)} %collective-permute-done.5.refs_1_), channel_id=1, source_target_pairs={{0,1},{1,0},{2,3},{3,2},{4,5},{5,4},{6,7},{7,6},{8,9},{9,8},{10,11... | collective-permute-start | bytes 24584 | tf_op jit(solution)/shard_map/ppermute | solution.py:354

commit v15 on v14

--- a/solution.py
+++ b/solution.py
@@ -292,9 +292,12 @@
         place = order.index(piece)
         places.append(place + odd * (order.index(piece ^ 1) - place) if halves else place)
 
-    def output_copy(block):
+    def output_copies(block):
         place = pl.ds(pl.multiple_of(8 * block, 8), 8)
-        return pltpu.make_async_copy(staged.at[:, place], out.at[:, place], sems.at[block])
+        return [
+            pltpu.make_async_copy(staged.at[k, place], out.at[k, place], sems.at[block, k])
+            for k in range(local_members)
+        ]
 
     def mix_block(block, carry):
         span = pl.ds(pl.multiple_of(8 * block, 8), 8)
@@ -312,11 +315,13 @@
             for k in range(local_members):
                 for u in range(2):
                     staged[k, span, spans[u]] = totals[k][u]
-        output_copy(block).start()
+        for copy in output_copies(block):
+            copy.start()
         return carry
 
     def wait_block(block, carry):
-        output_copy(block).wait()
+        for copy in output_copies(block):
+            copy.wait()
         return carry
 
     lax.fori_loop(0, elements // 8, mix_block, 0)
@@ -460,7 +465,7 @@
         )
         if direct:
             copies = [partial_sum] * (3 if paired else n_dom)
-            sums = spread(copies, n_dom, n_ens, bits=(2, 3, 1), crossing=0)
+            sums = spread(copies, n_dom, n_ens, bits=(2, 3, 1), crossing=1)
         else:
             sums = [lax.psum(partial_sum, "dom")]
         return call(
@@ -471,7 +476,7 @@
             [
                 pltpu.VMEM(state.shape, F32),
                 pltpu.VMEM((members * local_members, 8, 128), F32),
-                pltpu.SemaphoreType.DMA((elements // 8,)),
+                pltpu.SemaphoreType.DMA((elements // 8, local_members)),
             ],
             hbm,
         )

time: 27.9 us -> 28 us (level)
  waiting for transfers between devices: 10.2 us -> 11.3 us
  starting transfers between devices: 12.4 us -> 11.4 us
    ppermute x2, starting transfers between devices: 3.67 us -> 2.64 us  [spread(): far = lax.ppermute(far, ('dom', 'ens'), far_pairs)]
    ppermute x2, waiting for transfers between devices: 1.64 us -> 2.67 us  [spread(): near = lax.ppermute(near, ('dom', 'ens'), near_pairs)]
    ppermute x2, waiting for transfers between devices: 2.09 us -> 1.52 us  [spread(): far = lax.ppermute(far, ('dom', 'ens'), far_pairs)]
    ppermute x2, waiting for transfers between devices: 0.25 us -> 0.81 us  [spread(): other = lax.ppermute(near, 'ens', [(e, e ^ 1) for e in range(n_ens)])]
where the time goes in v15:
time: 28 us; the launch traced here: 27.8 us
  starting transfers between devices  11.4 us (41%)
  waiting for transfers between devices  11.3 us (40%)
  Pallas kernels  5.16 us (18%)
    ppermute x3, waiting for transfers between devices, gather_members(): pieces[key ^ bit] = lax.ppermute(pieces[key], 'ens', pairs)  5.44 us
    pallas_call x6, Pallas kernels, call(): pl.pallas_call(kernel, out_shape=out_shape, in_specs=specs or [vmem] * le...  5.16 us
    ppermute x2, starting transfers between devices, spread(): near = lax.ppermute(near, ('dom', 'ens'), near_pairs)  3.76 us
    ppermute x3, starting transfers between devices, gather_members(): pieces[key ^ bit] = lax.ppermute(pieces[key], 'ens', pairs)  3.04 us
    ppermute x2, waiting for transfers between devices, spread(): near = lax.ppermute(near, ('dom', 'ens'), near_pairs)  2.67 us
    ppermute x2, starting transfers between devices, spread(): far = lax.ppermute(far, ('dom', 'ens'), far_pairs)  2.64 us
    ppermute x2, waiting for transfers between devices, spread(): far = lax.ppermute(far, ('dom', 'ens'), far_pairs)  1.52 us
    ppermute x1, starting transfers between devices, on_device(): values.append(lax.ppermute(values[0], 'ens', pairs))  1.17 us
  transfers between devices with their start and end apart: 10, of which 6 were waited for; matrix products, arithmetic and copies ran while one was open for 0% of the time, Pallas kernels for 9%

profile of v15, /device:TPU:0, one launch (start us, length us, event | category | flops | bytes accessed | tf_op | source)
XLA Modules:
  0.0 27.8 jit_solution(15000513363409515170)
XLA Ops:
  0.0 3.0 %collective-permute-start.3 = (f32[4,32,512]{2,1,0:T(8,128)}, f32[4,32,512]{2,1,0:T(8,128)S(1)}, u32[]{:S(2)}, u32[]{:S(2)}) collective-permute-start(f32[4,32,512]{2,1,0:T(8,128)} %state.1), channel_id=1, source_target_pairs={{0,2},{1,3},{2,0},{3,1},{4,6},{5,7},{6,4},{7,5},{8,10},{9,11},{10,... | collective-permute-start | bytes 786440 | tf_op jit(solution)/shard_map/ppermute | solution.py:375
  3.0 1.0 %shard_map.65.refs_4_ = f32[4,32,512]{2,1,0:T(8,128)S(1)} custom-call(f32[4,32,512]{2,1,0:T(8,128)} %state.1), custom_call_target="tpu_custom_call" | custom-call | tf_op jit(solution)/shard_map/pallas_call | solution.py:393
  4.0 0.1 collective-permute-start.8
  4.0 5.4 %collective-permute-done.3.refs_0_.refs_6_ = f32[4,32,512]{2,1,0:T(8,128)S(1)} collective-permute-done((f32[4,32,512]{2,1,0:T(8,128)}, f32[4,32,512]{2,1,0:T(8,128)S(1)}, u32[]{:S(2)}, u32[]{:S(2)}) %collective-permute-start.3) | collective-permute-done | bytes 262176 | tf_op jit(solution)/shard_map/ppermute | solution.py:375
  9.5 0.0 collective-permute-start.9
  9.5 0.9 %shard_map.64 = (f32[8,128]{1,0:T(8,128)S(1)}, f32[8,128]{1,0:T(8,128)S(1)}, f32[8,128]{1,0:T(8,128)S(1)}) custom-call(s32[1,4]{1,0:T(1,128)} %refs_0_.1, f32[3,256]{1,0:T(4,128)} %refs_1_.1, s32[1,256]{1,0:T(1,128)} %bitcast.3, f32[1,256]{1,0:T(1,128)} %bitcast.4, f32[1,256]{1,0:T(1,128)} %bitcast.5), custom_call_target="tpu_custom_call" | custom-call | tf_op jit(solution)/shard_map/pallas_call | solution.py:393
  10.4 1.9 %collective-permute-start = (f32[8,128]{1,0:T(8,128)S(1)}, f32[8,128]{1,0:T(8,128)S(1)}, u32[]{:S(2)}, u32[]{:S(2)}) collective-permute-start(f32[8,128]{1,0:T(8,128)S(1)} %get-tuple-element.13), channel_id=1, source_target_pairs={{0,4},{1,13},{2,6},{3,15},{4,0},{5,9},{6,2},{7,11},{8,12},{9,5},{1... | collective-permute-start | bytes 12296 | tf_op jit(solution)/shard_map/ppermute | solution.py:357
  12.2 2.6 %collective-permute-start.1 = (f32[8,128]{1,0:T(8,128)S(1)}, f32[8,128]{1,0:T(8,128)S(1)}, u32[]{:S(2)}, u32[]{:S(2)}) collective-permute-start(f32[8,128]{1,0:T(8,128)S(1)} %get-tuple-element.14), channel_id=1, source_target_pairs={{0,8},{1,9},{2,10},{3,11},{4,12},{5,13},{6,14},{7,15},{8,0},{9,1},... | collective-permute-start | bytes 12296 | tf_op jit(solution)/shard_map/ppermute | solution.py:358
  14.8 0.0 collective-permute-done.refs_1_
  14.8 0.7 %collective-permute-start.2 = (f32[8,128]{1,0:T(8,128)S(1)}, f32[8,128]{1,0:T(8,128)S(1)}, u32[]{:S(2)}, u32[]{:S(2)}) collective-permute-start(f32[8,128]{1,0:T(8,128)S(1)} %collective-permute-done.refs_1_), channel_id=1, source_target_pairs={{0,1},{1,0},{2,3},{3,2},{4,5},{5,4},{6,7},{7,6},{8,9},{9,8},{10,11... | collective-permute-start | bytes 12296 | tf_op jit(solution)/shard_map/ppermute | solution.py:359
  15.5 1.3 %collective-permute-done.1.refs_2_ = f32[8,128]{1,0:T(8,128)S(1)} collective-permute-done((f32[8,128]{1,0:T(8,128)S(1)}, f32[8,128]{1,0:T(8,128)S(1)}, u32[]{:S(2)}, u32[]{:S(2)}) %collective-permute-start.1) | collective-permute-done | bytes 4128 | tf_op jit(solution)/shard_map/ppermute | solution.py:358
  16.8 0.0 collective-permute-done.2.refs_3_
  16.8 0.4 %shard_map.66 = (f32[8,256]{1,0:T(8,128)S(1)}, bf16[512,256]{1,0:T(8,128)(2,1)S(1)}, bf16[512,256]{1,0:T(8,128)(2,1)S(1)}, f32[4,256]{1,0:T(4,128)S(1)}) custom-call(f32[8,128]{1,0:T(8,128)S(1)} %get-tuple-element.12.refs_0_, f32[8,128]{1,0:T(8,128)S(1)} %collective-permute-done.refs_1_, f32[8,128]{1,0:T(8,128)S(1)} %collective-permute-done.1.refs_2_, ...), custom_call_target="tpu_custom_call" | custom-call | tf_op jit(solution)/shard_map/pallas_call | solution.py:393
  17.1 0.3 %shard_map.67.refs_1_ = f32[8,256]{1,0:T(8,128)S(1)} custom-call(f32[8,256]{1,0:T(8,128)S(1)} %get-tuple-element.15.sensors_ref.refs_0_, bf16[512,256]{1,0:T(8,128)(2,1)S(1)} %get-tuple-element.16.high_ref, bf16[512,256]{1,0:T(8,128)(2,1)S(1)} %get-tuple-element.17.low_ref, f32[4,256]{1,0:T(4,128)S(1)} %get-tuple-element.18.values_ref, ...), custom_call_target="tpu_custom_call" | custom-call | tf_op jit(solution)/shard_map/pallas_call | solution.py:393
  17.4 1.2 %collective-permute-start.4 = (f32[8,256]{1,0:T(8,128)S(1)}, f32[8,256]{1,0:T(8,128)S(1)}, u32[]{:S(2)}, u32[]{:S(2)}) collective-permute-start(f32[8,256]{1,0:T(8,128)S(1)} %shard_map.67.refs_1_), channel_id=1, source_target_pairs={{0,1},{1,0},{2,3},{3,2},{4,5},{5,4},{6,7},{7,6},{8,9},{9,8},{10,11... | collective-permute-start | bytes 24584 | tf_op jit(solution)/shard_map/ppermute | solution.py:462
  18.6 0.8 %collective-permute-done.4.refs_2_ = f32[8,256]{1,0:T(8,128)S(1)} collective-permute-done((f32[8,256]{1,0:T(8,128)S(1)}, f32[8,256]{1,0:T(8,128)S(1)}, u32[]{:S(2)}, u32[]{:S(2)}) %collective-permute-start.4) | collective-permute-done | bytes 8224 | tf_op jit(solution)/shard_map/ppermute | solution.py:462
  19.4 0.1 shard_map.68.refs_0_
  19.5 1.9 %collective-permute-start.5 = (f32[16,128]{1,0:T(8,128)S(1)}, f32[16,128]{1,0:T(8,128)S(1)}, u32[]{:S(2)}, u32[]{:S(2)}) collective-permute-start(f32[16,128]{1,0:T(8,128)S(1)} %shard_map.68.refs_0_), channel_id=1, source_target_pairs={{0,8},{1,13},{2,10},{3,15},{4,12},{5,9},{6,14},{7,11},{8,0},{9,5},... | collective-permute-start | bytes 24584 | tf_op jit(solution)/shard_map/ppermute | solution.py:357
  21.4 0.1 collective-permute-start.6
  21.4 2.7 %collective-permute-done.5.refs_1_ = f32[16,128]{1,0:T(8,128)S(1)} collective-permute-done((f32[16,128]{1,0:T(8,128)S(1)}, f32[16,128]{1,0:T(8,128)S(1)}, u32[]{:S(2)}, u32[]{:S(2)}) %collective-permute-start.5) | collective-permute-done | bytes 8224 | tf_op jit(solution)/shard_map/ppermute | solution.py:357
  24.1 0.1 collective-permute-start.7
  24.2 0.0 collective-permute-done.8.refs_5_
  24.2 0.3 collective-permute-done.6.refs_2_
  24.5 0.8 %collective-permute-done.7.refs_3_ = f32[16,128]{1,0:T(8,128)S(1)} collective-permute-done((f32[16,128]{1,0:T(8,128)S(1)}, f32[16,128]{1,0:T(8,128)S(1)}, u32[]{:S(2)}, u32[]{:S(2)}) %collective-permute-start.7) | collective-permute-done | bytes 8224 | tf_op jit(solution)/shard_map/ppermute | solution.py:359
  25.3 0.0 collective-permute-done.9.refs_7_
  25.3 2.6 %shard_map.69 = f32[4,32,512]{2,1,0:T(8,128)} custom-call(f32[16,128]{1,0:T(8,128)S(1)} %shard_map.68.refs_0_, f32[16,128]{1,0:T(8,128)S(1)} %collective-permute-done.5.refs_1_, f32[16,128]{1,0:T(8,128)S(1)} %collective-permute-done.6.refs_2_, f32[16,128]{1,0:T(8,128)S(1)} %collective-permute-done.7.refs_3_, f32[4,32,512]{2,1,0:T(8,128)S(1)} %shard_map.65.refs_4_, ...), custom_call_target="tpu_custom_call" | custom-call | tf_op jit(solution)/shard_map/pallas_call | solution.py:393
Async XLA Ops:
  0.0 9.5 %collective-permute-start.3 = (f32[4,32,512]{2,1,0:T(8,128)}, f32[4,32,512]{2,1,0:T(8,128)S(1)}, u32[]{:S(2)}, u32[]{:S(2)}) collective-permute-start(f32[4,32,512]{2,1,0:T(8,128)} %state.1), channel_id=1, source_target_pairs={{0,2},{1,3},{2,0},{3,1},{4,6},{5,7},{6,4},{7,5},{8,10},{9,11},{10,... | collective-permute-start | bytes 786440 | tf_op jit(solution)/shard_map/ppermute | solution.py:375
  4.0 20.2 %collective-permute-start.8 = (f32[4,32,512]{2,1,0:T(8,128)S(1)}, f32[4,32,512]{2,1,0:T(8,128)S(1)}, u32[]{:S(2)}, u32[]{:S(2)}) collective-permute-start(f32[4,32,512]{2,1,0:T(8,128)S(1)} %shard_map.65.refs_4_), channel_id=1, source_target_pairs={{0,1},{1,0},{2,3},{3,2},{4,5},{5,4},{6,7},{7,6},{8,9},{9,8},{10,11... | collective-permute-start | bytes 786440 | tf_op jit(solution)/shard_map/ppermute | solution.py:375
  9.5 15.8 %collective-permute-start.9 = (f32[4,32,512]{2,1,0:T(8,128)S(1)}, f32[4,32,512]{2,1,0:T(8,128)S(1)}, u32[]{:S(2)}, u32[]{:S(2)}) collective-permute-start(f32[4,32,512]{2,1,0:T(8,128)S(1)} %collective-permute-done.3.refs_0_.refs_6_), channel_id=1, source_target_pairs={{0,1},{1,0},{2,3},{3,2},{4,5},{5,4},{6,7},{7,6},{8,9},{9,8},{10,11... | collective-permute-start | bytes 786440 | tf_op jit(solution)/shard_map/ppermute | solution.py:375
  10.4 4.5 %collective-permute-start = (f32[8,128]{1,0:T(8,128)S(1)}, f32[8,128]{1,0:T(8,128)S(1)}, u32[]{:S(2)}, u32[]{:S(2)}) collective-permute-start(f32[8,128]{1,0:T(8,128)S(1)} %get-tuple-element.13), channel_id=1, source_target_pairs={{0,4},{1,13},{2,6},{3,15},{4,0},{5,9},{6,2},{7,11},{8,12},{9,5},{1... | collective-permute-start | bytes 12296 | tf_op jit(solution)/shard_map/ppermute | solution.py:357
  12.2 4.5 %collective-permute-start.1 = (f32[8,128]{1,0:T(8,128)S(1)}, f32[8,128]{1,0:T(8,128)S(1)}, u32[]{:S(2)}, u32[]{:S(2)}) collective-permute-start(f32[8,128]{1,0:T(8,128)S(1)} %get-tuple-element.14), channel_id=1, source_target_pairs={{0,8},{1,9},{2,10},{3,11},{4,12},{5,13},{6,14},{7,15},{8,0},{9,1},... | collective-permute-start | bytes 12296 | tf_op jit(solution)/shard_map/ppermute | solution.py:358
  14.8 1.9 %collective-permute-start.2 = (f32[8,128]{1,0:T(8,128)S(1)}, f32[8,128]{1,0:T(8,128)S(1)}, u32[]{:S(2)}, u32[]{:S(2)}) collective-permute-start(f32[8,128]{1,0:T(8,128)S(1)} %collective-permute-done.refs_1_), channel_id=1, source_target_pairs={{0,1},{1,0},{2,3},{3,2},{4,5},{5,4},{6,7},{7,6},{8,9},{9,8},{10,11... | collective-permute-start | bytes 12296 | tf_op jit(solution)/shard_map/ppermute | solution.py:359
  17.4 2.0 %collective-permute-start.4 = (f32[8,256]{1,0:T(8,128)S(1)}, f32[8,256]{1,0:T(8,128)S(1)}, u32[]{:S(2)}, u32[]{:S(2)}) collective-permute-start(f32[8,256]{1,0:T(8,128)S(1)} %shard_map.67.refs_1_), channel_id=1, source_target_pairs={{0,1},{1,0},{2,3},{3,2},{4,5},{5,4},{6,7},{7,6},{8,9},{9,8},{10,11... | collective-permute-start | bytes 24584 | tf_op jit(solution)/shard_map/ppermute | solution.py:462
  19.5 4.6 %collective-permute-start.5 = (f32[16,128]{1,0:T(8,128)S(1)}, f32[16,128]{1,0:T(8,128)S(1)}, u32[]{:S(2)}, u32[]{:S(2)}) collective-permute-start(f32[16,128]{1,0:T(8,128)S(1)} %shard_map.68.refs_0_), channel_id=1, source_target_pairs={{0,8},{1,13},{2,10},{3,15},{4,12},{5,9},{6,14},{7,11},{8,0},{9,5},... | collective-permute-start | bytes 24584 | tf_op jit(solution)/shard_map/ppermute | solution.py:357
  21.4 3.1 %collective-permute-start.6 = (f32[16,128]{1,0:T(8,128)S(1)}, f32[16,128]{1,0:T(8,128)S(1)}, u32[]{:S(2)}, u32[]{:S(2)}) collective-permute-start(f32[16,128]{1,0:T(8,128)S(1)} %shard_map.68.refs_0_), channel_id=1, source_target_pairs={{0,5},{1,4},{2,7},{3,6},{4,1},{5,0},{6,3},{7,2},{8,13},{9,12},{10,... | collective-permute-start | bytes 24584 | tf_op jit(solution)/shard_map/ppermute | solution.py:358
  24.1 1.2 %collective-permute-start.7 = (f32[16,128]{1,0:T(8,128)S(1)}, f32[16,128]{1,0:T(8,128)S(1)}, u32[]{:S(2)}, u32[]{:S(2)}) collective-permute-start(f32[16,128]{1,0:T(8,128)S(1)} %collective-permute-done.5.refs_1_), channel_id=1, source_target_pairs={{0,1},{1,0},{2,3},{3,2},{4,5},{5,4},{6,7},{7,6},{8,9},{9,8},{10,11... | collective-permute-start | bytes 24584 | tf_op jit(solution)/shard_map/ppermute | solution.py:359

commit v16 on v14

--- a/solution.py
+++ b/solution.py
@@ -100,8 +100,8 @@
         return jnp.where((column >= half) & (column < half + count), turned, 0.0)
 
     if paired:
-        near = jnp.where(is_odd(paired) == 0, 1, 3)
-        for out, bits, half in zip(outs, (0, near, 2), (0, CAP, 0)):
+        near = jnp.where(is_odd(paired) == 0, 2, 3)
+        for out, bits, half in zip(outs, (0, near, 1), (0, CAP, 0)):
             out[...] = tile(jnp.bitwise_xor(here, bits), half)
     elif direct:
         for shift in range(n_dom):
@@ -424,7 +424,7 @@
             ],
         )
         if direct:
-            tiles = spread(tiles, n_dom, n_ens)
+            tiles = spread(tiles, n_dom, n_ens, bits=(2, 3, 1), crossing=1)
         else:
             moved = lax.all_to_all(tiles[0], "dom", split_axis=0, concat_axis=0, tiled=True)
             tiles = [moved[d] for d in range(n_dom)]
@@ -460,7 +460,7 @@
         )
         if direct:
             copies = [partial_sum] * (3 if paired else n_dom)
-            sums = spread(copies, n_dom, n_ens, bits=(2, 3, 1), crossing=0)
+            sums = spread(copies, n_dom, n_ens, bits=(2, 3, 1), crossing=1)
         else:
             sums = [lax.psum(partial_sum, "dom")]
         return call(

time: 27.9 us -> 27.6 us (0.989)
  starting transfers between devices: 12.4 us -> 10.2 us
  waiting for transfers between devices: 10.2 us -> 12.1 us
    ppermute x2, starting transfers between devices: 3.67 us -> 0.45 us  [spread(): far = lax.ppermute(far, ('dom', 'ens'), far_pairs)]
    ppermute x2, waiting for transfers between devices: 1.64 us -> 4.02 us  [spread(): near = lax.ppermute(near, ('dom', 'ens'), near_pairs)]
    ppermute x2, waiting for transfers between devices: 2.09 us -> 0.96 us  [spread(): far = lax.ppermute(far, ('dom', 'ens'), far_pairs)]
    ppermute x2, starting transfers between devices: 3.76 us -> 4.69 us  [spread(): near = lax.ppermute(near, ('dom', 'ens'), near_pairs)]
    ppermute x2, waiting for transfers between devices: 0.25 us -> 0.85 us  [spread(): other = lax.ppermute(near, 'ens', [(e, e ^ 1) for e in range(n_ens)])]
  transfers between devices with their start and end apart: 10 -> 10, of which waited for: 6 -> 7; matrix products, arithmetic and copies ran while one was open for 0% -> 0% of each run, Pallas kernels for 9% -> 9%
where the time goes in v16:
time: 27.6 us; the launch traced here: 27.4 us
  waiting for transfers between devices  12.1 us (44%)
  starting transfers between devices  10.2 us (37%)
  Pallas kernels  5.06 us (18%)
    ppermute x3, waiting for transfers between devices, gather_members(): pieces[key ^ bit] = lax.ppermute(pieces[key], 'ens', pairs)  5.44 us
    pallas_call x6, Pallas kernels, call(): pl.pallas_call(kernel, out_shape=out_shape, in_specs=specs or [vmem] * le...  5.06 us
    ppermute x2, starting transfers between devices, spread(): near = lax.ppermute(near, ('dom', 'ens'), near_pairs)  4.69 us
    ppermute x2, waiting for transfers between devices, spread(): near = lax.ppermute(near, ('dom', 'ens'), near_pairs)  4.02 us
    ppermute x3, starting transfers between devices, gather_members(): pieces[key ^ bit] = lax.ppermute(pieces[key], 'ens', pairs)  3.04 us
    ppermute x1, starting transfers between devices, on_device(): values.append(lax.ppermute(values[0], 'ens', pairs))  1.28 us
    ppermute x2, waiting for transfers between devices, spread(): far = lax.ppermute(far, ('dom', 'ens'), far_pairs)  0.96 us
    ppermute x2, waiting for transfers between devices, spread(): other = lax.ppermute(near, 'ens', [(e, e ^ 1) for e in range(n_ens)])  0.85 us
  transfers between devices with their start and end apart: 10, of which 7 were waited for; matrix products, arithmetic and copies ran while one was open for 0% of the time, Pallas kernels for 9%

profile of v16, /device:TPU:0, one launch (start us, length us, event | category | flops | bytes accessed | tf_op | source)
XLA Modules:
  0.0 27.4 jit_solution(10772871715411544907)
XLA Ops:
  0.0 3.0 %collective-permute-start.3 = (f32[4,32,512]{2,1,0:T(8,128)}, f32[4,32,512]{2,1,0:T(8,128)S(1)}, u32[]{:S(2)}, u32[]{:S(2)}) collective-permute-start(f32[4,32,512]{2,1,0:T(8,128)} %state.1), channel_id=1, source_target_pairs={{0,2},{1,3},{2,0},{3,1},{4,6},{5,7},{6,4},{7,5},{8,10},{9,11},{10,... | collective-permute-start | bytes 786440 | tf_op jit(solution)/shard_map/ppermute | solution.py:370
  3.0 1.0 %shard_map.65.refs_4_ = f32[4,32,512]{2,1,0:T(8,128)S(1)} custom-call(f32[4,32,512]{2,1,0:T(8,128)} %state.1), custom_call_target="tpu_custom_call" | custom-call | tf_op jit(solution)/shard_map/pallas_call | solution.py:388
  4.0 0.1 collective-permute-start.8
  4.0 5.4 %collective-permute-done.3.refs_0_.refs_6_ = f32[4,32,512]{2,1,0:T(8,128)S(1)} collective-permute-done((f32[4,32,512]{2,1,0:T(8,128)}, f32[4,32,512]{2,1,0:T(8,128)S(1)}, u32[]{:S(2)}, u32[]{:S(2)}) %collective-permute-start.3) | collective-permute-done | bytes 262176 | tf_op jit(solution)/shard_map/ppermute | solution.py:370
  9.5 0.0 collective-permute-start.9
  9.5 0.9 %shard_map.64 = (f32[8,128]{1,0:T(8,128)S(1)}, f32[8,128]{1,0:T(8,128)S(1)}, f32[8,128]{1,0:T(8,128)S(1)}) custom-call(s32[1,4]{1,0:T(1,128)} %refs_0_.1, f32[3,256]{1,0:T(4,128)} %refs_1_.1, s32[1,256]{1,0:T(1,128)} %bitcast.3, f32[1,256]{1,0:T(1,128)} %bitcast.4, f32[1,256]{1,0:T(1,128)} %bitcast.5), custom_call_target="tpu_custom_call" | custom-call | tf_op jit(solution)/shard_map/pallas_call | solution.py:388
  10.4 2.9 %collective-permute-start = (f32[8,128]{1,0:T(8,128)S(1)}, f32[8,128]{1,0:T(8,128)S(1)}, u32[]{:S(2)}, u32[]{:S(2)}) collective-permute-start(f32[8,128]{1,0:T(8,128)S(1)} %get-tuple-element.13), channel_id=1, source_target_pairs={{0,8},{1,13},{2,10},{3,15},{4,12},{5,9},{6,14},{7,11},{8,0},{9,5},... | collective-permute-start | bytes 12296 | tf_op jit(solution)/shard_map/ppermute | solution.py:352
  13.3 0.4 %collective-permute-start.1 = (f32[8,128]{1,0:T(8,128)S(1)}, f32[8,128]{1,0:T(8,128)S(1)}, u32[]{:S(2)}, u32[]{:S(2)}) collective-permute-start(f32[8,128]{1,0:T(8,128)S(1)} %get-tuple-element.14), channel_id=1, source_target_pairs={{0,5},{1,4},{2,7},{3,6},{4,1},{5,0},{6,3},{7,2},{8,13},{9,12},{10,... | collective-permute-start | bytes 12296 | tf_op jit(solution)/shard_map/ppermute | solution.py:353
  13.7 1.3 %collective-permute-done.refs_1_ = f32[8,128]{1,0:T(8,128)S(1)} collective-permute-done((f32[8,128]{1,0:T(8,128)S(1)}, f32[8,128]{1,0:T(8,128)S(1)}, u32[]{:S(2)}, u32[]{:S(2)}) %collective-permute-start) | collective-permute-done | bytes 4128 | tf_op jit(solution)/shard_map/ppermute | solution.py:352
  14.9 0.6 %collective-permute-start.2 = (f32[8,128]{1,0:T(8,128)S(1)}, f32[8,128]{1,0:T(8,128)S(1)}, u32[]{:S(2)}, u32[]{:S(2)}) collective-permute-start(f32[8,128]{1,0:T(8,128)S(1)} %collective-permute-done.refs_1_), channel_id=1, source_target_pairs={{0,1},{1,0},{2,3},{3,2},{4,5},{5,4},{6,7},{7,6},{8,9},{9,8},{10,11... | collective-permute-start | bytes 12296 | tf_op jit(solution)/shard_map/ppermute | solution.py:354
  15.5 0.8 %collective-permute-done.1.refs_2_ = f32[8,128]{1,0:T(8,128)S(1)} collective-permute-done((f32[8,128]{1,0:T(8,128)S(1)}, f32[8,128]{1,0:T(8,128)S(1)}, u32[]{:S(2)}, u32[]{:S(2)}) %collective-permute-start.1) | collective-permute-done | bytes 4128 | tf_op jit(solution)/shard_map/ppermute | solution.py:353
  16.3 0.0 collective-permute-done.2.refs_3_
  16.3 0.3 %shard_map.66 = (f32[8,256]{1,0:T(8,128)S(1)}, bf16[512,256]{1,0:T(8,128)(2,1)S(1)}, bf16[512,256]{1,0:T(8,128)(2,1)S(1)}, f32[4,256]{1,0:T(4,128)S(1)}) custom-call(f32[8,128]{1,0:T(8,128)S(1)} %get-tuple-element.12.refs_0_, f32[8,128]{1,0:T(8,128)S(1)} %collective-permute-done.refs_1_, f32[8,128]{1,0:T(8,128)S(1)} %collective-permute-done.1.refs_2_, ...), custom_call_target="tpu_custom_call" | custom-call | tf_op jit(solution)/shard_map/pallas_call | solution.py:388
  16.7 0.3 %shard_map.67.refs_1_ = f32[8,256]{1,0:T(8,128)S(1)} custom-call(f32[8,256]{1,0:T(8,128)S(1)} %get-tuple-element.15.sensors_ref.refs_0_, bf16[512,256]{1,0:T(8,128)(2,1)S(1)} %get-tuple-element.16.high_ref, bf16[512,256]{1,0:T(8,128)(2,1)S(1)} %get-tuple-element.17.low_ref, f32[4,256]{1,0:T(4,128)S(1)} %get-tuple-element.18.values_ref, ...), custom_call_target="tpu_custom_call" | custom-call | tf_op jit(solution)/shard_map/pallas_call | solution.py:388
  17.0 1.3 %collective-permute-start.4 = (f32[8,256]{1,0:T(8,128)S(1)}, f32[8,256]{1,0:T(8,128)S(1)}, u32[]{:S(2)}, u32[]{:S(2)}) collective-permute-start(f32[8,256]{1,0:T(8,128)S(1)} %shard_map.67.refs_1_), channel_id=1, source_target_pairs={{0,1},{1,0},{2,3},{3,2},{4,5},{5,4},{6,7},{7,6},{8,9},{9,8},{10,11... | collective-permute-start | bytes 24584 | tf_op jit(solution)/shard_map/ppermute | solution.py:457
  18.2 0.8 %collective-permute-done.4.refs_2_ = f32[8,256]{1,0:T(8,128)S(1)} collective-permute-done((f32[8,256]{1,0:T(8,128)S(1)}, f32[8,256]{1,0:T(8,128)S(1)}, u32[]{:S(2)}, u32[]{:S(2)}) %collective-permute-start.4) | collective-permute-done | bytes 8224 | tf_op jit(solution)/shard_map/ppermute | solution.py:457
  19.1 0.1 shard_map.68.refs_0_
  19.2 1.8 %collective-permute-start.5 = (f32[16,128]{1,0:T(8,128)S(1)}, f32[16,128]{1,0:T(8,128)S(1)}, u32[]{:S(2)}, u32[]{:S(2)}) collective-permute-start(f32[16,128]{1,0:T(8,128)S(1)} %shard_map.68.refs_0_), channel_id=1, source_target_pairs={{0,8},{1,13},{2,10},{3,15},{4,12},{5,9},{6,14},{7,11},{8,0},{9,5},... | collective-permute-start | bytes 24584 | tf_op jit(solution)/shard_map/ppermute | solution.py:352
  21.0 0.1 collective-permute-start.6
  21.0 2.8 %collective-permute-done.5.refs_1_ = f32[16,128]{1,0:T(8,128)S(1)} collective-permute-done((f32[16,128]{1,0:T(8,128)S(1)}, f32[16,128]{1,0:T(8,128)S(1)}, u32[]{:S(2)}, u32[]{:S(2)}) %collective-permute-start.5) | collective-permute-done | bytes 8224 | tf_op jit(solution)/shard_map/ppermute | solution.py:352
  23.8 0.2 collective-permute-start.7
  23.9 0.0 collective-permute-done.8.refs_5_
  24.0 0.2 collective-permute-done.6.refs_2_
  24.1 0.8 %collective-permute-done.7.refs_3_ = f32[16,128]{1,0:T(8,128)S(1)} collective-permute-done((f32[16,128]{1,0:T(8,128)S(1)}, f32[16,128]{1,0:T(8,128)S(1)}, u32[]{:S(2)}, u32[]{:S(2)}) %collective-permute-start.7) | collective-permute-done | bytes 8224 | tf_op jit(solution)/shard_map/ppermute | solution.py:354
  24.9 0.0 collective-permute-done.9.refs_7_
  24.9 2.5 %shard_map.69 = f32[4,32,512]{2,1,0:T(8,128)} custom-call(f32[16,128]{1,0:T(8,128)S(1)} %shard_map.68.refs_0_, f32[16,128]{1,0:T(8,128)S(1)} %collective-permute-done.5.refs_1_, f32[16,128]{1,0:T(8,128)S(1)} %collective-permute-done.6.refs_2_, f32[16,128]{1,0:T(8,128)S(1)} %collective-permute-done.7.refs_3_, f32[4,32,512]{2,1,0:T(8,128)S(1)} %shard_map.65.refs_4_, ...), custom_call_target="tpu_custom_call" | custom-call | tf_op jit(solution)/shard_map/pallas_call | solution.py:388
Async XLA Ops:
  0.0 9.5 %collective-permute-start.3 = (f32[4,32,512]{2,1,0:T(8,128)}, f32[4,32,512]{2,1,0:T(8,128)S(1)}, u32[]{:S(2)}, u32[]{:S(2)}) collective-permute-start(f32[4,32,512]{2,1,0:T(8,128)} %state.1), channel_id=1, source_target_pairs={{0,2},{1,3},{2,0},{3,1},{4,6},{5,7},{6,4},{7,5},{8,10},{9,11},{10,... | collective-permute-start | bytes 786440 | tf_op jit(solution)/shard_map/ppermute | solution.py:370
  4.0 20.0 %collective-permute-start.8 = (f32[4,32,512]{2,1,0:T(8,128)S(1)}, f32[4,32,512]{2,1,0:T(8,128)S(1)}, u32[]{:S(2)}, u32[]{:S(2)}) collective-permute-start(f32[4,32,512]{2,1,0:T(8,128)S(1)} %shard_map.65.refs_4_), channel_id=1, source_target_pairs={{0,1},{1,0},{2,3},{3,2},{4,5},{5,4},{6,7},{7,6},{8,9},{9,8},{10,11... | collective-permute-start | bytes 786440 | tf_op jit(solution)/shard_map/ppermute | solution.py:370
  9.5 15.5 %collective-permute-start.9 = (f32[4,32,512]{2,1,0:T(8,128)S(1)}, f32[4,32,512]{2,1,0:T(8,128)S(1)}, u32[]{:S(2)}, u32[]{:S(2)}) collective-permute-start(f32[4,32,512]{2,1,0:T(8,128)S(1)} %collective-permute-done.3.refs_0_.refs_6_), channel_id=1, source_target_pairs={{0,1},{1,0},{2,3},{3,2},{4,5},{5,4},{6,7},{7,6},{8,9},{9,8},{10,11... | collective-permute-start | bytes 786440 | tf_op jit(solution)/shard_map/ppermute | solution.py:370
  10.4 4.6 %collective-permute-start = (f32[8,128]{1,0:T(8,128)S(1)}, f32[8,128]{1,0:T(8,128)S(1)}, u32[]{:S(2)}, u32[]{:S(2)}) collective-permute-start(f32[8,128]{1,0:T(8,128)S(1)} %get-tuple-element.13), channel_id=1, source_target_pairs={{0,8},{1,13},{2,10},{3,15},{4,12},{5,9},{6,14},{7,11},{8,0},{9,5},... | collective-permute-start | bytes 12296 | tf_op jit(solution)/shard_map/ppermute | solution.py:352
  13.3 3.0 %collective-permute-start.1 = (f32[8,128]{1,0:T(8,128)S(1)}, f32[8,128]{1,0:T(8,128)S(1)}, u32[]{:S(2)}, u32[]{:S(2)}) collective-permute-start(f32[8,128]{1,0:T(8,128)S(1)} %get-tuple-element.14), channel_id=1, source_target_pairs={{0,5},{1,4},{2,7},{3,6},{4,1},{5,0},{6,3},{7,2},{8,13},{9,12},{10,... | collective-permute-start | bytes 12296 | tf_op jit(solution)/shard_map/ppermute | solution.py:353
  14.9 1.4 %collective-permute-start.2 = (f32[8,128]{1,0:T(8,128)S(1)}, f32[8,128]{1,0:T(8,128)S(1)}, u32[]{:S(2)}, u32[]{:S(2)}) collective-permute-start(f32[8,128]{1,0:T(8,128)S(1)} %collective-permute-done.refs_1_), channel_id=1, source_target_pairs={{0,1},{1,0},{2,3},{3,2},{4,5},{5,4},{6,7},{7,6},{8,9},{9,8},{10,11... | collective-permute-start | bytes 12296 | tf_op jit(solution)/shard_map/ppermute | solution.py:354
  17.0 2.1 %collective-permute-start.4 = (f32[8,256]{1,0:T(8,128)S(1)}, f32[8,256]{1,0:T(8,128)S(1)}, u32[]{:S(2)}, u32[]{:S(2)}) collective-permute-start(f32[8,256]{1,0:T(8,128)S(1)} %shard_map.67.refs_1_), channel_id=1, source_target_pairs={{0,1},{1,0},{2,3},{3,2},{4,5},{5,4},{6,7},{7,6},{8,9},{9,8},{10,11... | collective-permute-start | bytes 24584 | tf_op jit(solution)/shard_map/ppermute | solution.py:457
  19.2 4.6 %collective-permute-start.5 = (f32[16,128]{1,0:T(8,128)S(1)}, f32[16,128]{1,0:T(8,128)S(1)}, u32[]{:S(2)}, u32[]{:S(2)}) collective-permute-start(f32[16,128]{1,0:T(8,128)S(1)} %shard_map.68.refs_0_), channel_id=1, source_target_pairs={{0,8},{1,13},{2,10},{3,15},{4,12},{5,9},{6,14},{7,11},{8,0},{9,5},... | collective-permute-start | bytes 24584 | tf_op jit(solution)/shard_map/ppermute | solution.py:352
  21.0 3.2 %collective-permute-start.6 = (f32[16,128]{1,0:T(8,128)S(1)}, f32[16,128]{1,0:T(8,128)S(1)}, u32[]{:S(2)}, u32[]{:S(2)}) collective-permute-start(f32[16,128]{1,0:T(8,128)S(1)} %shard_map.68.refs_0_), channel_id=1, source_target_pairs={{0,5},{1,4},{2,7},{3,6},{4,1},{5,0},{6,3},{7,2},{8,13},{9,12},{10,... | collective-permute-start | bytes 24584 | tf_op jit(solution)/shard_map/ppermute | solution.py:353
  23.8 1.2 %collective-permute-start.7 = (f32[16,128]{1,0:T(8,128)S(1)}, f32[16,128]{1,0:T(8,128)S(1)}, u32[]{:S(2)}, u32[]{:S(2)}) collective-permute-start(f32[16,128]{1,0:T(8,128)S(1)} %collective-permute-done.5.refs_1_), channel_id=1, source_target_pairs={{0,1},{1,0},{2,3},{3,2},{4,5},{5,4},{6,7},{7,6},{8,9},{9,8},{10,11... | collective-permute-start | bytes 24584 | tf_op jit(solution)/shard_map/ppermute | solution.py:354

commit v17 on v14

--- a/solution.py
+++ b/solution.py
@@ -291,9 +291,10 @@
     for piece in range(len(state_refs)):
         place = order.index(piece)
         places.append(place + odd * (order.index(piece ^ 1) - place) if halves else place)
+    tall = 8 * (elements // 8 // sems.shape[0])
 
     def output_copy(block):
-        place = pl.ds(pl.multiple_of(8 * block, 8), 8)
+        place = pl.ds(tall * block, tall)
         return pltpu.make_async_copy(staged.at[:, place], out.at[:, place], sems.at[block])
 
     def mix_block(block, carry):
@@ -312,15 +313,14 @@
             for k in range(local_members):
                 for u in range(2):
                     staged[k, span, spans[u]] = totals[k][u]
-        output_copy(block).start()
         return carry
 
-    def wait_block(block, carry):
-        output_copy(block).wait()
-        return carry
-
-    lax.fori_loop(0, elements // 8, mix_block, 0)
-    lax.fori_loop(0, elements // 8, wait_block, 0)
+    steps = tall // 8
+    for part in range(sems.shape[0]):
+        lax.fori_loop(part * steps, (part + 1) * steps, mix_block, 0)
+        output_copy(part).start()
+    for part in range(sems.shape[0]):
+        output_copy(part).wait()
 
 
 def has_halves(n_ens):
@@ -401,7 +401,7 @@
         return jax.ShapeDtypeStruct(dims, dtype)
 
     def on_device(state, coords, owner_local, counts, obs_value, obs_weight):
-        local_members, elements, nodes = state.shape
+        local_members, _, nodes = state.shape
         slots = coords.shape[1]
         members = local_members * n_ens
         tile_shape = (8, 2 * CAP)
@@ -460,7 +460,7 @@
         )
         if direct:
             copies = [partial_sum] * (3 if paired else n_dom)
-            sums = spread(copies, n_dom, n_ens, bits=(2, 3, 1), crossing=0)
+            sums = spread(copies, n_dom, n_ens, bits=(2, 3, 1), crossing=1)
         else:
             sums = [lax.psum(partial_sum, "dom")]
         return call(
@@ -471,7 +471,7 @@
             [
                 pltpu.VMEM(state.shape, F32),
                 pltpu.VMEM((members * local_members, 8, 128), F32),
-                pltpu.SemaphoreType.DMA((elements // 8,)),
+                pltpu.SemaphoreType.DMA((2,)),
             ],
             hbm,
         )

time: 27.9 us -> 27.9 us (level)
  waiting for transfers between devices: 10.2 us -> 11.3 us
  starting transfers between devices: 12.4 us -> 11.4 us
    ppermute x2, starting transfers between devices: 3.67 us -> 2.64 us  [spread(): far = lax.ppermute(far, ('dom', 'ens'), far_pairs)]
    ppermute x2, waiting for transfers between devices: 1.64 us -> 2.67 us  [spread(): near = lax.ppermute(near, ('dom', 'ens'), near_pairs)]
    ppermute x2, waiting for transfers between devices: 2.09 us -> 1.52 us  [spread(): far = lax.ppermute(far, ('dom', 'ens'), far_pairs)]
    ppermute x2, waiting for transfers between devices: 0.25 us -> 0.81 us  [spread(): other = lax.ppermute(near, 'ens', [(e, e ^ 1) for e in range(n_ens)])]
where the time goes in v17:
time: 27.9 us; the launch traced here: 27.8 us
  starting transfers between devices  11.4 us (41%)
  waiting for transfers between devices  11.3 us (41%)
  Pallas kernels  5.07 us (18%)
    ppermute x3, waiting for transfers between devices, gather_members(): pieces[key ^ bit] = lax.ppermute(pieces[key], 'ens', pairs)  5.44 us
    pallas_call x6, Pallas kernels, call(): pl.pallas_call(kernel, out_shape=out_shape, in_specs=specs or [vmem] * le...  5.07 us
    ppermute x2, starting transfers between devices, spread(): near = lax.ppermute(near, ('dom', 'ens'), near_pairs)  3.76 us
    ppermute x3, starting transfers between devices, gather_members(): pieces[key ^ bit] = lax.ppermute(pieces[key], 'ens', pairs)  3.04 us
    ppermute x2, waiting for transfers between devices, spread(): near = lax.ppermute(near, ('dom', 'ens'), near_pairs)  2.67 us
    ppermute x2, starting transfers between devices, spread(): far = lax.ppermute(far, ('dom', 'ens'), far_pairs)  2.64 us
    ppermute x2, waiting for transfers between devices, spread(): far = lax.ppermute(far, ('dom', 'ens'), far_pairs)  1.52 us
    ppermute x1, starting transfers between devices, on_device(): values.append(lax.ppermute(values[0], 'ens', pairs))  1.17 us
  transfers between devices with their start and end apart: 10, of which 6 were waited for; matrix products, arithmetic and copies ran while one was open for 0% of the time, Pallas kernels for 9%

profile of v17, /device:TPU:0, one launch (start us, length us, event | category | flops | bytes accessed | tf_op | source)
XLA Modules:
  0.0 27.8 jit_solution(8085782407144006966)
XLA Ops:
  0.0 3.0 %collective-permute-start.3 = (f32[4,32,512]{2,1,0:T(8,128)}, f32[4,32,512]{2,1,0:T(8,128)S(1)}, u32[]{:S(2)}, u32[]{:S(2)}) collective-permute-start(f32[4,32,512]{2,1,0:T(8,128)} %state.1), channel_id=1, source_target_pairs={{0,2},{1,3},{2,0},{3,1},{4,6},{5,7},{6,4},{7,5},{8,10},{9,11},{10,... | collective-permute-start | bytes 786440 | tf_op jit(solution)/shard_map/ppermute | solution.py:370
  3.0 1.0 %shard_map.65.refs_4_ = f32[4,32,512]{2,1,0:T(8,128)S(1)} custom-call(f32[4,32,512]{2,1,0:T(8,128)} %state.1), custom_call_target="tpu_custom_call" | custom-call | tf_op jit(solution)/shard_map/pallas_call | solution.py:388
  4.0 0.1 collective-permute-start.8
  4.0 5.4 %collective-permute-done.3.refs_0_.refs_6_ = f32[4,32,512]{2,1,0:T(8,128)S(1)} collective-permute-done((f32[4,32,512]{2,1,0:T(8,128)}, f32[4,32,512]{2,1,0:T(8,128)S(1)}, u32[]{:S(2)}, u32[]{:S(2)}) %collective-permute-start.3) | collective-permute-done | bytes 262176 | tf_op jit(solution)/shard_map/ppermute | solution.py:370
  9.5 0.0 collective-permute-start.9
  9.5 0.9 %shard_map.64 = (f32[8,128]{1,0:T(8,128)S(1)}, f32[8,128]{1,0:T(8,128)S(1)}, f32[8,128]{1,0:T(8,128)S(1)}) custom-call(s32[1,4]{1,0:T(1,128)} %refs_0_.1, f32[3,256]{1,0:T(4,128)} %refs_1_.1, s32[1,256]{1,0:T(1,128)} %bitcast.3, f32[1,256]{1,0:T(1,128)} %bitcast.4, f32[1,256]{1,0:T(1,128)} %bitcast.5), custom_call_target="tpu_custom_call" | custom-call | tf_op jit(solution)/shard_map/pallas_call | solution.py:388
  10.4 1.9 %collective-permute-start = (f32[8,128]{1,0:T(8,128)S(1)}, f32[8,128]{1,0:T(8,128)S(1)}, u32[]{:S(2)}, u32[]{:S(2)}) collective-permute-start(f32[8,128]{1,0:T(8,128)S(1)} %get-tuple-element.13), channel_id=1, source_target_pairs={{0,4},{1,13},{2,6},{3,15},{4,0},{5,9},{6,2},{7,11},{8,12},{9,5},{1... | collective-permute-start | bytes 12296 | tf_op jit(solution)/shard_map/ppermute | solution.py:352
  12.2 2.6 %collective-permute-start.1 = (f32[8,128]{1,0:T(8,128)S(1)}, f32[8,128]{1,0:T(8,128)S(1)}, u32[]{:S(2)}, u32[]{:S(2)}) collective-permute-start(f32[8,128]{1,0:T(8,128)S(1)} %get-tuple-element.14), channel_id=1, source_target_pairs={{0,8},{1,9},{2,10},{3,11},{4,12},{5,13},{6,14},{7,15},{8,0},{9,1},... | collective-permute-start | bytes 12296 | tf_op jit(solution)/shard_map/ppermute | solution.py:353
  14.8 0.0 collective-permute-done.refs_1_
  14.8 0.7 %collective-permute-start.2 = (f32[8,128]{1,0:T(8,128)S(1)}, f32[8,128]{1,0:T(8,128)S(1)}, u32[]{:S(2)}, u32[]{:S(2)}) collective-permute-start(f32[8,128]{1,0:T(8,128)S(1)} %collective-permute-done.refs_1_), channel_id=1, source_target_pairs={{0,1},{1,0},{2,3},{3,2},{4,5},{5,4},{6,7},{7,6},{8,9},{9,8},{10,11... | collective-permute-start | bytes 12296 | tf_op jit(solution)/shard_map/ppermute | solution.py:354
  15.5 1.3 %collective-permute-done.1.refs_2_ = f32[8,128]{1,0:T(8,128)S(1)} collective-permute-done((f32[8,128]{1,0:T(8,128)S(1)}, f32[8,128]{1,0:T(8,128)S(1)}, u32[]{:S(2)}, u32[]{:S(2)}) %collective-permute-start.1) | collective-permute-done | bytes 4128 | tf_op jit(solution)/shard_map/ppermute | solution.py:353
  16.8 0.0 collective-permute-done.2.refs_3_
  16.8 0.4 %shard_map.66 = (f32[8,256]{1,0:T(8,128)S(1)}, bf16[512,256]{1,0:T(8,128)(2,1)S(1)}, bf16[512,256]{1,0:T(8,128)(2,1)S(1)}, f32[4,256]{1,0:T(4,128)S(1)}) custom-call(f32[8,128]{1,0:T(8,128)S(1)} %get-tuple-element.12.refs_0_, f32[8,128]{1,0:T(8,128)S(1)} %collective-permute-done.refs_1_, f32[8,128]{1,0:T(8,128)S(1)} %collective-permute-done.1.refs_2_, ...), custom_call_target="tpu_custom_call" | custom-call | tf_op jit(solution)/shard_map/pallas_call | solution.py:388
  17.1 0.3 %shard_map.67.refs_1_ = f32[8,256]{1,0:T(8,128)S(1)} custom-call(f32[8,256]{1,0:T(8,128)S(1)} %get-tuple-element.15.sensors_ref.refs_0_, bf16[512,256]{1,0:T(8,128)(2,1)S(1)} %get-tuple-element.16.high_ref, bf16[512,256]{1,0:T(8,128)(2,1)S(1)} %get-tuple-element.17.low_ref, f32[4,256]{1,0:T(4,128)S(1)} %get-tuple-element.18.values_ref, ...), custom_call_target="tpu_custom_call" | custom-call | tf_op jit(solution)/shard_map/pallas_call | solution.py:388
  17.4 1.2 %collective-permute-start.4 = (f32[8,256]{1,0:T(8,128)S(1)}, f32[8,256]{1,0:T(8,128)S(1)}, u32[]{:S(2)}, u32[]{:S(2)}) collective-permute-start(f32[8,256]{1,0:T(8,128)S(1)} %shard_map.67.refs_1_), channel_id=1, source_target_pairs={{0,1},{1,0},{2,3},{3,2},{4,5},{5,4},{6,7},{7,6},{8,9},{9,8},{10,11... | collective-permute-start | bytes 24584 | tf_op jit(solution)/shard_map/ppermute | solution.py:457
  18.6 0.8 %collective-permute-done.4.refs_2_ = f32[8,256]{1,0:T(8,128)S(1)} collective-permute-done((f32[8,256]{1,0:T(8,128)S(1)}, f32[8,256]{1,0:T(8,128)S(1)}, u32[]{:S(2)}, u32[]{:S(2)}) %collective-permute-start.4) | collective-permute-done | bytes 8224 | tf_op jit(solution)/shard_map/ppermute | solution.py:457
  19.4 0.1 shard_map.68.refs_0_
  19.5 1.9 %collective-permute-start.5 = (f32[16,128]{1,0:T(8,128)S(1)}, f32[16,128]{1,0:T(8,128)S(1)}, u32[]{:S(2)}, u32[]{:S(2)}) collective-permute-start(f32[16,128]{1,0:T(8,128)S(1)} %shard_map.68.refs_0_), channel_id=1, source_target_pairs={{0,8},{1,13},{2,10},{3,15},{4,12},{5,9},{6,14},{7,11},{8,0},{9,5},... | collective-permute-start | bytes 24584 | tf_op jit(solution)/shard_map/ppermute | solution.py:352
  21.4 0.1 collective-permute-start.6
  21.4 2.7 %collective-permute-done.5.refs_1_ = f32[16,128]{1,0:T(8,128)S(1)} collective-permute-done((f32[16,128]{1,0:T(8,128)S(1)}, f32[16,128]{1,0:T(8,128)S(1)}, u32[]{:S(2)}, u32[]{:S(2)}) %collective-permute-start.5) | collective-permute-done | bytes 8224 | tf_op jit(solution)/shard_map/ppermute | solution.py:352
  24.1 0.1 collective-permute-start.7
  24.2 0.0 collective-permute-done.8.refs_5_
  24.2 0.3 collective-permute-done.6.refs_2_
  24.5 0.8 %collective-permute-done.7.refs_3_ = f32[16,128]{1,0:T(8,128)S(1)} collective-permute-done((f32[16,128]{1,0:T(8,128)S(1)}, f32[16,128]{1,0:T(8,128)S(1)}, u32[]{:S(2)}, u32[]{:S(2)}) %collective-permute-start.7) | collective-permute-done | bytes 8224 | tf_op jit(solution)/shard_map/ppermute | solution.py:354
  25.3 0.0 collective-permute-done.9.refs_7_
  25.3 2.5 %shard_map.69 = f32[4,32,512]{2,1,0:T(8,128)} custom-call(f32[16,128]{1,0:T(8,128)S(1)} %shard_map.68.refs_0_, f32[16,128]{1,0:T(8,128)S(1)} %collective-permute-done.5.refs_1_, f32[16,128]{1,0:T(8,128)S(1)} %collective-permute-done.6.refs_2_, f32[16,128]{1,0:T(8,128)S(1)} %collective-permute-done.7.refs_3_, f32[4,32,512]{2,1,0:T(8,128)S(1)} %shard_map.65.refs_4_, ...), custom_call_target="tpu_custom_call" | custom-call | tf_op jit(solution)/shard_map/pallas_call | solution.py:388
Async XLA Ops:
  0.0 9.5 %collective-permute-start.3 = (f32[4,32,512]{2,1,0:T(8,128)}, f32[4,32,512]{2,1,0:T(8,128)S(1)}, u32[]{:S(2)}, u32[]{:S(2)}) collective-permute-start(f32[4,32,512]{2,1,0:T(8,128)} %state.1), channel_id=1, source_target_pairs={{0,2},{1,3},{2,0},{3,1},{4,6},{5,7},{6,4},{7,5},{8,10},{9,11},{10,... | collective-permute-start | bytes 786440 | tf_op jit(solution)/shard_map/ppermute | solution.py:370
  4.0 20.2 %collective-permute-start.8 = (f32[4,32,512]{2,1,0:T(8,128)S(1)}, f32[4,32,512]{2,1,0:T(8,128)S(1)}, u32[]{:S(2)}, u32[]{:S(2)}) collective-permute-start(f32[4,32,512]{2,1,0:T(8,128)S(1)} %shard_map.65.refs_4_), channel_id=1, source_target_pairs={{0,1},{1,0},{2,3},{3,2},{4,5},{5,4},{6,7},{7,6},{8,9},{9,8},{10,11... | collective-permute-start | bytes 786440 | tf_op jit(solution)/shard_map/ppermute | solution.py:370
  9.5 15.8 %collective-permute-start.9 = (f32[4,32,512]{2,1,0:T(8,128)S(1)}, f32[4,32,512]{2,1,0:T(8,128)S(1)}, u32[]{:S(2)}, u32[]{:S(2)}) collective-permute-start(f32[4,32,512]{2,1,0:T(8,128)S(1)} %collective-permute-done.3.refs_0_.refs_6_), channel_id=1, source_target_pairs={{0,1},{1,0},{2,3},{3,2},{4,5},{5,4},{6,7},{7,6},{8,9},{9,8},{10,11... | collective-permute-start | bytes 786440 | tf_op jit(solution)/shard_map/ppermute | solution.py:370
  10.4 4.5 %collective-permute-start = (f32[8,128]{1,0:T(8,128)S(1)}, f32[8,128]{1,0:T(8,128)S(1)}, u32[]{:S(2)}, u32[]{:S(2)}) collective-permute-start(f32[8,128]{1,0:T(8,128)S(1)} %get-tuple-element.13), channel_id=1, source_target_pairs={{0,4},{1,13},{2,6},{3,15},{4,0},{5,9},{6,2},{7,11},{8,12},{9,5},{1... | collective-permute-start | bytes 12296 | tf_op jit(solution)/shard_map/ppermute | solution.py:352
  12.2 4.5 %collective-permute-start.1 = (f32[8,128]{1,0:T(8,128)S(1)}, f32[8,128]{1,0:T(8,128)S(1)}, u32[]{:S(2)}, u32[]{:S(2)}) collective-permute-start(f32[8,128]{1,0:T(8,128)S(1)} %get-tuple-element.14), channel_id=1, source_target_pairs={{0,8},{1,9},{2,10},{3,11},{4,12},{5,13},{6,14},{7,15},{8,0},{9,1},... | collective-permute-start | bytes 12296 | tf_op jit(solution)/shard_map/ppermute | solution.py:353
  14.8 1.9 %collective-permute-start.2 = (f32[8,128]{1,0:T(8,128)S(1)}, f32[8,128]{1,0:T(8,128)S(1)}, u32[]{:S(2)}, u32[]{:S(2)}) collective-permute-start(f32[8,128]{1,0:T(8,128)S(1)} %collective-permute-done.refs_1_), channel_id=1, source_target_pairs={{0,1},{1,0},{2,3},{3,2},{4,5},{5,4},{6,7},{7,6},{8,9},{9,8},{10,11... | collective-permute-start | bytes 12296 | tf_op jit(solution)/shard_map/ppermute | solution.py:354
  17.4 2.0 %collective-permute-start.4 = (f32[8,256]{1,0:T(8,128)S(1)}, f32[8,256]{1,0:T(8,128)S(1)}, u32[]{:S(2)}, u32[]{:S(2)}) collective-permute-start(f32[8,256]{1,0:T(8,128)S(1)} %shard_map.67.refs_1_), channel_id=1, source_target_pairs={{0,1},{1,0},{2,3},{3,2},{4,5},{5,4},{6,7},{7,6},{8,9},{9,8},{10,11... | collective-permute-start | bytes 24584 | tf_op jit(solution)/shard_map/ppermute | solution.py:457
  19.5 4.6 %collective-permute-start.5 = (f32[16,128]{1,0:T(8,128)S(1)}, f32[16,128]{1,0:T(8,128)S(1)}, u32[]{:S(2)}, u32[]{:S(2)}) collective-permute-start(f32[16,128]{1,0:T(8,128)S(1)} %shard_map.68.refs_0_), channel_id=1, source_target_pairs={{0,8},{1,13},{2,10},{3,15},{4,12},{5,9},{6,14},{7,11},{8,0},{9,5},... | collective-permute-start | bytes 24584 | tf_op jit(solution)/shard_map/ppermute | solution.py:352
  21.4 3.1 %collective-permute-start.6 = (f32[16,128]{1,0:T(8,128)S(1)}, f32[16,128]{1,0:T(8,128)S(1)}, u32[]{:S(2)}, u32[]{:S(2)}) collective-permute-start(f32[16,128]{1,0:T(8,128)S(1)} %shard_map.68.refs_0_), channel_id=1, source_target_pairs={{0,5},{1,4},{2,7},{3,6},{4,1},{5,0},{6,3},{7,2},{8,13},{9,12},{10,... | collective-permute-start | bytes 24584 | tf_op jit(solution)/shard_map/ppermute | solution.py:353
  24.1 1.2 %collective-permute-start.7 = (f32[16,128]{1,0:T(8,128)S(1)}, f32[16,128]{1,0:T(8,128)S(1)}, u32[]{:S(2)}, u32[]{:S(2)}) collective-permute-start(f32[16,128]{1,0:T(8,128)S(1)} %collective-permute-done.5.refs_1_), channel_id=1, source_target_pairs={{0,1},{1,0},{2,3},{3,2},{4,5},{5,4},{6,7},{7,6},{8,9},{9,8},{10,11... | collective-permute-start | bytes 24584 | tf_op jit(solution)/shard_map/ppermute | solution.py:354
